TPU v7x, 32 devices: a whole 2x2x4 slice. The times are simulated.
32 devices in a mesh: fsdp: 8 (over y, x, core), tp: 4 (over z).
Axes of the slice: x: 2, y: 2, z: 4, core: 2. Of those that a mesh axis runs over, the one named last changes fastest.
Arguments:
- emb: bfloat16 [8192, 1536], P(('fsdp', 'tp')), may hold values from -0.5 to 0.5
- segment_ids: int32 [16, 512], P('fsdp'), may hold values from 0 to 3, never falling along the last dimension, each value on 1 to 256 neighbouring positions
- routes: int32 [8192, 8], P('fsdp'), may hold values from 0 to 39, all different within a row; in each aligned block of 1024 rows (0 to 1023, 1024 to 2047, ...) at most 408 rows name the same one
- norm1_gain: bfloat16 [1536], replicated, may hold values from 0.5 to 1.5
- w_query: bfloat16 [1536, 1536], P('fsdp', 'tp'), may hold values from -0.625 to 0.625
- w_key: bfloat16 [1536, 512], P('fsdp', 'tp'), may hold values from -0.625 to 0.625
- w_value: bfloat16 [1536, 512], P('fsdp', 'tp'), may hold values from -0.15625 to 0.15625
- w_out: bfloat16 [1536, 1536], P('fsdp', 'tp'), may hold values from -1.25 to 1.25
- norm2_gain: bfloat16 [1536], replicated, may hold values from 0.5 to 1.5
- w_router: bfloat16 [1536, 40], P('fsdp'), may hold values from -0.15625 to 0.15625
- w_gate: bfloat16 [40, 1536, 512], P('tp', 'fsdp'), may hold values from -0.15625 to 0.15625
- w_up: bfloat16 [40, 1536, 512], P('tp', 'fsdp'), may hold values from -0.15625 to 0.15625
- w_down: bfloat16 [40, 1536, 512], P('tp', 'fsdp'), may hold values from -3 to 3
- cotangent: bfloat16 [8192, 1536], P(('fsdp', 'tp')), may hold values from -6 to 6
Outputs:
- out: bfloat16 [8192, 1536], P(('fsdp', 'tp'))
- grad_emb: float32 [8192, 1536], P(('fsdp', 'tp'))
- grad_norm1_gain: float32 [1536], replicated
- grad_w_query: float32 [1536, 1536], P('fsdp', 'tp')
- grad_w_key: float32 [1536, 512], P('fsdp', 'tp')
- grad_w_value: float32 [1536, 512], P('fsdp', 'tp')
- grad_w_out: float32 [1536, 1536], P('fsdp', 'tp')
- grad_norm2_gain: float32 [1536], replicated
- grad_w_router: float32 [1536, 40], P('fsdp')
- grad_w_gate: float32 [40, 1536, 512], P('tp', 'fsdp')
- grad_w_up: float32 [40, 1536, 512], P('tp', 'fsdp')
- grad_w_down: float32 [40, 1536, 512], P('tp', 'fsdp')
Inputs may be any that keep to these rules, and one draw needn't show every extreme that they name: `routes`: in each aligned block of 1024 rows no expert is named by more than 408 rows, a bound that some block reaches. `segment_ids`: along a sequence the numbers never fall; a document spans at most 256 tokens, and one spans exactly 256.
All inputs are finite; a program needn't handle non-finite values.
Results may differ from a plain program's by a relative error of at most 0.015.
Values may be sent and summed in bfloat16 or wider, within the bound.
A program may use at most 384 MiB of HBM per device.

v0:
```python
import jax
import jax.numpy as jnp
from jax import lax
from jax.sharding import PartitionSpec as P

HEAD_DIM = 64
SEQ = 512


emb_scale = 12.0
resid_scale = 0.22
attn_scale = 0.015625
norm_eps = 1e-06
rope_base = 10000.0
masked_value = -1e30


def contract_last(left_op, right_op):
    return lax.dot_general(
        left_op, right_op, (((1,), (1,)), ((), ())), preferred_element_type=jnp.float32
    )


def contract_first(left_op, right_op):
    return lax.dot_general(
        left_op, right_op, (((0,), (0,)), ((), ())), preferred_element_type=jnp.float32
    )


def rms_forward(values, gain_vec):
    inverse = lax.rsqrt(jnp.mean(values * values, axis=-1, keepdims=True) + norm_eps)
    return (values * inverse * gain_vec, inverse)


def rms_backward(incoming, values, inverse, gain_vec):
    scaled = values * inverse
    gain_grad = jnp.sum(incoming * scaled, axis=0)
    weighted = incoming * gain_vec
    row_inner = jnp.mean(weighted * scaled, axis=-1, keepdims=True)
    return (inverse * (weighted - scaled * row_inner), gain_grad)


def rotary_tables(row_count, head_width):
    half_width = head_width // 2
    positions = (jnp.arange(row_count) % SEQ).astype(jnp.float32)
    frequency = rope_base ** (-jnp.arange(half_width).astype(jnp.float32) * 2.0 / head_width)
    angles = positions[:, None] * frequency[None, :]
    return (jnp.cos(angles)[:, None, :], jnp.sin(angles)[:, None, :])


def rotate(values, cosine_table, sine_table):
    half_width = values.shape[-1] // 2
    lead_half = values[..., :half_width]
    tail_half = values[..., half_width:]
    return jnp.concatenate(
        [
            lead_half * cosine_table - tail_half * sine_table,
            tail_half * cosine_table + lead_half * sine_table,
        ],
        axis=-1,
    )


def attention_scores(queries, key_rows, segments):
    length, heads_here, head_width = queries.shape
    kv_here = key_rows.shape[1]
    grouped = queries.reshape(length, kv_here, heads_here // kv_here, head_width)
    scores = (
        jnp.einsum("qkgd,tkd->kgqt", grouped, key_rows, preferred_element_type=jnp.float32)
        * attn_scale
    )
    places = jnp.arange(length)
    allowed = (places[:, None] >= places[None, :]) & (segments[:, None] == segments[None, :])
    return (jnp.where(allowed, scores, masked_value), grouped)


def attend_forward(pieces):
    queries, key_rows, value_rows, segments = pieces
    scores, grouped = attention_scores(queries, key_rows, segments)
    row_top = jnp.max(scores, axis=-1, keepdims=True)
    raised = jnp.exp(scores - row_top)
    row_total = jnp.sum(raised, axis=-1, keepdims=True)
    probs_low = (raised / row_total).astype(jnp.bfloat16)
    mixed_out = jnp.einsum(
        "kgqt,tkd->qkgd", probs_low, value_rows, preferred_element_type=jnp.float32
    )
    return (
        mixed_out.astype(jnp.bfloat16).reshape(queries.shape[0], -1),
        (row_top + jnp.log(row_total))[..., 0],
    )


def attend_backward(pieces):
    queries, key_rows, value_rows, segments, logsum, mixed_grad = pieces
    scores, grouped = attention_scores(queries, key_rows, segments)
    attn_probs = jnp.exp(scores - logsum[..., None])
    grad_grouped = mixed_grad.reshape(grouped.shape)
    probs_grad = jnp.einsum(
        "qkgd,tkd->kgqt", grad_grouped, value_rows, preferred_element_type=jnp.float32
    )
    row_inner = jnp.sum(attn_probs * probs_grad, axis=-1, keepdims=True)
    score_grad = (attn_probs * (probs_grad - row_inner)).astype(jnp.bfloat16)
    query_grad = (
        jnp.einsum("kgqt,tkd->qkgd", score_grad, key_rows, preferred_element_type=jnp.float32)
        * attn_scale
    )
    key_grad = (
        jnp.einsum("kgqt,qkgd->tkd", score_grad, grouped, preferred_element_type=jnp.float32)
        * attn_scale
    )
    value_grad = jnp.einsum(
        "kgqt,qkgd->tkd",
        attn_probs.astype(jnp.bfloat16),
        grad_grouped,
        preferred_element_type=jnp.float32,
    )
    return (query_grad.reshape(queries.shape), key_grad, value_grad)


def route_slots(expert, group_routes, group_gates, capacity):
    hit_mask = group_routes == expert
    member = jnp.any(hit_mask, axis=1)
    weight = jnp.sum(jnp.where(hit_mask, group_gates.astype(jnp.float32), 0.0), axis=1)
    member_int = member.astype(jnp.int32)
    slot_index = jnp.cumsum(member_int) - 1
    target = jnp.where(member, slot_index, capacity)
    row_ids = jnp.arange(member.shape[0], dtype=jnp.int32)
    slot_rows = jnp.zeros((capacity,), jnp.int32).at[target].set(row_ids, mode="drop")
    filled = jnp.arange(capacity) < jnp.sum(member_int)
    slot_scale = jnp.where(filled, jnp.take(weight, slot_rows, axis=0), 0.0)
    picked = jnp.where(filled[:, None], jnp.take(hit_mask, slot_rows, axis=0), False).astype(
        jnp.float32
    )
    return (slot_rows, slot_scale, picked)


def local(
    emb,
    segment_ids,
    routes,
    norm1_gain,
    w_query,
    w_key,
    w_value,
    w_out,
    norm2_gain,
    w_router,
    w_gate,
    w_up,
    w_down,
    cotangent,
):
    local_rows = emb.shape[0]
    query_w, key_w, value_w, out_w, router_w, gate_w, up_w, down_w = (
        lax.all_gather(w_query, "fsdp", axis=0, tiled=True),
        lax.all_gather(w_key, "fsdp", axis=0, tiled=True),
        lax.all_gather(w_value, "fsdp", axis=0, tiled=True),
        lax.all_gather(w_out, "fsdp", axis=0, tiled=True),
        lax.all_gather(w_router, "fsdp", axis=0, tiled=True),
        lax.all_gather(w_gate, "fsdp", axis=1, tiled=True),
        lax.all_gather(w_up, "fsdp", axis=1, tiled=True),
        lax.all_gather(w_down, "fsdp", axis=1, tiled=True),
    )
    gain_one = norm1_gain.astype(jnp.float32)
    gain_two = norm2_gain.astype(jnp.float32)
    start_x = emb.astype(jnp.float32) * emb_scale
    normed_one, inverse_one = rms_forward(start_x, gain_one)
    group_rows = lax.all_gather(normed_one.astype(jnp.bfloat16), "tp", axis=0, tiled=True)
    group_size = group_rows.shape[0]
    seq_count = group_size // SEQ
    heads_here = query_w.shape[1] // HEAD_DIM
    kv_here = key_w.shape[1] // HEAD_DIM
    cosine_table, sine_table = rotary_tables(group_size, HEAD_DIM)
    query_proj = jnp.dot(group_rows, query_w, preferred_element_type=jnp.float32).reshape(
        group_size, heads_here, HEAD_DIM
    )
    key_proj = jnp.dot(group_rows, key_w, preferred_element_type=jnp.float32).reshape(
        group_size, kv_here, HEAD_DIM
    )
    queries = rotate(query_proj, cosine_table, sine_table).astype(jnp.bfloat16)
    key_rows = rotate(key_proj, cosine_table, sine_table).astype(jnp.bfloat16)
    value_rows = jnp.dot(group_rows, value_w, preferred_element_type=jnp.float32).astype(
        jnp.bfloat16
    )
    seq_queries = queries.reshape(seq_count, SEQ, heads_here, HEAD_DIM)
    seq_keys = key_rows.reshape(seq_count, SEQ, kv_here, HEAD_DIM)
    seq_values = value_rows.reshape(seq_count, SEQ, kv_here, HEAD_DIM)
    mixed_out, logsum = lax.map(attend_forward, (seq_queries, seq_keys, seq_values, segment_ids))
    mixed_rows = mixed_out.reshape(group_size, heads_here * HEAD_DIM)
    attn_branch = lax.psum_scatter(
        contract_last(mixed_rows, out_w), "tp", scatter_dimension=0, tiled=True
    )
    mid_x = start_x + resid_scale * attn_branch
    normed_two, inverse_two = rms_forward(mid_x, gain_two)
    normed_low = normed_two.astype(jnp.bfloat16)
    logits = jnp.dot(normed_low, router_w, preferred_element_type=jnp.float32)
    tp_index = lax.axis_index("tp")
    own_routes = lax.dynamic_slice_in_dim(routes, tp_index * local_rows, local_rows, 0)
    expert_count = router_w.shape[1]
    chosen = (own_routes[:, :, None] == jnp.arange(expert_count)[None, None, :]).astype(jnp.float32)
    selected = jnp.sum(chosen * logits[:, None, :], axis=-1)
    sel_top = jnp.max(selected, axis=-1, keepdims=True)
    sel_raised = jnp.exp(selected - sel_top)
    gates = sel_raised / jnp.sum(sel_raised, axis=-1, keepdims=True)
    moe_rows, group_gates = (
        lax.all_gather(normed_low, "tp", axis=0, tiled=True),
        lax.all_gather(gates.astype(jnp.bfloat16), "tp", axis=0, tiled=True),
    )
    experts_here = gate_w.shape[0]
    capacity = group_size * routes.shape[1] // expert_count * 2
    expert_ids = tp_index * experts_here + jnp.arange(experts_here, dtype=jnp.int32)

    def expert_forward(running, inputs):
        gate_one, up_one, down_one, expert = inputs
        slot_rows, slot_scale, picked = route_slots(expert, routes, group_gates, capacity)
        rows_taken = jnp.take(moe_rows, slot_rows, axis=0)
        gate_pre = jnp.dot(rows_taken, gate_one, preferred_element_type=jnp.float32)
        up_pre = jnp.dot(rows_taken, up_one, preferred_element_type=jnp.float32)
        act_low = (gate_pre * jax.nn.sigmoid(gate_pre) * up_pre).astype(jnp.bfloat16)
        expert_out = contract_last(act_low, down_one)
        running = running.at[slot_rows].add(expert_out * slot_scale[:, None])
        return (running, (slot_rows, slot_scale, picked, gate_pre, up_pre, act_low, expert_out))

    moe_start = jnp.zeros((group_size, moe_rows.shape[1]), jnp.float32)
    moe_part, kept = lax.scan(expert_forward, moe_start, (gate_w, up_w, down_w, expert_ids))
    moe_sum = lax.psum_scatter(moe_part, "tp", scatter_dimension=0, tiled=True)
    out = (mid_x + resid_scale * moe_sum).astype(jnp.bfloat16)
    out_grad = cotangent.astype(jnp.float32)
    moe_grad = (resid_scale * out_grad).astype(jnp.bfloat16)
    moe_grad_rows = lax.all_gather(moe_grad, "tp", axis=0, tiled=True)
    gate_back, up_back, down_back = (gate_w, up_w, down_w)

    def expert_backward(running, inputs):
        rows_grad, gates_part = running
        (
            gate_one,
            up_one,
            down_one,
            slot_rows,
            slot_scale,
            picked,
            gate_pre,
            up_pre,
            act_low,
            expert_out,
        ) = inputs
        rows_taken = jnp.take(moe_rows, slot_rows, axis=0)
        taken_grad = jnp.take(moe_grad_rows, slot_rows, axis=0).astype(jnp.float32)
        slot_grad = jnp.sum(expert_out * taken_grad, axis=1)
        gates_part = gates_part.at[slot_rows].add(picked * slot_grad[:, None])
        scaled_grad = (taken_grad * slot_scale[:, None]).astype(jnp.bfloat16)
        down_grad = contract_first(scaled_grad, act_low)
        act_grad = jnp.dot(scaled_grad, down_one, preferred_element_type=jnp.float32)
        sig_gate = jax.nn.sigmoid(gate_pre)
        gate_grad = (act_grad * up_pre * sig_gate * (1.0 + gate_pre * (1.0 - sig_gate))).astype(
            jnp.bfloat16
        )
        up_grad = (act_grad * gate_pre * sig_gate).astype(jnp.bfloat16)
        gate_w_grad = contract_first(rows_taken, gate_grad)
        up_w_grad = contract_first(rows_taken, up_grad)
        input_grad = contract_last(gate_grad, gate_one) + contract_last(up_grad, up_one)
        rows_grad = rows_grad.at[slot_rows].add(input_grad)
        return ((rows_grad, gates_part), (gate_w_grad, up_w_grad, down_grad))

    back_start = (
        jnp.zeros((group_size, moe_rows.shape[1]), jnp.float32),
        jnp.zeros((group_size, routes.shape[1]), jnp.float32),
    )
    (rows_grad_part, gates_grad_part), (gate_grads, up_grads, down_grads) = lax.scan(
        expert_backward, back_start, (gate_back, up_back, down_back) + kept
    )
    rows_grad_sum, gates_grad = (
        lax.psum_scatter(rows_grad_part, "tp", scatter_dimension=0, tiled=True),
        lax.psum_scatter(gates_grad_part, "tp", scatter_dimension=0, tiled=True),
    )
    gates_inner = jnp.sum(gates * gates_grad, axis=-1, keepdims=True)
    selected_grad = gates * (gates_grad - gates_inner)
    logits_grad = jnp.sum(chosen * selected_grad[:, :, None], axis=1).astype(jnp.bfloat16)
    router_grad_part = contract_first(normed_low, logits_grad)
    normed_two_grad = rows_grad_sum + contract_last(logits_grad, router_w)
    mid_from_norm, gain_two_grad = rms_backward(normed_two_grad, mid_x, inverse_two, gain_two)
    mid_grad = out_grad + mid_from_norm
    branch_grad = (resid_scale * mid_grad).astype(jnp.bfloat16)
    branch_grad_rows = lax.all_gather(branch_grad, "tp", axis=0, tiled=True)
    out_w_grad = contract_first(branch_grad_rows, mixed_rows)
    mixed_grad = jnp.dot(branch_grad_rows, out_w, preferred_element_type=jnp.float32).astype(
        jnp.bfloat16
    )
    query_grad, key_grad, value_grad = lax.map(
        attend_backward,
        (
            seq_queries,
            seq_keys,
            seq_values,
            segment_ids,
            logsum,
            mixed_grad.reshape(seq_count, SEQ, -1),
        ),
    )
    query_proj_grad = (
        rotate(query_grad.reshape(group_size, heads_here, HEAD_DIM), cosine_table, -sine_table)
        .astype(jnp.bfloat16)
        .reshape(group_size, -1)
    )
    key_proj_grad = (
        rotate(key_grad.reshape(group_size, kv_here, HEAD_DIM), cosine_table, -sine_table)
        .astype(jnp.bfloat16)
        .reshape(group_size, -1)
    )
    value_proj_grad = value_grad.reshape(group_size, -1).astype(jnp.bfloat16)
    query_w_grad = contract_first(group_rows, query_proj_grad)
    key_w_grad = contract_first(group_rows, key_proj_grad)
    value_w_grad = contract_first(group_rows, value_proj_grad)
    total_grad = contract_last(query_proj_grad, query_w)
    total_grad = total_grad + contract_last(key_proj_grad, key_w)
    normed_one_grad = lax.psum_scatter(
        total_grad + contract_last(value_proj_grad, value_w), "tp", scatter_dimension=0, tiled=True
    )
    start_from_norm, gain_one_grad = rms_backward(normed_one_grad, start_x, inverse_one, gain_one)
    grad_emb = emb_scale * (mid_grad + start_from_norm)
    gain_one_sum, gain_two_sum, router_sum = lax.psum(
        (gain_one_grad, gain_two_grad, router_grad_part), ("fsdp", "tp")
    )
    router_rows = w_router.shape[0]
    router_own = lax.dynamic_slice_in_dim(
        router_sum, lax.axis_index("fsdp") * router_rows, router_rows, 0
    )
    query_sum, key_sum, value_sum, out_sum = (
        lax.psum_scatter(query_w_grad, "fsdp", scatter_dimension=0, tiled=True),
        lax.psum_scatter(key_w_grad, "fsdp", scatter_dimension=0, tiled=True),
        lax.psum_scatter(value_w_grad, "fsdp", scatter_dimension=0, tiled=True),
        lax.psum_scatter(out_w_grad, "fsdp", scatter_dimension=0, tiled=True),
    )
    gate_sum, up_sum, down_sum = (
        lax.psum_scatter(gate_grads, "fsdp", scatter_dimension=1, tiled=True),
        lax.psum_scatter(up_grads, "fsdp", scatter_dimension=1, tiled=True),
        lax.psum_scatter(down_grads, "fsdp", scatter_dimension=1, tiled=True),
    )
    return (
        out,
        grad_emb,
        gain_one_sum,
        query_sum,
        key_sum,
        value_sum,
        out_sum,
        gain_two_sum,
        router_own,
        gate_sum,
        up_sum,
        down_sum,
    )


def solution(mesh):
    return jax.shard_map(
        local,
        mesh=mesh,
        in_specs=(
            P(("fsdp", "tp"), None),
            P("fsdp", None),
            P("fsdp", None),
            P(),
            P("fsdp", "tp"),
            P("fsdp", "tp"),
            P("fsdp", "tp"),
            P("fsdp", "tp"),
            P(),
            P("fsdp", None),
            P("tp", "fsdp", None),
            P("tp", "fsdp", None),
            P("tp", "fsdp", None),
            P(("fsdp", "tp"), None),
        ),
        out_specs=(
            P(("fsdp", "tp"), None),
            P(("fsdp", "tp"), None),
            P(),
            P("fsdp", "tp"),
            P("fsdp", "tp"),
            P("fsdp", "tp"),
            P("fsdp", "tp"),
            P(),
            P("fsdp", None),
            P("tp", "fsdp", None),
            P("tp", "fsdp", None),
            P("tp", "fsdp", None),
        ),
        check_vma=False,
    )
```

profile of v0, /device:TPU:0, one launch (start us, length us, event | category | flops | bytes accessed | tf_op | source)
XLA Modules:
  0.0 2861.0 jit_solution(5613374487226321994)
XLA Ops:
  37.2 41.9 %all-gather.11.cloned.1.call-done = bf16[1024,1536]{1,0:T(8,128)(2,1)} async-done(((bf16[256,1536]{1,0:T(8,128)(2,1)}), bf16[1024,1536]{1,0:T(8,128)(2,1)}) %all-gather.11.cloned.1.call-update) | async-done | bytes 3145744 | tf_op jit(solution)/shard_map/all_gather | solution.py:168
  88.8 14.8 all-gather.13.cloned.1.call-done
  108.3 13.1 while.70
  136.1 110.3 %reduce-scatter.13.cloned.1.call-done = f32[256,1536]{1,0:T(8,128)} async-done(((f32[1024,1536]{1,0:T(8,128)}), f32[256,1536]{1,0:T(8,128)}) %reduce-scatter.13.cloned.1.call-update) | async-done | bytes 1572880 | tf_op jit(solution)/shard_map/reduce_scatter | solution.py:190
  266.3 14.2 all_gather.49
  280.8 34.1 %all-gather.17.cloned.1.call-done = bf16[1024,1536]{1,0:T(8,128)(2,1)} async-done(((bf16[256,1536]{1,0:T(8,128)(2,1)}), bf16[1024,1536]{1,0:T(8,128)(2,1)}) %all-gather.17.cloned.1.call-update) | async-done | bytes 3145744 | tf_op jit(solution)/shard_map/all_gather | solution.py:206
  314.8 85.7 %all-gather.19.cloned.1.call-done = bf16[10,1536,512]{2,1,0:T(8,128)(2,1)} async-done(((bf16[10,192,512]{2,1,0:T(8,128)(2,1)}), bf16[10,1536,512]{2,1,0:T(8,128)(2,1)}) %all-gather.19.cloned.1.call-update) | async-done | bytes 15728656 | tf_op jit(solution)/shard_map/all_gather | solution.py:160
  400.6 87.2 %all-gather.21.cloned.1.call-done = bf16[10,1536,512]{2,1,0:T(8,128)(2,1)} async-done(((bf16[10,192,512]{2,1,0:T(8,128)(2,1)}), bf16[10,1536,512]{2,1,0:T(8,128)(2,1)}) %all-gather.21.cloned.1.call-update) | async-done | bytes 15728656 | tf_op jit(solution)/shard_map/all_gather | solution.py:161
  487.8 87.2 %all-gather.23.cloned.1.call-done = bf16[10,1536,512]{2,1,0:T(8,128)(2,1)} async-done(((bf16[10,192,512]{2,1,0:T(8,128)(2,1)}), bf16[10,1536,512]{2,1,0:T(8,128)(2,1)}) %all-gather.23.cloned.1.call-update) | async-done | bytes 15728656 | tf_op jit(solution)/shard_map/all_gather | solution.py:162
  578.5 468.3 %while.71 = (s32[]{:T(128)}, f32[1024,1536]{1,0:T(8,128)}, s32[10,408]{1,0:T(8,128)}, f32[10,408]{1,0:T(8,128)}, f32[10,408,8]{2,1,0:T(8,128)}, /*index=5*/f32[1...) while((s32[]{:T(128)}, f32[1024,1536]{1,0:T(8,128)}, ...), condition=%wide.region_18.20_spmd, body=%wide.region_10.19_spmd.sunk | while | flops 1929139968 | bytes 35207396 | solution.py:225
  614.2 11.3 scatter_custom_fusion.17
  707.9 11.2 scatter_custom_fusion.17
  754.7 11.2 scatter_custom_fusion.17
  801.5 11.2 scatter_custom_fusion.17
  1051.0 504.1 %while.72 = (s32[]{:T(128)}, f32[1024,1536]{1,0:T(8,128)}, f32[1024,8]{1,0:T(8,128)}, f32[10,1536,512]{2,1,0:T(8,128)}, f32[10,1536,512]{2,1,0:T(8,128)}, /*inde...) while((s32[]{:T(128)}, f32[1024,1536]{1,0:T(8,128)}, ...), condition=%wide.region_24.26_spmd, body=%wide.region_20.25_spmd.sunk | while | flops 3863125760 | bytes 57883772 | solution.py:269
  1557.7 18.9 reduce-scatter.19.cloned.1.call-done
  1578.1 109.8 %reduce-scatter.17.cloned.1.call-done = f32[256,1536]{1,0:T(8,128)} async-done(((f32[1024,1536]{1,0:T(8,128)}), f32[256,1536]{1,0:T(8,128)}) %reduce-scatter.17.cloned.1.call-update) | async-done | bytes 1572880 | tf_op jit(solution)/shard_map/reduce_scatter | solution.py:273
  1693.7 62.9 %all-gather.27.cloned.1.call-done = bf16[1024,1536]{1,0:T(8,128)(2,1)} async-done(((bf16[256,1536]{1,0:T(8,128)(2,1)}), bf16[1024,1536]{1,0:T(8,128)(2,1)}) %all-gather.27.cloned.1.call-update) | async-done | bytes 3145744 | tf_op jit(solution)/shard_map/all_gather | solution.py:284
  1761.6 65.1 %while.73 = (s32[]{:T(128)}, f32[2,512,6,64]{1,0,3,2:T(2,128)}, f32[2,512,2,64]{1,0,3,2:T(2,128)}, bf16[2,512,2,64]{1,3,2,0:T(8,128)(2,1)}, bf16[2,512,2,64]{1,3...) while((s32[]{:T(128)}, f32[2,512,6,64]{1,0,3,2:T(2,128)}, ...), condition=%wide.region_32.34_spmd, body=%wide.region_30.33_spmd.sunk | while | flops 1031271424 | bytes 58161316 | solution.py:289
  1779.1 15.0 dynamic_update_slice.116
  1811.6 15.0 dynamic_update_slice.116
  1859.1 27.0 all-reduce.3.cloned.1.call-done
  1887.6 111.7 %reduce-scatter.21.cloned.1.call-done = f32[256,1536]{1,0:T(8,128)} async-done(((f32[1024,1536]{1,0:T(8,128)}), f32[256,1536]{1,0:T(8,128)}) %reduce-scatter.21.cloned.1.call-update) | async-done | bytes 1572880 | tf_op jit(solution)/shard_map/reduce_scatter | solution.py:316
  2001.3 45.1 %all-reduce = (f32[1536]{0:T(1024)}, f32[1536]{0:T(1024)}) all-reduce(f32[1536]{0:T(1024)S(1)} %get-tuple-element.575, f32[1536]{0:T(1024)S(1)} %get-tuple-element.573), channel_id=1, replica_groups=mesh['fsdp'=8,'tp'=4] {'fsdp','tp'}, use_global_device_ids=true, to_apply=%region_36.38 | all-reduce | flops 3072 | bytes 24576 | tf_op jit(solution)/shard_map/psum | solution.py:321
  2046.4 67.5 %reduce-scatter.15.cloned.1.call-done = f32[256,1536]{1,0:T(8,128)} async-done(((f32[1024,1536]{1,0:T(8,128)}), f32[256,1536]{1,0:T(8,128)}) %reduce-scatter.15.cloned.1.call-update) | async-done | bytes 1572880 | tf_op jit(solution)/shard_map/reduce_scatter | solution.py:226
  2118.5 34.4 %reduce-scatter.25.cloned.1.call-done = f32[192,128]{1,0:T(8,128)} async-done(((f32[1536,128]{1,0:T(8,128)}), f32[192,128]{1,0:T(8,128)}) %reduce-scatter.25.cloned.1.call-update) | async-done | bytes 98320 | tf_op jit(solution)/shard_map/reduce_scatter | solution.py:330
  2152.9 38.6 %reduce-scatter.27.cloned.1.call-done = f32[192,128]{1,0:T(8,128)} async-done(((f32[1536,128]{1,0:T(8,128)}), f32[192,128]{1,0:T(8,128)}) %reduce-scatter.27.cloned.1.call-update) | async-done | bytes 98320 | tf_op jit(solution)/shard_map/reduce_scatter | solution.py:331
  2191.5 46.2 %reduce-scatter.29.cloned.1.call-done = f32[192,384]{1,0:T(8,128)} async-done(((f32[1536,384]{1,0:T(8,128)}), f32[192,384]{1,0:T(8,128)}) %reduce-scatter.29.cloned.1.call-update) | async-done | bytes 294928 | tf_op jit(solution)/shard_map/reduce_scatter | solution.py:332
  2237.7 46.3 %reduce-scatter.23.cloned.1.call-done = f32[192,384]{1,0:T(8,128)} async-done(((f32[1536,384]{1,0:T(8,128)}), f32[192,384]{1,0:T(8,128)}) %reduce-scatter.23.cloned.1.call-update) | async-done | bytes 294928 | tf_op jit(solution)/shard_map/reduce_scatter | solution.py:329
  2283.9 189.9 %reduce-scatter.35.cloned.1.call-done = f32[10,192,512]{2,1,0:T(8,128)} async-done(((f32[10,1536,512]{2,1,0:T(8,128)}), f32[10,192,512]{2,1,0:T(8,128)}) %reduce-scatter.35.cloned.1.call-update) | async-done | bytes 3932176 | tf_op jit(solution)/shard_map/reduce_scatter | solution.py:337
  2473.9 190.0 %reduce-scatter.31.cloned.1.call-done = f32[10,192,512]{2,1,0:T(8,128)} async-done(((f32[10,1536,512]{2,1,0:T(8,128)}), f32[10,192,512]{2,1,0:T(8,128)}) %reduce-scatter.31.cloned.1.call-update) | async-done | bytes 3932176 | tf_op jit(solution)/shard_map/reduce_scatter | solution.py:335
  2663.9 190.0 %reduce-scatter.33.cloned.1.call-done = f32[10,192,512]{2,1,0:T(8,128)} async-done(((f32[10,1536,512]{2,1,0:T(8,128)}), f32[10,192,512]{2,1,0:T(8,128)}) %reduce-scatter.33.cloned.1.call-update) | async-done | bytes 3932176 | tf_op jit(solution)/shard_map/reduce_scatter | solution.py:336
  (944 shorter events, 1114.8 us)
Async XLA Ops:
  7.2 71.9 %all-gather.11.cloned.1.call-start = ((), (), s32[]{:S(2)}) async-start(), calls=%async_computation.12 | async-start | bytes 3932160 | tf_op jit(solution)/shard_map/all_gather | solution.py:168
  12.8 90.8 %all-gather.13.cloned.1.call-start = ((), (), s32[]{:S(2)}) async-start(), calls=%async_computation.13 | async-start | bytes 1327104 | tf_op jit(solution)/shard_map/all_gather | solution.py:155
  13.5 115.9 %all-gather.15.cloned.1.call-start = ((), (), s32[]{:S(2)}) async-start(), calls=%async_computation.14 | async-start | bytes 1327104 | tf_op jit(solution)/shard_map/all_gather | solution.py:158
  14.3 232.2 %reduce-scatter.13.cloned.1.call-start = ((), (), s32[]{:S(2)}) async-start(), calls=%async_computation.15 | async-start | bytes 7864320 | tf_op jit(solution)/shard_map/reduce_scatter | solution.py:190
  135.5 179.3 %all-gather.17.cloned.1.call-start = ((), (), s32[]{:S(2)}) async-start(), calls=%async_computation.16 | async-start | bytes 3932160 | tf_op jit(solution)/shard_map/all_gather | solution.py:206
  250.5 150.1 %all-gather.19.cloned.1.call-start = ((), (), s32[]{:S(2)}) async-start(), calls=%async_computation.17 | async-start | bytes 17694720 | tf_op jit(solution)/shard_map/all_gather | solution.py:160
  251.1 236.7 %all-gather.21.cloned.1.call-start = ((), (), s32[]{:S(2)}) async-start(), calls=%async_computation.18 | async-start | bytes 17694720 | tf_op jit(solution)/shard_map/all_gather | solution.py:161
  251.9 323.2 %all-gather.23.cloned.1.call-start = ((), (), s32[]{:S(2)}) async-start(), calls=%async_computation.19 | async-start | bytes 17694720 | tf_op jit(solution)/shard_map/all_gather | solution.py:162
  252.6 794.2 %all-gather.25.cloned.1.call-start = ((), (), s32[]{:S(2)}) async-start(), calls=%async_computation.21 | async-start | bytes 3932160 | tf_op jit(solution)/shard_map/all_gather | solution.py:230
  253.7 1322.9 %reduce-scatter.19.cloned.1.call-start = ((), (), s32[]{:S(2)}) async-start(), calls=%async_computation.23 | async-start | bytes 40960 | tf_op jit(solution)/shard_map/reduce_scatter | solution.py:274
  314.8 263.6 %copy-start = (bf16[1024,1536]{1,0:T(8,128)(2,1)S(1)}, bf16[1024,1536]{1,0:T(8,128)(2,1)}, u32[]{:S(2)}) copy-start(bf16[1024,1536]{1,0:T(8,128)(2,1)} %all-gather.17.cloned.1.call-done) | copy-start | bytes 9437188
  1556.9 130.9 %reduce-scatter.17.cloned.1.call-start = ((), (), s32[]{:S(2)}) async-start(), calls=%async_computation.22 | async-start | bytes 7864320 | tf_op jit(solution)/shard_map/reduce_scatter | solution.py:273
  1557.0 130.8 %copy-start.4 = (f32[256,1536]{1,0:T(8,128)S(1)}, f32[256,1536]{1,0:T(8,128)}, u32[]{:S(2)}) copy-start(f32[256,1536]{1,0:T(8,128)} %copy-done.3) | copy-start | bytes 4718596
  1557.0 130.8 %copy-start.41 = (bf16[1536,40]{0,1:T(8,128)(2,1)S(1)}, bf16[1536,40]{0,1:T(8,128)(2,1)}, u32[]{:S(2)}) copy-start(bf16[1536,40]{0,1:T(8,128)(2,1)} %copy-done.40) | copy-start | bytes 368644
  1557.7 133.4 %copy-start.21 = (bf16[256,1536]{1,0:T(8,128)(2,1)S(1)}, bf16[256,1536]{1,0:T(8,128)(2,1)}, u32[]{:S(2)}) copy-start(bf16[256,1536]{1,0:T(8,128)(2,1)} %param.37) | copy-start | bytes 2359300
  1557.7 199.0 %all-gather.27.cloned.1.call-start = ((), (), s32[]{:S(2)}) async-start(), calls=%async_computation.24 | async-start | bytes 3932160 | tf_op jit(solution)/shard_map/all_gather | solution.py:284
  1692.6 193.5 %all-reduce.3.cloned.1.call-start = ((), (), s32[]{:S(2)}) async-start(), calls=%async_computation.30 | async-start | bytes 491520 | tf_op jit(solution)/shard_map/psum | solution.py:321
  1693.7 305.7 %reduce-scatter.21.cloned.1.call-start = ((), (), s32[]{:S(2)}) async-start(), calls=%async_computation.25 | async-start | bytes 7864320 | tf_op jit(solution)/shard_map/reduce_scatter | solution.py:316
  1840.3 273.6 %reduce-scatter.15.cloned.1.call-start = ((), (), s32[]{:S(2)}) async-start(), calls=%async_computation.20 | async-start | bytes 7864320 | tf_op jit(solution)/shard_map/reduce_scatter | solution.py:226
  1840.9 312.1 %reduce-scatter.25.cloned.1.call-start = ((), (), s32[]{:S(2)}) async-start(), calls=%async_computation.27 | async-start | bytes 884736 | tf_op jit(solution)/shard_map/reduce_scatter | solution.py:330
  1844.2 347.3 %reduce-scatter.27.cloned.1.call-start = ((), (), s32[]{:S(2)}) async-start(), calls=%async_computation.28 | async-start | bytes 884736 | tf_op jit(solution)/shard_map/reduce_scatter | solution.py:331
  1847.1 390.6 %reduce-scatter.29.cloned.1.call-start = ((), (), s32[]{:S(2)}) async-start(), calls=%async_computation.29 | async-start | bytes 2654208 | tf_op jit(solution)/shard_map/reduce_scatter | solution.py:332
  1852.5 431.5 %reduce-scatter.23.cloned.1.call-start = ((), (), s32[]{:S(2)}) async-start(), calls=%async_computation.26 | async-start | bytes 2654208 | tf_op jit(solution)/shard_map/reduce_scatter | solution.py:329
  1857.0 616.9 %reduce-scatter.35.cloned.1.call-start = ((), (), s32[]{:S(2)}) async-start(), calls=%async_computation.33 | async-start | bytes 35389440 | tf_op jit(solution)/shard_map/reduce_scatter | solution.py:337
  1857.5 806.3 %reduce-scatter.31.cloned.1.call-start = ((), (), s32[]{:S(2)}) async-start(), calls=%async_computation.31 | async-start | bytes 35389440 | tf_op jit(solution)/shard_map/reduce_scatter | solution.py:335
  1858.3 995.7 %reduce-scatter.33.cloned.1.call-start = ((), (), s32[]{:S(2)}) async-start(), calls=%async_computation.32 | async-start | bytes 35389440 | tf_op jit(solution)/shard_map/reduce_scatter | solution.py:336
  1858.3 141.0 %copy-start.13 = (bf16[256,1536]{1,0:T(8,128)(2,1)S(1)}, bf16[256,1536]{1,0:T(8,128)(2,1)}, u32[]{:S(2)}) copy-start(bf16[256,1536]{1,0:T(8,128)(2,1)} %param.24) | copy-start | bytes 2359300
  1858.3 141.0 %copy-start.49 = (f32[1536]{0:T(1024)S(1)}, f32[1536]{0:T(1024)}, u32[]{:S(2)}) copy-start(f32[1536]{0:T(1024)} %copy-done.48) | copy-start | bytes 18436
  1858.3 141.0 %copy-start.65 = (f32[256]{0:T(256)S(1)}, f32[256]{0:T(256)}, u32[]{:S(2)}) copy-start(f32[256]{0:T(256)} %copy-done.64) | copy-start | bytes 3076
  1858.4 255.5 %copy-start.67 = (f32[256]{0:T(256)S(1)}, f32[256]{0:T(256)}, u32[]{:S(2)}) copy-start(f32[256]{0:T(256)} %get-tuple-element.715) | copy-start | bytes 3076
  1859.0 254.8 %copy-start.5 = (f32[256,1536]{1,0:T(8,128)S(1)}, f32[256,1536]{1,0:T(8,128)}, u32[]{:S(2)}) copy-start(f32[256,1536]{1,0:T(8,128)} %copy-done.3) | copy-start | bytes 4718596
  1859.0 254.8 %copy-start.22 = (bf16[256,1536]{1,0:T(8,128)(2,1)S(1)}, bf16[256,1536]{1,0:T(8,128)(2,1)}, u32[]{:S(2)}) copy-start(bf16[256,1536]{1,0:T(8,128)(2,1)} %param.37) | copy-start | bytes 2359300
  (153 other events, 1550.2 us)
Sparse Core Ops, SparseCore 0:
  12.9 66.1 all-gather.10
  81.0 22.5 all-gather.12
  105.5 23.9 all-gather.14
  135.6 110.7 reduce-scatter.12
  250.6 64.1 all-gather.16
  316.6 83.9 all-gather.18
  402.5 85.2 all-gather.20
  489.7 85.2 all-gather.22
  577.2 63.4 all-gather.24
  1557.0 19.4 reduce-scatter.18
  1578.9 108.9 reduce-scatter.16
  1692.7 63.9 all-gather.26
  1762.2 123.8 all-reduce.2
  1888.2 111.0 reduce-scatter.20
  2001.5 112.3 reduce-scatter.14
  2117.4 35.4 reduce-scatter.24
  2156.5 34.9 reduce-scatter.26
  2195.3 42.3 reduce-scatter.28
  2241.6 42.3 reduce-scatter.22
  2288.0 185.8 reduce-scatter.34
  2478.1 185.7 reduce-scatter.30
  2668.1 185.8 reduce-scatter.32
where the time goes:
time: 2880 us; the launch traced here: 2860 us
  waiting for transfers between devices  1610 us (56%)
  other arithmetic  411 us (14%)
  matrix products  385 us (13%)
  local copies, waits for them, and re-layouts  348 us (12%)
  blocking collectives  90.5 us (3%)
    reduce_scatter x1, waiting for transfers between devices, local(): lax.psum_scatter(up_grads, 'fsdp', scatter_dimension=1, tiled=True)  190 us
    reduce_scatter x1, waiting for transfers between devices, local(): lax.psum_scatter(gate_grads, 'fsdp', scatter_dimension=1, tiled=True)  190 us
    reduce_scatter x1, waiting for transfers between devices, local(): lax.psum_scatter(down_grads, 'fsdp', scatter_dimension=1, tiled=True)  190 us
    dot_general x35, matrix products, contract_last(): lax.dot_general(left_op, right_op, (((1,), (1,)), ((), ())), preferred_el...  122 us
    dot_general x35, matrix products, contract_first(): lax.dot_general(left_op, right_op, (((0,), (0,)), ((), ())), preferred_el...  117 us
    scatter-add x10, other arithmetic, expert_forward(): running = running.at[slot_rows].add(expert_out * slot_scale[:, None])  112 us
    reduce_scatter x1, waiting for transfers between devices, local(): lax.psum_scatter(total_grad + contract_last(value_proj_grad, value_w), 't...  112 us
    reduce_scatter x1, waiting for transfers between devices, local(): lax.psum_scatter(contract_last(mixed_rows, out_w), 'tp', scatter_dimensio...  110 us
  transfers between devices with their start and end apart: 22, of which 21 were waited for; matrix products, arithmetic and copies ran while one was open for 21% of the time, Pallas kernels for 0%

commit v1 on v0

v1 whole, which is shorter than its diff:
```python
import functools

import jax
import jax.numpy as jnp
from jax import lax
from jax.experimental import pallas as pl
from jax.experimental.pallas import tpu as pltpu
from jax.sharding import PartitionSpec as P

HEAD_DIM = 64
SEQ = 512


emb_scale = 12.0
resid_scale = 0.22
attn_scale = 0.015625
norm_eps = 1e-06
rope_base = 10000.0
masked_value = -1e30


def contract_last(left_op, right_op):
    return lax.dot_general(
        left_op, right_op, (((1,), (1,)), ((), ())), preferred_element_type=jnp.float32
    )


def contract_first(left_op, right_op):
    return lax.dot_general(
        left_op, right_op, (((0,), (0,)), ((), ())), preferred_element_type=jnp.float32
    )


def rms_forward(values, gain_vec):
    inverse = lax.rsqrt(jnp.mean(values * values, axis=-1, keepdims=True) + norm_eps)
    return (values * inverse * gain_vec, inverse)


def rms_backward(incoming, values, inverse, gain_vec):
    scaled = values * inverse
    gain_grad = jnp.sum(incoming * scaled, axis=0)
    weighted = incoming * gain_vec
    row_inner = jnp.mean(weighted * scaled, axis=-1, keepdims=True)
    return (inverse * (weighted - scaled * row_inner), gain_grad)


def rotary_tables(row_count, head_width):
    half_width = head_width // 2
    positions = (jnp.arange(row_count) % SEQ).astype(jnp.float32)
    frequency = rope_base ** (-jnp.arange(half_width).astype(jnp.float32) * 2.0 / head_width)
    angles = positions[:, None] * frequency[None, :]
    return (jnp.cos(angles)[:, None, :], jnp.sin(angles)[:, None, :])


def rotate(values, cosine_table, sine_table):
    half_width = values.shape[-1] // 2
    lead_half = values[..., :half_width]
    tail_half = values[..., half_width:]
    return jnp.concatenate(
        [
            lead_half * cosine_table - tail_half * sine_table,
            tail_half * cosine_table + lead_half * sine_table,
        ],
        axis=-1,
    )


def attention_scores(queries, key_rows, segments):
    length, heads_here, head_width = queries.shape
    kv_here = key_rows.shape[1]
    grouped = queries.reshape(length, kv_here, heads_here // kv_here, head_width)
    scores = (
        jnp.einsum("qkgd,tkd->kgqt", grouped, key_rows, preferred_element_type=jnp.float32)
        * attn_scale
    )
    places = jnp.arange(length)
    allowed = (places[:, None] >= places[None, :]) & (segments[:, None] == segments[None, :])
    return (jnp.where(allowed, scores, masked_value), grouped)


def attend_forward(pieces):
    queries, key_rows, value_rows, segments = pieces
    scores, grouped = attention_scores(queries, key_rows, segments)
    row_top = jnp.max(scores, axis=-1, keepdims=True)
    raised = jnp.exp(scores - row_top)
    row_total = jnp.sum(raised, axis=-1, keepdims=True)
    probs_low = (raised / row_total).astype(jnp.bfloat16)
    mixed_out = jnp.einsum(
        "kgqt,tkd->qkgd", probs_low, value_rows, preferred_element_type=jnp.float32
    )
    return (
        mixed_out.astype(jnp.bfloat16).reshape(queries.shape[0], -1),
        (row_top + jnp.log(row_total))[..., 0],
    )


def attend_backward(pieces):
    queries, key_rows, value_rows, segments, logsum, mixed_grad = pieces
    scores, grouped = attention_scores(queries, key_rows, segments)
    attn_probs = jnp.exp(scores - logsum[..., None])
    grad_grouped = mixed_grad.reshape(grouped.shape)
    probs_grad = jnp.einsum(
        "qkgd,tkd->kgqt", grad_grouped, value_rows, preferred_element_type=jnp.float32
    )
    row_inner = jnp.sum(attn_probs * probs_grad, axis=-1, keepdims=True)
    score_grad = (attn_probs * (probs_grad - row_inner)).astype(jnp.bfloat16)
    query_grad = (
        jnp.einsum("kgqt,tkd->qkgd", score_grad, key_rows, preferred_element_type=jnp.float32)
        * attn_scale
    )
    key_grad = (
        jnp.einsum("kgqt,qkgd->tkd", score_grad, grouped, preferred_element_type=jnp.float32)
        * attn_scale
    )
    value_grad = jnp.einsum(
        "kgqt,qkgd->tkd",
        attn_probs.astype(jnp.bfloat16),
        grad_grouped,
        preferred_element_type=jnp.float32,
    )
    return (query_grad.reshape(queries.shape), key_grad, value_grad)


def line_barrier(me, count):
    barrier = pltpu.get_barrier_semaphore()

    @pl.when(me > 0)
    def _():
        pl.semaphore_signal(barrier, inc=1, device_id={"tp": me - 1})

    @pl.when(me < count - 1)
    def _():
        pl.semaphore_signal(barrier, inc=1, device_id={"tp": me + 1})

    pl.semaphore_wait(barrier, jnp.where((me > 0) & (me < count - 1), 2, 1))


def line_gather_kernel(count, x_ref, o_ref, send_sem, recv_sem, own_sem):
    rows = x_ref.shape[0]
    me = lax.axis_index("tp")
    line_barrier(me, count)

    def part(chunk):
        return o_ref.at[pl.ds(pl.multiple_of(chunk * rows, rows), rows)]

    def hop(way, step, chunk):
        return pltpu.make_async_remote_copy(
            src_ref=x_ref if step == 0 else part(chunk),
            dst_ref=part(chunk),
            send_sem=send_sem.at[way, step],
            recv_sem=recv_sem.at[way, step],
            device_id={"tp": me + 1 if way == 0 else me - 1},
        )

    own = pltpu.make_async_copy(x_ref, part(me), own_sem)
    sends = [[(me >= step) & (me < count - 1) for step in range(count - 1)],
             [(me + step < count) & (me > 0) for step in range(count - 1)]]
    gets = [[me - 1 - step >= 0 for step in range(count - 1)],
            [me + 1 + step < count for step in range(count - 1)]]
    for step in range(count - 1):

        @pl.when(sends[0][step])
        def _():
            hop(0, step, me - step).start()

        @pl.when(sends[1][step])
        def _():
            hop(1, step, me + step).start()

        if step == 0:
            own.start()

        @pl.when(gets[0][step])
        def _():
            hop(0, step, me - 1 - step).wait_recv()

        @pl.when(gets[1][step])
        def _():
            hop(1, step, me + 1 + step).wait_recv()

    own.wait()
    for step in range(count - 1):

        @pl.when(sends[0][step])
        def _():
            hop(0, step, me - step).wait_send()

        @pl.when(sends[1][step])
        def _():
            hop(1, step, me + step).wait_send()


def line_gather(rows_in, count, ident):
    rows, width = rows_in.shape
    return pl.pallas_call(
        functools.partial(line_gather_kernel, count),
        out_shape=jax.ShapeDtypeStruct((rows * count, width), rows_in.dtype),
        in_specs=[pl.BlockSpec(memory_space=pltpu.VMEM)],
        out_specs=pl.BlockSpec(memory_space=pl.ANY),
        scratch_shapes=[
            pltpu.SemaphoreType.DMA((2, count - 1)),
            pltpu.SemaphoreType.DMA((2, count - 1)),
            pltpu.SemaphoreType.DMA,
        ],
        compiler_params=pltpu.CompilerParams(collective_id=ident, has_side_effects=True),
        cost_estimate=pl.CostEstimate(flops=0, transcendentals=0, bytes_accessed=150_000_000),
    )(rows_in)


def line_scatter_kernel(count, x_ref, o_ref, recv, send, send_sem, recv_sem):
    rows = o_ref.shape[0]
    me = lax.axis_index("tp")
    line_barrier(me, count)

    def block(dest):
        return x_ref[pl.ds(pl.multiple_of(dest * rows, rows), rows), :].astype(jnp.float32)

    def hop(way, step):
        return pltpu.make_async_remote_copy(
            src_ref=send.at[way, step],
            dst_ref=recv.at[way, step],
            send_sem=send_sem.at[way, step],
            recv_sem=recv_sem.at[way, step],
            device_id={"tp": me + 1 if way == 0 else me - 1},
        )

    behind = (me, count - 1 - me)
    has_next = (me < count - 1, me > 0)
    has_prev = (me > 0, me < count - 1)
    for step in range(count - 1):
        for way in range(2):
            dest = count - 1 - step + me if way == 0 else step - (count - 1 - me)

            @pl.when(has_next[way] & (step >= behind[way]) & (behind[way] == 0))
            def _():
                send[way, step] = block(dest).astype(send.dtype)
                hop(way, step).start()

            if step > 0:

                @pl.when(has_next[way] & (step >= behind[way]) & (behind[way] > 0))
                def _():
                    total = block(dest) + recv[way, step - 1].astype(jnp.float32)
                    send[way, step] = total.astype(send.dtype)
                    hop(way, step).start()

        for way in range(2):

            @pl.when(has_prev[way] & (step >= behind[way] - 1))
            def _():
                hop(way, step).wait_recv()

    o_ref[...] = block(me)
    for way in range(2):

        @pl.when(has_prev[way])
        def _():
            o_ref[...] += recv[way, count - 2].astype(jnp.float32)

    for step in range(count - 1):
        for way in range(2):

            @pl.when(has_next[way] & (step >= behind[way]))
            def _():
                hop(way, step).wait_send()


def line_scatter(partial_rows, count, ident):
    rows, width = partial_rows.shape[0] // count, partial_rows.shape[1]
    return pl.pallas_call(
        functools.partial(line_scatter_kernel, count),
        out_shape=jax.ShapeDtypeStruct((rows, width), jnp.float32),
        in_specs=[pl.BlockSpec(memory_space=pltpu.VMEM)],
        out_specs=pl.BlockSpec(memory_space=pltpu.VMEM),
        scratch_shapes=[
            pltpu.VMEM((2, count - 1, rows, width), jnp.bfloat16),
            pltpu.VMEM((2, count - 1, rows, width), jnp.bfloat16),
            pltpu.SemaphoreType.DMA((2, count - 1)),
            pltpu.SemaphoreType.DMA((2, count - 1)),
        ],
        compiler_params=pltpu.CompilerParams(
            collective_id=ident, has_side_effects=True, vmem_limit_bytes=56 << 20
        ),
        cost_estimate=pl.CostEstimate(flops=0, transcendentals=0, bytes_accessed=150_000_000),
    )(partial_rows)


SLOTS = 256


def experts_kernel(
    first_expert,
    capacity,
    meta,
    place_row,
    place_cols,
    gate_row,
    x_ref,
    g_ref,
    weights,
    y_ref,
    dx_ref,
    grads,
):
    step = pl.program_id(0)
    expert = step + first_expert
    group, width = x_ref.shape
    tail = dx_ref.shape[1] - width

    @pl.when(step == 0)
    def _():
        y_ref[...] = jnp.zeros_like(y_ref)
        dx_ref[...] = jnp.zeros_like(dx_ref)

    lanes = lax.broadcasted_iota(jnp.int32, place_cols.shape, 1)
    place_col = jnp.sum(jnp.where(lanes == expert, place_cols[...], 0), axis=1, keepdims=True)
    column = expert + meta[meta.shape[0] - 1]
    mark = jnp.where(lax.broadcasted_iota(jnp.int32, (1, tail), 1) == column, 1.0, 0.0)

    def run(base, span):
        slots = lax.broadcasted_iota(jnp.int32, (span, group), 0) + base
        hit = slots == place_row[0]
        pick = jnp.where(hit, 1.0, 0.0).astype(jnp.bfloat16)
        scale = jnp.sum(jnp.where(hit, gate_row[0], 0.0), axis=1, keepdims=True)
        x_taken = jnp.dot(pick, x_ref[...], preferred_element_type=jnp.float32).astype(jnp.bfloat16)
        g_taken = jnp.dot(pick, g_ref[...], preferred_element_type=jnp.float32).astype(jnp.bfloat16)
        gate_pre = jnp.dot(x_taken, weights[0, 0], preferred_element_type=jnp.float32)
        up_pre = jnp.dot(x_taken, weights[0, 1], preferred_element_type=jnp.float32)
        raw = jnp.dot(g_taken, weights[0, 2], preferred_element_type=jnp.float32)
        sig = jax.nn.sigmoid(gate_pre)
        silu = gate_pre * sig
        act = (silu * up_pre).astype(jnp.bfloat16).astype(jnp.float32)
        slot_grad = jnp.sum(act * raw, axis=1, keepdims=True)
        act_grad = raw * scale
        act_scaled = (act * scale).astype(jnp.bfloat16)
        gate_grad = (act_grad * up_pre * sig * (1.0 + gate_pre * (1.0 - sig))).astype(jnp.bfloat16)
        up_grad = (act_grad * silu).astype(jnp.bfloat16)
        extra = (slot_grad * mark).astype(jnp.bfloat16)
        rows_out = contract_last(act_scaled, weights[0, 2]).astype(jnp.bfloat16)
        rows_in = (
            contract_last(gate_grad, weights[0, 0]) + contract_last(up_grad, weights[0, 1])
        ).astype(jnp.bfloat16)
        for slot, left_op, right_op in (
            (0, x_taken, gate_grad),
            (1, x_taken, up_grad),
            (2, g_taken, act_scaled),
        ):
            grad = contract_first(left_op, right_op)
            if base > 0:
                grad = grad + grads[0, slot].astype(jnp.float32)
            grads[0, slot] = grad.astype(jnp.bfloat16)
        block = min(256, group)
        for start in range(0, group, block):
            back = jnp.where(
                lax.broadcasted_iota(jnp.int32, (block, span), 1) + base
                == place_col[start : start + block],
                1.0,
                0.0,
            ).astype(jnp.bfloat16)
            for target, low_col, addend in (
                (y_ref, 0, rows_out),
                (dx_ref, 0, rows_in),
                (dx_ref, width, extra),
            ):
                area = (slice(start, start + block), slice(low_col, low_col + addend.shape[1]))
                target[area] = (
                    target[area].astype(jnp.float32)
                    + jnp.dot(back, addend, preferred_element_type=jnp.float32)
                ).astype(target.dtype)

    run(0, min(SLOTS, capacity))
    for base in range(SLOTS, capacity, SLOTS):
        span = min(SLOTS, -(-(capacity - base) // 16) * 16)

        @pl.when(meta[expert] > base)
        def _():
            run(base, span)


def experts_step(meta, place_rows, place_cols, gate_rows, x_rows, g_rows, weights, first, capacity):
    group, width = x_rows.shape
    count, _, _, hidden = weights.shape
    keep = jnp.float32 if group <= 1024 else jnp.bfloat16
    tail = 128

    def whole(shape):
        return pl.BlockSpec(
            shape, lambda step, meta: (0,) * len(shape), pipeline_mode=pl.Buffered(1)
        )

    def row(shape):
        return pl.BlockSpec(shape, lambda step, meta: (step + first, 0, 0))

    def big():
        return pl.BlockSpec((1, 3, width, hidden), lambda step, meta: (step, 0, 0, 0))

    return pl.pallas_call(
        functools.partial(experts_kernel, first, capacity),
        grid_spec=pltpu.PrefetchScalarGridSpec(
            num_scalar_prefetch=1,
            grid=(count,),
            in_specs=[
                row((1, 1, group)),
                whole(place_cols.shape),
                row((1, 1, group)),
                whole(x_rows.shape),
                whole(g_rows.shape),
                big(),
            ],
            out_specs=[
                whole((group, width)),
                whole((group, width + tail)),
                big(),
            ],
        ),
        out_shape=[
            jax.ShapeDtypeStruct((group, width), keep),
            jax.ShapeDtypeStruct((group, width + tail), keep),
            jax.ShapeDtypeStruct(weights.shape, jnp.bfloat16),
        ],
        compiler_params=pltpu.CompilerParams(
            dimension_semantics=("arbitrary",), vmem_limit_bytes=63 << 20
        ),
        cost_estimate=pl.CostEstimate(
            flops=count * 17 * 2 * 408 * width * hidden,
            transcendentals=count * 408 * hidden,
            bytes_accessed=count * 12 * width * hidden,
        ),
    )(meta, place_rows, place_cols, gate_rows, x_rows, g_rows, weights)


CHUNKS = 2


def local(
    emb,
    segment_ids,
    routes,
    norm1_gain,
    w_query,
    w_key,
    w_value,
    w_out,
    norm2_gain,
    w_router,
    w_gate,
    w_up,
    w_down,
    cotangent,
):
    local_rows = emb.shape[0]
    tp_count = lax.axis_size("tp")
    tp_index = lax.axis_index("tp")
    experts_here = w_gate.shape[0]
    attn_w = lax.all_gather(
        jnp.concatenate([w_query, w_key, w_value, w_out, jnp.pad(w_router, ((0, 0), (0, 128 - w_router.shape[1])))], axis=1),
        "fsdp", axis=0, tiled=True)
    q_width, kv_width = w_query.shape[1], w_key.shape[1]
    query_w = attn_w[:, :q_width]
    key_w = attn_w[:, q_width : q_width + kv_width]
    value_w = attn_w[:, q_width + kv_width : q_width + 2 * kv_width]
    out_w = attn_w[:, q_width + 2 * kv_width : 2 * q_width + 2 * kv_width]
    expert_count = w_router.shape[1]
    router_w = attn_w[:, 2 * q_width + 2 * kv_width :]
    stacked = jnp.stack([w_gate, w_up, w_down], axis=1)
    edges = [experts_here * part // CHUNKS for part in range(CHUNKS + 1)]
    pieces = []
    for low, high in zip(edges[:-1], edges[1:]):
        pieces.append(lax.all_gather(stacked[low:high], "fsdp", axis=2, tiled=True))

    gain_one = norm1_gain.astype(jnp.float32)
    gain_two = norm2_gain.astype(jnp.float32)
    start_x = emb.astype(jnp.float32) * emb_scale
    normed_one, inverse_one = rms_forward(start_x, gain_one)
    group_rows = line_gather(normed_one.astype(jnp.bfloat16), tp_count, 0)
    out_grad = cotangent.astype(jnp.float32)
    moe_grad_rows = line_gather((resid_scale * out_grad).astype(jnp.bfloat16), tp_count, 1)
    group_size = group_rows.shape[0]
    seq_count = group_size // SEQ
    heads_here = query_w.shape[1] // HEAD_DIM
    kv_here = key_w.shape[1] // HEAD_DIM

    capacity = group_size * routes.shape[1] // expert_count * 2
    all_experts = jnp.arange(expert_count, dtype=jnp.int32)
    member_all = jnp.any(routes[:, :, None] == all_experts[None, None, :], axis=1)
    own_member = lax.dynamic_slice_in_dim(member_all, tp_index * local_rows, local_rows, 0)
    member = lax.dynamic_slice_in_dim(member_all, tp_index * experts_here, experts_here, 1)
    ids = jnp.arange(group_size)
    earlier = (ids[:, None] > ids[None, :]).astype(jnp.bfloat16)
    ranks = jnp.dot(earlier, member.astype(jnp.bfloat16), preferred_element_type=jnp.float32)
    places = jnp.where(member, ranks.astype(jnp.int32), -1)
    meta = jnp.concatenate(
        [jnp.sum(member.astype(jnp.int32), axis=0), (tp_index * experts_here)[None]]
    )

    cosine_table, sine_table = rotary_tables(group_size, HEAD_DIM)
    query_proj = jnp.dot(group_rows, query_w, preferred_element_type=jnp.float32).reshape(
        group_size, heads_here, HEAD_DIM
    )
    key_proj = jnp.dot(group_rows, key_w, preferred_element_type=jnp.float32).reshape(
        group_size, kv_here, HEAD_DIM
    )
    queries = rotate(query_proj, cosine_table, sine_table).astype(jnp.bfloat16)
    key_rows = rotate(key_proj, cosine_table, sine_table).astype(jnp.bfloat16)
    value_rows = jnp.dot(group_rows, value_w, preferred_element_type=jnp.float32).astype(
        jnp.bfloat16
    )
    seq_queries = queries.reshape(seq_count, SEQ, heads_here, HEAD_DIM)
    seq_keys = key_rows.reshape(seq_count, SEQ, kv_here, HEAD_DIM)
    seq_values = value_rows.reshape(seq_count, SEQ, kv_here, HEAD_DIM)
    mixed_out, logsum = lax.map(attend_forward, (seq_queries, seq_keys, seq_values, segment_ids))
    mixed_rows = mixed_out.reshape(group_size, heads_here * HEAD_DIM)
    attn_branch = line_scatter(contract_last(mixed_rows, out_w), tp_count, 2)
    mid_x = start_x + resid_scale * attn_branch
    normed_two, inverse_two = rms_forward(mid_x, gain_two)
    normed_low = normed_two.astype(jnp.bfloat16)
    moe_rows = line_gather(normed_low, tp_count, 3)

    def gates_of(rows, inside):
        logits = jnp.dot(rows, router_w, preferred_element_type=jnp.float32)[:, :expert_count]
        top = jnp.max(jnp.where(inside, logits, masked_value), axis=-1, keepdims=True)
        raised = jnp.where(inside, jnp.exp(jnp.where(inside, logits - top, 0.0)), 0.0)
        return raised / jnp.sum(raised, axis=-1, keepdims=True)

    gates = gates_of(normed_low, own_member)
    gates_here = lax.dynamic_slice_in_dim(
        gates_of(moe_rows, member_all).astype(jnp.bfloat16).astype(jnp.float32),
        tp_index * experts_here, experts_here, 1)
    place_rows = places.T[:, None, :]
    gate_rows = gates_here.T[:, None, :]

    outs = []
    for first, piece in zip(edges[:-1], pieces):
        outs.append(experts_step(
            meta, place_rows, places, gate_rows, moe_rows, moe_grad_rows, piece, first, capacity))
    grad_sums = []
    behind = None
    for part in outs:
        grads = part[2]
        if behind is not None:
            grads, _ = lax.optimization_barrier((grads, behind))
        behind = lax.psum_scatter(grads, "fsdp", scatter_dimension=2, tiled=True)
        grad_sums.append(behind)
    y_part = functools.reduce(lambda one, two: one + two, [part[0] for part in outs])
    dx_part = functools.reduce(lambda one, two: one + two, [part[1] for part in outs])
    dx_sum = line_scatter(dx_part, tp_count, 4)
    rows_grad_sum = dx_sum[:, : emb.shape[1]]
    gates_grad = dx_sum[:, emb.shape[1] : emb.shape[1] + expert_count]
    gates_inner = jnp.sum(gates * gates_grad, axis=-1, keepdims=True)
    logits_grad = (gates * (gates_grad - gates_inner)).astype(jnp.bfloat16)
    router_grad_part = contract_first(normed_low, logits_grad)
    normed_two_grad = rows_grad_sum + contract_last(logits_grad, router_w[:, :expert_count])
    mid_from_norm, gain_two_grad = rms_backward(normed_two_grad, mid_x, inverse_two, gain_two)
    mid_grad = out_grad + mid_from_norm
    branch_grad = (resid_scale * mid_grad).astype(jnp.bfloat16)
    branch_grad_rows = line_gather(branch_grad, tp_count, 5)
    moe_sum = line_scatter(y_part, tp_count, 6)
    out = (mid_x + resid_scale * moe_sum).astype(jnp.bfloat16)
    out_w_grad = contract_first(branch_grad_rows, mixed_rows)
    mixed_grad = jnp.dot(branch_grad_rows, out_w, preferred_element_type=jnp.float32).astype(
        jnp.bfloat16
    )
    query_grad, key_grad, value_grad = lax.map(
        attend_backward,
        (
            seq_queries,
            seq_keys,
            seq_values,
            segment_ids,
            logsum,
            mixed_grad.reshape(seq_count, SEQ, -1),
        ),
    )
    query_proj_grad = (
        rotate(query_grad.reshape(group_size, heads_here, HEAD_DIM), cosine_table, -sine_table)
        .astype(jnp.bfloat16)
        .reshape(group_size, -1)
    )
    key_proj_grad = (
        rotate(key_grad.reshape(group_size, kv_here, HEAD_DIM), cosine_table, -sine_table)
        .astype(jnp.bfloat16)
        .reshape(group_size, -1)
    )
    value_proj_grad = value_grad.reshape(group_size, -1).astype(jnp.bfloat16)
    qkv_grad = jnp.concatenate([query_proj_grad, key_proj_grad, value_proj_grad], axis=1)
    qkv_w_grad = contract_first(group_rows, qkv_grad)
    qkv_w = attn_w[:, : q_width + 2 * kv_width]
    normed_one_grad = line_scatter(contract_last(qkv_grad, qkv_w), tp_count, 7)
    start_from_norm, gain_one_grad = rms_backward(normed_one_grad, start_x, inverse_one, gain_one)
    grad_emb = emb_scale * (mid_grad + start_from_norm)
    attn_grads = jnp.concatenate([qkv_w_grad, out_w_grad], axis=1).astype(jnp.bfloat16)
    attn_grads, grad_sums[-1] = lax.optimization_barrier((attn_grads, grad_sums[-1]))
    attn_sum = lax.psum_scatter(attn_grads, "fsdp", scatter_dimension=0, tiled=True).astype(jnp.float32)
    gain_one_sum, gain_two_sum, router_sum = lax.psum(
        (gain_one_grad, gain_two_grad, router_grad_part), ("fsdp", "tp")
    )
    router_rows = w_router.shape[0]
    router_own = lax.dynamic_slice_in_dim(
        router_sum, lax.axis_index("fsdp") * router_rows, router_rows, 0
    )
    expert_sum = jnp.concatenate(grad_sums, axis=0).astype(jnp.float32)
    return (
        out,
        grad_emb,
        gain_one_sum,
        attn_sum[:, :q_width],
        attn_sum[:, q_width : q_width + kv_width],
        attn_sum[:, q_width + kv_width : q_width + 2 * kv_width],
        attn_sum[:, q_width + 2 * kv_width :],
        gain_two_sum,
        router_own,
        expert_sum[:, 0],
        expert_sum[:, 1],
        expert_sum[:, 2],
    )


def solution(mesh):
    return jax.shard_map(
        local,
        mesh=mesh,
        in_specs=(
            P(("fsdp", "tp"), None),
            P("fsdp", None),
            P("fsdp", None),
            P(),
            P("fsdp", "tp"),
            P("fsdp", "tp"),
            P("fsdp", "tp"),
            P("fsdp", "tp"),
            P(),
            P("fsdp", None),
            P("tp", "fsdp", None),
            P("tp", "fsdp", None),
            P("tp", "fsdp", None),
            P(("fsdp", "tp"), None),
        ),
        out_specs=(
            P(("fsdp", "tp"), None),
            P(("fsdp", "tp"), None),
            P(),
            P("fsdp", "tp"),
            P("fsdp", "tp"),
            P("fsdp", "tp"),
            P("fsdp", "tp"),
            P(),
            P("fsdp", None),
            P("tp", "fsdp", None),
            P("tp", "fsdp", None),
            P("tp", "fsdp", None),
        ),
        check_vma=False,
    )
```

time: 2880 us -> 969 us (0.34)
  waiting for transfers between devices: 1610 us -> 107 us
  Pallas kernels: 0 us -> 553 us
  other arithmetic: 411 us -> 54.2 us
  matrix products: 385 us -> 91.1 us
  local copies, waits for them, and re-layouts: 348 us -> 96.6 us
  blocking collectives: 90.5 us -> 41 us
    reduce_scatter x12 -> x2, waiting for transfers between devices: 1150 us -> 106 us  [local(): behind = lax.psum_scatter(grads, 'fsdp', scatter_dimension=2, tiled=True)]
    pallas_call x0 -> x10, Pallas kernels: none -> 553 us  [the longest x4 228 us: line_scatter(): pl.pallas_call(functools.partial(line_scatter_kernel, count), out_shape=j...]
    all_gather x9 -> x3, waiting for transfers between devices: 422 us -> 0.02 us  [the longest x2 0.02 us: local(): pieces.append(lax.all_gather(stacked[low:high], 'fsdp', axis=2, tiled=True))]
    scatter-add x30 -> x0, other arithmetic: 274 us -> none  [the longest x10 112 us: expert_forward(): running = running.at[slot_rows].add(expert_out * slot_scale[:, None])]
    gather x50 -> x0, local copies, waits for them, and re-layouts: 161 us -> none  [the longest x10 65.8 us: expert_backward(): taken_grad = jnp.take(moe_grad_rows, slot_rows, axis=0).astype(jnp.float32)]
    dot_general x35 -> x3, matrix products: 122 us -> 15.3 us  [contract_last(): lax.dot_general(left_op, right_op, (((1,), (1,)), ((), ())), preferred_el...]
    dot_general x35 -> x3, matrix products: 117 us -> 10.2 us  [contract_first(): lax.dot_general(left_op, right_op, (((0,), (0,)), ((), ())), preferred_el...]
    dot_general x31 -> x3, matrix products: 113 us -> 5.92 us  [the longest x2 4.43 us: gates_of(): jnp.dot(rows, router_w, preferred_element_type=jnp.float32)]
  transfers between devices with their start and end apart: 22 -> 7, of which waited for: 21 -> 1; matrix products, arithmetic and copies ran while one was open for 21% -> 24% of each run, Pallas kernels for 0% -> 58%
where the time goes in v1:
time: 969 us; the launch traced here: 959 us
  Pallas kernels  553 us (57%)
  waiting for transfers between devices  107 us (11%)
  local copies, waits for them, and re-layouts  96.6 us (10%)
  matrix products  91.1 us (9%)
  other arithmetic  54.2 us (6%)
  blocking collectives  41 us (4%)
  between operations  15.3 us (2%)
    pallas_call x4, Pallas kernels, line_scatter(): pl.pallas_call(functools.partial(line_scatter_kernel, count), out_shape=j...  228 us
    pallas_call x4, Pallas kernels, line_gather(): pl.pallas_call(functools.partial(line_gather_kernel, count), out_shape=ja...  219 us
    pallas_call x2, Pallas kernels, experts_step(): pl.pallas_call(functools.partial(experts_kernel, first, capacity), grid_s...  107 us
    reduce_scatter x2, waiting for transfers between devices, local(): behind = lax.psum_scatter(grads, 'fsdp', scatter_dimension=2, tiled=True)  106 us
    dynamic_update_slice x8, local copies, waits for them, and re-layouts, local(): lax.map(attend_backward, (seq_queries, seq_keys, seq_values, segment_ids,...  45.5 us
    psum x1, blocking collectives, local(): lax.psum((gain_one_grad, gain_two_grad, router_grad_part), ('fsdp', 'tp'))  41 us
  transfers between devices with their start and end apart: 7, of which 1 were waited for; matrix products, arithmetic and copies ran while one was open for 24% of the time, Pallas kernels for 58%

profile of v1, /device:TPU:0, one launch (start us, length us, event | category | flops | bytes accessed | tf_op | source)
XLA Modules:
  0.0 959.4 jit_solution(17631948113092541864)
XLA Ops:
  22.3 58.8 %shard_map.229 = bf16[1024,1536]{1,0:T(8,128)(2,1)} custom-call(bf16[256,1536]{1,0:T(8,128)(2,1)} %fusion.55.x_ref), custom_call_target="tpu_custom_call" | custom-call | bytes 150000000 | tf_op jit(solution)/shard_map/pallas_call | solution.py:195
  86.0 52.4 %shard_map.232.g_ref = bf16[1024,1536]{1,0:T(8,128)(2,1)} custom-call(bf16[256,1536]{1,0:T(8,128)(2,1)} %fusion.62.x_ref), custom_call_target="tpu_custom_call" | custom-call | bytes 150000000 | tf_op jit(solution)/shard_map/pallas_call | solution.py:195
  155.4 15.3 %while.26 = (s32[]{:T(128)}, bf16[2,512,384]{2,1,0:T(8,128)(2,1)S(1)}, f32[2,2,3,512]{3,2,1,0:T(4,128)S(1)}, bf16[2,512,2,64]{1,3,2,0:T(8,128)(2,1)S(1)}, s32[2,...) while((s32[]{:T(128)}, ...), condition=%wide.region_4.5_spmd, body=%wide.region_1.4_spmd.sunk | while | flops 422507520 | bytes 23456360 | solution.py:511
  170.7 6.1 fusion.69.x_ref
  176.8 52.2 %shard_map.230 = f32[256,1536]{1,0:T(8,128)} custom-call(f32[1024,1536]{1,0:T(8,128)} %fusion.69.x_ref), custom_call_target="tpu_custom_call" | custom-call | bytes 150000000 | tf_op jit(solution)/shard_map/pallas_call | solution.py:270
  233.1 54.4 %shard_map.231.x_ref = bf16[1024,1536]{1,0:T(8,128)(2,1)} custom-call(bf16[256,1536]{1,0:T(8,128)(2,1)} %multiply_convert_fusion.1.x_ref), custom_call_target="tpu_custom_call" | custom-call | bytes 150000000 | tf_op jit(solution)/shard_map/pallas_call | solution.py:195
  291.2 56.4 %shard_map.233 = (f32[1024,1536]{1,0:T(8,128)}, f32[1024,1664]{1,0:T(8,128)}, bf16[5,3,1536,512]{3,2,1,0:T(8,128)(2,1)}) custom-call(s32[11]{0:T(128)} %pad_add_fusion.meta, s32[10,1,1024]{2,1,0:T(1,128)} %copy.116.place_row, s32[1024,10]{1,0:T(8,128)} %fusion.65.place_cols, f32[10,1,1024]{2,1,0:T(1,128)} %broadcast_in_dim.109.gate_row, ...), custom_call_target="tpu_custom_call" | custom-call | flops 54546923520 | bytes 47185920 | tf_op jit(solution)/shard_map/pallas_call | solution.py:397
  347.8 50.6 %shard_map.234 = (f32[1024,1536]{1,0:T(8,128)}, f32[1024,1664]{1,0:T(8,128)}, bf16[5,3,1536,512]{3,2,1,0:T(8,128)(2,1)}) custom-call(s32[11]{0:T(128)} %pad_add_fusion.meta, s32[10,1,1024]{2,1,0:T(1,128)} %copy.116.place_row, s32[1024,10]{1,0:T(8,128)} %fusion.65.place_cols, f32[10,1,1024]{2,1,0:T(1,128)} %broadcast_in_dim.109.gate_row, ...), custom_call_target="tpu_custom_call" | custom-call | flops 54546923520 | bytes 47185920 | tf_op jit(solution)/shard_map/pallas_call | solution.py:397
  398.4 106.3 %reduce-scatter.6.cloned.1.call-done = bf16[5,3,192,512]{3,2,1,0:T(8,128)(2,1)} async-done(((bf16[5,3,1536,512]{3,2,1,0:T(8,128)(2,1)}), bf16[5,3,192,512]{3,2,1,0:T(8,128)(2,1)}) %reduce-scatter.6.cloned.1.call-update) | async-done | bytes 2949136 | tf_op jit(solution)/shard_map/reduce_scatter | solution.py:542
  507.5 8.7 add.143.x_ref
  516.2 64.9 %shard_map.236 = f32[256,1664]{1,0:T(8,128)} custom-call(f32[1024,1664]{1,0:T(8,128)} %add.143.x_ref), custom_call_target="tpu_custom_call" | custom-call | bytes 150000000 | tf_op jit(solution)/shard_map/pallas_call | solution.py:270
  587.9 53.0 %shard_map.237 = bf16[1024,1536]{1,0:T(8,128)(2,1)} custom-call(bf16[256,1536]{1,0:T(8,128)(2,1)} %multiply_convert_fusion.x_ref), custom_call_target="tpu_custom_call" | custom-call | bytes 150000000 | tf_op jit(solution)/shard_map/pallas_call | solution.py:195
  645.0 93.5 %while.27 = (s32[]{:T(128)}, f32[2,512,6,64]{1,0,3,2:T(2,128)}, f32[2,512,2,64]{1,0,3,2:T(2,128)}, bf16[2,512,2,64]{1,3,2,0:T(8,128)(2,1)}, bf16[2,512,2,64]{1,3...) while((s32[]{:T(128)}, f32[2,512,6,64]{1,0,3,2:T(2,128)}, ...), condition=%wide.region_16.17_spmd, body=%wide.region_14.16_spmd.sunk | while | flops 1031271424 | bytes 86470960 | solution.py:563
  646.4 4.8 fusion.150
  653.1 5.1 fusion.152
  663.4 15.0 %dynamic_update_slice.30 = f32[2,512,6,64]{1,0,3,2:T(2,128)} dynamic-update-slice(f32[2,512,6,64]{1,0,3,2:T(2,128)} %get-tuple-element.469, f32[1,512,6,64]{1,0,3,2:T(1,128)} %copy.174, s32[]{:T(128)} %get-tuple-element.468, s32[]{:T(128)} %constant.63.clone.1..sunk, s32[]{:T(128)} %constant.63.clone.1..sunk, s32[]{:T(128)} %constant.63.clone.1..sunk) | dynamic-update-slice | bytes 1572868 | tf_op jit(solution)/shard_map/while/body/jit(dynamic_update_index_in_dim)/dynamic_update_slice | solution.py:563
  680.8 5.8 dynamic_update_slice.31
  686.5 5.3 fusion.155
  693.1 4.8 fusion.150
  699.8 5.1 fusion.152
  710.1 15.0 %dynamic_update_slice.30 = f32[2,512,6,64]{1,0,3,2:T(2,128)} dynamic-update-slice(f32[2,512,6,64]{1,0,3,2:T(2,128)} %get-tuple-element.469, f32[1,512,6,64]{1,0,3,2:T(1,128)} %copy.174, s32[]{:T(128)} %get-tuple-element.468, s32[]{:T(128)} %constant.63.clone.1..sunk, s32[]{:T(128)} %constant.63.clone.1..sunk, s32[]{:T(128)} %constant.63.clone.1..sunk) | dynamic-update-slice | bytes 1572868 | tf_op jit(solution)/shard_map/while/body/jit(dynamic_update_index_in_dim)/dynamic_update_slice | solution.py:563
  727.5 5.8 dynamic_update_slice.31
  733.3 5.3 fusion.155
  746.3 4.7 convolution_convert_fusion.1
  758.9 6.3 fusion.46.x_ref
  765.2 55.1 %shard_map.238 = f32[256,1536]{1,0:T(8,128)} custom-call(f32[1024,1536]{1,0:T(8,128)} %fusion.46.x_ref), custom_call_target="tpu_custom_call" | custom-call | bytes 150000000 | tf_op jit(solution)/shard_map/pallas_call | solution.py:270
  820.4 6.8 add.141.x_ref
  827.3 55.5 %shard_map.235 = f32[256,1536]{1,0:T(8,128)} custom-call(f32[1024,1536]{1,0:T(8,128)} %add.141.x_ref), custom_call_target="tpu_custom_call" | custom-call | bytes 150000000 | tf_op jit(solution)/shard_map/pallas_call | solution.py:270
  883.4 41.0 %all-reduce.1 = (f32[1536]{0:T(1024)}, f32[1536]{0:T(1024)}) all-reduce(f32[1536]{0:T(1024)S(1)} %get-tuple-element.245, f32[1536]{0:T(1024)S(1)} %copy-done.42), channel_id=1, replica_groups=mesh['fsdp'=8,'tp'=4] {'fsdp','tp'}, use_global_device_ids=true, to_apply=%region_19.20 | all-reduce | flops 3072 | bytes 24576 | tf_op jit(solution)/shard_map/psum | solution.py:594
  924.4 4.7 fusion.60
  930.7 7.8 maximum_convert_fusion
  938.5 9.4 slice_bitcast_fusion
  (269 shorter events, 116.6 us)
Async XLA Ops:
  7.2 133.2 %all-gather.4.cloned.1.call-start = ((), (), s32[]{:S(2)}) async-start(), calls=%async_computation.3 | async-start | bytes 3981312 | tf_op jit(solution)/shard_map/all_gather | solution.py:455
  12.4 278.9 %all-gather.6.cloned.1.call-start = ((), (), s32[]{:S(2)}) async-start(), calls=%async_computation.4 | async-start | bytes 26542080 | tf_op jit(solution)/shard_map/all_gather | solution.py:469
  19.2 328.6 %all-gather.8.cloned.1.call-start = ((), (), s32[]{:S(2)}) async-start(), calls=%async_computation.5 | async-start | bytes 26542080 | tf_op jit(solution)/shard_map/all_gather | solution.py:469
  19.9 484.8 %reduce-scatter.6.cloned.1.call-start = ((), (), s32[]{:S(2)}) async-start(), calls=%async_computation.6 | async-start | bytes 26542080 | tf_op jit(solution)/shard_map/reduce_scatter | solution.py:542
  20.3 60.8 %copy-start.31 = (f32[1536]{0:T(1024)}, f32[1536]{0:T(1024)S(1)}, u32[]{:S(2)}) copy-start(f32[1536]{0:T(1024)S(1)} %convert_element_type.169) | copy-start | bytes 18436
  20.6 60.6 %copy-start.45 = (bf16[1536]{0:T(1024)(128)(2,1)S(1)}, bf16[1536]{0:T(1024)(128)(2,1)}, u32[]{:S(2)}) copy-start(bf16[1536]{0:T(1024)(128)(2,1)} %param.26) | copy-start | bytes 9220
  20.6 60.6 %copy-start.35 = (s32[1024,8]{0,1:T(8,128)S(1)}, s32[1024,8]{0,1:T(8,128)}, u32[]{:S(2)}) copy-start(s32[1024,8]{0,1:T(8,128)} %param.20) | copy-start | bytes 98308
  21.2 60.0 %copy-start.38 = (f32[256]{0:T(256)}, f32[256]{0:T(256)S(1)}, u32[]{:S(2)}) copy-start(f32[256]{0:T(256)S(1)} %get-tuple-element.314) | copy-start | bytes 3076
  22.3 62.7 %copy-start.9 = (bf16[256,1536]{1,0:T(8,128)(2,1)S(1)}, bf16[256,1536]{1,0:T(8,128)(2,1)}, u32[]{:S(2)}) copy-start(bf16[256,1536]{1,0:T(8,128)(2,1)} %param.31) | copy-start | bytes 2359300
  81.2 504.1 %copy-start.33 = (f32[1536]{0:T(1024)}, f32[1536]{0:T(1024)S(1)}, u32[]{:S(2)}) copy-start(f32[1536]{0:T(1024)S(1)} %convert_element_type.176) | copy-start | bytes 18436
  230.9 354.4 %copy-start.36 = (f32[256]{0:T(256)}, f32[256]{0:T(256)S(1)}, u32[]{:S(2)}) copy-start(f32[256]{0:T(256)S(1)} %add_rsqrt_fusion) | copy-start | bytes 3076
  347.7 407.1 %reduce-scatter.8.cloned.1.call-start = ((), (), s32[]{:S(2)}) async-start(), calls=%async_computation.7 | async-start | bytes 26542080 | tf_op jit(solution)/shard_map/reduce_scatter | solution.py:542
  504.7 424.4 %all-reduce.4.cloned.1.call-start = ((), (), s32[]{:S(2)}) async-start(), calls=%async_computation.8 | async-start | bytes 491520 | tf_op jit(solution)/shard_map/psum | solution.py:594
  505.8 76.5 %copy-start.26 = (pred[256,40]{1,0:T(32,128)(4,1)}, pred[256,40]{1,0:T(32,128)(4,1)S(1)}, u32[]{:S(2)}) copy-start(pred[256,40]{1,0:T(32,128)(4,1)S(1)} %copy.155) | copy-start | bytes 30724
  507.3 75.1 %copy-start.46 = (f32[256]{0:T(256)}, f32[256]{0:T(256)S(1)}, u32[]{:S(2)}) copy-start(f32[256]{0:T(256)S(1)} %get-tuple-element.317) | copy-start | bytes 3076
  507.5 74.9 %copy-start.48 = (f32[256]{0:T(256)}, f32[256]{0:T(256)S(1)}, u32[]{:S(2)}) copy-start(f32[256]{0:T(256)S(1)} %fusion.80) | copy-start | bytes 3076
  516.2 66.2 %copy-start.3 = (f32[256,1536]{1,0:T(8,128)S(1)}, f32[256,1536]{1,0:T(8,128)}, u32[]{:S(2)}) copy-start(f32[256,1536]{1,0:T(8,128)} %copy-done.2) | copy-start | bytes 4718596
  585.3 55.6 %copy-start.40 = (f32[256]{0:T(256)}, f32[256]{0:T(256)S(1)}, u32[]{:S(2)}) copy-start(f32[256]{0:T(256)S(1)} %broadcast_multiply_fusion.2) | copy-start | bytes 3076
  751.0 196.8 %reduce-scatter.10.cloned.1.call-start = ((), (), s32[]{:S(2)}) async-start(), calls=%async_computation.9 | async-start | bytes 3538944
  757.8 62.6 %slice-start.2 = ((s8[6291456]{0:T(1024)(128)(4,1)}), s8[2097152]{0:T(1024)(128)(4,1)S(1)}, s32[]{:S(2)}) async-start(s8[6291456]{0:T(1024)(128)(4,1)} %bitcast.233), calls=%async_computation.12 | async-start | bytes 4194304
  758.9 61.4 %slice-start.3 = ((s8[6291456]{0:T(1024)(128)(4,1)}), s8[4194304]{0:T(1024)(128)(4,1)S(1)}, s32[]{:S(2)}) async-start(s8[6291456]{0:T(1024)(128)(4,1)} %bitcast.233), calls=%async_computation.13 | async-start | bytes 8388608
  827.2 55.6 %copy-start.6 = (bf16[256,1536]{1,0:T(8,128)(2,1)S(1)}, bf16[256,1536]{1,0:T(8,128)(2,1)}, u32[]{:S(2)}) copy-start(bf16[256,1536]{1,0:T(8,128)(2,1)} %param.18) | copy-start | bytes 2359300
  827.2 55.6 %copy-start.7 = (f32[256,1536]{1,0:T(8,128)S(1)}, f32[256,1536]{1,0:T(8,128)}, u32[]{:S(2)}) copy-start(f32[256,1536]{1,0:T(8,128)} %shard_map.238) | copy-start | bytes 4718596
  827.2 55.6 %copy-start.32 = (f32[1536]{0:T(1024)S(1)}, f32[1536]{0:T(1024)}, u32[]{:S(2)}) copy-start(f32[1536]{0:T(1024)} %copy-done.31) | copy-start | bytes 18436
  827.2 55.6 %copy-start.39 = (f32[256]{0:T(256)S(1)}, f32[256]{0:T(256)}, u32[]{:S(2)}) copy-start(f32[256]{0:T(256)} %copy-done.38) | copy-start | bytes 3076
  827.2 56.2 %copy-start.42 = (f32[1536]{0:T(1024)S(1)}, f32[1536]{0:T(1024)}, u32[]{:S(2)}) copy-start(f32[1536]{0:T(1024)} %get-tuple-element.243) | copy-start | bytes 18436
  827.2 97.2 %copy-start.11 = (bf16[256,1536]{1,0:T(8,128)(2,1)S(1)}, bf16[256,1536]{1,0:T(8,128)(2,1)}, u32[]{:S(2)}) copy-start(bf16[256,1536]{1,0:T(8,128)(2,1)} %param.31) | copy-start | bytes 2359300
  827.2 97.1 %copy-start.34 = (f32[1536]{0:T(1024)S(1)}, f32[1536]{0:T(1024)}, u32[]{:S(2)}) copy-start(f32[1536]{0:T(1024)} %copy-done.33) | copy-start | bytes 18436
  827.3 97.1 %copy-start.37 = (f32[256]{0:T(256)S(1)}, f32[256]{0:T(256)}, u32[]{:S(2)}) copy-start(f32[256]{0:T(256)} %copy-done.36) | copy-start | bytes 3076
  827.3 97.1 %copy-start.41 = (f32[256]{0:T(256)S(1)}, f32[256]{0:T(256)}, u32[]{:S(2)}) copy-start(f32[256]{0:T(256)} %copy-done.40) | copy-start | bytes 3076
  827.3 97.1 %copy-start.43 = (f32[256]{0:T(256)S(1)}, f32[256]{0:T(256)}, u32[]{:S(2)}) copy-start(f32[256]{0:T(256)} %get-tuple-element.313) | copy-start | bytes 3076
  882.9 41.6 %copy-start.4 = (f32[256,1536]{1,0:T(8,128)S(1)}, f32[256,1536]{1,0:T(8,128)}, u32[]{:S(2)}) copy-start(f32[256,1536]{1,0:T(8,128)} %copy-done.2) | copy-start | bytes 4718596
  (37 other events, 146.2 us)
Sparse Core Ops, SparseCore 0:
  12.5 36.5 all-gather.3
  51.6 118.5 all-gather.5
  172.7 118.5 all-gather.7
  347.8 156.8 reduce-scatter.5
  508.2 148.3 reduce-scatter.7
  751.1 124.3 all-reduce.3
  878.9 46.9 reduce-scatter.9

commit v2 on v1

--- a/solution.py
+++ b/solution.py
@@ -42,83 +42,6 @@
     weighted = incoming * gain_vec
     row_inner = jnp.mean(weighted * scaled, axis=-1, keepdims=True)
     return (inverse * (weighted - scaled * row_inner), gain_grad)
-
-
-def rotary_tables(row_count, head_width):
-    half_width = head_width // 2
-    positions = (jnp.arange(row_count) % SEQ).astype(jnp.float32)
-    frequency = rope_base ** (-jnp.arange(half_width).astype(jnp.float32) * 2.0 / head_width)
-    angles = positions[:, None] * frequency[None, :]
-    return (jnp.cos(angles)[:, None, :], jnp.sin(angles)[:, None, :])
-
-
-def rotate(values, cosine_table, sine_table):
-    half_width = values.shape[-1] // 2
-    lead_half = values[..., :half_width]
-    tail_half = values[..., half_width:]
-    return jnp.concatenate(
-        [
-            lead_half * cosine_table - tail_half * sine_table,
-            tail_half * cosine_table + lead_half * sine_table,
-        ],
-        axis=-1,
-    )
-
-
-def attention_scores(queries, key_rows, segments):
-    length, heads_here, head_width = queries.shape
-    kv_here = key_rows.shape[1]
-    grouped = queries.reshape(length, kv_here, heads_here // kv_here, head_width)
-    scores = (
-        jnp.einsum("qkgd,tkd->kgqt", grouped, key_rows, preferred_element_type=jnp.float32)
-        * attn_scale
-    )
-    places = jnp.arange(length)
-    allowed = (places[:, None] >= places[None, :]) & (segments[:, None] == segments[None, :])
-    return (jnp.where(allowed, scores, masked_value), grouped)
-
-
-def attend_forward(pieces):
-    queries, key_rows, value_rows, segments = pieces
-    scores, grouped = attention_scores(queries, key_rows, segments)
-    row_top = jnp.max(scores, axis=-1, keepdims=True)
-    raised = jnp.exp(scores - row_top)
-    row_total = jnp.sum(raised, axis=-1, keepdims=True)
-    probs_low = (raised / row_total).astype(jnp.bfloat16)
-    mixed_out = jnp.einsum(
-        "kgqt,tkd->qkgd", probs_low, value_rows, preferred_element_type=jnp.float32
-    )
-    return (
-        mixed_out.astype(jnp.bfloat16).reshape(queries.shape[0], -1),
-        (row_top + jnp.log(row_total))[..., 0],
-    )
-
-
-def attend_backward(pieces):
-    queries, key_rows, value_rows, segments, logsum, mixed_grad = pieces
-    scores, grouped = attention_scores(queries, key_rows, segments)
-    attn_probs = jnp.exp(scores - logsum[..., None])
-    grad_grouped = mixed_grad.reshape(grouped.shape)
-    probs_grad = jnp.einsum(
-        "qkgd,tkd->kgqt", grad_grouped, value_rows, preferred_element_type=jnp.float32
-    )
-    row_inner = jnp.sum(attn_probs * probs_grad, axis=-1, keepdims=True)
-    score_grad = (attn_probs * (probs_grad - row_inner)).astype(jnp.bfloat16)
-    query_grad = (
-        jnp.einsum("kgqt,tkd->qkgd", score_grad, key_rows, preferred_element_type=jnp.float32)
-        * attn_scale
-    )
-    key_grad = (
-        jnp.einsum("kgqt,qkgd->tkd", score_grad, grouped, preferred_element_type=jnp.float32)
-        * attn_scale
-    )
-    value_grad = jnp.einsum(
-        "kgqt,qkgd->tkd",
-        attn_probs.astype(jnp.bfloat16),
-        grad_grouped,
-        preferred_element_type=jnp.float32,
-    )
-    return (query_grad.reshape(queries.shape), key_grad, value_grad)
 
 
 def line_barrier(me, count):
@@ -429,6 +352,376 @@
     )(meta, place_rows, place_cols, gate_rows, x_rows, g_rows, weights)
 
 
+def rotate_head(values, cosine, sine, sign):
+    half = values.shape[-1] // 2
+    other = jnp.concatenate([values[:, half:], values[:, :half]], axis=1)
+    return values * cosine + other * (sine * sign)
+
+
+def segment_bias(seg_row, seg_col):
+    shape = (seg_col.shape[0], seg_row.shape[1])
+    keys = lax.broadcasted_iota(jnp.int32, shape, 0)
+    queries = lax.broadcasted_iota(jnp.int32, shape, 1)
+    return jnp.where((keys <= queries) & (seg_col == seg_row), 0.0, masked_value)
+
+
+def attend_kernel(
+    x_ref,
+    w_ref,
+    seg_row,
+    seg_col,
+    cos_ref,
+    sin_ref,
+    q_ref,
+    k_ref,
+    v_ref,
+    mixed_ref,
+    logsum_ref,
+    branch_ref,
+    bias,
+    v_turned,
+    mixed_heads,
+):
+    heads, kv_heads = q_ref.shape[0], k_ref.shape[0]
+    per_kv = heads // kv_heads
+    block = SEQ // 2
+    edge = (heads + 2 * kv_heads) * HEAD_DIM
+    proj = jnp.dot(x_ref[...], w_ref[:, :edge], preferred_element_type=jnp.float32)
+    cosine, sine = cos_ref[...], sin_ref[...]
+    for head in range(heads + 2 * kv_heads):
+        part = proj[:, head * HEAD_DIM : (head + 1) * HEAD_DIM]
+        if head < heads:
+            q_ref[head] = rotate_head(part, cosine, sine, 1.0).astype(jnp.bfloat16)
+        elif head < heads + kv_heads:
+            k_ref[head - heads] = rotate_head(part, cosine, sine, 1.0).astype(jnp.bfloat16)
+        else:
+            v_ref[head - heads - kv_heads] = part.astype(jnp.bfloat16)
+            v_turned[head - heads - kv_heads] = part.T.astype(jnp.bfloat16)
+    bias[...] = segment_bias(seg_row[0], seg_col[0])
+
+    def one_head(head, carry):
+        kv = head // per_kv
+        for part in range(2):
+            span, low = block * (part + 1), block * part
+            scores = contract_last(k_ref[kv, :span], q_ref[head, low : low + block]) * attn_scale
+            scores = scores + bias[:span, low : low + block]
+            top = jnp.max(scores, axis=0, keepdims=True)
+            raised = jnp.exp(scores - top)
+            total = jnp.sum(raised, axis=0, keepdims=True)
+            probs = (raised * (1.0 / total)).astype(jnp.bfloat16)
+            turned = jnp.dot(v_turned[kv, :, :span], probs, preferred_element_type=jnp.float32)
+            mixed_heads[head, low : low + block, :] = turned.T.astype(jnp.bfloat16)
+            logsum_ref[0, pl.ds(head, 1), low : low + block] = top + jnp.log(total)
+        return carry
+
+    lax.fori_loop(0, heads, one_head, 0)
+    for head in range(heads):
+        mixed_ref[:, head * HEAD_DIM : (head + 1) * HEAD_DIM] = mixed_heads[head]
+    branch_ref[...] = contract_last(
+        mixed_ref[...], w_ref[:, edge : edge + heads * HEAD_DIM]
+    ).astype(jnp.bfloat16)
+
+
+def attend_back_kernel(
+    x_ref,
+    w_ref,
+    seg_row,
+    seg_col,
+    cos_ref,
+    sin_ref,
+    q_ref,
+    k_ref,
+    v_ref,
+    mixed_ref,
+    logsum_ref,
+    branch_grad,
+    dx_ref,
+    dw_ref,
+    bias,
+    k_turned,
+    mixed_grads,
+    q_grads,
+    kv_grads,
+    qkv_grad,
+    dw_acc,
+):
+    heads, kv_heads = q_ref.shape[0], k_ref.shape[0]
+    per_kv = heads // kv_heads
+    block = SEQ // 2
+    edge = (heads + 2 * kv_heads) * HEAD_DIM
+    step = pl.program_id(0)
+    out_edge = edge + heads * HEAD_DIM
+    grad = jnp.dot(
+        branch_grad[...], w_ref[:, edge:out_edge], preferred_element_type=jnp.float32
+    ).astype(jnp.bfloat16)
+    for head in range(heads):
+        mixed_grads[head] = grad[:, head * HEAD_DIM : (head + 1) * HEAD_DIM]
+    for kv in range(kv_heads):
+        k_turned[kv] = k_ref[kv].astype(jnp.float32).T.astype(jnp.bfloat16)
+    bias[...] = segment_bias(seg_row[0], seg_col[0])
+    kv_grads[...] = jnp.zeros_like(kv_grads)
+
+    def one_head(head, carry):
+        kv = head // per_kv
+        for part in range(2):
+            span, low = block * (part + 1), block * part
+            high = low + block
+            scores = contract_last(k_ref[kv, :span], q_ref[head, low:high]) * attn_scale
+            scores = scores + bias[:span, low:high]
+            probs = jnp.exp(scores - logsum_ref[0, pl.ds(head, 1), low:high])
+            probs_grad = contract_last(v_ref[kv, :span], mixed_grads[head, low:high])
+            inner = jnp.sum(probs * probs_grad, axis=0, keepdims=True)
+            score_grad = (probs * (probs_grad - inner)).astype(jnp.bfloat16)
+            turned = jnp.dot(k_turned[kv, :, :span], score_grad, preferred_element_type=jnp.float32)
+            q_grads[head, low:high, :] = turned.T * attn_scale
+            kv_grads[0, kv, :span, :] += jnp.dot(
+                score_grad, q_ref[head, low:high], preferred_element_type=jnp.float32
+            )
+            kv_grads[1, kv, :span, :] += jnp.dot(
+                probs.astype(jnp.bfloat16), mixed_grads[head, low:high],
+                preferred_element_type=jnp.float32,
+            )
+        return carry
+
+    lax.fori_loop(0, heads, one_head, 0)
+    cosine, sine = cos_ref[...], sin_ref[...]
+    for head in range(heads + 2 * kv_heads):
+        if head < heads:
+            part = rotate_head(q_grads[head], cosine, sine, -1.0)
+        elif head < heads + kv_heads:
+            part = rotate_head(kv_grads[0, head - heads] * attn_scale, cosine, sine, -1.0)
+        else:
+            part = kv_grads[1, head - heads - kv_heads]
+        qkv_grad[:, head * HEAD_DIM : (head + 1) * HEAD_DIM] = part.astype(jnp.bfloat16)
+    dx_ref[...] = contract_last(qkv_grad[...], w_ref[:, :edge]).astype(jnp.bfloat16)
+    qkv_part = contract_first(x_ref[...], qkv_grad[...])
+    out_part = contract_first(branch_grad[...], mixed_ref[...])
+
+    @pl.when(step == 0)
+    def _():
+        dw_acc[:, :edge] = qkv_part
+        dw_acc[:, edge:out_edge] = out_part
+
+    @pl.when(step > 0)
+    def _():
+        dw_acc[:, :edge] += qkv_part
+        dw_acc[:, edge:out_edge] += out_part
+
+    @pl.when(step == pl.num_programs(0) - 1)
+    def _():
+        dw_ref[...] = dw_acc[...].astype(jnp.bfloat16)
+
+
+def fixed(shape):
+    return pl.BlockSpec(shape, lambda seq: (0,) * len(shape), pipeline_mode=pl.Buffered(1))
+
+
+def by_row(width):
+    return pl.BlockSpec((SEQ, width), lambda seq: (seq, 0))
+
+
+def by_head(heads):
+    return pl.BlockSpec((heads, SEQ, HEAD_DIM), lambda seq: (0, seq, 0))
+
+
+def attend_tables():
+    half = HEAD_DIM // 2
+    positions = jnp.arange(SEQ).astype(jnp.float32)
+    frequency = rope_base ** (-jnp.arange(half).astype(jnp.float32) * 2.0 / HEAD_DIM)
+    angles = positions[:, None] * frequency[None, :]
+    cosine, sine = jnp.cos(angles), jnp.sin(angles)
+    return (
+        jnp.concatenate([cosine, cosine], axis=1),
+        jnp.concatenate([-sine, sine], axis=1),
+    )
+
+
+def attend(rows, weights, segments, tables, heads, kv_heads):
+    group, width = rows.shape
+    seqs = group // SEQ
+    return pl.pallas_call(
+        attend_kernel,
+        grid=(seqs,),
+        in_specs=[
+            by_row(width),
+            fixed(weights.shape),
+            pl.BlockSpec((1, 1, SEQ), lambda seq: (seq, 0, 0)),
+            pl.BlockSpec((1, SEQ, 1), lambda seq: (seq, 0, 0)),
+            fixed(tables[0].shape),
+            fixed(tables[1].shape),
+        ],
+        out_specs=[
+            by_head(heads),
+            by_head(kv_heads),
+            by_head(kv_heads),
+            by_row(heads * HEAD_DIM),
+            pl.BlockSpec((1, heads, SEQ), lambda seq: (seq, 0, 0)),
+            by_row(width),
+        ],
+        out_shape=[
+            jax.ShapeDtypeStruct((heads, group, HEAD_DIM), jnp.bfloat16),
+            jax.ShapeDtypeStruct((kv_heads, group, HEAD_DIM), jnp.bfloat16),
+            jax.ShapeDtypeStruct((kv_heads, group, HEAD_DIM), jnp.bfloat16),
+            jax.ShapeDtypeStruct((group, heads * HEAD_DIM), jnp.bfloat16),
+            jax.ShapeDtypeStruct((seqs, heads, SEQ), jnp.float32),
+            jax.ShapeDtypeStruct((group, width), jnp.bfloat16),
+        ],
+        scratch_shapes=[
+            pltpu.VMEM((SEQ, SEQ), jnp.float32),
+            pltpu.VMEM((kv_heads, HEAD_DIM, SEQ), jnp.bfloat16),
+            pltpu.VMEM((heads, SEQ, HEAD_DIM), jnp.bfloat16),
+        ],
+        compiler_params=pltpu.CompilerParams(
+            dimension_semantics=("arbitrary",), vmem_limit_bytes=56 << 20
+        ),
+        cost_estimate=pl.CostEstimate(
+            flops=10_000_000_000, transcendentals=3_000_000, bytes_accessed=60_000_000
+        ),
+    )(rows, weights, segments[:, None, :], segments[:, :, None], *tables)
+
+
+def attend_back(rows, weights, segments, tables, kept, branch_grad):
+    queries, keys, values, mixed, logsum = kept
+    group, width = rows.shape
+    heads, kv_heads = queries.shape[0], keys.shape[0]
+    used = 2 * (heads + kv_heads) * HEAD_DIM
+    return pl.pallas_call(
+        attend_back_kernel,
+        grid=(group // SEQ,),
+        in_specs=[
+            by_row(width),
+            fixed(weights.shape),
+            pl.BlockSpec((1, 1, SEQ), lambda seq: (seq, 0, 0)),
+            pl.BlockSpec((1, SEQ, 1), lambda seq: (seq, 0, 0)),
+            fixed(tables[0].shape),
+            fixed(tables[1].shape),
+            by_head(heads),
+            by_head(kv_heads),
+            by_head(kv_heads),
+            by_row(heads * HEAD_DIM),
+            pl.BlockSpec((1, heads, SEQ), lambda seq: (seq, 0, 0)),
+            by_row(width),
+        ],
+        out_specs=[by_row(width), fixed((width, used))],
+        out_shape=[
+            jax.ShapeDtypeStruct((group, width), jnp.bfloat16),
+            jax.ShapeDtypeStruct((width, used), jnp.bfloat16),
+        ],
+        scratch_shapes=[
+            pltpu.VMEM((SEQ, SEQ), jnp.float32),
+            pltpu.VMEM((kv_heads, HEAD_DIM, SEQ), jnp.bfloat16),
+            pltpu.VMEM((heads, SEQ, HEAD_DIM), jnp.bfloat16),
+            pltpu.VMEM((heads, SEQ, HEAD_DIM), jnp.float32),
+            pltpu.VMEM((2, kv_heads, SEQ, HEAD_DIM), jnp.float32),
+            pltpu.VMEM((SEQ, used - heads * HEAD_DIM), jnp.bfloat16),
+            pltpu.VMEM((width, used), jnp.float32),
+        ],
+        compiler_params=pltpu.CompilerParams(
+            dimension_semantics=("arbitrary",), vmem_limit_bytes=60 << 20
+        ),
+        cost_estimate=pl.CostEstimate(
+            flops=20_000_000_000, transcendentals=3_000_000, bytes_accessed=100_000_000
+        ),
+    )(rows, weights, segments[:, None, :], segments[:, :, None], *tables,
+      queries, keys, values, mixed, logsum, branch_grad)
+
+
+def total_kernel(tp_count, fsdp_count, x_ref, o_ref, tp_got, fsdp_got, send_sem, recv_sem):
+    tp_me, fsdp_me = lax.axis_index("tp"), lax.axis_index("fsdp")
+    barrier = pltpu.get_barrier_semaphore()
+    for shift in range(1, tp_count):
+        pl.semaphore_signal(barrier, inc=1, device_id={"tp": lax.rem(tp_me + shift, tp_count)})
+    for shift in range(1, fsdp_count):
+        pl.semaphore_signal(
+            barrier, inc=1, device_id={"fsdp": lax.rem(fsdp_me + shift, fsdp_count)}
+        )
+    pl.semaphore_wait(barrier, tp_count + fsdp_count - 2)
+
+    def exchange(axis, me, count, source, got, base):
+        copies = []
+        for shift in range(1, count):
+            copies.append(
+                pltpu.make_async_remote_copy(
+                    src_ref=source,
+                    dst_ref=got.at[me],
+                    send_sem=send_sem.at[base + shift],
+                    recv_sem=recv_sem.at[base + shift],
+                    device_id={axis: lax.rem(me + shift, count)},
+                )
+            )
+            copies[-1].start()
+        got[me] = source[...]
+        for copy in copies:
+            copy.wait()
+        total = got[0]
+        for index in range(1, count):
+            total = total + got[index]
+        return total
+
+    o_ref[...] = exchange("tp", tp_me, tp_count, x_ref, tp_got, 0)
+    o_ref[...] = exchange("fsdp", fsdp_me, fsdp_count, o_ref, fsdp_got, tp_count)
+
+
+def total_everywhere(values, ident):
+    tp_count, fsdp_count = lax.axis_size("tp"), lax.axis_size("fsdp")
+    return pl.pallas_call(
+        functools.partial(total_kernel, tp_count, fsdp_count),
+        out_shape=jax.ShapeDtypeStruct(values.shape, values.dtype),
+        in_specs=[pl.BlockSpec(memory_space=pltpu.VMEM)],
+        out_specs=pl.BlockSpec(memory_space=pltpu.VMEM),
+        scratch_shapes=[
+            pltpu.VMEM((tp_count,) + values.shape, values.dtype),
+            pltpu.VMEM((fsdp_count,) + values.shape, values.dtype),
+            pltpu.SemaphoreType.DMA((tp_count + fsdp_count,)),
+            pltpu.SemaphoreType.DMA((tp_count + fsdp_count,)),
+        ],
+        compiler_params=pltpu.CompilerParams(collective_id=ident, has_side_effects=True),
+    )(values)
+
+
+def widen_kernel(packed, *refs):
+    for slot, target in enumerate(refs[-3:]):
+        target[0] = packed[0, slot].astype(jnp.float32)
+
+
+def widen(packed, count, first, held):
+    span, _, rows, width = packed.shape
+    shape = jax.ShapeDtypeStruct((count, rows, width), jnp.float32)
+    return pl.pallas_call(
+        widen_kernel,
+        grid=(span,),
+        in_specs=[pl.BlockSpec((1, 3, rows, width), lambda step: (step, 0, 0, 0))]
+        + [pl.BlockSpec(memory_space=pl.ANY)] * len(held),
+        out_specs=[pl.BlockSpec((1, rows, width), lambda step: (step + first, 0, 0))] * 3,
+        out_shape=[shape] * 3,
+        input_output_aliases={1 + index: index for index in range(len(held))},
+    )(packed, *held)
+
+
+def shifted_gather(block, count, me):
+    rows = block.shape[0]
+    whole = jnp.zeros((rows * count, block.shape[1]), block.dtype)
+    whole = lax.dynamic_update_slice_in_dim(whole, block, me * rows, 0)
+    for shift in range(1, count):
+        got = lax.ppermute(block, "tp", [(i, (i + shift) % count) for i in range(count)])
+        whole = lax.dynamic_update_slice_in_dim(
+            whole, got, lax.rem(me + count - shift, count) * rows, 0
+        )
+    return whole
+
+
+def shifted_scatter(partial_rows, count, me):
+    rows = partial_rows.shape[0] // count
+    total = lax.dynamic_slice_in_dim(partial_rows, me * rows, rows, 0).astype(jnp.float32)
+    for shift in range(1, count):
+        block = lax.dynamic_slice_in_dim(
+            partial_rows, lax.rem(me + shift, count) * rows, rows, 0
+        ).astype(jnp.bfloat16)
+        got = lax.ppermute(block, "tp", [(i, (i + shift) % count) for i in range(count)])
+        total = total + got.astype(jnp.float32)
+    return total
+
+
 CHUNKS = 2
 
 
@@ -448,25 +741,29 @@
     w_down,
     cotangent,
 ):
-    local_rows = emb.shape[0]
+    local_rows, width = emb.shape
     tp_count = lax.axis_size("tp")
     tp_index = lax.axis_index("tp")
     experts_here = w_gate.shape[0]
+    expert_count = w_router.shape[1]
+    q_width, kv_width = w_query.shape[1], w_key.shape[1]
+    used = 2 * (q_width + kv_width)
+    lane_pad = 128 - expert_count
     attn_w = lax.all_gather(
-        jnp.concatenate([w_query, w_key, w_value, w_out, jnp.pad(w_router, ((0, 0), (0, 128 - w_router.shape[1])))], axis=1),
-        "fsdp", axis=0, tiled=True)
-    q_width, kv_width = w_query.shape[1], w_key.shape[1]
-    query_w = attn_w[:, :q_width]
-    key_w = attn_w[:, q_width : q_width + kv_width]
-    value_w = attn_w[:, q_width + kv_width : q_width + 2 * kv_width]
-    out_w = attn_w[:, q_width + 2 * kv_width : 2 * q_width + 2 * kv_width]
-    expert_count = w_router.shape[1]
-    router_w = attn_w[:, 2 * q_width + 2 * kv_width :]
+        jnp.concatenate(
+            [w_query, w_key, w_value, w_out, jnp.pad(w_router, ((0, 0), (0, lane_pad)))], axis=1
+        ),
+        "fsdp",
+        axis=0,
+        tiled=True,
+    )
+    router_w = attn_w[:, used : used + expert_count]
     stacked = jnp.stack([w_gate, w_up, w_down], axis=1)
     edges = [experts_here * part // CHUNKS for part in range(CHUNKS + 1)]
-    pieces = []
-    for low, high in zip(edges[:-1], edges[1:]):
-        pieces.append(lax.all_gather(stacked[low:high], "fsdp", axis=2, tiled=True))
+    pieces = [
+        lax.all_gather(stacked[low:high], "fsdp", axis=2, tiled=True)
+        for low, high in zip(edges[:-1], edges[1:])
+    ]
 
     gain_one = norm1_gain.astype(jnp.float32)
     gain_two = norm2_gain.astype(jnp.float32)
@@ -474,11 +771,8 @@
     normed_one, inverse_one = rms_forward(start_x, gain_one)
     group_rows = line_gather(normed_one.astype(jnp.bfloat16), tp_count, 0)
     out_grad = cotangent.astype(jnp.float32)
-    moe_grad_rows = line_gather((resid_scale * out_grad).astype(jnp.bfloat16), tp_count, 1)
+    moe_grad_rows = shifted_gather((resid_scale * out_grad).astype(jnp.bfloat16), tp_count, tp_index)
     group_size = group_rows.shape[0]
-    seq_count = group_size // SEQ
-    heads_here = query_w.shape[1] // HEAD_DIM
-    kv_here = key_w.shape[1] // HEAD_DIM
 
     capacity = group_size * routes.shape[1] // expert_count * 2
     all_experts = jnp.arange(expert_count, dtype=jnp.int32)
@@ -493,31 +787,17 @@
         [jnp.sum(member.astype(jnp.int32), axis=0), (tp_index * experts_here)[None]]
     )
 
-    cosine_table, sine_table = rotary_tables(group_size, HEAD_DIM)
-    query_proj = jnp.dot(group_rows, query_w, preferred_element_type=jnp.float32).reshape(
-        group_size, heads_here, HEAD_DIM
-    )
-    key_proj = jnp.dot(group_rows, key_w, preferred_element_type=jnp.float32).reshape(
-        group_size, kv_here, HEAD_DIM
-    )
-    queries = rotate(query_proj, cosine_table, sine_table).astype(jnp.bfloat16)
-    key_rows = rotate(key_proj, cosine_table, sine_table).astype(jnp.bfloat16)
-    value_rows = jnp.dot(group_rows, value_w, preferred_element_type=jnp.float32).astype(
-        jnp.bfloat16
-    )
-    seq_queries = queries.reshape(seq_count, SEQ, heads_here, HEAD_DIM)
-    seq_keys = key_rows.reshape(seq_count, SEQ, kv_here, HEAD_DIM)
-    seq_values = value_rows.reshape(seq_count, SEQ, kv_here, HEAD_DIM)
-    mixed_out, logsum = lax.map(attend_forward, (seq_queries, seq_keys, seq_values, segment_ids))
-    mixed_rows = mixed_out.reshape(group_size, heads_here * HEAD_DIM)
-    attn_branch = line_scatter(contract_last(mixed_rows, out_w), tp_count, 2)
+    tables = attend_tables()
+    heads_here, kv_here = q_width // HEAD_DIM, kv_width // HEAD_DIM
+    *kept, branch_part = attend(group_rows, attn_w, segment_ids, tables, heads_here, kv_here)
+    attn_branch = line_scatter(branch_part, tp_count, 2)
     mid_x = start_x + resid_scale * attn_branch
     normed_two, inverse_two = rms_forward(mid_x, gain_two)
     normed_low = normed_two.astype(jnp.bfloat16)
     moe_rows = line_gather(normed_low, tp_count, 3)
 
     def gates_of(rows, inside):
-        logits = jnp.dot(rows, router_w, preferred_element_type=jnp.float32)[:, :expert_count]
+        logits = jnp.dot(rows, router_w, preferred_element_type=jnp.float32)
         top = jnp.max(jnp.where(inside, logits, masked_value), axis=-1, keepdims=True)
         raised = jnp.where(inside, jnp.exp(jnp.where(inside, logits - top, 0.0)), 0.0)
         return raised / jnp.sum(raised, axis=-1, keepdims=True)
@@ -525,93 +805,76 @@
     gates = gates_of(normed_low, own_member)
     gates_here = lax.dynamic_slice_in_dim(
         gates_of(moe_rows, member_all).astype(jnp.bfloat16).astype(jnp.float32),
-        tp_index * experts_here, experts_here, 1)
+        tp_index * experts_here,
+        experts_here,
+        1,
+    )
     place_rows = places.T[:, None, :]
     gate_rows = gates_here.T[:, None, :]
 
     outs = []
     for first, piece in zip(edges[:-1], pieces):
-        outs.append(experts_step(
-            meta, place_rows, places, gate_rows, moe_rows, moe_grad_rows, piece, first, capacity))
-    grad_sums = []
-    behind = None
-    for part in outs:
-        grads = part[2]
-        if behind is not None:
-            grads, _ = lax.optimization_barrier((grads, behind))
-        behind = lax.psum_scatter(grads, "fsdp", scatter_dimension=2, tiled=True)
-        grad_sums.append(behind)
+        outs.append(
+            experts_step(
+                meta,
+                place_rows,
+                places,
+                gate_rows,
+                moe_rows,
+                moe_grad_rows,
+                piece,
+                first,
+                capacity,
+            )
+        )
+    grad_sums = [
+        lax.psum_scatter(part[2], "fsdp", scatter_dimension=2, tiled=True) for part in outs
+    ]
     y_part = functools.reduce(lambda one, two: one + two, [part[0] for part in outs])
     dx_part = functools.reduce(lambda one, two: one + two, [part[1] for part in outs])
     dx_sum = line_scatter(dx_part, tp_count, 4)
-    rows_grad_sum = dx_sum[:, : emb.shape[1]]
-    gates_grad = dx_sum[:, emb.shape[1] : emb.shape[1] + expert_count]
+    moe_sum = shifted_scatter(y_part, tp_count, tp_index)
+    out = (mid_x + resid_scale * moe_sum).astype(jnp.bfloat16)
+    gates_grad = dx_sum[:, width : width + expert_count]
     gates_inner = jnp.sum(gates * gates_grad, axis=-1, keepdims=True)
     logits_grad = (gates * (gates_grad - gates_inner)).astype(jnp.bfloat16)
-    router_grad_part = contract_first(normed_low, logits_grad)
-    normed_two_grad = rows_grad_sum + contract_last(logits_grad, router_w[:, :expert_count])
+    normed_two_grad = dx_sum[:, :width] + contract_last(logits_grad, router_w)
     mid_from_norm, gain_two_grad = rms_backward(normed_two_grad, mid_x, inverse_two, gain_two)
     mid_grad = out_grad + mid_from_norm
     branch_grad = (resid_scale * mid_grad).astype(jnp.bfloat16)
-    branch_grad_rows = line_gather(branch_grad, tp_count, 5)
-    moe_sum = line_scatter(y_part, tp_count, 6)
-    out = (mid_x + resid_scale * moe_sum).astype(jnp.bfloat16)
-    out_w_grad = contract_first(branch_grad_rows, mixed_rows)
-    mixed_grad = jnp.dot(branch_grad_rows, out_w, preferred_element_type=jnp.float32).astype(
-        jnp.bfloat16
-    )
-    query_grad, key_grad, value_grad = lax.map(
-        attend_backward,
-        (
-            seq_queries,
-            seq_keys,
-            seq_values,
-            segment_ids,
-            logsum,
-            mixed_grad.reshape(seq_count, SEQ, -1),
-        ),
-    )
-    query_proj_grad = (
-        rotate(query_grad.reshape(group_size, heads_here, HEAD_DIM), cosine_table, -sine_table)
-        .astype(jnp.bfloat16)
-        .reshape(group_size, -1)
-    )
-    key_proj_grad = (
-        rotate(key_grad.reshape(group_size, kv_here, HEAD_DIM), cosine_table, -sine_table)
-        .astype(jnp.bfloat16)
-        .reshape(group_size, -1)
-    )
-    value_proj_grad = value_grad.reshape(group_size, -1).astype(jnp.bfloat16)
-    qkv_grad = jnp.concatenate([query_proj_grad, key_proj_grad, value_proj_grad], axis=1)
-    qkv_w_grad = contract_first(group_rows, qkv_grad)
-    qkv_w = attn_w[:, : q_width + 2 * kv_width]
-    normed_one_grad = line_scatter(contract_last(qkv_grad, qkv_w), tp_count, 7)
+    sent = line_gather(
+        jnp.concatenate([branch_grad, jnp.pad(logits_grad, ((0, 0), (0, lane_pad)))], axis=1),
+        tp_count,
+        5,
+    )
+    router_grad = contract_first(moe_rows, sent[:, width:])
+    dx_one, attn_dw = attend_back(
+        group_rows, attn_w, segment_ids, tables, kept, sent
+    )
+    attn_grads = jnp.concatenate([attn_dw, router_grad.astype(jnp.bfloat16)], axis=1)
+    normed_one_grad = line_scatter(dx_one, tp_count, 7)
     start_from_norm, gain_one_grad = rms_backward(normed_one_grad, start_x, inverse_one, gain_one)
     grad_emb = emb_scale * (mid_grad + start_from_norm)
-    attn_grads = jnp.concatenate([qkv_w_grad, out_w_grad], axis=1).astype(jnp.bfloat16)
-    attn_grads, grad_sums[-1] = lax.optimization_barrier((attn_grads, grad_sums[-1]))
-    attn_sum = lax.psum_scatter(attn_grads, "fsdp", scatter_dimension=0, tiled=True).astype(jnp.float32)
-    gain_one_sum, gain_two_sum, router_sum = lax.psum(
-        (gain_one_grad, gain_two_grad, router_grad_part), ("fsdp", "tp")
-    )
-    router_rows = w_router.shape[0]
-    router_own = lax.dynamic_slice_in_dim(
-        router_sum, lax.axis_index("fsdp") * router_rows, router_rows, 0
-    )
-    expert_sum = jnp.concatenate(grad_sums, axis=0).astype(jnp.float32)
+    gain_sums = total_everywhere(
+        jnp.concatenate([gain_one_grad, gain_two_grad]).reshape(8, -1), 8
+    ).reshape(2, width)
+    attn_sum = lax.psum_scatter(attn_grads, "fsdp", scatter_dimension=0, tiled=True).astype(
+        jnp.float32
+    )
+    expert_sums = ()
+    for first, part in zip(edges[:-1], grad_sums):
+        expert_sums = widen(part, experts_here, first, expert_sums)
     return (
         out,
         grad_emb,
-        gain_one_sum,
+        gain_sums[0],
         attn_sum[:, :q_width],
         attn_sum[:, q_width : q_width + kv_width],
         attn_sum[:, q_width + kv_width : q_width + 2 * kv_width],
-        attn_sum[:, q_width + 2 * kv_width :],
-        gain_two_sum,
-        router_own,
-        expert_sum[:, 0],
-        expert_sum[:, 1],
-        expert_sum[:, 2],
+        attn_sum[:, q_width + 2 * kv_width : used],
+        gain_sums[1],
+        attn_sum[:, used : used + expert_count],
+        *expert_sums,
     )
 
 

time: 969 us -> 977 us (level)
  waiting for transfers between devices: 107 us -> 199 us
  Pallas kernels: 553 us -> 638 us
  matrix products: 91.1 us -> 11.1 us
  local copies, waits for them, and re-layouts: 96.6 us -> 32.6 us
  blocking collectives: 41 us -> 0 us
  starting transfers between devices: 0.28 us -> 26.2 us
  other arithmetic: 54.2 us -> 41.5 us
    pallas_call x0 -> x5, Pallas kernels: none -> 122 us  [the longest x1 59.6 us: total_everywhere(): pl.pallas_call(functools.partial(total_kernel, tp_count, fsdp_count), out...]
    reduce_scatter x2 -> x3, waiting for transfers between devices: 106 us -> 197 us  [the longest x2 197 us: local(): lax.psum_scatter(part[2], 'fsdp', scatter_dimension=2, tiled=True)]
    dot_general x20 -> x2, matrix products: 64.2 us -> 4.49 us  [gates_of(): logits = jnp.dot(rows, router_w, preferred_element_type=jnp.float32)]
    pallas_call x4 -> x3, Pallas kernels: 228 us -> 173 us  [line_scatter(): pl.pallas_call(functools.partial(line_scatter_kernel, count), out_shape=j...]
    psum x1 -> x0, blocking collectives: 41 us -> none  [local(): lax.psum((gain_one_grad, gain_two_grad, router_grad_part), ('fsdp', 'tp'))]
    dynamic_update_slice x12 -> x3, local copies, waits for them, and re-layouts: 46 us -> 6.19 us  [shifted_gather(): lax.dynamic_update_slice_in_dim(whole, got, lax.rem(me + count - shift, c...]
    ppermute x0 -> x6, starting transfers between devices: none -> 26 us  [the longest x3 18.9 us: shifted_scatter(): lax.ppermute(block, 'tp', [(i, (i + shift) % count) for i in range(count)])]
    pallas_call x2, Pallas kernels: 107 us -> 129 us  [experts_step(): pl.pallas_call(functools.partial(experts_kernel, first, capacity), grid_s...]
  transfers between devices with their start and end apart: 7 -> 12, of which waited for: 1 -> 2; matrix products, arithmetic and copies ran while one was open for 24% -> 6% of each run, Pallas kernels for 58% -> 44%
where the time goes in v2:
time: 977 us; the launch traced here: 963 us
  Pallas kernels  638 us (65%)
  waiting for transfers between devices  199 us (20%)
  other arithmetic  41.5 us (4%)
  local copies, waits for them, and re-layouts  32.6 us (3%)
  starting transfers between devices  26.2 us (3%)
  between operations  15 us (2%)
  matrix products  11.1 us (1%)
    pallas_call x3, Pallas kernels, line_gather(): pl.pallas_call(functools.partial(line_gather_kernel, count), out_shape=ja...  213 us
    reduce_scatter x2, waiting for transfers between devices, local(): lax.psum_scatter(part[2], 'fsdp', scatter_dimension=2, tiled=True)  197 us
    pallas_call x3, Pallas kernels, line_scatter(): pl.pallas_call(functools.partial(line_scatter_kernel, count), out_shape=j...  173 us
    pallas_call x2, Pallas kernels, experts_step(): pl.pallas_call(functools.partial(experts_kernel, first, capacity), grid_s...  129 us
    pallas_call x1, Pallas kernels, total_everywhere(): pl.pallas_call(functools.partial(total_kernel, tp_count, fsdp_count), out...  59.6 us
    pallas_call x1, Pallas kernels, attend_back(): pl.pallas_call(attend_back_kernel, grid=(group // SEQ,), in_specs=[by_row...  32.2 us
    pallas_call x1, Pallas kernels, attend(): pl.pallas_call(attend_kernel, grid=(seqs,), in_specs=[by_row(width), fixe...  19.7 us
  transfers between devices with their start and end apart: 12, of which 2 were waited for; matrix products, arithmetic and copies ran while one was open for 6% of the time, Pallas kernels for 44%

profile of v2, /device:TPU:0, one launch (start us, length us, event | category | flops | bytes accessed | tf_op | source)
XLA Modules:
  0.0 962.9 jit_solution(13126424784442578742)
XLA Ops:
  12.4 3.5 pad_maximum_fusion
  16.0 3.2 fusion.33
  20.5 3.1 collective-permute-start
  23.6 2.6 collective-permute-start.1
  33.7 112.6 %shard_map.229.x_ref = bf16[1024,1536]{1,0:T(8,128)(2,1)} custom-call(bf16[256,1536]{1,0:T(8,128)(2,1)} %fusion.9.x_ref), custom_call_target="tpu_custom_call" | custom-call | bytes 150000000 | tf_op jit(solution)/shard_map/pallas_call | solution.py:118
  151.6 2.1 constant_dynamic-update-slice_fusion.6
  153.6 2.1 constant_dynamic-update-slice_fusion.5
  155.7 2.1 constant_dynamic-update-slice_fusion.4.g_ref
  157.8 19.7 %shard_map.230 = (bf16[6,1024,64]{2,1,0:T(8,128)(2,1)}, bf16[2,1024,64]{2,1,0:T(8,128)(2,1)}, bf16[2,1024,64]{2,1,0:T(8,128)(2,1)}, bf16[1024,384]{1,0:T(8,128)(...) custom-call(bf16[1024,1536]{1,0:T(8,128)(2,1)} %shard_map.229.x_ref, ...), custom_call_target="tpu_custom_call" | custom-call | flops 10000000000 | bytes 60000000 | tf_op jit(solution)/shard_map/pallas_call | solution.py:542
  177.5 54.3 %shard_map.231 = f32[256,1536]{1,0:T(8,128)} custom-call(bf16[1024,1536]{1,0:T(8,128)(2,1)} %get-tuple-element.32.x_ref), custom_call_target="tpu_custom_call" | custom-call | bytes 150000000 | tf_op jit(solution)/shard_map/pallas_call | solution.py:193
  235.8 54.6 %shard_map.232.x_ref = bf16[1024,1536]{1,0:T(8,128)(2,1)} custom-call(bf16[256,1536]{1,0:T(8,128)(2,1)} %multiply_convert_fusion.1.x_ref), custom_call_target="tpu_custom_call" | custom-call | bytes 150000000 | tf_op jit(solution)/shard_map/pallas_call | solution.py:118
  290.4 3.1 select_reduce_fusion
  295.9 66.0 %shard_map.234 = (f32[1024,1536]{1,0:T(8,128)}, f32[1024,1664]{1,0:T(8,128)}, bf16[5,3,1536,512]{3,2,1,0:T(8,128)(2,1)}) custom-call(s32[11]{0:T(128)} %pad_add_fusion.meta, s32[10,1,1024]{2,1,0:T(1,128)} %copy.74.place_row, s32[1024,10]{1,0:T(8,128)} %fusion.19.place_cols, f32[10,1,1024]{2,1,0:T(1,128)} %broadcast_in_dim.66.gate_row, ...), custom_call_target="tpu_custom_call" | custom-call | flops 54546923520 | bytes 47185920 | tf_op jit(solution)/shard_map/pallas_call | solution.py:320
  361.9 63.0 %shard_map.233 = (f32[1024,1536]{1,0:T(8,128)}, f32[1024,1664]{1,0:T(8,128)}, bf16[5,3,1536,512]{3,2,1,0:T(8,128)(2,1)}) custom-call(s32[11]{0:T(128)} %pad_add_fusion.meta, s32[10,1,1024]{2,1,0:T(1,128)} %copy.74.place_row, s32[1024,10]{1,0:T(8,128)} %fusion.19.place_cols, f32[10,1,1024]{2,1,0:T(1,128)} %broadcast_in_dim.66.gate_row, ...), custom_call_target="tpu_custom_call" | custom-call | flops 54546923520 | bytes 47185920 | tf_op jit(solution)/shard_map/pallas_call | solution.py:320
  424.9 8.4 add.105.x_ref
  433.2 63.2 %shard_map.235 = f32[256,1664]{1,0:T(8,128)} custom-call(f32[1024,1664]{1,0:T(8,128)} %add.105.x_ref), custom_call_target="tpu_custom_call" | custom-call | bytes 150000000 | tf_op jit(solution)/shard_map/pallas_call | solution.py:193
  498.7 2.2 multiply_reduce_fusion
  503.0 46.1 %shard_map.236.branch_grad = bf16[1024,1664]{1,0:T(8,128)(2,1)} custom-call(bf16[256,1664]{1,0:T(8,128)(2,1)} %fusion.20.x_ref), custom_call_target="tpu_custom_call" | custom-call | bytes 150000000 | tf_op jit(solution)/shard_map/pallas_call | solution.py:118
  549.2 2.9 convolution_convert_fusion
  552.1 32.2 %shard_map.237 = (bf16[1024,1536]{1,0:T(8,128)(2,1)}, bf16[1536,1024]{1,0:T(8,128)(2,1)}) custom-call(bf16[1024,1536]{1,0:T(8,128)(2,1)} %shard_map.229.x_ref, bf16[1536,1152]{1,0:T(8,128)(2,1)} %all-gather.4.cloned.1.call-done.w_ref, s32[2,1,512]{2,1,0:T(1,128)} %broadcast_in_dim.32.seg_row, s32[2,512,1]{2,1,0:T(8,128)} %copy.71.seg_col, ...), custom_call_target="tpu_custom_call" | custom-call | flops 20000000000 | bytes 100000000 | tf_op jit(solution)/shard_map/pallas_call | solution.py:588
  584.3 4.1 pad_maximum_fusion.1
  589.6 55.4 %shard_map.238 = f32[256,1536]{1,0:T(8,128)} custom-call(bf16[1024,1536]{1,0:T(8,128)(2,1)} %get-tuple-element.42.x_ref), custom_call_target="tpu_custom_call" | custom-call | bytes 150000000 | tf_op jit(solution)/shard_map/pallas_call | solution.py:193
  645.0 6.0 add.100
  651.0 2.6 copy-done.4
  655.1 16.3 %collective-permute-start.3 = (bf16[256,1536]{1,0:T(8,128)(2,1)}, bf16[256,1536]{1,0:T(8,128)(2,1)}, u32[]{:S(2)}, u32[]{:S(2)}) collective-permute-start(bf16[256,1536]{1,0:T(8,128)(2,1)} %get-tuple-element.108), channel_id=1, source_target_pairs={{0,1},{1,2},{2,3},{3,0},{4,5},{5,6},{6,7},{7,4},{8,9},{9,10},{10,1... | collective-permute-start | bytes 2359304 | tf_op jit(solution)/shard_map/ppermute | solution.py:720
  671.4 2.6 collective-permute-start.5
  675.2 59.6 %shard_map.239 = f32[8,384]{1,0:T(8,128)} custom-call(f32[8,384]{1,0:T(8,128)} %pad_maximum_fusion.4.x_ref), custom_call_target="tpu_custom_call" | custom-call | tf_op jit(solution)/shard_map/pallas_call | solution.py:667
  736.9 6.0 fusion.14
  747.7 50.5 %reduce-scatter.8.cloned.1.call-done.packed = bf16[5,3,192,512]{3,2,1,0:T(8,128)(2,1)} async-done(((bf16[5,3,1536,512]{3,2,1,0:T(8,128)(2,1)}), bf16[5,3,192,512]{3,2,1,0:T(8,128)(2,1)}) %reduce-scatter.8.cloned.1.call-update) | async-done | bytes 2949136 | tf_op jit(solution)/shard_map/reduce_scatter | solution.py:831
  798.2 5.4 shard_map.240
  803.6 146.6 %reduce-scatter.6.cloned.1.call-done.packed = bf16[5,3,192,512]{3,2,1,0:T(8,128)(2,1)} async-done(((bf16[5,3,1536,512]{3,2,1,0:T(8,128)(2,1)}), bf16[5,3,192,512]{3,2,1,0:T(8,128)(2,1)}) %reduce-scatter.6.cloned.1.call-update) | async-done | bytes 2949136 | tf_op jit(solution)/shard_map/reduce_scatter | solution.py:831
  950.2 5.4 shard_map.241
  (118 shorter events, 40.5 us)
Async XLA Ops:
  7.2 150.6 %all-gather.4.cloned.1.call-start = ((), (), s32[]{:S(2)}) async-start(), calls=%async_computation.3 | async-start | bytes 3981312 | tf_op jit(solution)/shard_map/all_gather | solution.py:752
  11.6 0.8 copy-start.10
  12.4 283.5 %all-gather.8.cloned.1.call-start = ((), (), s32[]{:S(2)}) async-start(), calls=%async_computation.5 | async-start | bytes 26542080 | tf_op jit(solution)/shard_map/all_gather | solution.py:764
  19.2 1.1 copy-start.7
  19.2 342.7 %all-gather.6.cloned.1.call-start = ((), (), s32[]{:S(2)}) async-start(), calls=%async_computation.4 | async-start | bytes 26542080 | tf_op jit(solution)/shard_map/all_gather | solution.py:764
  19.3 8.3 copy-start.18
  19.3 8.3 copy-start.13
  20.0 8.2 copy-start.2
  20.0 722.9 %reduce-scatter.4.cloned.1.call-start = ((), (), s32[]{:S(2)}) async-start(), calls=%async_computation.6 | async-start | bytes 3981312 | tf_op jit(solution)/shard_map/reduce_scatter | solution.py:861
  20.5 131.1 %collective-permute-start = (bf16[256,1536]{1,0:T(8,128)(2,1)S(1)}, bf16[256,1536]{1,0:T(8,128)(2,1)}, u32[]{:S(2)}, u32[]{:S(2)}) collective-permute-start(bf16[256,1536]{1,0:T(8,128)(2,1)S(1)} %fusion.16), channel_id=1, source_target_pairs={{0,1},{1,2},{2,3},{3,0},{4,5},{5,6},{6,7},{7,4},{8,9},{9,10},{10,1... | collective-permute-start | bytes 2359304 | tf_op jit(solution)/shard_map/ppermute | solution.py:706
  23.6 130.1 %collective-permute-start.1 = (bf16[256,1536]{1,0:T(8,128)(2,1)S(1)}, bf16[256,1536]{1,0:T(8,128)(2,1)}, u32[]{:S(2)}, u32[]{:S(2)}) collective-permute-start(bf16[256,1536]{1,0:T(8,128)(2,1)S(1)} %fusion.16), channel_id=1, source_target_pairs={{0,2},{1,3},{2,0},{3,1},{4,6},{5,7},{6,4},{7,5},{8,10},{9,11},{10,... | collective-permute-start | bytes 2359304 | tf_op jit(solution)/shard_map/ppermute | solution.py:706
  26.2 129.5 %collective-permute-start.2 = (bf16[256,1536]{1,0:T(8,128)(2,1)S(1)}, bf16[256,1536]{1,0:T(8,128)(2,1)}, u32[]{:S(2)}, u32[]{:S(2)}) collective-permute-start(bf16[256,1536]{1,0:T(8,128)(2,1)S(1)} %fusion.16), channel_id=1, source_target_pairs={{0,3},{1,0},{2,1},{3,2},{4,7},{5,4},{6,5},{7,6},{8,11},{9,8},{10,9... | collective-permute-start | bytes 2359304 | tf_op jit(solution)/shard_map/ppermute | solution.py:706
  27.5 1.9 copy-start.11
  29.1 0.6 copy-start.15
  29.5 4.2 copy-start.8
  33.7 112.7 %copy-start.14 = (s32[2,512]{1,0:T(2,128)S(1)}, s32[2,512]{1,0:T(2,128)}, u32[]{:S(2)}) copy-start(s32[2,512]{1,0:T(2,128)} %param.15) | copy-start | bytes 12292
  33.7 114.3 %copy-start.19 = (bf16[1536]{0:T(1024)(128)(2,1)S(1)}, bf16[1536]{0:T(1024)(128)(2,1)}, u32[]{:S(2)}) copy-start(bf16[1536]{0:T(1024)(128)(2,1)} %param.22) | copy-start | bytes 9220
  233.5 1.1 copy-start
  290.4 3.8 copy-start.9
  433.2 65.4 %copy-start.1 = (f32[256,1536]{1,0:T(8,128)S(1)}, f32[256,1536]{1,0:T(8,128)}, u32[]{:S(2)}) copy-start(f32[256,1536]{1,0:T(8,128)} %copy-done) | copy-start | bytes 4718596
  500.8 1.2 copy-start.5
  588.4 209.8 %reduce-scatter.8.cloned.1.call-start = ((), (), s32[]{:S(2)}) async-start(), calls=%async_computation.8 | async-start | bytes 26542080 | tf_op jit(solution)/shard_map/reduce_scatter | solution.py:831
  589.0 361.2 %reduce-scatter.6.cloned.1.call-start = ((), (), s32[]{:S(2)}) async-start(), calls=%async_computation.7 | async-start | bytes 26542080 | tf_op jit(solution)/shard_map/reduce_scatter | solution.py:831
  651.0 2.6 copy-start.4
  653.6 20.4 %copy-start.3 = (bf16[256,1536]{1,0:T(8,128)(2,1)S(1)}, bf16[256,1536]{1,0:T(8,128)(2,1)}, u32[]{:S(2)}) copy-start(bf16[256,1536]{1,0:T(8,128)(2,1)} %param.14) | copy-start | bytes 2359300
  653.6 20.4 %copy-start.6 = (f32[256,1536]{1,0:T(8,128)S(1)}, f32[256,1536]{1,0:T(8,128)}, u32[]{:S(2)}) copy-start(f32[256,1536]{1,0:T(8,128)} %shard_map.238) | copy-start | bytes 4718596
  653.6 20.4 %copy-start.12 = (f32[1536]{0:T(1024)S(1)}, f32[1536]{0:T(1024)}, u32[]{:S(2)}) copy-start(f32[1536]{0:T(1024)} %copy-done.11) | copy-start | bytes 18436
  653.6 20.4 %copy-start.16 = (f32[256]{0:T(256)S(1)}, f32[256]{0:T(256)}, u32[]{:S(2)}) copy-start(f32[256]{0:T(256)} %copy-done.15) | copy-start | bytes 3076
  655.1 81.8 %copy-start.17 = (f32[256]{0:T(256)S(1)}, f32[256]{0:T(256)}, u32[]{:S(2)}) copy-start(f32[256]{0:T(256)} %get-tuple-element.124) | copy-start | bytes 3076
  655.1 81.8 %collective-permute-start.3 = (bf16[256,1536]{1,0:T(8,128)(2,1)}, bf16[256,1536]{1,0:T(8,128)(2,1)}, u32[]{:S(2)}, u32[]{:S(2)}) collective-permute-start(bf16[256,1536]{1,0:T(8,128)(2,1)} %get-tuple-element.108), channel_id=1, source_target_pairs={{0,1},{1,2},{2,3},{3,0},{4,5},{5,6},{6,7},{7,4},{8,9},{9,10},{10,1... | collective-permute-start | bytes 2359304 | tf_op jit(solution)/shard_map/ppermute | solution.py:720
  671.4 65.5 %collective-permute-start.4 = (bf16[256,1536]{1,0:T(8,128)(2,1)}, bf16[256,1536]{1,0:T(8,128)(2,1)}, u32[]{:S(2)}, u32[]{:S(2)}) collective-permute-start(bf16[256,1536]{1,0:T(8,128)(2,1)} %get-tuple-element.110), channel_id=1, source_target_pairs={{0,2},{1,3},{2,0},{3,1},{4,6},{5,7},{6,4},{7,5},{8,10},{9,11},{10,... | collective-permute-start | bytes 2359304 | tf_op jit(solution)/shard_map/ppermute | solution.py:720
  671.4 65.5 %collective-permute-start.5 = (bf16[256,1536]{1,0:T(8,128)(2,1)}, bf16[256,1536]{1,0:T(8,128)(2,1)}, u32[]{:S(2)}, u32[]{:S(2)}) collective-permute-start(bf16[256,1536]{1,0:T(8,128)(2,1)} %get-tuple-element.109), channel_id=1, source_target_pairs={{0,3},{1,0},{2,1},{3,2},{4,7},{5,4},{6,5},{7,6},{8,11},{9,8},{10,9... | collective-permute-start | bytes 2359304 | tf_op jit(solution)/shard_map/ppermute | solution.py:720
Sparse Core Ops, SparseCore 0:
  12.5 36.5 all-gather.3
  51.6 118.5 all-gather.7
  172.1 118.5 all-gather.5
  588.5 56.6 reduce-scatter.3
  648.8 149.4 reduce-scatter.7
  801.7 148.4 reduce-scatter.5

commit v3 on v2

--- a/solution.py
+++ b/solution.py
@@ -44,9 +44,7 @@
     return (inverse * (weighted - scaled * row_inner), gain_grad)
 
 
-def line_barrier(me, count):
-    barrier = pltpu.get_barrier_semaphore()
-
+def line_signal(barrier, me, count):
     @pl.when(me > 0)
     def _():
         pl.semaphore_signal(barrier, inc=1, device_id={"tp": me - 1})
@@ -55,62 +53,110 @@
     def _():
         pl.semaphore_signal(barrier, inc=1, device_id={"tp": me + 1})
 
-    pl.semaphore_wait(barrier, jnp.where((me > 0) & (me < count - 1), 2, 1))
-
-
-def line_gather_kernel(count, x_ref, o_ref, send_sem, recv_sem, own_sem):
-    rows = x_ref.shape[0]
-    me = lax.axis_index("tp")
-    line_barrier(me, count)
-
-    def part(chunk):
-        return o_ref.at[pl.ds(pl.multiple_of(chunk * rows, rows), rows)]
-
-    def hop(way, step, chunk):
+    return jnp.where((me > 0) & (me < count - 1), 2, 1)
+
+
+class Plane:
+    def __init__(self, count):
+        self.me = lax.axis_index("fsdp")
+        self.core = lax.rem(self.me, 2)
+        self.chip = lax.div(self.me, 2)
+        self.chips = count // 2
+        self.partner = self.me + 1 - 2 * self.core
+
+    def chip_at(self, shift):
+        return lax.rem(self.chip + shift + self.chips, self.chips)
+
+    def peer(self, shift):
+        return self.chip_at(shift) * 2 + self.core
+
+    def signal(self, barrier):
+        for shift in range(1, self.chips):
+            pl.semaphore_signal(barrier, inc=1, device_id={"fsdp": self.peer(shift)})
+        pl.semaphore_signal(barrier, inc=1, device_id={"fsdp": self.partner})
+        return self.chips
+
+
+def rows_of(ref, index, rows):
+    return ref.at[pl.ds(pl.multiple_of(index * rows, rows), rows)]
+
+
+class LineGather:
+    def __init__(self, count, x_ref, o_ref, send_sem, recv_sem, own_sem):
+        self.count, self.x_ref, self.o_ref = count, x_ref, o_ref
+        self.send_sem, self.recv_sem = send_sem, recv_sem
+        self.rows = x_ref.shape[0]
+        me = self.me = lax.axis_index("tp")
+        self.own = pltpu.make_async_copy(x_ref, rows_of(o_ref, me, self.rows), own_sem)
+        steps = range(count - 1)
+        self.sends = [
+            [(me >= step) & (me < count - 1) for step in steps],
+            [(me + step < count) & (me > 0) for step in steps],
+        ]
+        self.gets = [
+            [me - 1 - step >= 0 for step in steps],
+            [me + 1 + step < count for step in steps],
+        ]
+
+    def hop(self, way, step, chunk):
+        part = rows_of(self.o_ref, chunk, self.rows)
         return pltpu.make_async_remote_copy(
-            src_ref=x_ref if step == 0 else part(chunk),
-            dst_ref=part(chunk),
-            send_sem=send_sem.at[way, step],
-            recv_sem=recv_sem.at[way, step],
-            device_id={"tp": me + 1 if way == 0 else me - 1},
+            src_ref=self.x_ref if step == 0 else part,
+            dst_ref=part,
+            send_sem=self.send_sem.at[way, step],
+            recv_sem=self.recv_sem.at[way, step],
+            device_id={"tp": self.me + 1 if way == 0 else self.me - 1},
         )
 
-    own = pltpu.make_async_copy(x_ref, part(me), own_sem)
-    sends = [[(me >= step) & (me < count - 1) for step in range(count - 1)],
-             [(me + step < count) & (me > 0) for step in range(count - 1)]]
-    gets = [[me - 1 - step >= 0 for step in range(count - 1)],
-            [me + 1 + step < count for step in range(count - 1)]]
+    def start(self, step):
+        @pl.when(self.sends[0][step])
+        def _():
+            self.hop(0, step, self.me - step).start()
+
+        @pl.when(self.sends[1][step])
+        def _():
+            self.hop(1, step, self.me + step).start()
+
+        if step == 0:
+            self.own.start()
+
+    def arrive(self, step):
+        @pl.when(self.gets[0][step])
+        def _():
+            self.hop(0, step, self.me - 1 - step).wait_recv()
+
+        @pl.when(self.gets[1][step])
+        def _():
+            self.hop(1, step, self.me + 1 + step).wait_recv()
+
+    def finish(self):
+        self.own.wait()
+        for step in range(self.count - 1):
+
+            @pl.when(self.sends[0][step])
+            def _():
+                self.hop(0, step, self.me - step).wait_send()
+
+            @pl.when(self.sends[1][step])
+            def _():
+                self.hop(1, step, self.me + step).wait_send()
+
+
+def line_gather_kernel(count, x_ref, o_ref, *sems):
+    barrier = pltpu.get_barrier_semaphore()
+    pl.semaphore_wait(barrier, line_signal(barrier, lax.axis_index("tp"), count))
+    line = LineGather(count, x_ref, o_ref, *sems)
     for step in range(count - 1):
-
-        @pl.when(sends[0][step])
-        def _():
-            hop(0, step, me - step).start()
-
-        @pl.when(sends[1][step])
-        def _():
-            hop(1, step, me + step).start()
-
-        if step == 0:
-            own.start()
-
-        @pl.when(gets[0][step])
-        def _():
-            hop(0, step, me - 1 - step).wait_recv()
-
-        @pl.when(gets[1][step])
-        def _():
-            hop(1, step, me + 1 + step).wait_recv()
-
-    own.wait()
-    for step in range(count - 1):
-
-        @pl.when(sends[0][step])
-        def _():
-            hop(0, step, me - step).wait_send()
-
-        @pl.when(sends[1][step])
-        def _():
-            hop(1, step, me + step).wait_send()
+        line.start(step)
+        line.arrive(step)
+    line.finish()
+
+
+def line_sems(count):
+    return [
+        pltpu.SemaphoreType.DMA((2, count - 1)),
+        pltpu.SemaphoreType.DMA((2, count - 1)),
+    ]
 
 
 def line_gather(rows_in, count, ident):
@@ -120,92 +166,295 @@
         out_shape=jax.ShapeDtypeStruct((rows * count, width), rows_in.dtype),
         in_specs=[pl.BlockSpec(memory_space=pltpu.VMEM)],
         out_specs=pl.BlockSpec(memory_space=pl.ANY),
-        scratch_shapes=[
-            pltpu.SemaphoreType.DMA((2, count - 1)),
-            pltpu.SemaphoreType.DMA((2, count - 1)),
-            pltpu.SemaphoreType.DMA,
-        ],
+        scratch_shapes=line_sems(count) + [pltpu.SemaphoreType.DMA],
         compiler_params=pltpu.CompilerParams(collective_id=ident, has_side_effects=True),
         cost_estimate=pl.CostEstimate(flops=0, transcendentals=0, bytes_accessed=150_000_000),
     )(rows_in)
 
 
-def line_scatter_kernel(count, x_ref, o_ref, recv, send, send_sem, recv_sem):
-    rows = o_ref.shape[0]
-    me = lax.axis_index("tp")
-    line_barrier(me, count)
-
-    def block(dest):
-        return x_ref[pl.ds(pl.multiple_of(dest * rows, rows), rows), :].astype(jnp.float32)
-
-    def hop(way, step):
+def gather_both_kernel(
+    tp_count, fsdp_count, x_ref, w_ref, o_ref, wo_ref,
+    line_send, line_recv, own_sem, out_send, out_recv, on_send, on_recv, kept_sem,
+):
+    plane = Plane(fsdp_count)
+    barrier = pltpu.get_barrier_semaphore()
+    waits = line_signal(barrier, lax.axis_index("tp"), tp_count) + plane.signal(barrier)
+    pl.semaphore_wait(barrier, waits)
+    line = LineGather(tp_count, x_ref, o_ref, line_send, line_recv, own_sem)
+    rows = w_ref.shape[0]
+
+    def outward(shift, target, source_device):
         return pltpu.make_async_remote_copy(
-            src_ref=send.at[way, step],
-            dst_ref=recv.at[way, step],
-            send_sem=send_sem.at[way, step],
-            recv_sem=recv_sem.at[way, step],
-            device_id={"tp": me + 1 if way == 0 else me - 1},
+            src_ref=w_ref,
+            dst_ref=rows_of(wo_ref, source_device, rows),
+            send_sem=out_send.at[shift],
+            recv_sem=out_recv.at[shift],
+            device_id={"fsdp": target},
         )
 
-    behind = (me, count - 1 - me)
-    has_next = (me < count - 1, me > 0)
-    has_prev = (me > 0, me < count - 1)
-    for step in range(count - 1):
+    def onward(shift, source_device):
+        part = rows_of(wo_ref, source_device, rows)
+        return pltpu.make_async_remote_copy(
+            src_ref=part,
+            dst_ref=part,
+            send_sem=on_send.at[shift - 1],
+            recv_sem=on_recv.at[shift - 1],
+            device_id={"fsdp": plane.partner},
+        )
+
+    kept = pltpu.make_async_copy(w_ref, rows_of(wo_ref, plane.me, rows), kept_sem)
+    line.start(0)
+    for shift in range(1, plane.chips):
+        outward(shift, plane.peer(shift), plane.me).start()
+    outward(0, plane.partner, plane.me).start()
+    kept.start()
+    for shift in range(1, plane.chips):
+        outward(shift, plane.peer(shift), plane.peer(-shift)).wait_recv()
+        onward(shift, plane.peer(-shift)).start()
+    line.arrive(0)
+    for step in range(1, tp_count - 1):
+        line.start(step)
+        line.arrive(step)
+    outward(0, plane.partner, plane.partner).wait_recv()
+    for shift in range(1, plane.chips):
+        onward(shift, plane.chip_at(-shift) * 2 + 1 - plane.core).wait_recv()
+    for shift in range(1, plane.chips):
+        outward(shift, plane.peer(shift), plane.me).wait_send()
+        onward(shift, plane.peer(-shift)).wait_send()
+    outward(0, plane.partner, plane.me).wait_send()
+    kept.wait()
+    line.finish()
+
+
+def gather_both(rows_in, weights, tp_count, fsdp_count, ident):
+    chips = fsdp_count // 2
+    return pl.pallas_call(
+        functools.partial(gather_both_kernel, tp_count, fsdp_count),
+        out_shape=[
+            jax.ShapeDtypeStruct((rows_in.shape[0] * tp_count, rows_in.shape[1]), rows_in.dtype),
+            jax.ShapeDtypeStruct((weights.shape[0] * fsdp_count, weights.shape[1]), weights.dtype),
+        ],
+        in_specs=[pl.BlockSpec(memory_space=pltpu.VMEM)] * 2,
+        out_specs=[pl.BlockSpec(memory_space=pl.ANY)] * 2,
+        scratch_shapes=line_sems(tp_count)
+        + [
+            pltpu.SemaphoreType.DMA,
+            pltpu.SemaphoreType.DMA((chips,)),
+            pltpu.SemaphoreType.DMA((chips,)),
+            pltpu.SemaphoreType.DMA((chips - 1,)),
+            pltpu.SemaphoreType.DMA((chips - 1,)),
+            pltpu.SemaphoreType.DMA,
+        ],
+        compiler_params=pltpu.CompilerParams(collective_id=ident, has_side_effects=True),
+        cost_estimate=pl.CostEstimate(flops=0, transcendentals=0, bytes_accessed=150_000_000),
+    )(rows_in, weights)
+
+
+class LineScatter:
+    def __init__(self, count, x_refs, o_ref, recv, send, send_sem, recv_sem):
+        self.count, self.x_refs, self.o_ref = count, x_refs, o_ref
+        self.recv, self.send = recv, send
+        self.send_sem, self.recv_sem = send_sem, recv_sem
+        self.rows = o_ref.shape[0]
+        me = self.me = lax.axis_index("tp")
+        self.behind = (me, count - 1 - me)
+        self.has_next = (me < count - 1, me > 0)
+        self.has_prev = (me > 0, me < count - 1)
+
+    def block(self, dest):
+        area = pl.ds(pl.multiple_of(dest * self.rows, self.rows), self.rows)
+        total = self.x_refs[0][area, :].astype(jnp.float32)
+        for x_ref in self.x_refs[1:]:
+            total = total + x_ref[area, :].astype(jnp.float32)
+        return total
+
+    def hop(self, way, step):
+        return pltpu.make_async_remote_copy(
+            src_ref=self.send.at[way, step],
+            dst_ref=self.recv.at[way, step],
+            send_sem=self.send_sem.at[way, step],
+            recv_sem=self.recv_sem.at[way, step],
+            device_id={"tp": self.me + 1 if way == 0 else self.me - 1},
+        )
+
+    def start(self, step):
+        count, me, send = self.count, self.me, self.send
         for way in range(2):
             dest = count - 1 - step + me if way == 0 else step - (count - 1 - me)
-
-            @pl.when(has_next[way] & (step >= behind[way]) & (behind[way] == 0))
+            active = self.has_next[way] & (step >= self.behind[way])
+
+            @pl.when(active & (self.behind[way] == 0))
             def _():
-                send[way, step] = block(dest).astype(send.dtype)
-                hop(way, step).start()
+                send[way, step] = self.block(dest).astype(send.dtype)
+                self.hop(way, step).start()
 
             if step > 0:
 
-                @pl.when(has_next[way] & (step >= behind[way]) & (behind[way] > 0))
+                @pl.when(active & (self.behind[way] > 0))
                 def _():
-                    total = block(dest) + recv[way, step - 1].astype(jnp.float32)
+                    total = self.block(dest) + self.recv[way, step - 1].astype(jnp.float32)
                     send[way, step] = total.astype(send.dtype)
-                    hop(way, step).start()
-
+                    self.hop(way, step).start()
+
+    def arrive(self, step):
         for way in range(2):
 
-            @pl.when(has_prev[way] & (step >= behind[way] - 1))
+            @pl.when(self.has_prev[way] & (step >= self.behind[way] - 1))
             def _():
-                hop(way, step).wait_recv()
-
-    o_ref[...] = block(me)
-    for way in range(2):
-
-        @pl.when(has_prev[way])
-        def _():
-            o_ref[...] += recv[way, count - 2].astype(jnp.float32)
-
+                self.hop(way, step).wait_recv()
+
+    def finish(self):
+        self.o_ref[...] = self.block(self.me)
+        for way in range(2):
+
+            @pl.when(self.has_prev[way])
+            def _():
+                self.o_ref[...] += self.recv[way, self.count - 2].astype(jnp.float32)
+
+        for step in range(self.count - 1):
+            for way in range(2):
+
+                @pl.when(self.has_next[way] & (step >= self.behind[way]))
+                def _():
+                    self.hop(way, step).wait_send()
+
+
+def line_scatter_kernel(count, parts, *refs):
+    barrier = pltpu.get_barrier_semaphore()
+    pl.semaphore_wait(barrier, line_signal(barrier, lax.axis_index("tp"), count))
+    line = LineScatter(count, refs[:parts], *refs[parts:])
     for step in range(count - 1):
-        for way in range(2):
-
-            @pl.when(has_next[way] & (step >= behind[way]))
-            def _():
-                hop(way, step).wait_send()
-
-
-def line_scatter(partial_rows, count, ident):
-    rows, width = partial_rows.shape[0] // count, partial_rows.shape[1]
+        line.start(step)
+        line.arrive(step)
+    line.finish()
+
+
+def line_buffers(count, rows, width):
+    return [
+        pltpu.VMEM((2, count - 1, rows, width), jnp.bfloat16),
+        pltpu.VMEM((2, count - 1, rows, width), jnp.bfloat16),
+    ] + line_sems(count)
+
+
+def line_scatter(parts, count, ident):
+    rows, width = parts[0].shape[0] // count, parts[0].shape[1]
     return pl.pallas_call(
-        functools.partial(line_scatter_kernel, count),
+        functools.partial(line_scatter_kernel, count, len(parts)),
         out_shape=jax.ShapeDtypeStruct((rows, width), jnp.float32),
-        in_specs=[pl.BlockSpec(memory_space=pltpu.VMEM)],
+        in_specs=[pl.BlockSpec(memory_space=pltpu.VMEM)] * len(parts),
         out_specs=pl.BlockSpec(memory_space=pltpu.VMEM),
-        scratch_shapes=[
-            pltpu.VMEM((2, count - 1, rows, width), jnp.bfloat16),
-            pltpu.VMEM((2, count - 1, rows, width), jnp.bfloat16),
-            pltpu.SemaphoreType.DMA((2, count - 1)),
-            pltpu.SemaphoreType.DMA((2, count - 1)),
-        ],
+        scratch_shapes=line_buffers(count, rows, width),
         compiler_params=pltpu.CompilerParams(
-            collective_id=ident, has_side_effects=True, vmem_limit_bytes=56 << 20
+            collective_id=ident, has_side_effects=True, vmem_limit_bytes=60 << 20
         ),
         cost_estimate=pl.CostEstimate(flops=0, transcendentals=0, bytes_accessed=150_000_000),
-    )(partial_rows)
+    )(*parts)
+
+
+def scatter_both_kernel(
+    tp_count, fsdp_count, x_ref, w_ref, o_ref, wo_ref,
+    line_recv, line_send, line_send_sem, line_recv_sem,
+    pair_got, chip_sums, chip_got, pair_send, pair_recv, chip_send, chip_recv,
+):
+    plane = Plane(fsdp_count)
+    barrier = pltpu.get_barrier_semaphore()
+    waits = line_signal(barrier, lax.axis_index("tp"), tp_count) + plane.signal(barrier)
+    pl.semaphore_wait(barrier, waits)
+    line = LineScatter(
+        tp_count, [x_ref], o_ref, line_recv, line_send, line_send_sem, line_recv_sem
+    )
+    rows = wo_ref.shape[0]
+
+    def to_pair(shift):
+        return pltpu.make_async_remote_copy(
+            src_ref=rows_of(w_ref, plane.chip_at(shift) * 2 + 1 - plane.core, rows),
+            dst_ref=pair_got.at[shift],
+            send_sem=pair_send.at[shift],
+            recv_sem=pair_recv.at[shift],
+            device_id={"fsdp": plane.partner},
+        )
+
+    def to_chip(shift):
+        return pltpu.make_async_remote_copy(
+            src_ref=chip_sums.at[shift - 1],
+            dst_ref=chip_got.at[shift - 1],
+            send_sem=chip_send.at[shift - 1],
+            recv_sem=chip_recv.at[shift - 1],
+            device_id={"fsdp": plane.peer(shift)},
+        )
+
+    def both_cores(shift):
+        own = pl.ds(pl.multiple_of(plane.peer(shift) * rows, rows), rows)
+        return w_ref[own, :].astype(jnp.float32) + pair_got[shift].astype(jnp.float32)
+
+    line.start(0)
+    order = list(range(1, plane.chips)) + [0]
+    for shift in order:
+        to_pair(shift).start()
+    for shift in order:
+        to_pair(shift).wait_recv()
+        if shift > 0:
+            chip_sums[shift - 1] = both_cores(shift).astype(chip_sums.dtype)
+            to_chip(shift).start()
+    line.arrive(0)
+    for step in range(1, tp_count - 1):
+        line.start(step)
+        line.arrive(step)
+    total = both_cores(0)
+    for shift in range(1, plane.chips):
+        to_chip(shift).wait_recv()
+        total = total + chip_got[shift - 1].astype(jnp.float32)
+    wo_ref[...] = total
+    line.finish()
+    for shift in order:
+        to_pair(shift).wait_send()
+        if shift > 0:
+            to_chip(shift).wait_send()
+
+
+def scatter_both(partial_rows, weight_grads, tp_count, fsdp_count, ident):
+    rows, width = partial_rows.shape[0] // tp_count, partial_rows.shape[1]
+    w_rows, w_width = weight_grads.shape[0] // fsdp_count, weight_grads.shape[1]
+    chips = fsdp_count // 2
+    return pl.pallas_call(
+        functools.partial(scatter_both_kernel, tp_count, fsdp_count),
+        out_shape=[
+            jax.ShapeDtypeStruct((rows, width), jnp.float32),
+            jax.ShapeDtypeStruct((w_rows, w_width), jnp.float32),
+        ],
+        in_specs=[pl.BlockSpec(memory_space=pltpu.VMEM)] * 2,
+        out_specs=[pl.BlockSpec(memory_space=pltpu.VMEM)] * 2,
+        scratch_shapes=line_buffers(tp_count, rows, width)
+        + [
+            pltpu.VMEM((chips, w_rows, w_width), jnp.bfloat16),
+            pltpu.VMEM((chips - 1, w_rows, w_width), jnp.bfloat16),
+            pltpu.VMEM((chips - 1, w_rows, w_width), jnp.bfloat16),
+            pltpu.SemaphoreType.DMA((chips,)),
+            pltpu.SemaphoreType.DMA((chips,)),
+            pltpu.SemaphoreType.DMA((chips - 1,)),
+            pltpu.SemaphoreType.DMA((chips - 1,)),
+        ],
+        compiler_params=pltpu.CompilerParams(
+            collective_id=ident, has_side_effects=True, vmem_limit_bytes=60 << 20
+        ),
+        cost_estimate=pl.CostEstimate(flops=0, transcendentals=0, bytes_accessed=150_000_000),
+    )(partial_rows, weight_grads)
+
+
+def pack_kernel(*refs):
+    for slot, source in enumerate(refs[:-1]):
+        refs[-1][0, slot] = source[0]
+
+
+def pack(stacks, low, high):
+    _, rows, width = stacks[0].shape
+    return pl.pallas_call(
+        pack_kernel,
+        grid=(high - low,),
+        in_specs=[pl.BlockSpec((1, rows, width), lambda step: (step + low, 0, 0))] * len(stacks),
+        out_specs=pl.BlockSpec((1, len(stacks), rows, width), lambda step: (step, 0, 0, 0)),
+        out_shape=jax.ShapeDtypeStruct((high - low, len(stacks), rows, width), jnp.bfloat16),
+    )(*stacks)
 
 
 SLOTS = 256
@@ -221,10 +470,12 @@
     x_ref,
     g_ref,
     weights,
-    y_ref,
-    dx_ref,
+    y_out,
+    dx_out,
     grads,
+    *totals,
 ):
+    y_ref, dx_ref = totals or (y_out, dx_out)
     step = pl.program_id(0)
     expert = step + first_expert
     group, width = x_ref.shape
@@ -299,11 +550,16 @@
         def _():
             run(base, span)
 
-
-def experts_step(meta, place_rows, place_cols, gate_rows, x_rows, g_rows, weights, first, capacity):
+    @pl.when((step == pl.num_programs(0) - 1) & (len(totals) > 0))
+    def _():
+        y_out[...] = y_ref[...].astype(y_out.dtype)
+        dx_out[...] = dx_ref[...].astype(dx_out.dtype)
+
+
+def experts_step(meta, place_rows, place_cols, gate_rows, x_rows, g_rows, weights, first, count, skip, capacity):
     group, width = x_rows.shape
-    count, _, _, hidden = weights.shape
-    keep = jnp.float32 if group <= 1024 else jnp.bfloat16
+    hidden = weights.shape[-1]
+    totals = [pltpu.VMEM((group, width), jnp.float32), pltpu.VMEM((group, width + 128), jnp.float32)]
     tail = 128
 
     def whole(shape):
@@ -314,8 +570,8 @@
     def row(shape):
         return pl.BlockSpec(shape, lambda step, meta: (step + first, 0, 0))
 
-    def big():
-        return pl.BlockSpec((1, 3, width, hidden), lambda step, meta: (step, 0, 0, 0))
+    def big(offset):
+        return pl.BlockSpec((1, 3, width, hidden), lambda step, meta: (step + offset, 0, 0, 0))
 
     return pl.pallas_call(
         functools.partial(experts_kernel, first, capacity),
@@ -328,18 +584,19 @@
                 row((1, 1, group)),
                 whole(x_rows.shape),
                 whole(g_rows.shape),
-                big(),
+                big(skip),
             ],
             out_specs=[
                 whole((group, width)),
                 whole((group, width + tail)),
-                big(),
+                big(0),
             ],
+            scratch_shapes=totals if group <= 1024 else [],
         ),
         out_shape=[
-            jax.ShapeDtypeStruct((group, width), keep),
-            jax.ShapeDtypeStruct((group, width + tail), keep),
-            jax.ShapeDtypeStruct(weights.shape, jnp.bfloat16),
+            jax.ShapeDtypeStruct((group, width), jnp.bfloat16),
+            jax.ShapeDtypeStruct((group, width + tail), jnp.bfloat16),
+            jax.ShapeDtypeStruct((count, 3, width, hidden), jnp.bfloat16),
         ],
         compiler_params=pltpu.CompilerParams(
             dimension_semantics=("arbitrary",), vmem_limit_bytes=63 << 20
@@ -434,6 +691,7 @@
     v_ref,
     mixed_ref,
     logsum_ref,
+    moe_rows,
     branch_grad,
     dx_ref,
     dw_ref,
@@ -451,8 +709,9 @@
     edge = (heads + 2 * kv_heads) * HEAD_DIM
     step = pl.program_id(0)
     out_edge = edge + heads * HEAD_DIM
+    width = x_ref.shape[1]
     grad = jnp.dot(
-        branch_grad[...], w_ref[:, edge:out_edge], preferred_element_type=jnp.float32
+        branch_grad[:, :width], w_ref[:, edge:out_edge], preferred_element_type=jnp.float32
     ).astype(jnp.bfloat16)
     for head in range(heads):
         mixed_grads[head] = grad[:, head * HEAD_DIM : (head + 1) * HEAD_DIM]
@@ -494,18 +753,20 @@
             part = kv_grads[1, head - heads - kv_heads]
         qkv_grad[:, head * HEAD_DIM : (head + 1) * HEAD_DIM] = part.astype(jnp.bfloat16)
     dx_ref[...] = contract_last(qkv_grad[...], w_ref[:, :edge]).astype(jnp.bfloat16)
-    qkv_part = contract_first(x_ref[...], qkv_grad[...])
-    out_part = contract_first(branch_grad[...], mixed_ref[...])
-
-    @pl.when(step == 0)
-    def _():
-        dw_acc[:, :edge] = qkv_part
-        dw_acc[:, edge:out_edge] = out_part
-
-    @pl.when(step > 0)
-    def _():
-        dw_acc[:, :edge] += qkv_part
-        dw_acc[:, edge:out_edge] += out_part
+    for low, high, left_op, right_op in (
+        (0, edge, x_ref[...], qkv_grad[...]),
+        (edge, out_edge, branch_grad[:, :width], mixed_ref[...]),
+        (out_edge, dw_acc.shape[1], moe_rows[...], branch_grad[:, width:]),
+    ):
+        part = contract_first(left_op, right_op)
+
+        @pl.when(step == 0)
+        def _():
+            dw_acc[:, low:high] = part
+
+        @pl.when(step > 0)
+        def _():
+            dw_acc[:, low:high] += part
 
     @pl.when(step == pl.num_programs(0) - 1)
     def _():
@@ -580,11 +841,12 @@
     )(rows, weights, segments[:, None, :], segments[:, :, None], *tables)
 
 
-def attend_back(rows, weights, segments, tables, kept, branch_grad):
+def attend_back(rows, weights, segments, tables, kept, moe_rows, branch_grad):
     queries, keys, values, mixed, logsum = kept
     group, width = rows.shape
     heads, kv_heads = queries.shape[0], keys.shape[0]
-    used = 2 * (heads + kv_heads) * HEAD_DIM
+    used = weights.shape[1]
+    edge = (heads + 2 * kv_heads) * HEAD_DIM
     return pl.pallas_call(
         attend_back_kernel,
         grid=(group // SEQ,),
@@ -601,6 +863,7 @@
             by_row(heads * HEAD_DIM),
             pl.BlockSpec((1, heads, SEQ), lambda seq: (seq, 0, 0)),
             by_row(width),
+            by_row(branch_grad.shape[1]),
         ],
         out_specs=[by_row(width), fixed((width, used))],
         out_shape=[
@@ -613,7 +876,7 @@
             pltpu.VMEM((heads, SEQ, HEAD_DIM), jnp.bfloat16),
             pltpu.VMEM((heads, SEQ, HEAD_DIM), jnp.float32),
             pltpu.VMEM((2, kv_heads, SEQ, HEAD_DIM), jnp.float32),
-            pltpu.VMEM((SEQ, used - heads * HEAD_DIM), jnp.bfloat16),
+            pltpu.VMEM((SEQ, edge), jnp.bfloat16),
             pltpu.VMEM((width, used), jnp.float32),
         ],
         compiler_params=pltpu.CompilerParams(
@@ -623,7 +886,7 @@
             flops=20_000_000_000, transcendentals=3_000_000, bytes_accessed=100_000_000
         ),
     )(rows, weights, segments[:, None, :], segments[:, :, None], *tables,
-      queries, keys, values, mixed, logsum, branch_grad)
+      queries, keys, values, mixed, logsum, moe_rows, branch_grad)
 
 
 def total_kernel(tp_count, fsdp_count, x_ref, o_ref, tp_got, fsdp_got, send_sem, recv_sem):
@@ -722,7 +985,8 @@
     return total
 
 
-CHUNKS = 2
+GATHERS = 2
+RUNS = (0, 2, 5, 10)
 
 
 def local(
@@ -749,29 +1013,30 @@
     q_width, kv_width = w_query.shape[1], w_key.shape[1]
     used = 2 * (q_width + kv_width)
     lane_pad = 128 - expert_count
-    attn_w = lax.all_gather(
-        jnp.concatenate(
-            [w_query, w_key, w_value, w_out, jnp.pad(w_router, ((0, 0), (0, lane_pad)))], axis=1
-        ),
-        "fsdp",
-        axis=0,
-        tiled=True,
-    )
-    router_w = attn_w[:, used : used + expert_count]
-    stacked = jnp.stack([w_gate, w_up, w_down], axis=1)
-    edges = [experts_here * part // CHUNKS for part in range(CHUNKS + 1)]
+    edges = [experts_here * part // GATHERS for part in range(GATHERS + 1)]
     pieces = [
-        lax.all_gather(stacked[low:high], "fsdp", axis=2, tiled=True)
+        lax.all_gather(pack([w_gate, w_up, w_down], low, high), "fsdp", axis=2, tiled=True)
         for low, high in zip(edges[:-1], edges[1:])
     ]
-
     gain_one = norm1_gain.astype(jnp.float32)
     gain_two = norm2_gain.astype(jnp.float32)
     start_x = emb.astype(jnp.float32) * emb_scale
     normed_one, inverse_one = rms_forward(start_x, gain_one)
-    group_rows = line_gather(normed_one.astype(jnp.bfloat16), tp_count, 0)
+    fsdp_count = lax.axis_size("fsdp")
+    group_rows, attn_w = gather_both(
+        normed_one.astype(jnp.bfloat16),
+        jnp.concatenate(
+            [w_query, w_key, w_value, w_out, jnp.pad(w_router, ((0, 0), (0, lane_pad)))], axis=1
+        ),
+        tp_count,
+        fsdp_count,
+        0,
+    )
+    router_w = attn_w[:, used : used + expert_count]
     out_grad = cotangent.astype(jnp.float32)
-    moe_grad_rows = shifted_gather((resid_scale * out_grad).astype(jnp.bfloat16), tp_count, tp_index)
+    moe_grad = (resid_scale * out_grad).astype(jnp.bfloat16)
+    moe_grad, group_rows = lax.optimization_barrier((moe_grad, group_rows))
+    moe_grad_rows = shifted_gather(moe_grad, tp_count, tp_index)
     group_size = group_rows.shape[0]
 
     capacity = group_size * routes.shape[1] // expert_count * 2
@@ -790,7 +1055,7 @@
     tables = attend_tables()
     heads_here, kv_here = q_width // HEAD_DIM, kv_width // HEAD_DIM
     *kept, branch_part = attend(group_rows, attn_w, segment_ids, tables, heads_here, kv_here)
-    attn_branch = line_scatter(branch_part, tp_count, 2)
+    attn_branch = line_scatter([branch_part], tp_count, 2)
     mid_x = start_x + resid_scale * attn_branch
     normed_two, inverse_two = rms_forward(mid_x, gain_two)
     normed_low = normed_two.astype(jnp.bfloat16)
@@ -813,7 +1078,9 @@
     gate_rows = gates_here.T[:, None, :]
 
     outs = []
-    for first, piece in zip(edges[:-1], pieces):
+    runs = sorted({edge * experts_here // RUNS[-1] for edge in RUNS} | set(edges))
+    for first, last in zip(runs[:-1], runs[1:]):
+        home = max(index for index in range(GATHERS) if edges[index] <= first)
         outs.append(
             experts_step(
                 meta,
@@ -822,19 +1089,17 @@
                 gate_rows,
                 moe_rows,
                 moe_grad_rows,
-                piece,
+                pieces[home],
                 first,
+                last - first,
+                first - edges[home],
                 capacity,
             )
         )
     grad_sums = [
         lax.psum_scatter(part[2], "fsdp", scatter_dimension=2, tiled=True) for part in outs
     ]
-    y_part = functools.reduce(lambda one, two: one + two, [part[0] for part in outs])
-    dx_part = functools.reduce(lambda one, two: one + two, [part[1] for part in outs])
-    dx_sum = line_scatter(dx_part, tp_count, 4)
-    moe_sum = shifted_scatter(y_part, tp_count, tp_index)
-    out = (mid_x + resid_scale * moe_sum).astype(jnp.bfloat16)
+    dx_sum = line_scatter([part[1] for part in outs], tp_count, 4)
     gates_grad = dx_sum[:, width : width + expert_count]
     gates_inner = jnp.sum(gates * gates_grad, axis=-1, keepdims=True)
     logits_grad = (gates * (gates_grad - gates_inner)).astype(jnp.bfloat16)
@@ -847,22 +1112,21 @@
         tp_count,
         5,
     )
-    router_grad = contract_first(moe_rows, sent[:, width:])
-    dx_one, attn_dw = attend_back(
-        group_rows, attn_w, segment_ids, tables, kept, sent
+    y_parts, sent = lax.optimization_barrier(([part[0] for part in outs], sent))
+    y_part = functools.reduce(
+        lambda one, two: one + two, [part.astype(jnp.float32) for part in y_parts]
     )
-    attn_grads = jnp.concatenate([attn_dw, router_grad.astype(jnp.bfloat16)], axis=1)
-    normed_one_grad = line_scatter(dx_one, tp_count, 7)
+    moe_sum = shifted_scatter(y_part, tp_count, tp_index)
+    out = (mid_x + resid_scale * moe_sum).astype(jnp.bfloat16)
+    dx_one, attn_grads = attend_back(group_rows, attn_w, segment_ids, tables, kept, moe_rows, sent)
+    normed_one_grad, attn_sum = scatter_both(dx_one, attn_grads, tp_count, fsdp_count, 7)
     start_from_norm, gain_one_grad = rms_backward(normed_one_grad, start_x, inverse_one, gain_one)
     grad_emb = emb_scale * (mid_grad + start_from_norm)
     gain_sums = total_everywhere(
         jnp.concatenate([gain_one_grad, gain_two_grad]).reshape(8, -1), 8
     ).reshape(2, width)
-    attn_sum = lax.psum_scatter(attn_grads, "fsdp", scatter_dimension=0, tiled=True).astype(
-        jnp.float32
-    )
     expert_sums = ()
-    for first, part in zip(edges[:-1], grad_sums):
+    for first, part in zip(runs[:-1], grad_sums):
         expert_sums = widen(part, experts_here, first, expert_sums)
     return (
         out,

time: 977 us -> 766 us (0.78)
  waiting for transfers between devices: 199 us -> 61.2 us
  Pallas kernels: 638 us -> 615 us
  starting transfers between devices: 26.2 us -> 6.16 us
  other arithmetic: 41.5 us -> 26.8 us
    reduce_scatter x2 -> x3, waiting for transfers between devices: 197 us -> 0.01 us  [local(): lax.psum_scatter(part[2], 'fsdp', scatter_dimension=2, tiled=True)]
    pallas_call x3 -> x6, Pallas kernels: 173 us -> 306 us  [the longest x2 151 us: line_scatter(): pl.pallas_call(functools.partial(line_scatter_kernel, count, len(parts)),...]
    pallas_call x3 -> x2, Pallas kernels: 213 us -> 108 us  [line_gather(): pl.pallas_call(functools.partial(line_gather_kernel, count), out_shape=ja...]
    ppermute x3, waiting for transfers between devices: 0.01 us -> 61.1 us  [shifted_scatter(): lax.ppermute(block, 'tp', [(i, (i + shift) % count) for i in range(count)])]
    pallas_call x1, Pallas kernels: 59.6 us -> 16.1 us  [total_everywhere(): pl.pallas_call(functools.partial(total_kernel, tp_count, fsdp_count), out...]
    ppermute x3, starting transfers between devices: 18.9 us -> 3.83 us  [shifted_scatter(): lax.ppermute(block, 'tp', [(i, (i + shift) % count) for i in range(count)])]
    pallas_call x2 -> x3, Pallas kernels: 129 us -> 116 us  [experts_step(): pl.pallas_call(functools.partial(experts_kernel, first, capacity), grid_s...]
  transfers between devices with their start and end apart: 12 -> 11, of which waited for: 2 -> 3; matrix products, arithmetic and copies ran while one was open for 6% -> 7% of each run, Pallas kernels for 44% -> 80%
where the time goes in v3:
time: 766 us; the launch traced here: 757 us
  Pallas kernels  615 us (80%)
  waiting for transfers between devices  61.2 us (8%)
  other arithmetic  26.8 us (3%)
  local copies, waits for them, and re-layouts  26.1 us (3%)
  between operations  14.4 us (2%)
    pallas_call x2, Pallas kernels, line_scatter(): pl.pallas_call(functools.partial(line_scatter_kernel, count, len(parts)),...  151 us
    pallas_call x3, Pallas kernels, experts_step(): pl.pallas_call(functools.partial(experts_kernel, first, capacity), grid_s...  116 us
    pallas_call x2, Pallas kernels, line_gather(): pl.pallas_call(functools.partial(line_gather_kernel, count), out_shape=ja...  108 us
    pallas_call x1, Pallas kernels, gather_both(): pl.pallas_call(functools.partial(gather_both_kernel, tp_count, fsdp_count...  81.8 us
    pallas_call x1, Pallas kernels, scatter_both(): pl.pallas_call(functools.partial(scatter_both_kernel, tp_count, fsdp_coun...  62.7 us
    ppermute x3, waiting for transfers between devices, shifted_scatter(): lax.ppermute(block, 'tp', [(i, (i + shift) % count) for i in range(count)])  61.1 us
    pallas_call x1, Pallas kernels, attend_back(): pl.pallas_call(attend_back_kernel, grid=(group // SEQ,), in_specs=[by_row...  37.3 us
    pallas_call x1, Pallas kernels, attend(): pl.pallas_call(attend_kernel, grid=(seqs,), in_specs=[by_row(width), fixe...  19.8 us
  transfers between devices with their start and end apart: 11, of which 3 were waited for; matrix products, arithmetic and copies ran while one was open for 7% of the time, Pallas kernels for 80%

profile of v3, /device:TPU:0, one launch (start us, length us, event | category | flops | bytes accessed | tf_op | source)
XLA Modules:
  0.0 757.2 jit_solution(4105144234182394969)
XLA Ops:
  7.2 4.9 shard_map.233
  12.2 5.0 shard_map.236
  21.1 81.8 %shard_map.229 = (bf16[1024,1536]{1,0:T(8,128)(2,1)}, bf16[1536,1152]{1,0:T(8,128)(2,1)}) custom-call(bf16[256,1536]{1,0:T(8,128)(2,1)} %fusion.9.x_ref, bf16[192,1152]{1,0:T(8,128)(2,1)} %copy-done.10), custom_call_target="tpu_custom_call" | custom-call | bytes 150000000 | tf_op jit(solution)/shard_map/pallas_call | solution.py:231
  109.3 19.8 %shard_map.230 = (bf16[6,1024,64]{2,1,0:T(8,128)(2,1)}, bf16[2,1024,64]{2,1,0:T(8,128)(2,1)}, bf16[2,1024,64]{2,1,0:T(8,128)(2,1)}, bf16[1024,384]{1,0:T(8,128)(...) custom-call(bf16[1024,1536]{1,0:T(8,128)(2,1)} %get-tuple-element.49.x_ref, ...), custom_call_target="tpu_custom_call" | custom-call | flops 10000000000 | bytes 60000000 | tf_op jit(solution)/shard_map/pallas_call | solution.py:803
  129.2 77.0 %shard_map.231 = f32[256,1536]{1,0:T(8,128)} custom-call(bf16[1024,1536]{1,0:T(8,128)(2,1)} %get-tuple-element.51.refs_0_), custom_call_target="tpu_custom_call" | custom-call | bytes 150000000 | tf_op jit(solution)/shard_map/pallas_call | solution.py:341
  206.1 2.3 multiply_reduce_fusion.2
  210.7 51.3 %shard_map.232.x_ref.moe_rows = bf16[1024,1536]{1,0:T(8,128)(2,1)} custom-call(bf16[256,1536]{1,0:T(8,128)(2,1)} %multiply_convert_fusion.1.x_ref), custom_call_target="tpu_custom_call" | custom-call | bytes 150000000 | tf_op jit(solution)/shard_map/pallas_call | solution.py:164
  262.7 3.3 select_reduce_fusion
  268.3 1.9 broadcast_in_dim.67
  271.2 2.1 constant_dynamic-update-slice_fusion.6
  273.3 2.1 constant_dynamic-update-slice_fusion.5
  276.4 26.0 %shard_map.234 = (bf16[1024,1536]{1,0:T(8,128)(2,1)}, bf16[1024,1664]{1,0:T(8,128)(2,1)}, bf16[2,3,1536,512]{3,2,1,0:T(8,128)(2,1)}) custom-call(s32[11]{0:T(128)} %pad_add_fusion.meta, s32[10,1,1024]{2,1,0:T(1,128)} %copy.79.place_row, s32[1024,10]{1,0:T(8,128)} %copy-done.11, f32[10,1,1024]{2,1,0:T(1,128)} %broadcast_in_dim.66.gate_row, ...), custom_call_target="tpu_custom_call" | custom-call | flops 21818769408 | bytes 18874368 | tf_op jit(solution)/shard_map/pallas_call | solution.py:576
  302.4 40.4 %shard_map.235 = (bf16[1024,1536]{1,0:T(8,128)(2,1)}, bf16[1024,1664]{1,0:T(8,128)(2,1)}, bf16[3,3,1536,512]{3,2,1,0:T(8,128)(2,1)}) custom-call(s32[11]{0:T(128)} %pad_add_fusion.meta, s32[10,1,1024]{2,1,0:T(1,128)} %copy.79.place_row, s32[1024,10]{1,0:T(8,128)} %copy-done.11, f32[10,1,1024]{2,1,0:T(1,128)} %broadcast_in_dim.66.gate_row, ...), custom_call_target="tpu_custom_call" | custom-call | flops 32728154112 | bytes 28311552 | tf_op jit(solution)/shard_map/pallas_call | solution.py:576
  342.9 49.4 %shard_map.237 = (bf16[1024,1536]{1,0:T(8,128)(2,1)}, bf16[1024,1664]{1,0:T(8,128)(2,1)}, bf16[5,3,1536,512]{3,2,1,0:T(8,128)(2,1)}) custom-call(s32[11]{0:T(128)} %pad_add_fusion.meta, s32[10,1,1024]{2,1,0:T(1,128)} %copy.79.place_row, s32[1024,10]{1,0:T(8,128)} %copy-done.11, f32[10,1,1024]{2,1,0:T(1,128)} %broadcast_in_dim.66.gate_row, ...), custom_call_target="tpu_custom_call" | custom-call | flops 54546923520 | bytes 47185920 | tf_op jit(solution)/shard_map/pallas_call | solution.py:576
  395.1 74.3 %shard_map.238 = f32[256,1664]{1,0:T(8,128)} custom-call(bf16[1024,1664]{1,0:T(8,128)(2,1)} %get-tuple-element.56.refs_0_, bf16[1024,1664]{1,0:T(8,128)(2,1)} %get-tuple-element.57.refs_1_, bf16[1024,1664]{1,0:T(8,128)(2,1)} %get-tuple-element.58.refs_2_), custom_call_target="tpu_custom_call" | custom-call | bytes 150000000 | tf_op jit(solution)/shard_map/pallas_call | solution.py:341
  471.7 2.2 multiply_reduce_fusion
  473.9 2.2 multiply_convert_fusion
  477.1 57.1 %shard_map.239.branch_grad = bf16[1024,1664]{1,0:T(8,128)(2,1)} custom-call(bf16[256,1664]{1,0:T(8,128)(2,1)} %fusion.20.x_ref), custom_call_target="tpu_custom_call" | custom-call | bytes 150000000 | tf_op jit(solution)/shard_map/pallas_call | solution.py:164
  534.2 37.3 %shard_map.240 = (bf16[1024,1536]{1,0:T(8,128)(2,1)}, bf16[1536,1152]{1,0:T(8,128)(2,1)}) custom-call(bf16[1024,1536]{1,0:T(8,128)(2,1)} %get-tuple-element.49.x_ref, bf16[1536,1152]{1,0:T(8,128)(2,1)} %get-tuple-element.50.w_ref, s32[2,1,512]{2,1,0:T(1,128)} %broadcast_in_dim.32.seg_row, s32[2,512,1]{2,1,0:T(8,128)} %copy.76.seg_col, ...), custom_call_target="tpu_custom_call" | custom-call | flops 20000000000 | bytes 100000000 | tf_op jit(solution)/shard_map/pallas_call | solution.py:850
  571.6 62.7 %shard_map.241 = (f32[256,1536]{1,0:T(8,128)}, f32[192,1152]{1,0:T(8,128)}) custom-call(bf16[1024,1536]{1,0:T(8,128)(2,1)} %get-tuple-element.68.x_ref, bf16[1536,1152]{1,0:T(8,128)(2,1)} %get-tuple-element.69.w_ref), custom_call_target="tpu_custom_call" | custom-call | bytes 150000000 | tf_op jit(solution)/shard_map/pallas_call | solution.py:419
  634.3 2.0 fusion.15
  636.9 16.1 %shard_map.242 = f32[8,384]{1,0:T(8,128)} custom-call(f32[8,384]{1,0:T(8,128)} %pad_maximum_fusion.2.x_ref), custom_call_target="tpu_custom_call" | custom-call | tf_op jit(solution)/shard_map/pallas_call | solution.py:930
  652.9 5.0 convert_add_fusion
  658.0 2.7 copy-done.4
  662.8 3.2 collective-permute-start.5
  672.4 12.3 %collective-permute-done.3 = bf16[256,1536]{1,0:T(8,128)(2,1)} collective-permute-done((bf16[256,1536]{1,0:T(8,128)(2,1)}, bf16[256,1536]{1,0:T(8,128)(2,1)}, u32[]{:S(2)}, u32[]{:S(2)}) %collective-permute-start.3) | collective-permute-done | bytes 786464 | tf_op jit(solution)/shard_map/ppermute | solution.py:983
  684.7 15.4 %collective-permute-done.5 = bf16[256,1536]{1,0:T(8,128)(2,1)} collective-permute-done((bf16[256,1536]{1,0:T(8,128)(2,1)}, bf16[256,1536]{1,0:T(8,128)(2,1)}, u32[]{:S(2)}, u32[]{:S(2)}) %collective-permute-start.5) | collective-permute-done | bytes 786464 | tf_op jit(solution)/shard_map/ppermute | solution.py:983
  700.2 33.4 %collective-permute-done.4 = bf16[256,1536]{1,0:T(8,128)(2,1)} collective-permute-done((bf16[256,1536]{1,0:T(8,128)(2,1)}, bf16[256,1536]{1,0:T(8,128)(2,1)}, u32[]{:S(2)}, u32[]{:S(2)}) %collective-permute-start.4) | collective-permute-done | bytes 786464 | tf_op jit(solution)/shard_map/ppermute | solution.py:983
  733.6 5.2 fusion.14
  738.8 2.5 shard_map.243
  741.3 3.8 shard_map.244
  745.0 5.4 shard_map.245
  (128 shorter events, 32.8 us)
Async XLA Ops:
  7.2 269.2 %all-gather.3.cloned.1.call-start = ((), (), s32[]{:S(2)}) async-start(), calls=%async_computation.3 | async-start | bytes 26542080 | tf_op jit(solution)/shard_map/all_gather | solution.py:1018
  12.2 330.7 %all-gather.5.cloned.1.call-start = ((), (), s32[]{:S(2)}) async-start(), calls=%async_computation.4 | async-start | bytes 26542080 | tf_op jit(solution)/shard_map/all_gather | solution.py:1018
  17.2 1.0 copy-start.13
  17.2 1.3 copy-start.2
  17.3 721.5 %reduce-scatter.8.cloned.1.call-start = ((), (), s32[]{:S(2)}) async-start(), calls=%async_computation.7 | async-start | bytes 10616832 | tf_op jit(solution)/shard_map/reduce_scatter | solution.py:1100
  17.9 3.1 copy-start.14
  18.6 2.5 copy-start.10
  18.9 84.1 %copy-start.7 = (bf16[256,1536]{1,0:T(8,128)(2,1)S(1)}, bf16[256,1536]{1,0:T(8,128)(2,1)}, u32[]{:S(2)}) copy-start(bf16[256,1536]{1,0:T(8,128)(2,1)} %param.27) | copy-start | bytes 2359300
  21.1 84.2 %copy-start.21 = (s32[2,512]{1,0:T(2,128)S(1)}, s32[2,512]{1,0:T(2,128)}, u32[]{:S(2)}) copy-start(s32[2,512]{1,0:T(2,128)} %param.15) | copy-start | bytes 12292
  21.1 84.7 %copy-start.26 = (bf16[1536]{0:T(1024)(128)(2,1)S(1)}, bf16[1536]{0:T(1024)(128)(2,1)}, u32[]{:S(2)}) copy-start(bf16[1536]{0:T(1024)(128)(2,1)} %param.22) | copy-start | bytes 9220
  21.1 84.7 %copy-start.19 = (s32[1024,8]{0,1:T(8,128)S(1)}, s32[1024,8]{0,1:T(8,128)}, u32[]{:S(2)}) copy-start(s32[1024,8]{0,1:T(8,128)} %param.16) | copy-start | bytes 98308
  103.1 172.3 %collective-permute-start.2 = (bf16[256,1536]{1,0:T(8,128)(2,1)S(1)}, bf16[256,1536]{1,0:T(8,128)(2,1)S(1)}, u32[]{:S(2)}, u32[]{:S(2)}) collective-permute-start(bf16[256,1536]{1,0:T(8,128)(2,1)S(1)} %fusion.16), channel_id=1, source_target_pairs={{0,3},{1,0},{2,1},{3,2},{4,7},{5,4},{6,5},{7,6},{8,11},{9,8},{10,9... | collective-permute-start | bytes 2359304 | tf_op jit(solution)/shard_map/ppermute | solution.py:969
  104.6 168.7 %collective-permute-start.1 = (bf16[256,1536]{1,0:T(8,128)(2,1)S(1)}, bf16[256,1536]{1,0:T(8,128)(2,1)}, u32[]{:S(2)}, u32[]{:S(2)}) collective-permute-start(bf16[256,1536]{1,0:T(8,128)(2,1)S(1)} %fusion.16), channel_id=1, source_target_pairs={{0,2},{1,3},{2,0},{3,1},{4,6},{5,7},{6,4},{7,5},{8,10},{9,11},{10,... | collective-permute-start | bytes 2359304 | tf_op jit(solution)/shard_map/ppermute | solution.py:969
  104.6 166.6 %collective-permute-start = (bf16[256,1536]{1,0:T(8,128)(2,1)S(1)}, bf16[256,1536]{1,0:T(8,128)(2,1)}, u32[]{:S(2)}, u32[]{:S(2)}) collective-permute-start(bf16[256,1536]{1,0:T(8,128)(2,1)S(1)} %fusion.16), channel_id=1, source_target_pairs={{0,1},{1,2},{2,3},{3,0},{4,5},{5,6},{6,7},{7,4},{8,9},{9,10},{10,1... | collective-permute-start | bytes 2359304 | tf_op jit(solution)/shard_map/ppermute | solution.py:969
  208.4 1.2 copy-start
  262.7 4.2 copy-start.11
  302.4 438.9 %reduce-scatter.6.cloned.1.call-start = ((), (), s32[]{:S(2)}) async-start(), calls=%async_computation.6 | async-start | bytes 15925248 | tf_op jit(solution)/shard_map/reduce_scatter | solution.py:1100
  342.9 402.2 %reduce-scatter.4.cloned.1.call-start = ((), (), s32[]{:S(2)}) async-start(), calls=%async_computation.5 | async-start | bytes 26542080 | tf_op jit(solution)/shard_map/reduce_scatter | solution.py:1100
  392.3 1.1 copy-start.9
  395.1 76.6 %copy-start.1 = (f32[256,1536]{1,0:T(8,128)S(1)}, f32[256,1536]{1,0:T(8,128)}, u32[]{:S(2)}) copy-start(f32[256,1536]{1,0:T(8,128)} %copy-done) | copy-start | bytes 4718596
  473.9 2.2 copy-start.5
  571.6 62.7 %copy-start.3 = (bf16[256,1536]{1,0:T(8,128)(2,1)S(1)}, bf16[256,1536]{1,0:T(8,128)(2,1)}, u32[]{:S(2)}) copy-start(bf16[256,1536]{1,0:T(8,128)(2,1)} %param.14) | copy-start | bytes 2359300
  571.6 62.7 %copy-start.15 = (f32[1536]{0:T(1024)S(1)}, f32[1536]{0:T(1024)}, u32[]{:S(2)}) copy-start(f32[1536]{0:T(1024)} %copy-done.14) | copy-start | bytes 18436
  571.6 62.7 %copy-start.23 = (f32[256]{0:T(256)S(1)}, f32[256]{0:T(256)}, u32[]{:S(2)}) copy-start(f32[256]{0:T(256)} %copy-done.22) | copy-start | bytes 3076
  658.0 2.7 copy-start.4
  660.7 5.3 copy-start.18
  660.7 72.9 %copy-start.8 = (bf16[256,1536]{1,0:T(8,128)(2,1)S(1)}, bf16[256,1536]{1,0:T(8,128)(2,1)}, u32[]{:S(2)}) copy-start(bf16[256,1536]{1,0:T(8,128)(2,1)} %param.27) | copy-start | bytes 2359300
  662.1 71.4 %copy-start.24 = (f32[256]{0:T(256)S(1)}, f32[256]{0:T(256)}, u32[]{:S(2)}) copy-start(f32[256]{0:T(256)} %get-tuple-element.154) | copy-start | bytes 3076
  662.1 22.6 %collective-permute-start.3 = (bf16[256,1536]{1,0:T(8,128)(2,1)}, bf16[256,1536]{1,0:T(8,128)(2,1)}, u32[]{:S(2)}, u32[]{:S(2)}) collective-permute-start(bf16[256,1536]{1,0:T(8,128)(2,1)} %get-tuple-element.140), channel_id=1, source_target_pairs={{0,1},{1,2},{2,3},{3,0},{4,5},{5,6},{6,7},{7,4},{8,9},{9,10},{10,1... | collective-permute-start | bytes 2359304 | tf_op jit(solution)/shard_map/ppermute | solution.py:983
  662.8 37.3 %collective-permute-start.5 = (bf16[256,1536]{1,0:T(8,128)(2,1)}, bf16[256,1536]{1,0:T(8,128)(2,1)}, u32[]{:S(2)}, u32[]{:S(2)}) collective-permute-start(bf16[256,1536]{1,0:T(8,128)(2,1)} %get-tuple-element.141), channel_id=1, source_target_pairs={{0,3},{1,0},{2,1},{3,2},{4,7},{5,4},{6,5},{7,6},{8,11},{9,8},{10,9... | collective-permute-start | bytes 2359304 | tf_op jit(solution)/shard_map/ppermute | solution.py:983
  666.0 67.6 %collective-permute-start.4 = (bf16[256,1536]{1,0:T(8,128)(2,1)}, bf16[256,1536]{1,0:T(8,128)(2,1)}, u32[]{:S(2)}, u32[]{:S(2)}) collective-permute-start(bf16[256,1536]{1,0:T(8,128)(2,1)} %get-tuple-element.142), channel_id=1, source_target_pairs={{0,2},{1,3},{2,0},{3,1},{4,6},{5,7},{6,4},{7,5},{8,10},{9,11},{10,... | collective-permute-start | bytes 2359304 | tf_op jit(solution)/shard_map/ppermute | solution.py:983
  668.8 64.8 %copy-start.6 = (f32[256,1536]{1,0:T(8,128)S(1)}, f32[256,1536]{1,0:T(8,128)}, u32[]{:S(2)}) copy-start(f32[256,1536]{1,0:T(8,128)} %copy-done.5) | copy-start | bytes 4718596
  (6 other events, 4.8 us)
Sparse Core Ops, SparseCore 0:
  12.3 139.8 all-gather.2
  154.6 118.5 all-gather.4
  302.5 86.6 reduce-scatter.7
  392.6 99.5 reduce-scatter.5
  495.7 168.3 reduce-scatter.3

commit v4 on v3

--- a/solution.py
+++ b/solution.py
@@ -29,19 +29,6 @@
     return lax.dot_general(
         left_op, right_op, (((0,), (0,)), ((), ())), preferred_element_type=jnp.float32
     )
-
-
-def rms_forward(values, gain_vec):
-    inverse = lax.rsqrt(jnp.mean(values * values, axis=-1, keepdims=True) + norm_eps)
-    return (values * inverse * gain_vec, inverse)
-
-
-def rms_backward(incoming, values, inverse, gain_vec):
-    scaled = values * inverse
-    gain_grad = jnp.sum(incoming * scaled, axis=0)
-    weighted = incoming * gain_vec
-    row_inner = jnp.mean(weighted * scaled, axis=-1, keepdims=True)
-    return (inverse * (weighted - scaled * row_inner), gain_grad)
 
 
 def line_signal(barrier, me, count):
@@ -82,12 +69,11 @@
 
 
 class LineGather:
-    def __init__(self, count, x_ref, o_ref, send_sem, recv_sem, own_sem):
-        self.count, self.x_ref, self.o_ref = count, x_ref, o_ref
+    def __init__(self, count, o_ref, send_sem, recv_sem):
+        self.count, self.o_ref = count, o_ref
         self.send_sem, self.recv_sem = send_sem, recv_sem
-        self.rows = x_ref.shape[0]
+        self.rows = o_ref.shape[0] // count
         me = self.me = lax.axis_index("tp")
-        self.own = pltpu.make_async_copy(x_ref, rows_of(o_ref, me, self.rows), own_sem)
         steps = range(count - 1)
         self.sends = [
             [(me >= step) & (me < count - 1) for step in steps],
@@ -101,7 +87,7 @@
     def hop(self, way, step, chunk):
         part = rows_of(self.o_ref, chunk, self.rows)
         return pltpu.make_async_remote_copy(
-            src_ref=self.x_ref if step == 0 else part,
+            src_ref=part,
             dst_ref=part,
             send_sem=self.send_sem.at[way, step],
             recv_sem=self.recv_sem.at[way, step],
@@ -117,9 +103,6 @@
         def _():
             self.hop(1, step, self.me + step).start()
 
-        if step == 0:
-            self.own.start()
-
     def arrive(self, step):
         @pl.when(self.gets[0][step])
         def _():
@@ -130,7 +113,6 @@
             self.hop(1, step, self.me + 1 + step).wait_recv()
 
     def finish(self):
-        self.own.wait()
         for step in range(self.count - 1):
 
             @pl.when(self.sends[0][step])
@@ -140,16 +122,6 @@
             @pl.when(self.sends[1][step])
             def _():
                 self.hop(1, step, self.me + step).wait_send()
-
-
-def line_gather_kernel(count, x_ref, o_ref, *sems):
-    barrier = pltpu.get_barrier_semaphore()
-    pl.semaphore_wait(barrier, line_signal(barrier, lax.axis_index("tp"), count))
-    line = LineGather(count, x_ref, o_ref, *sems)
-    for step in range(count - 1):
-        line.start(step)
-        line.arrive(step)
-    line.finish()
 
 
 def line_sems(count):
@@ -157,97 +129,6 @@
         pltpu.SemaphoreType.DMA((2, count - 1)),
         pltpu.SemaphoreType.DMA((2, count - 1)),
     ]
-
-
-def line_gather(rows_in, count, ident):
-    rows, width = rows_in.shape
-    return pl.pallas_call(
-        functools.partial(line_gather_kernel, count),
-        out_shape=jax.ShapeDtypeStruct((rows * count, width), rows_in.dtype),
-        in_specs=[pl.BlockSpec(memory_space=pltpu.VMEM)],
-        out_specs=pl.BlockSpec(memory_space=pl.ANY),
-        scratch_shapes=line_sems(count) + [pltpu.SemaphoreType.DMA],
-        compiler_params=pltpu.CompilerParams(collective_id=ident, has_side_effects=True),
-        cost_estimate=pl.CostEstimate(flops=0, transcendentals=0, bytes_accessed=150_000_000),
-    )(rows_in)
-
-
-def gather_both_kernel(
-    tp_count, fsdp_count, x_ref, w_ref, o_ref, wo_ref,
-    line_send, line_recv, own_sem, out_send, out_recv, on_send, on_recv, kept_sem,
-):
-    plane = Plane(fsdp_count)
-    barrier = pltpu.get_barrier_semaphore()
-    waits = line_signal(barrier, lax.axis_index("tp"), tp_count) + plane.signal(barrier)
-    pl.semaphore_wait(barrier, waits)
-    line = LineGather(tp_count, x_ref, o_ref, line_send, line_recv, own_sem)
-    rows = w_ref.shape[0]
-
-    def outward(shift, target, source_device):
-        return pltpu.make_async_remote_copy(
-            src_ref=w_ref,
-            dst_ref=rows_of(wo_ref, source_device, rows),
-            send_sem=out_send.at[shift],
-            recv_sem=out_recv.at[shift],
-            device_id={"fsdp": target},
-        )
-
-    def onward(shift, source_device):
-        part = rows_of(wo_ref, source_device, rows)
-        return pltpu.make_async_remote_copy(
-            src_ref=part,
-            dst_ref=part,
-            send_sem=on_send.at[shift - 1],
-            recv_sem=on_recv.at[shift - 1],
-            device_id={"fsdp": plane.partner},
-        )
-
-    kept = pltpu.make_async_copy(w_ref, rows_of(wo_ref, plane.me, rows), kept_sem)
-    line.start(0)
-    for shift in range(1, plane.chips):
-        outward(shift, plane.peer(shift), plane.me).start()
-    outward(0, plane.partner, plane.me).start()
-    kept.start()
-    for shift in range(1, plane.chips):
-        outward(shift, plane.peer(shift), plane.peer(-shift)).wait_recv()
-        onward(shift, plane.peer(-shift)).start()
-    line.arrive(0)
-    for step in range(1, tp_count - 1):
-        line.start(step)
-        line.arrive(step)
-    outward(0, plane.partner, plane.partner).wait_recv()
-    for shift in range(1, plane.chips):
-        onward(shift, plane.chip_at(-shift) * 2 + 1 - plane.core).wait_recv()
-    for shift in range(1, plane.chips):
-        outward(shift, plane.peer(shift), plane.me).wait_send()
-        onward(shift, plane.peer(-shift)).wait_send()
-    outward(0, plane.partner, plane.me).wait_send()
-    kept.wait()
-    line.finish()
-
-
-def gather_both(rows_in, weights, tp_count, fsdp_count, ident):
-    chips = fsdp_count // 2
-    return pl.pallas_call(
-        functools.partial(gather_both_kernel, tp_count, fsdp_count),
-        out_shape=[
-            jax.ShapeDtypeStruct((rows_in.shape[0] * tp_count, rows_in.shape[1]), rows_in.dtype),
-            jax.ShapeDtypeStruct((weights.shape[0] * fsdp_count, weights.shape[1]), weights.dtype),
-        ],
-        in_specs=[pl.BlockSpec(memory_space=pltpu.VMEM)] * 2,
-        out_specs=[pl.BlockSpec(memory_space=pl.ANY)] * 2,
-        scratch_shapes=line_sems(tp_count)
-        + [
-            pltpu.SemaphoreType.DMA,
-            pltpu.SemaphoreType.DMA((chips,)),
-            pltpu.SemaphoreType.DMA((chips,)),
-            pltpu.SemaphoreType.DMA((chips - 1,)),
-            pltpu.SemaphoreType.DMA((chips - 1,)),
-            pltpu.SemaphoreType.DMA,
-        ],
-        compiler_params=pltpu.CompilerParams(collective_id=ident, has_side_effects=True),
-        cost_estimate=pl.CostEstimate(flops=0, transcendentals=0, bytes_accessed=150_000_000),
-    )(rows_in, weights)
 
 
 class LineScatter:
@@ -303,7 +184,7 @@
             def _():
                 self.hop(way, step).wait_recv()
 
-    def finish(self):
+    def collect(self):
         self.o_ref[...] = self.block(self.me)
         for way in range(2):
 
@@ -311,22 +192,13 @@
             def _():
                 self.o_ref[...] += self.recv[way, self.count - 2].astype(jnp.float32)
 
+    def finish(self):
         for step in range(self.count - 1):
             for way in range(2):
 
                 @pl.when(self.has_next[way] & (step >= self.behind[way]))
                 def _():
                     self.hop(way, step).wait_send()
-
-
-def line_scatter_kernel(count, parts, *refs):
-    barrier = pltpu.get_barrier_semaphore()
-    pl.semaphore_wait(barrier, line_signal(barrier, lax.axis_index("tp"), count))
-    line = LineScatter(count, refs[:parts], *refs[parts:])
-    for step in range(count - 1):
-        line.start(step)
-        line.arrive(step)
-    line.finish()
 
 
 def line_buffers(count, rows, width):
@@ -336,34 +208,224 @@
     ] + line_sems(count)
 
 
-def line_scatter(parts, count, ident):
-    rows, width = parts[0].shape[0] // count, parts[0].shape[1]
+def own_rows(rows):
+    return pl.ds(pl.multiple_of(lax.axis_index("tp") * rows, rows), rows)
+
+
+def inverse_norm(values):
+    return lax.rsqrt(jnp.mean(values * values, axis=-1, keepdims=True) + norm_eps)
+
+
+def rms_back(incoming, values, gain_row):
+    inverse = inverse_norm(values)
+    scaled = values * inverse
+    gain_grad = jnp.sum(incoming * scaled, axis=0, keepdims=True)
+    weighted = incoming * gain_row
+    row_inner = jnp.mean(weighted * scaled, axis=-1, keepdims=True)
+    return inverse * (weighted - scaled * row_inner), gain_grad
+
+
+def enter_kernel(count):
+    barrier = pltpu.get_barrier_semaphore()
+    pl.semaphore_wait(barrier, line_signal(barrier, lax.axis_index("tp"), count))
+
+
+def remote_params(ident, limit=60):
+    return pltpu.CompilerParams(
+        collective_id=ident, has_side_effects=True, vmem_limit_bytes=limit << 20
+    )
+
+
+IN_VMEM = pl.BlockSpec(memory_space=pltpu.VMEM)
+IN_PLACE = pl.BlockSpec(memory_space=pl.ANY)
+TRANSFER = pl.CostEstimate(flops=0, transcendentals=0, bytes_accessed=150_000_000)
+
+
+def norm_gather_kernel(count, emb_ref, gain_ref, rows_ref, *sems):
+    enter_kernel(count)
+    line = LineGather(count, rows_ref, *sems)
+    start_x = emb_ref[...].astype(jnp.float32) * emb_scale
+    normed = start_x * inverse_norm(start_x) * gain_ref[...]
+    rows_ref[own_rows(line.rows), :] = normed.astype(jnp.bfloat16)
+    for step in range(count - 1):
+        line.start(step)
+        line.arrive(step)
+    line.finish()
+
+
+def norm_gather(emb, gain_row, count, ident):
+    rows, width = emb.shape
     return pl.pallas_call(
-        functools.partial(line_scatter_kernel, count, len(parts)),
-        out_shape=jax.ShapeDtypeStruct((rows, width), jnp.float32),
-        in_specs=[pl.BlockSpec(memory_space=pltpu.VMEM)] * len(parts),
-        out_specs=pl.BlockSpec(memory_space=pltpu.VMEM),
-        scratch_shapes=line_buffers(count, rows, width),
-        compiler_params=pltpu.CompilerParams(
-            collective_id=ident, has_side_effects=True, vmem_limit_bytes=60 << 20
-        ),
-        cost_estimate=pl.CostEstimate(flops=0, transcendentals=0, bytes_accessed=150_000_000),
-    )(*parts)
-
-
-def scatter_both_kernel(
-    tp_count, fsdp_count, x_ref, w_ref, o_ref, wo_ref,
-    line_recv, line_send, line_send_sem, line_recv_sem,
-    pair_got, chip_sums, chip_got, pair_send, pair_recv, chip_send, chip_recv,
+        functools.partial(norm_gather_kernel, count),
+        out_shape=jax.ShapeDtypeStruct((rows * count, width), jnp.bfloat16),
+        in_specs=[IN_VMEM] * 2,
+        out_specs=IN_VMEM,
+        scratch_shapes=line_sems(count),
+        compiler_params=remote_params(ident, 32),
+        cost_estimate=TRANSFER,
+    )(emb, gain_row)
+
+
+def mid_kernel(
+    count, part_ref, emb_ref, gain_ref, router_ref, mask_ref,
+    mid_ref, rows_ref, gates_ref, own_gates,
+    recv, send, sum_send, sum_recv, row_send, row_recv,
 ):
+    enter_kernel(count)
+    total = LineScatter(count, [part_ref], mid_ref, recv, send, sum_send, sum_recv)
+    line = LineGather(count, rows_ref, row_send, row_recv)
+    rows = line.rows
+    for step in range(count - 1):
+        total.start(step)
+        total.arrive(step)
+    total.collect()
+    mid = emb_ref[...].astype(jnp.float32) * emb_scale + resid_scale * mid_ref[...]
+    mid_ref[...] = mid
+    own = own_rows(rows)
+    rows_ref[own, :] = (mid * inverse_norm(mid) * gain_ref[...]).astype(jnp.bfloat16)
+
+    def find_gates(chunk):
+        area = pl.ds(pl.multiple_of(chunk * rows, rows), rows)
+        logits = jnp.dot(rows_ref[area, :], router_ref[...], preferred_element_type=jnp.float32)
+        inside = mask_ref[area, :] > 0.0
+        top = jnp.max(jnp.where(inside, logits, masked_value), axis=-1, keepdims=True)
+        raised = jnp.where(inside, jnp.exp(jnp.where(inside, logits - top, 0.0)), 0.0)
+        gates = raised / jnp.sum(raised, axis=-1, keepdims=True)
+        gates_ref[:, area] = gates.T
+        return gates
+
+    for step in range(count - 1):
+        line.start(step)
+        if step == 0:
+            own_gates[...] = find_gates(line.me)
+        line.arrive(step)
+
+        @pl.when(line.gets[0][step])
+        def _():
+            find_gates(line.me - 1 - step)
+
+        @pl.when(line.gets[1][step])
+        def _():
+            find_gates(line.me + 1 + step)
+
+    line.finish()
+    total.finish()
+
+
+def find_mid(part, emb, gain_row, weights, used, mask, count, ident):
+    rows, width = emb.shape
+    group = rows * count
+    return pl.pallas_call(
+        functools.partial(mid_kernel, count),
+        grid=(1,),
+        out_shape=[
+            jax.ShapeDtypeStruct((rows, width), jnp.float32),
+            jax.ShapeDtypeStruct((group, width), jnp.bfloat16),
+            jax.ShapeDtypeStruct((128, group), jnp.float32),
+            jax.ShapeDtypeStruct((rows, 128), jnp.float32),
+        ],
+        in_specs=[
+            IN_VMEM,
+            IN_VMEM,
+            IN_VMEM,
+            pl.BlockSpec((width, 128), lambda step: (0, used // 128)),
+            IN_VMEM,
+        ],
+        out_specs=[IN_VMEM] * 4,
+        scratch_shapes=line_buffers(count, rows, width) + line_sems(count),
+        compiler_params=remote_params(ident),
+        cost_estimate=TRANSFER,
+    )(part, emb, gain_row, weights, mask)
+
+
+def moe_back_kernel(count, runs, *refs):
+    dx_parts, y_parts, refs = refs[:runs], refs[runs : 2 * runs], refs[2 * runs :]
+    (
+        mid_ref, cotangent_ref, own_gates, gain_ref, router_ref,
+        y_ref, mid_grad, gain_grad, sent_ref,
+        sum_ref, recv, send, sum_send, sum_recv, row_send, row_recv,
+    ) = refs
+    enter_kernel(count)
+    total = LineScatter(count, dx_parts, sum_ref, recv, send, sum_send, sum_recv)
+    line = LineGather(count, sent_ref, row_send, row_recv)
+    rows, width = mid_ref.shape
+    for step in range(count - 1):
+        total.start(step)
+        if step == 0:
+            for chunk in range(count):
+                area = slice(chunk * rows, (chunk + 1) * rows)
+                whole = y_parts[0][area, :].astype(jnp.float32)
+                for y_part in y_parts[1:]:
+                    whole = whole + y_part[area, :].astype(jnp.float32)
+                y_ref[area, :] = whole.astype(y_ref.dtype)
+        total.arrive(step)
+    total.collect()
+    gates = own_gates[...]
+    gates_grad = sum_ref[:, width:]
+    gates_inner = jnp.sum(gates * gates_grad, axis=-1, keepdims=True)
+    logits_grad = (gates * (gates_grad - gates_inner)).astype(jnp.bfloat16)
+    incoming = sum_ref[:, :width] + contract_last(logits_grad, router_ref[...])
+    from_norm, gain_part = rms_back(incoming, mid_ref[...], gain_ref[...])
+    grad = cotangent_ref[...].astype(jnp.float32) + from_norm
+    mid_grad[...] = grad
+    gain_grad[...] = gain_part
+    own = own_rows(rows)
+    sent_ref[own, :width] = (resid_scale * grad).astype(jnp.bfloat16)
+    sent_ref[own, width:] = logits_grad
+    for step in range(count - 1):
+        line.start(step)
+        line.arrive(step)
+    line.finish()
+    total.finish()
+
+
+def find_mid_grad(dx_parts, y_parts, mid, cotangent, own_gates, gain_row, weights, used, count, ident):
+    rows, width = mid.shape
+    runs, group = len(dx_parts), rows * count
+    wide = dx_parts[0].shape[1]
+    return pl.pallas_call(
+        functools.partial(moe_back_kernel, count, runs),
+        grid=(1,),
+        out_shape=[
+            jax.ShapeDtypeStruct((group, width), jnp.bfloat16),
+            jax.ShapeDtypeStruct((rows, width), jnp.float32),
+            jax.ShapeDtypeStruct((1, width), jnp.float32),
+            jax.ShapeDtypeStruct((group, wide), jnp.bfloat16),
+        ],
+        in_specs=[IN_VMEM] * (2 * runs + 4)
+        + [pl.BlockSpec((width, 128), lambda step: (0, used // 128))],
+        out_specs=[IN_VMEM] * 4,
+        scratch_shapes=[pltpu.VMEM((rows, wide), jnp.float32)]
+        + line_buffers(count, rows, wide)
+        + line_sems(count),
+        compiler_params=remote_params(ident, 62),
+        cost_estimate=TRANSFER,
+    )(*dx_parts, *y_parts, mid, cotangent, own_gates, gain_row, weights)
+
+
+def finish_kernel(tp_count, fsdp_count, runs, *refs):
+    x_ref, w_ref, emb_ref, gain_ref, mid_grad, gain_two = refs[:6]
+    packed, refs = refs[6 : 6 + runs], refs[6 + runs :]
+    (
+        grad_ref, w_sum, gains_ref, *wide,
+        line_recv, line_send, line_send_sem, line_recv_sem,
+        pair_got, chip_sums, chip_got, pair_send, pair_recv, chip_send, chip_recv,
+        tp_got, fsdp_got, small_send, small_recv, narrow, broad, in_sem, out_sem,
+    ) = refs
     plane = Plane(fsdp_count)
+    tp_me, fsdp_me = lax.axis_index("tp"), plane.me
     barrier = pltpu.get_barrier_semaphore()
-    waits = line_signal(barrier, lax.axis_index("tp"), tp_count) + plane.signal(barrier)
-    pl.semaphore_wait(barrier, waits)
+    for shift in range(1, tp_count):
+        pl.semaphore_signal(barrier, inc=1, device_id={"tp": lax.rem(tp_me + shift, tp_count)})
+    for shift in range(1, fsdp_count):
+        pl.semaphore_signal(
+            barrier, inc=1, device_id={"fsdp": lax.rem(fsdp_me + shift, fsdp_count)}
+        )
+    pl.semaphore_wait(barrier, tp_count + fsdp_count - 2)
     line = LineScatter(
-        tp_count, [x_ref], o_ref, line_recv, line_send, line_send_sem, line_recv_sem
+        tp_count, [x_ref], grad_ref, line_recv, line_send, line_send_sem, line_recv_sem
     )
-    rows = wo_ref.shape[0]
+    rows = w_sum.shape[0]
 
     def to_pair(shift):
         return pltpu.make_async_remote_copy(
@@ -386,6 +448,49 @@
     def both_cores(shift):
         own = pl.ds(pl.multiple_of(plane.peer(shift) * rows, rows), rows)
         return w_ref[own, :].astype(jnp.float32) + pair_got[shift].astype(jnp.float32)
+
+    def exchange(axis, me, count, got, base):
+        copies = []
+        for shift in range(1, count):
+            copies.append(
+                pltpu.make_async_remote_copy(
+                    src_ref=gains_ref,
+                    dst_ref=got.at[me],
+                    send_sem=small_send.at[base + shift],
+                    recv_sem=small_recv.at[base + shift],
+                    device_id={axis: lax.rem(me + shift, count)},
+                )
+            )
+            copies[-1].start()
+        got[me] = gains_ref[...]
+        for copy in copies:
+            copy.wait()
+        total = got[0]
+        for index in range(1, count):
+            total = total + got[index]
+        return total
+
+    def widen_run(run):
+        base = sum(packed[index].shape[0] for index in range(run))
+
+        def one(index, carry):
+            fetch = pltpu.make_async_copy(packed[run].at[index], narrow, in_sem)
+            fetch.start()
+            fetch.wait()
+            puts = []
+            for slot in range(3):
+                broad[slot] = narrow[slot].astype(jnp.float32)
+                puts.append(
+                    pltpu.make_async_copy(
+                        broad.at[slot], wide[slot].at[base + index], out_sem.at[slot]
+                    )
+                )
+                puts[-1].start()
+            for put in puts:
+                put.wait()
+            return carry
+
+        lax.fori_loop(0, packed[run].shape[0], one, 0)
 
     line.start(0)
     order = list(range(1, plane.chips)) + [0]
@@ -396,15 +501,29 @@
         if shift > 0:
             chip_sums[shift - 1] = both_cores(shift).astype(chip_sums.dtype)
             to_chip(shift).start()
+    if runs > 0:
+        widen_run(0)
     line.arrive(0)
     for step in range(1, tp_count - 1):
         line.start(step)
+        if step < runs:
+            widen_run(step)
         line.arrive(step)
+    line.collect()
+    from_norm, gain_one = rms_back(
+        grad_ref[...], emb_ref[...].astype(jnp.float32) * emb_scale, gain_ref[...]
+    )
+    gains_ref[...] = jnp.zeros_like(gains_ref)
+    gains_ref[0:1, :] = gain_one
+    gains_ref[1:2, :] = gain_two[...]
+    grad_ref[...] = emb_scale * (mid_grad[...] + from_norm)
     total = both_cores(0)
     for shift in range(1, plane.chips):
         to_chip(shift).wait_recv()
         total = total + chip_got[shift - 1].astype(jnp.float32)
-    wo_ref[...] = total
+    w_sum[...] = total
+    gains_ref[...] = exchange("tp", tp_me, tp_count, tp_got, 0)
+    gains_ref[...] = exchange("fsdp", fsdp_me, fsdp_count, fsdp_got, tp_count)
     line.finish()
     for shift in order:
         to_pair(shift).wait_send()
@@ -412,18 +531,23 @@
             to_chip(shift).wait_send()
 
 
-def scatter_both(partial_rows, weight_grads, tp_count, fsdp_count, ident):
-    rows, width = partial_rows.shape[0] // tp_count, partial_rows.shape[1]
+def finish(dx_rows, weight_grads, emb, gain_row, mid_grad, gain_two, packed, experts, ident):
+    tp_count, fsdp_count = lax.axis_size("tp"), lax.axis_size("fsdp")
+    rows, width = emb.shape
     w_rows, w_width = weight_grads.shape[0] // fsdp_count, weight_grads.shape[1]
-    chips = fsdp_count // 2
+    chips, runs = fsdp_count // 2, len(packed)
+    shares, hidden = packed[0].shape[2:] if runs else (8, 128)
+    wide = [jax.ShapeDtypeStruct((experts, shares, hidden), jnp.float32)] * (3 if runs else 0)
     return pl.pallas_call(
-        functools.partial(scatter_both_kernel, tp_count, fsdp_count),
+        functools.partial(finish_kernel, tp_count, fsdp_count, runs),
         out_shape=[
             jax.ShapeDtypeStruct((rows, width), jnp.float32),
             jax.ShapeDtypeStruct((w_rows, w_width), jnp.float32),
-        ],
-        in_specs=[pl.BlockSpec(memory_space=pltpu.VMEM)] * 2,
-        out_specs=[pl.BlockSpec(memory_space=pltpu.VMEM)] * 2,
+            jax.ShapeDtypeStruct((8, width), jnp.float32),
+            *wide,
+        ],
+        in_specs=[IN_VMEM] * 6 + [IN_PLACE] * runs,
+        out_specs=[IN_VMEM] * 3 + [IN_PLACE] * len(wide),
         scratch_shapes=line_buffers(tp_count, rows, width)
         + [
             pltpu.VMEM((chips, w_rows, w_width), jnp.bfloat16),
@@ -433,28 +557,72 @@
             pltpu.SemaphoreType.DMA((chips,)),
             pltpu.SemaphoreType.DMA((chips - 1,)),
             pltpu.SemaphoreType.DMA((chips - 1,)),
-        ],
-        compiler_params=pltpu.CompilerParams(
-            collective_id=ident, has_side_effects=True, vmem_limit_bytes=60 << 20
-        ),
-        cost_estimate=pl.CostEstimate(flops=0, transcendentals=0, bytes_accessed=150_000_000),
-    )(partial_rows, weight_grads)
-
-
-def pack_kernel(*refs):
-    for slot, source in enumerate(refs[:-1]):
-        refs[-1][0, slot] = source[0]
+            pltpu.VMEM((tp_count, 8, width), jnp.float32),
+            pltpu.VMEM((fsdp_count, 8, width), jnp.float32),
+            pltpu.SemaphoreType.DMA((tp_count + fsdp_count,)),
+            pltpu.SemaphoreType.DMA((tp_count + fsdp_count,)),
+            pltpu.VMEM((3, shares, hidden), jnp.bfloat16),
+            pltpu.VMEM((3, shares, hidden), jnp.float32),
+            pltpu.SemaphoreType.DMA,
+            pltpu.SemaphoreType.DMA((3,)),
+        ],
+        compiler_params=remote_params(ident),
+        cost_estimate=TRANSFER,
+    )(dx_rows, weight_grads, emb, gain_row, mid_grad, gain_two, *packed)
+
+
+def pack_kernel(low, *refs):
+    sources, target, held, in_sem, out_sem = refs[:-4], *refs[-4:]
+    span = target.shape[0]
+    gets = [
+        pltpu.make_async_copy(source.at[pl.ds(low, span)], held.at[slot], in_sem.at[slot])
+        for slot, source in enumerate(sources)
+    ]
+    puts = [
+        pltpu.make_async_copy(held.at[slot], target.at[:, slot], out_sem.at[slot])
+        for slot in range(len(sources))
+    ]
+    for get in gets:
+        get.start()
+    for get, put in zip(gets, puts):
+        get.wait()
+        put.start()
+    for put in puts:
+        put.wait()
 
 
 def pack(stacks, low, high):
     _, rows, width = stacks[0].shape
+    count, span = len(stacks), high - low
     return pl.pallas_call(
-        pack_kernel,
-        grid=(high - low,),
-        in_specs=[pl.BlockSpec((1, rows, width), lambda step: (step + low, 0, 0))] * len(stacks),
-        out_specs=pl.BlockSpec((1, len(stacks), rows, width), lambda step: (step, 0, 0, 0)),
-        out_shape=jax.ShapeDtypeStruct((high - low, len(stacks), rows, width), jnp.bfloat16),
+        functools.partial(pack_kernel, low),
+        in_specs=[IN_PLACE] * count,
+        out_specs=IN_PLACE,
+        out_shape=jax.ShapeDtypeStruct((span, count, rows, width), jnp.bfloat16),
+        scratch_shapes=[
+            pltpu.VMEM((count, span, rows, width), jnp.bfloat16),
+            pltpu.SemaphoreType.DMA((count,)),
+            pltpu.SemaphoreType.DMA((count,)),
+        ],
     )(*stacks)
+
+
+def join_kernel(*refs):
+    low = 0
+    for source in refs[:-1]:
+        refs[-1][:, low : low + source.shape[1]] = source[...]
+        low += source.shape[1]
+    if low < refs[-1].shape[1]:
+        refs[-1][:, low:] = jnp.zeros((refs[-1].shape[0], refs[-1].shape[1] - low), jnp.bfloat16)
+
+
+def join(parts, width):
+    return pl.pallas_call(
+        join_kernel,
+        in_specs=[IN_VMEM] * len(parts),
+        out_specs=IN_VMEM,
+        out_shape=jax.ShapeDtypeStruct((parts[0].shape[0], width), jnp.bfloat16),
+    )(*parts)
 
 
 SLOTS = 256
@@ -466,16 +634,12 @@
     meta,
     place_row,
     place_cols,
-    gate_row,
+    gate_rows,
     x_ref,
-    g_ref,
     weights,
-    y_out,
-    dx_out,
-    grads,
-    *totals,
+    *refs,
 ):
-    y_ref, dx_ref = totals or (y_out, dx_out)
+    g_blocks, (y_ref, dx_ref, grads, g_ref, g_sem) = refs[:-5], refs[-5:]
     step = pl.program_id(0)
     expert = step + first_expert
     group, width = x_ref.shape
@@ -483,19 +647,28 @@
 
     @pl.when(step == 0)
     def _():
+        count, rows = len(g_blocks), g_blocks[0].shape[0]
+        copies = []
+        for shift, block in enumerate(g_blocks):
+            home = lax.rem(meta[meta.shape[0] - 1] + count - shift, count)
+            copies.append(pltpu.make_async_copy(block, rows_of(g_ref, home, rows), g_sem.at[shift]))
+            copies[-1].start()
         y_ref[...] = jnp.zeros_like(y_ref)
         dx_ref[...] = jnp.zeros_like(dx_ref)
+        for copy in copies:
+            copy.wait()
 
     lanes = lax.broadcasted_iota(jnp.int32, place_cols.shape, 1)
     place_col = jnp.sum(jnp.where(lanes == expert, place_cols[...], 0), axis=1, keepdims=True)
-    column = expert + meta[meta.shape[0] - 1]
+    column = expert + meta[meta.shape[0] - 2]
+    gate_row = gate_rows[pl.ds(column, 1), :].astype(jnp.bfloat16).astype(jnp.float32)
     mark = jnp.where(lax.broadcasted_iota(jnp.int32, (1, tail), 1) == column, 1.0, 0.0)
 
     def run(base, span):
         slots = lax.broadcasted_iota(jnp.int32, (span, group), 0) + base
         hit = slots == place_row[0]
         pick = jnp.where(hit, 1.0, 0.0).astype(jnp.bfloat16)
-        scale = jnp.sum(jnp.where(hit, gate_row[0], 0.0), axis=1, keepdims=True)
+        scale = jnp.sum(jnp.where(hit, gate_row, 0.0), axis=1, keepdims=True)
         x_taken = jnp.dot(pick, x_ref[...], preferred_element_type=jnp.float32).astype(jnp.bfloat16)
         g_taken = jnp.dot(pick, g_ref[...], preferred_element_type=jnp.float32).astype(jnp.bfloat16)
         gate_pre = jnp.dot(x_taken, weights[0, 0], preferred_element_type=jnp.float32)
@@ -550,16 +723,10 @@
         def _():
             run(base, span)
 
-    @pl.when((step == pl.num_programs(0) - 1) & (len(totals) > 0))
-    def _():
-        y_out[...] = y_ref[...].astype(y_out.dtype)
-        dx_out[...] = dx_ref[...].astype(dx_out.dtype)
-
-
-def experts_step(meta, place_rows, place_cols, gate_rows, x_rows, g_rows, weights, first, count, skip, capacity):
+
+def experts_step(meta, place_rows, place_cols, gate_rows, x_rows, g_blocks, weights, first, count, skip, capacity):
     group, width = x_rows.shape
     hidden = weights.shape[-1]
-    totals = [pltpu.VMEM((group, width), jnp.float32), pltpu.VMEM((group, width + 128), jnp.float32)]
     tail = 128
 
     def whole(shape):
@@ -581,17 +748,20 @@
             in_specs=[
                 row((1, 1, group)),
                 whole(place_cols.shape),
-                row((1, 1, group)),
+                whole(gate_rows.shape),
                 whole(x_rows.shape),
-                whole(g_rows.shape),
                 big(skip),
-            ],
+            ]
+            + [IN_PLACE] * len(g_blocks),
             out_specs=[
                 whole((group, width)),
                 whole((group, width + tail)),
                 big(0),
             ],
-            scratch_shapes=totals if group <= 1024 else [],
+            scratch_shapes=[
+                pltpu.VMEM((group, width), jnp.bfloat16),
+                pltpu.SemaphoreType.DMA((len(g_blocks),)),
+            ],
         ),
         out_shape=[
             jax.ShapeDtypeStruct((group, width), jnp.bfloat16),
@@ -606,7 +776,7 @@
             transcendentals=count * 408 * hidden,
             bytes_accessed=count * 12 * width * hidden,
         ),
-    )(meta, place_rows, place_cols, gate_rows, x_rows, g_rows, weights)
+    )(meta, place_rows, place_cols, gate_rows, x_rows, weights, *g_blocks)
 
 
 def rotate_head(values, cosine, sine, sign):
@@ -889,59 +1059,6 @@
       queries, keys, values, mixed, logsum, moe_rows, branch_grad)
 
 
-def total_kernel(tp_count, fsdp_count, x_ref, o_ref, tp_got, fsdp_got, send_sem, recv_sem):
-    tp_me, fsdp_me = lax.axis_index("tp"), lax.axis_index("fsdp")
-    barrier = pltpu.get_barrier_semaphore()
-    for shift in range(1, tp_count):
-        pl.semaphore_signal(barrier, inc=1, device_id={"tp": lax.rem(tp_me + shift, tp_count)})
-    for shift in range(1, fsdp_count):
-        pl.semaphore_signal(
-            barrier, inc=1, device_id={"fsdp": lax.rem(fsdp_me + shift, fsdp_count)}
-        )
-    pl.semaphore_wait(barrier, tp_count + fsdp_count - 2)
-
-    def exchange(axis, me, count, source, got, base):
-        copies = []
-        for shift in range(1, count):
-            copies.append(
-                pltpu.make_async_remote_copy(
-                    src_ref=source,
-                    dst_ref=got.at[me],
-                    send_sem=send_sem.at[base + shift],
-                    recv_sem=recv_sem.at[base + shift],
-                    device_id={axis: lax.rem(me + shift, count)},
-                )
-            )
-            copies[-1].start()
-        got[me] = source[...]
-        for copy in copies:
-            copy.wait()
-        total = got[0]
-        for index in range(1, count):
-            total = total + got[index]
-        return total
-
-    o_ref[...] = exchange("tp", tp_me, tp_count, x_ref, tp_got, 0)
-    o_ref[...] = exchange("fsdp", fsdp_me, fsdp_count, o_ref, fsdp_got, tp_count)
-
-
-def total_everywhere(values, ident):
-    tp_count, fsdp_count = lax.axis_size("tp"), lax.axis_size("fsdp")
-    return pl.pallas_call(
-        functools.partial(total_kernel, tp_count, fsdp_count),
-        out_shape=jax.ShapeDtypeStruct(values.shape, values.dtype),
-        in_specs=[pl.BlockSpec(memory_space=pltpu.VMEM)],
-        out_specs=pl.BlockSpec(memory_space=pltpu.VMEM),
-        scratch_shapes=[
-            pltpu.VMEM((tp_count,) + values.shape, values.dtype),
-            pltpu.VMEM((fsdp_count,) + values.shape, values.dtype),
-            pltpu.SemaphoreType.DMA((tp_count + fsdp_count,)),
-            pltpu.SemaphoreType.DMA((tp_count + fsdp_count,)),
-        ],
-        compiler_params=pltpu.CompilerParams(collective_id=ident, has_side_effects=True),
-    )(values)
-
-
 def widen_kernel(packed, *refs):
     for slot, target in enumerate(refs[-3:]):
         target[0] = packed[0, slot].astype(jnp.float32)
@@ -961,16 +1078,11 @@
     )(packed, *held)
 
 
-def shifted_gather(block, count, me):
-    rows = block.shape[0]
-    whole = jnp.zeros((rows * count, block.shape[1]), block.dtype)
-    whole = lax.dynamic_update_slice_in_dim(whole, block, me * rows, 0)
-    for shift in range(1, count):
-        got = lax.ppermute(block, "tp", [(i, (i + shift) % count) for i in range(count)])
-        whole = lax.dynamic_update_slice_in_dim(
-            whole, got, lax.rem(me + count - shift, count) * rows, 0
-        )
-    return whole
+def shifted_blocks(block, count):
+    return [block] + [
+        lax.ppermute(block, "tp", [(i, (i + shift) % count) for i in range(count)])
+        for shift in range(1, count)
+    ]
 
 
 def shifted_scatter(partial_rows, count, me):
@@ -985,7 +1097,6 @@
     return total
 
 
-GATHERS = 2
 RUNS = (0, 2, 5, 10)
 
 
@@ -1005,82 +1116,55 @@
     w_down,
     cotangent,
 ):
-    local_rows, width = emb.shape
-    tp_count = lax.axis_size("tp")
-    tp_index = lax.axis_index("tp")
+    local_rows, _ = emb.shape
+    tp_count, tp_index = lax.axis_size("tp"), lax.axis_index("tp")
     experts_here = w_gate.shape[0]
     expert_count = w_router.shape[1]
     q_width, kv_width = w_query.shape[1], w_key.shape[1]
     used = 2 * (q_width + kv_width)
-    lane_pad = 128 - expert_count
-    edges = [experts_here * part // GATHERS for part in range(GATHERS + 1)]
+    group_size = local_rows * tp_count
+    gathers = 2 if group_size <= 1024 else 1
+
+    moe_grad = (resid_scale * cotangent.astype(jnp.float32)).astype(jnp.bfloat16)
+    moe_grad_blocks = shifted_blocks(moe_grad, tp_count)
+    attn_w = lax.all_gather(
+        join([w_query, w_key, w_value, w_out, w_router], used + 128), "fsdp", axis=0, tiled=True
+    )
+    edges = [experts_here * part // gathers for part in range(gathers + 1)]
     pieces = [
         lax.all_gather(pack([w_gate, w_up, w_down], low, high), "fsdp", axis=2, tiled=True)
         for low, high in zip(edges[:-1], edges[1:])
     ]
-    gain_one = norm1_gain.astype(jnp.float32)
-    gain_two = norm2_gain.astype(jnp.float32)
-    start_x = emb.astype(jnp.float32) * emb_scale
-    normed_one, inverse_one = rms_forward(start_x, gain_one)
-    fsdp_count = lax.axis_size("fsdp")
-    group_rows, attn_w = gather_both(
-        normed_one.astype(jnp.bfloat16),
-        jnp.concatenate(
-            [w_query, w_key, w_value, w_out, jnp.pad(w_router, ((0, 0), (0, lane_pad)))], axis=1
-        ),
-        tp_count,
-        fsdp_count,
-        0,
-    )
-    router_w = attn_w[:, used : used + expert_count]
-    out_grad = cotangent.astype(jnp.float32)
-    moe_grad = (resid_scale * out_grad).astype(jnp.bfloat16)
-    moe_grad, group_rows = lax.optimization_barrier((moe_grad, group_rows))
-    moe_grad_rows = shifted_gather(moe_grad, tp_count, tp_index)
-    group_size = group_rows.shape[0]
+    gain_one = norm1_gain.astype(jnp.float32)[None, :]
+    gain_two = norm2_gain.astype(jnp.float32)[None, :]
+    group_rows = norm_gather(emb, gain_one, tp_count, 0)
 
     capacity = group_size * routes.shape[1] // expert_count * 2
-    all_experts = jnp.arange(expert_count, dtype=jnp.int32)
-    member_all = jnp.any(routes[:, :, None] == all_experts[None, None, :], axis=1)
-    own_member = lax.dynamic_slice_in_dim(member_all, tp_index * local_rows, local_rows, 0)
+    lanes = jnp.arange(128, dtype=jnp.int32)
+    member_all = jnp.any(routes[:, :, None] == lanes[None, None, :], axis=1)
     member = lax.dynamic_slice_in_dim(member_all, tp_index * experts_here, experts_here, 1)
     ids = jnp.arange(group_size)
     earlier = (ids[:, None] > ids[None, :]).astype(jnp.bfloat16)
     ranks = jnp.dot(earlier, member.astype(jnp.bfloat16), preferred_element_type=jnp.float32)
     places = jnp.where(member, ranks.astype(jnp.int32), -1)
     meta = jnp.concatenate(
-        [jnp.sum(member.astype(jnp.int32), axis=0), (tp_index * experts_here)[None]]
+        [jnp.sum(member.astype(jnp.int32), axis=0), jnp.stack([tp_index * experts_here, tp_index])]
     )
+    place_rows = places.T[:, None, :]
 
     tables = attend_tables()
     heads_here, kv_here = q_width // HEAD_DIM, kv_width // HEAD_DIM
     *kept, branch_part = attend(group_rows, attn_w, segment_ids, tables, heads_here, kv_here)
-    attn_branch = line_scatter([branch_part], tp_count, 2)
-    mid_x = start_x + resid_scale * attn_branch
-    normed_two, inverse_two = rms_forward(mid_x, gain_two)
-    normed_low = normed_two.astype(jnp.bfloat16)
-    moe_rows = line_gather(normed_low, tp_count, 3)
-
-    def gates_of(rows, inside):
-        logits = jnp.dot(rows, router_w, preferred_element_type=jnp.float32)
-        top = jnp.max(jnp.where(inside, logits, masked_value), axis=-1, keepdims=True)
-        raised = jnp.where(inside, jnp.exp(jnp.where(inside, logits - top, 0.0)), 0.0)
-        return raised / jnp.sum(raised, axis=-1, keepdims=True)
-
-    gates = gates_of(normed_low, own_member)
-    gates_here = lax.dynamic_slice_in_dim(
-        gates_of(moe_rows, member_all).astype(jnp.bfloat16).astype(jnp.float32),
-        tp_index * experts_here,
-        experts_here,
-        1,
+    mid_x, moe_rows, gate_rows, own_gates = find_mid(
+        branch_part, emb, gain_two, attn_w, used, member_all.astype(jnp.float32), tp_count, 1
     )
-    place_rows = places.T[:, None, :]
-    gate_rows = gates_here.T[:, None, :]
 
     outs = []
-    runs = sorted({edge * experts_here // RUNS[-1] for edge in RUNS} | set(edges))
+    runs = edges
+    if gathers > 1:
+        runs = sorted({edge * experts_here // RUNS[-1] for edge in RUNS} | set(edges))
     for first, last in zip(runs[:-1], runs[1:]):
-        home = max(index for index in range(GATHERS) if edges[index] <= first)
+        home = max(index for index in range(gathers) if edges[index] <= first)
         outs.append(
             experts_step(
                 meta,
@@ -1088,7 +1172,7 @@
                 places,
                 gate_rows,
                 moe_rows,
-                moe_grad_rows,
+                moe_grad_blocks,
                 pieces[home],
                 first,
                 last - first,
@@ -1099,35 +1183,33 @@
     grad_sums = [
         lax.psum_scatter(part[2], "fsdp", scatter_dimension=2, tiled=True) for part in outs
     ]
-    dx_sum = line_scatter([part[1] for part in outs], tp_count, 4)
-    gates_grad = dx_sum[:, width : width + expert_count]
-    gates_inner = jnp.sum(gates * gates_grad, axis=-1, keepdims=True)
-    logits_grad = (gates * (gates_grad - gates_inner)).astype(jnp.bfloat16)
-    normed_two_grad = dx_sum[:, :width] + contract_last(logits_grad, router_w)
-    mid_from_norm, gain_two_grad = rms_backward(normed_two_grad, mid_x, inverse_two, gain_two)
-    mid_grad = out_grad + mid_from_norm
-    branch_grad = (resid_scale * mid_grad).astype(jnp.bfloat16)
-    sent = line_gather(
-        jnp.concatenate([branch_grad, jnp.pad(logits_grad, ((0, 0), (0, lane_pad)))], axis=1),
+    y_part, mid_grad, gain_two_grad, sent = find_mid_grad(
+        [part[1] for part in outs],
+        [part[0] for part in outs],
+        mid_x,
+        cotangent,
+        own_gates,
+        gain_two,
+        attn_w,
+        used,
         tp_count,
-        5,
-    )
-    y_parts, sent = lax.optimization_barrier(([part[0] for part in outs], sent))
-    y_part = functools.reduce(
-        lambda one, two: one + two, [part.astype(jnp.float32) for part in y_parts]
+        2,
     )
     moe_sum = shifted_scatter(y_part, tp_count, tp_index)
     out = (mid_x + resid_scale * moe_sum).astype(jnp.bfloat16)
     dx_one, attn_grads = attend_back(group_rows, attn_w, segment_ids, tables, kept, moe_rows, sent)
-    normed_one_grad, attn_sum = scatter_both(dx_one, attn_grads, tp_count, fsdp_count, 7)
-    start_from_norm, gain_one_grad = rms_backward(normed_one_grad, start_x, inverse_one, gain_one)
-    grad_emb = emb_scale * (mid_grad + start_from_norm)
-    gain_sums = total_everywhere(
-        jnp.concatenate([gain_one_grad, gain_two_grad]).reshape(8, -1), 8
-    ).reshape(2, width)
-    expert_sums = ()
-    for first, part in zip(runs[:-1], grad_sums):
-        expert_sums = widen(part, experts_here, first, expert_sums)
+    grad_emb, attn_sum, gain_sums, *expert_sums = finish(
+        dx_one,
+        attn_grads,
+        emb,
+        gain_one,
+        mid_grad,
+        gain_two_grad,
+        grad_sums[:-1],
+        experts_here,
+        3,
+    )
+    expert_sums = widen(grad_sums[-1], experts_here, runs[-2], expert_sums)
     return (
         out,
         grad_emb,

time: 766 us -> 728 us (0.950)
  waiting for transfers between devices: 61.2 us -> 27.8 us
  other arithmetic: 26.8 us -> 12.3 us
  Pallas kernels: 615 us -> 623 us
    ppermute x3, waiting for transfers between devices: 61.1 us -> 27.7 us  [shifted_scatter(): lax.ppermute(block, 'tp', [(i, (i + shift) % count) for i in range(count)])]
    pallas_call x9 -> x7, Pallas kernels: 430 us -> 444 us  [the longest x1 139 us: find_mid_grad(): pl.pallas_call(functools.partial(moe_back_kernel, count, runs), grid=(1,)...]
    unnamed x63 -> x37, local copies, waits for them, and re-layouts: 7.74 us -> 17.1 us
  transfers between devices with their start and end apart: 11 -> 12, of which waited for: 3 -> 1; matrix products, arithmetic and copies ran while one was open for 7% -> 4% of each run, Pallas kernels for 80% -> 86%
where the time goes in v4:
time: 728 us; the launch traced here: 718 us
  Pallas kernels  623 us (86%)
  local copies, waits for them, and re-layouts  29 us (4%)
  waiting for transfers between devices  27.8 us (4%)
  between operations  14.9 us (2%)
  other arithmetic  12.3 us (2%)
  starting transfers between devices  10.2 us (1%)
    pallas_call x1, Pallas kernels, find_mid_grad(): pl.pallas_call(functools.partial(moe_back_kernel, count, runs), grid=(1,)...  139 us
    pallas_call x3, Pallas kernels, experts_step(): pl.pallas_call(functools.partial(experts_kernel, first, capacity), grid_s...  117 us
    pallas_call x1, Pallas kernels, find_mid(): pl.pallas_call(functools.partial(mid_kernel, count), grid=(1,), out_shape...  110 us
    pallas_call x1, Pallas kernels, norm_gather(): pl.pallas_call(functools.partial(norm_gather_kernel, count), out_shape=ja...  109 us
    pallas_call x1, Pallas kernels, finish(): pl.pallas_call(functools.partial(finish_kernel, tp_count, fsdp_count, run...  78.5 us
    pallas_call x1, Pallas kernels, attend_back(): pl.pallas_call(attend_back_kernel, grid=(group // SEQ,), in_specs=[by_row...  36.7 us
    ppermute x3, waiting for transfers between devices, shifted_scatter(): lax.ppermute(block, 'tp', [(i, (i + shift) % count) for i in range(count)])  27.7 us
    pallas_call x1, Pallas kernels, attend(): pl.pallas_call(attend_kernel, grid=(seqs,), in_specs=[by_row(width), fixe...  19.7 us
  transfers between devices with their start and end apart: 12, of which 1 were waited for; matrix products, arithmetic and copies ran while one was open for 4% of the time, Pallas kernels for 86%

profile of v4, /device:TPU:0, one launch (start us, length us, event | category | flops | bytes accessed | tf_op | source)
XLA Modules:
  0.0 717.8 jit_solution(12232707914103932133)
XLA Ops:
  7.2 1.4 copy.54.refs_4_
  8.7 1.8 shard_map.230
  10.6 2.8 shard_map.233
  13.5 2.8 shard_map.236
  17.6 5.1 collective-permute-start.2
  22.8 1.0 collective-permute-start
  25.0 1.0 copy.56.seg_col
  26.3 5.8 fusion
  34.5 108.8 %shard_map.229.x_ref = bf16[1024,1536]{1,0:T(8,128)(2,1)S(1)} custom-call(bf16[256,1536]{1,0:T(8,128)(2,1)S(1)} %copy-done, f32[1,1536]{1,0:T(1,128)S(1)} %reshape.36.gain_ref.refs_3_), custom_call_target="tpu_custom_call" | custom-call | bytes 150000000 | tf_op jit(solution)/shard_map/pallas_call | solution.py:258
  143.3 1.7 copy-done.1
  146.8 1.0 pad_maximum_fusion
  147.8 19.7 %shard_map.231 = (bf16[6,1024,64]{2,1,0:T(8,128)(2,1)}, bf16[2,1024,64]{2,1,0:T(8,128)(2,1)}, bf16[2,1024,64]{2,1,0:T(8,128)(2,1)}, bf16[1024,384]{1,0:T(8,128)(...) custom-call(bf16[1024,1536]{1,0:T(8,128)(2,1)} %copy-done.1, ...), custom_call_target="tpu_custom_call" | custom-call | flops 10000000000 | bytes 60000000 | tf_op jit(solution)/shard_map/pallas_call | solution.py:973
  167.5 110.4 %shard_map.232 = (f32[256,1536]{1,0:T(8,128)}, bf16[1024,1536]{1,0:T(8,128)(2,1)}, f32[128,1024]{1,0:T(8,128)}, f32[256,128]{1,0:T(8,128)}) custom-call(bf16[1024,1536]{1,0:T(8,128)(2,1)} %get-tuple-element.46.part_ref, bf16[256,1536]{1,0:T(8,128)(2,1)} %refs_2_.7, f32[1,1536]{1,0:T(1,128)} %reshape.37.gain_ref.refs_9_, ...), custom_call_target="tpu_custom_call" | custom-call | bytes 150000000 | tf_op jit(solution)/shard_map/pallas_call | solution.py:318
  278.9 26.5 %shard_map.234 = (bf16[1024,1536]{1,0:T(8,128)(2,1)}, bf16[1024,1664]{1,0:T(8,128)(2,1)}, bf16[2,3,1536,512]{3,2,1,0:T(8,128)(2,1)}) custom-call(s32[12]{0:T(128)} %pad_add_fusion.meta, s32[10,1,1024]{2,1,0:T(1,128)} %copy.59.place_row, s32[1024,10]{1,0:T(8,128)} %copy-done.9, f32[128,1024]{1,0:T(8,128)} %get-tuple-element.48.gate_rows, ...), custom_call_target="tpu_custom_call" | custom-call | flops 21818769408 | bytes 18874368 | tf_op jit(solution)/shard_map/pallas_call | solution.py:743
  305.4 40.6 %shard_map.235 = (bf16[1024,1536]{1,0:T(8,128)(2,1)}, bf16[1024,1664]{1,0:T(8,128)(2,1)}, bf16[3,3,1536,512]{3,2,1,0:T(8,128)(2,1)}) custom-call(s32[12]{0:T(128)} %pad_add_fusion.meta, s32[10,1,1024]{2,1,0:T(1,128)} %copy.59.place_row, s32[1024,10]{1,0:T(8,128)} %copy-done.9, f32[128,1024]{1,0:T(8,128)} %get-tuple-element.48.gate_rows, ...), custom_call_target="tpu_custom_call" | custom-call | flops 32728154112 | bytes 28311552 | tf_op jit(solution)/shard_map/pallas_call | solution.py:743
  346.1 49.5 %shard_map.237 = (bf16[1024,1536]{1,0:T(8,128)(2,1)}, bf16[1024,1664]{1,0:T(8,128)(2,1)}, bf16[5,3,1536,512]{3,2,1,0:T(8,128)(2,1)}) custom-call(s32[12]{0:T(128)} %pad_add_fusion.meta, s32[10,1,1024]{2,1,0:T(1,128)} %copy.59.place_row, s32[1024,10]{1,0:T(8,128)} %copy-done.9, f32[128,1024]{1,0:T(8,128)} %get-tuple-element.48.gate_rows, ...), custom_call_target="tpu_custom_call" | custom-call | flops 54546923520 | bytes 47185920 | tf_op jit(solution)/shard_map/pallas_call | solution.py:743
  395.7 138.8 %shard_map.238 = (bf16[1024,1536]{1,0:T(8,128)(2,1)}, f32[256,1536]{1,0:T(8,128)}, f32[1,1536]{1,0:T(1,128)}, bf16[1024,1664]{1,0:T(8,128)(2,1)}) custom-call(bf16[1024,1664]{1,0:T(8,128)(2,1)} %get-tuple-element.50.refs_0_, bf16[1024,1664]{1,0:T(8,128)(2,1)} %get-tuple-element.51.refs_1_, bf16[1024,1664]{1,0:T(8,128)(2,1)} %get-tuple-element.52.refs_2_, ...), custom_call_target="tpu_custom_call" | custom-call | bytes 150000000 | tf_op jit(solution)/shard_map/pallas_call | solution.py:386
  534.6 2.9 constant_dynamic-slice_fusion.2
  537.5 3.8 collective-permute-start.5
  541.3 36.7 %shard_map.239 = (bf16[1024,1536]{1,0:T(8,128)(2,1)}, bf16[1536,1152]{1,0:T(8,128)(2,1)}) custom-call(bf16[1024,1536]{1,0:T(8,128)(2,1)} %copy-done.1, bf16[1536,1152]{1,0:T(8,128)(2,1)} %all-gather.4.cloned.1.call-done.w_ref.router_ref.refs_10_, s32[2,1,512]{2,1,0:T(1,128)} %broadcast_in_dim.33.seg_row, s32[2,512,1]{2,1,0:T(8,128)} %copy.56.seg_col, ...), custom_call_target="tpu_custom_call" | custom-call | flops 20000000000 | bytes 100000000 | tf_op jit(solution)/shard_map/pallas_call | solution.py:1020
  578.0 27.7 %collective-permute-done.4 = bf16[256,1536]{1,0:T(8,128)(2,1)} collective-permute-done((bf16[256,1536]{1,0:T(8,128)(2,1)S(1)}, bf16[256,1536]{1,0:T(8,128)(2,1)}, u32[]{:S(2)}, u32[]{:S(2)}) %collective-permute-start.4) | collective-permute-done | bytes 786464 | tf_op jit(solution)/shard_map/ppermute | solution.py:1095
  605.7 2.8 add_convert_fusion
  608.5 78.5 %shard_map.240 = (f32[256,1536]{1,0:T(8,128)}, f32[192,1152]{1,0:T(8,128)}, f32[8,1536]{1,0:T(8,128)}, f32[10,192,512]{2,1,0:T(8,128)}, f32[10,192,512]{2,1,0:T(8,128)}, /*index=5*/f32[10,192,512]{2,1,0:T(8,128)}) custom-call(bf16[1024,1536]{1,0:T(8,128)(2,1)} %get-tuple-element.64.refs_0_, bf16[1536,1152]{1,0:T(8,128)(2,1)} %get-tuple-element.65.refs_1_, ...), custom_call_target="tpu_custom_call" | custom-call | bytes 150000000 | tf_op jit(solution)/shard_map/pallas_call | solution.py:541
  688.6 1.5 slice_reduce_fusion
  690.1 1.6 fusion.8
  691.8 1.9 fusion.7
  693.7 5.6 shard_map.241
  699.2 1.1 copy.72
  700.4 4.6 copy.73
  705.0 2.0 copy.74
  707.0 1.5 copy-done.4
  708.5 1.9 copy.75
  (69 shorter events, 9.7 us)
Async XLA Ops:
  7.2 140.6 %all-gather.4.cloned.1.call-start = ((), (), s32[]{:S(2)}) async-start(), calls=%async_computation.3 | async-start | bytes 3981312 | tf_op jit(solution)/shard_map/all_gather | solution.py:1130
  10.5 268.3 %all-gather.6.cloned.1.call-start = ((), (), s32[]{:S(2)}) async-start(), calls=%async_computation.4 | async-start | bytes 26542080 | tf_op jit(solution)/shard_map/all_gather | solution.py:1135
  13.5 332.7 %all-gather.8.cloned.1.call-start = ((), (), s32[]{:S(2)}) async-start(), calls=%async_computation.5 | async-start | bytes 26542080 | tf_op jit(solution)/shard_map/all_gather | solution.py:1135
  16.4 1.1 copy-start.6
  16.4 7.4 %copy-start.11 = (s32[2,512]{1,0:T(2,128)S(1)}, s32[2,512]{1,0:T(2,128)}, u32[]{:S(2)}) copy-start(s32[2,512]{1,0:T(2,128)} %param.15) | copy-start | bytes 12292
  16.4 8.0 %copy-start.12 = (bf16[1536]{0:T(1024)(128)(2,1)S(1)}, bf16[1536]{0:T(1024)(128)(2,1)}, u32[]{:S(2)}) copy-start(bf16[1536]{0:T(1024)(128)(2,1)} %param.17) | copy-start | bytes 9220
  16.4 8.0 %copy-start.13 = (bf16[1536]{0:T(1024)(128)(2,1)S(1)}, bf16[1536]{0:T(1024)(128)(2,1)}, u32[]{:S(2)}) copy-start(bf16[1536]{0:T(1024)(128)(2,1)} %param.22) | copy-start | bytes 9220
  16.4 9.6 %copy-start.10 = (s32[1024,8]{0,1:T(8,128)S(1)}, s32[1024,8]{0,1:T(8,128)}, u32[]{:S(2)}) copy-start(s32[1024,8]{0,1:T(8,128)} %param.16) | copy-start | bytes 98308
  16.5 18.1 %copy-start = (bf16[256,1536]{1,0:T(8,128)(2,1)S(1)}, bf16[256,1536]{1,0:T(8,128)(2,1)}, u32[]{:S(2)}) copy-start(bf16[256,1536]{1,0:T(8,128)(2,1)} %refs_2_.7) | copy-start | bytes 2359300
  16.5 592.0 %reduce-scatter.4.cloned.1.call-start = ((), (), s32[]{:S(2)}) async-start(), calls=%async_computation.6 | async-start | bytes 10616832 | tf_op jit(solution)/shard_map/reduce_scatter | solution.py:1184
  17.6 125.7 %copy-start.8 = (bf16[256,1536]{1,0:T(8,128)(2,1)}, bf16[256,1536]{1,0:T(8,128)(2,1)S(1)}, u32[]{:S(2)}) copy-start(bf16[256,1536]{1,0:T(8,128)(2,1)S(1)} %multiply_convert_fusion.refs_0_) | copy-start | bytes 2359300
  17.6 260.3 %collective-permute-start.2 = (bf16[256,1536]{1,0:T(8,128)(2,1)S(1)}, bf16[256,1536]{1,0:T(8,128)(2,1)S(1)}, u32[]{:S(2)}, u32[]{:S(2)}) collective-permute-start(bf16[256,1536]{1,0:T(8,128)(2,1)S(1)} %multiply_convert_fusion.refs_0_), channel_id=1, source_target_pairs={{0,3},{1,0},{2,1},{3,2},{4,7},{5,4},{6,5},{7,6},{8,11},{9,8},{10,9... | collective-permute-start | bytes 2359304 | tf_op jit(solution)/shard_map/ppermute | solution.py:1083
  22.8 255.2 %collective-permute-start.1 = (bf16[256,1536]{1,0:T(8,128)(2,1)S(1)}, bf16[256,1536]{1,0:T(8,128)(2,1)}, u32[]{:S(2)}, u32[]{:S(2)}) collective-permute-start(bf16[256,1536]{1,0:T(8,128)(2,1)S(1)} %multiply_convert_fusion.refs_0_), channel_id=1, source_target_pairs={{0,2},{1,3},{2,0},{3,1},{4,6},{5,7},{6,4},{7,5},{8,10},{9,11},{10,... | collective-permute-start | bytes 2359304 | tf_op jit(solution)/shard_map/ppermute | solution.py:1083
  22.8 255.2 %collective-permute-start = (bf16[256,1536]{1,0:T(8,128)(2,1)S(1)}, bf16[256,1536]{1,0:T(8,128)(2,1)}, u32[]{:S(2)}, u32[]{:S(2)}) collective-permute-start(bf16[256,1536]{1,0:T(8,128)(2,1)S(1)} %multiply_convert_fusion.refs_0_), channel_id=1, source_target_pairs={{0,1},{1,2},{2,3},{3,0},{4,5},{5,6},{6,7},{7,4},{8,9},{9,10},{10,1... | collective-permute-start | bytes 2359304 | tf_op jit(solution)/shard_map/ppermute | solution.py:1083
  24.4 118.9 %copy-start.2 = (f32[1,1536]{1,0:T(1,128)}, f32[1,1536]{1,0:T(1,128)S(1)}, u32[]{:S(2)}) copy-start(f32[1,1536]{1,0:T(1,128)S(1)} %reshape.36.gain_ref.refs_3_) | copy-start | bytes 18436
  33.7 114.1 %copy-start.9 = (s32[1024,10]{1,0:T(8,128)}, s32[1024,10]{1,0:T(8,128)S(1)}, u32[]{:S(2)}) copy-start(s32[1024,10]{1,0:T(8,128)S(1)} %fusion.3.place_cols) | copy-start | bytes 122884
  143.3 1.7 copy-start.1
  278.0 0.9 copy-start.14
  305.3 303.1 %reduce-scatter.6.cloned.1.call-start = ((), (), s32[]{:S(2)}) async-start(), calls=%async_computation.7 | async-start | bytes 15925248 | tf_op jit(solution)/shard_map/reduce_scatter | solution.py:1184
  346.1 347.6 %reduce-scatter.8.cloned.1.call-start = ((), (), s32[]{:S(2)}) async-start(), calls=%async_computation.8 | async-start | bytes 26542080 | tf_op jit(solution)/shard_map/reduce_scatter | solution.py:1184
  537.5 40.5 %collective-permute-start.3 = (bf16[256,1536]{1,0:T(8,128)(2,1)}, bf16[256,1536]{1,0:T(8,128)(2,1)S(1)}, u32[]{:S(2)}, u32[]{:S(2)}) collective-permute-start(bf16[256,1536]{1,0:T(8,128)(2,1)} %get-tuple-element.130), channel_id=1, source_target_pairs={{0,1},{1,2},{2,3},{3,0},{4,5},{5,6},{6,7},{7,4},{8,9},{9,10},{10,1... | collective-permute-start | bytes 2359304 | tf_op jit(solution)/shard_map/ppermute | solution.py:1095
  537.5 40.5 %collective-permute-start.5 = (bf16[256,1536]{1,0:T(8,128)(2,1)}, bf16[256,1536]{1,0:T(8,128)(2,1)S(1)}, u32[]{:S(2)}, u32[]{:S(2)}) collective-permute-start(bf16[256,1536]{1,0:T(8,128)(2,1)} %get-tuple-element.131), channel_id=1, source_target_pairs={{0,3},{1,0},{2,1},{3,2},{4,7},{5,4},{6,5},{7,6},{8,11},{9,8},{10,9... | collective-permute-start | bytes 2359304 | tf_op jit(solution)/shard_map/ppermute | solution.py:1095
  541.3 64.4 %collective-permute-start.4 = (bf16[256,1536]{1,0:T(8,128)(2,1)S(1)}, bf16[256,1536]{1,0:T(8,128)(2,1)}, u32[]{:S(2)}, u32[]{:S(2)}) collective-permute-start(bf16[256,1536]{1,0:T(8,128)(2,1)S(1)} %get-tuple-element.132), channel_id=1, source_target_pairs={{0,2},{1,3},{2,0},{3,1},{4,6},{5,7},{6,4},{7,5},{8,10},{9,11},{10,... | collective-permute-start | bytes 2359304 | tf_op jit(solution)/shard_map/ppermute | solution.py:1095
  541.3 64.4 %copy-start.5 = (f32[256,1536]{1,0:T(8,128)S(1)}, f32[256,1536]{1,0:T(8,128)}, u32[]{:S(2)}) copy-start(f32[256,1536]{1,0:T(8,128)} %get-tuple-element.47.refs_6_) | copy-start | bytes 4718596
  693.7 5.6 copy-start.7
  700.4 4.6 copy-start.3
  705.0 3.5 copy-start.4
Sparse Core Ops, SparseCore 0:
  10.6 36.5 all-gather.3
  49.7 118.5 all-gather.5
  170.8 118.5 all-gather.7
  305.5 85.4 reduce-scatter.3
  394.4 99.5 reduce-scatter.5
  497.5 167.3 reduce-scatter.7

commit v5 on v4

--- a/solution.py
+++ b/solution.py
@@ -241,7 +241,9 @@
 TRANSFER = pl.CostEstimate(flops=0, transcendentals=0, bytes_accessed=150_000_000)
 
 
-def norm_gather_kernel(count, emb_ref, gain_ref, rows_ref, *sems):
+def norm_gather_kernel(
+    count, emb_ref, gain_ref, routes_ref, rows_ref, mask_ref, cols_ref, turned_ref, counts_ref, *sems
+):
     enter_kernel(count)
     line = LineGather(count, rows_ref, *sems)
     start_x = emb_ref[...].astype(jnp.float32) * emb_scale
@@ -249,21 +251,55 @@
     rows_ref[own_rows(line.rows), :] = normed.astype(jnp.bfloat16)
     for step in range(count - 1):
         line.start(step)
+        if step == 0:
+            place_routes(line.rows, routes_ref, mask_ref, cols_ref, turned_ref, counts_ref)
         line.arrive(step)
     line.finish()
 
 
-def norm_gather(emb, gain_row, count, ident):
+def place_routes(rows, routes_ref, mask_ref, cols_ref, turned_ref, counts_ref):
+    group, lanes = mask_ref.shape
+    columns = lax.broadcasted_iota(jnp.int32, (rows, lanes), 1)
+    for low in range(0, group, rows):
+        area = slice(low, low + rows)
+        mask = jnp.zeros((rows, lanes), jnp.float32)
+        for choice in range(routes_ref.shape[1]):
+            mask = jnp.where(routes_ref[area, choice : choice + 1] == columns, 1.0, mask)
+        mask_ref[area, :] = mask
+    counts_ref[...] = jnp.sum(mask_ref[...], axis=0, keepdims=True).astype(jnp.int32)
+    member = mask_ref[...].astype(jnp.bfloat16)
+    for low in range(0, group, rows):
+        area = slice(low, low + rows)
+        here = lax.broadcasted_iota(jnp.int32, (rows, group), 0) + low
+        earlier = here > lax.broadcasted_iota(jnp.int32, (rows, group), 1)
+        ranks = jnp.dot(
+            jnp.where(earlier, 1.0, 0.0).astype(jnp.bfloat16),
+            member,
+            preferred_element_type=jnp.float32,
+        )
+        places = jnp.where(mask_ref[area, :] > 0.0, ranks, -1.0)
+        cols_ref[area, :] = places.astype(jnp.int32)
+        turned_ref[:, area] = places.T.astype(jnp.int32)
+
+
+def norm_gather(emb, gain_row, routes, count, ident):
     rows, width = emb.shape
+    group = rows * count
     return pl.pallas_call(
         functools.partial(norm_gather_kernel, count),
-        out_shape=jax.ShapeDtypeStruct((rows * count, width), jnp.bfloat16),
-        in_specs=[IN_VMEM] * 2,
-        out_specs=IN_VMEM,
+        out_shape=[
+            jax.ShapeDtypeStruct((group, width), jnp.bfloat16),
+            jax.ShapeDtypeStruct((group, 128), jnp.float32),
+            jax.ShapeDtypeStruct((group, 128), jnp.int32),
+            jax.ShapeDtypeStruct((128, group), jnp.int32),
+            jax.ShapeDtypeStruct((1, 128), jnp.int32),
+        ],
+        in_specs=[IN_VMEM] * 3,
+        out_specs=[IN_VMEM] * 5,
         scratch_shapes=line_sems(count),
-        compiler_params=remote_params(ident, 32),
+        compiler_params=remote_params(ident, 48),
         cost_estimate=TRANSFER,
-    )(emb, gain_row)
+    )(emb, gain_row, routes)
 
 
 def mid_kernel(
@@ -403,14 +439,13 @@
     )(*dx_parts, *y_parts, mid, cotangent, own_gates, gain_row, weights)
 
 
-def finish_kernel(tp_count, fsdp_count, runs, *refs):
-    x_ref, w_ref, emb_ref, gain_ref, mid_grad, gain_two = refs[:6]
-    packed, refs = refs[6 : 6 + runs], refs[6 + runs :]
+def finish_kernel(tp_count, fsdp_count, *refs):
+    x_ref, w_ref, emb_ref, gain_ref, mid_grad, gain_two, *refs = refs
     (
-        grad_ref, w_sum, gains_ref, *wide,
+        grad_ref, w_sum, gains_ref,
         line_recv, line_send, line_send_sem, line_recv_sem,
         pair_got, chip_sums, chip_got, pair_send, pair_recv, chip_send, chip_recv,
-        tp_got, fsdp_got, small_send, small_recv, narrow, broad, in_sem, out_sem,
+        tp_got, fsdp_got, small_send, small_recv,
     ) = refs
     plane = Plane(fsdp_count)
     tp_me, fsdp_me = lax.axis_index("tp"), plane.me
@@ -470,28 +505,6 @@
             total = total + got[index]
         return total
 
-    def widen_run(run):
-        base = sum(packed[index].shape[0] for index in range(run))
-
-        def one(index, carry):
-            fetch = pltpu.make_async_copy(packed[run].at[index], narrow, in_sem)
-            fetch.start()
-            fetch.wait()
-            puts = []
-            for slot in range(3):
-                broad[slot] = narrow[slot].astype(jnp.float32)
-                puts.append(
-                    pltpu.make_async_copy(
-                        broad.at[slot], wide[slot].at[base + index], out_sem.at[slot]
-                    )
-                )
-                puts[-1].start()
-            for put in puts:
-                put.wait()
-            return carry
-
-        lax.fori_loop(0, packed[run].shape[0], one, 0)
-
     line.start(0)
     order = list(range(1, plane.chips)) + [0]
     for shift in order:
@@ -501,13 +514,9 @@
         if shift > 0:
             chip_sums[shift - 1] = both_cores(shift).astype(chip_sums.dtype)
             to_chip(shift).start()
-    if runs > 0:
-        widen_run(0)
     line.arrive(0)
     for step in range(1, tp_count - 1):
         line.start(step)
-        if step < runs:
-            widen_run(step)
         line.arrive(step)
     line.collect()
     from_norm, gain_one = rms_back(
@@ -531,23 +540,20 @@
             to_chip(shift).wait_send()
 
 
-def finish(dx_rows, weight_grads, emb, gain_row, mid_grad, gain_two, packed, experts, ident):
+def finish(dx_rows, weight_grads, emb, gain_row, mid_grad, gain_two, ident):
     tp_count, fsdp_count = lax.axis_size("tp"), lax.axis_size("fsdp")
     rows, width = emb.shape
     w_rows, w_width = weight_grads.shape[0] // fsdp_count, weight_grads.shape[1]
-    chips, runs = fsdp_count // 2, len(packed)
-    shares, hidden = packed[0].shape[2:] if runs else (8, 128)
-    wide = [jax.ShapeDtypeStruct((experts, shares, hidden), jnp.float32)] * (3 if runs else 0)
+    chips = fsdp_count // 2
     return pl.pallas_call(
-        functools.partial(finish_kernel, tp_count, fsdp_count, runs),
+        functools.partial(finish_kernel, tp_count, fsdp_count),
         out_shape=[
             jax.ShapeDtypeStruct((rows, width), jnp.float32),
             jax.ShapeDtypeStruct((w_rows, w_width), jnp.float32),
             jax.ShapeDtypeStruct((8, width), jnp.float32),
-            *wide,
-        ],
-        in_specs=[IN_VMEM] * 6 + [IN_PLACE] * runs,
-        out_specs=[IN_VMEM] * 3 + [IN_PLACE] * len(wide),
+        ],
+        in_specs=[IN_VMEM] * 6,
+        out_specs=[IN_VMEM] * 3,
         scratch_shapes=line_buffers(tp_count, rows, width)
         + [
             pltpu.VMEM((chips, w_rows, w_width), jnp.bfloat16),
@@ -561,14 +567,10 @@
             pltpu.VMEM((fsdp_count, 8, width), jnp.float32),
             pltpu.SemaphoreType.DMA((tp_count + fsdp_count,)),
             pltpu.SemaphoreType.DMA((tp_count + fsdp_count,)),
-            pltpu.VMEM((3, shares, hidden), jnp.bfloat16),
-            pltpu.VMEM((3, shares, hidden), jnp.float32),
-            pltpu.SemaphoreType.DMA,
-            pltpu.SemaphoreType.DMA((3,)),
         ],
         compiler_params=remote_params(ident),
         cost_estimate=TRANSFER,
-    )(dx_rows, weight_grads, emb, gain_row, mid_grad, gain_two, *packed)
+    )(dx_rows, weight_grads, emb, gain_row, mid_grad, gain_two)
 
 
 def pack_kernel(low, *refs):
@@ -608,21 +610,23 @@
 
 
 def join_kernel(*refs):
+    *sources, last, target = refs
     low = 0
-    for source in refs[:-1]:
-        refs[-1][:, low : low + source.shape[1]] = source[...]
+    for source in sources:
+        target[:, low : low + source.shape[1]] = source[...]
         low += source.shape[1]
-    if low < refs[-1].shape[1]:
-        refs[-1][:, low:] = jnp.zeros((refs[-1].shape[0], refs[-1].shape[1] - low), jnp.bfloat16)
-
-
-def join(parts, width):
+    router = last[...].astype(jnp.float32).T.astype(jnp.bfloat16)
+    target[:, low:] = jnp.zeros((target.shape[0], target.shape[1] - low), jnp.bfloat16)
+    target[:, low : low + router.shape[1]] = router
+
+
+def join(parts, last_turned, width):
     return pl.pallas_call(
         join_kernel,
-        in_specs=[IN_VMEM] * len(parts),
+        in_specs=[IN_VMEM] * (len(parts) + 1),
         out_specs=IN_VMEM,
         out_shape=jax.ShapeDtypeStruct((parts[0].shape[0], width), jnp.bfloat16),
-    )(*parts)
+    )(*parts, last_turned)
 
 
 SLOTS = 256
@@ -632,7 +636,7 @@
     first_expert,
     capacity,
     meta,
-    place_row,
+    place_rows,
     place_cols,
     gate_rows,
     x_ref,
@@ -658,15 +662,16 @@
         for copy in copies:
             copy.wait()
 
+    column = expert + meta[meta.shape[0] - 2]
     lanes = lax.broadcasted_iota(jnp.int32, place_cols.shape, 1)
-    place_col = jnp.sum(jnp.where(lanes == expert, place_cols[...], 0), axis=1, keepdims=True)
-    column = expert + meta[meta.shape[0] - 2]
+    place_col = jnp.sum(jnp.where(lanes == column, place_cols[...], 0), axis=1, keepdims=True)
+    place_row = place_rows[pl.ds(column, 1), :]
     gate_row = gate_rows[pl.ds(column, 1), :].astype(jnp.bfloat16).astype(jnp.float32)
     mark = jnp.where(lax.broadcasted_iota(jnp.int32, (1, tail), 1) == column, 1.0, 0.0)
 
     def run(base, span):
         slots = lax.broadcasted_iota(jnp.int32, (span, group), 0) + base
-        hit = slots == place_row[0]
+        hit = slots == place_row
         pick = jnp.where(hit, 1.0, 0.0).astype(jnp.bfloat16)
         scale = jnp.sum(jnp.where(hit, gate_row, 0.0), axis=1, keepdims=True)
         x_taken = jnp.dot(pick, x_ref[...], preferred_element_type=jnp.float32).astype(jnp.bfloat16)
@@ -719,7 +724,7 @@
     for base in range(SLOTS, capacity, SLOTS):
         span = min(SLOTS, -(-(capacity - base) // 16) * 16)
 
-        @pl.when(meta[expert] > base)
+        @pl.when(meta[column] > base)
         def _():
             run(base, span)
 
@@ -733,9 +738,6 @@
         return pl.BlockSpec(
             shape, lambda step, meta: (0,) * len(shape), pipeline_mode=pl.Buffered(1)
         )
-
-    def row(shape):
-        return pl.BlockSpec(shape, lambda step, meta: (step + first, 0, 0))
 
     def big(offset):
         return pl.BlockSpec((1, 3, width, hidden), lambda step, meta: (step + offset, 0, 0, 0))
@@ -746,7 +748,7 @@
             num_scalar_prefetch=1,
             grid=(count,),
             in_specs=[
-                row((1, 1, group)),
+                whole(place_rows.shape),
                 whole(place_cols.shape),
                 whole(gate_rows.shape),
                 whole(x_rows.shape),
@@ -785,8 +787,11 @@
     return values * cosine + other * (sine * sign)
 
 
-def segment_bias(seg_row, seg_col):
-    shape = (seg_col.shape[0], seg_row.shape[1])
+def segment_bias(seg_row):
+    length = seg_row.shape[1]
+    shape = (length, length)
+    seg_row = seg_row.astype(jnp.float32)
+    seg_col = jnp.broadcast_to(seg_row, (128, length)).T[:, :1]
     keys = lax.broadcasted_iota(jnp.int32, shape, 0)
     queries = lax.broadcasted_iota(jnp.int32, shape, 1)
     return jnp.where((keys <= queries) & (seg_col == seg_row), 0.0, masked_value)
@@ -796,7 +801,6 @@
     x_ref,
     w_ref,
     seg_row,
-    seg_col,
     cos_ref,
     sin_ref,
     q_ref,
@@ -824,7 +828,7 @@
         else:
             v_ref[head - heads - kv_heads] = part.astype(jnp.bfloat16)
             v_turned[head - heads - kv_heads] = part.T.astype(jnp.bfloat16)
-    bias[...] = segment_bias(seg_row[0], seg_col[0])
+    bias[...] = segment_bias(seg_row[0])
 
     def one_head(head, carry):
         kv = head // per_kv
@@ -853,7 +857,6 @@
     x_ref,
     w_ref,
     seg_row,
-    seg_col,
     cos_ref,
     sin_ref,
     q_ref,
@@ -887,7 +890,7 @@
         mixed_grads[head] = grad[:, head * HEAD_DIM : (head + 1) * HEAD_DIM]
     for kv in range(kv_heads):
         k_turned[kv] = k_ref[kv].astype(jnp.float32).T.astype(jnp.bfloat16)
-    bias[...] = segment_bias(seg_row[0], seg_col[0])
+    bias[...] = segment_bias(seg_row[0])
     kv_grads[...] = jnp.zeros_like(kv_grads)
 
     def one_head(head, carry):
@@ -977,7 +980,6 @@
             by_row(width),
             fixed(weights.shape),
             pl.BlockSpec((1, 1, SEQ), lambda seq: (seq, 0, 0)),
-            pl.BlockSpec((1, SEQ, 1), lambda seq: (seq, 0, 0)),
             fixed(tables[0].shape),
             fixed(tables[1].shape),
         ],
@@ -1008,7 +1010,7 @@
         cost_estimate=pl.CostEstimate(
             flops=10_000_000_000, transcendentals=3_000_000, bytes_accessed=60_000_000
         ),
-    )(rows, weights, segments[:, None, :], segments[:, :, None], *tables)
+    )(rows, weights, segments[:, None, :], *tables)
 
 
 def attend_back(rows, weights, segments, tables, kept, moe_rows, branch_grad):
@@ -1024,7 +1026,6 @@
             by_row(width),
             fixed(weights.shape),
             pl.BlockSpec((1, 1, SEQ), lambda seq: (seq, 0, 0)),
-            pl.BlockSpec((1, SEQ, 1), lambda seq: (seq, 0, 0)),
             fixed(tables[0].shape),
             fixed(tables[1].shape),
             by_head(heads),
@@ -1055,27 +1056,37 @@
         cost_estimate=pl.CostEstimate(
             flops=20_000_000_000, transcendentals=3_000_000, bytes_accessed=100_000_000
         ),
-    )(rows, weights, segments[:, None, :], segments[:, :, None], *tables,
+    )(rows, weights, segments[:, None, :], *tables,
       queries, keys, values, mixed, logsum, moe_rows, branch_grad)
 
 
-def widen_kernel(packed, *refs):
-    for slot, target in enumerate(refs[-3:]):
-        target[0] = packed[0, slot].astype(jnp.float32)
-
-
-def widen(packed, count, first, held):
-    span, _, rows, width = packed.shape
-    shape = jax.ShapeDtypeStruct((count, rows, width), jnp.float32)
+def widen_kernel(edges, *refs):
+    step = pl.program_id(0)
+    packed, targets = refs[:-3], refs[-3:]
+    for part, low, high in zip(packed, edges[:-1], edges[1:]):
+
+        @pl.when((step >= low) & (step < high))
+        def _():
+            for slot, target in enumerate(targets):
+                target[0] = part[0, slot].astype(jnp.float32)
+
+
+def widen(packed, edges):
+    _, _, rows, width = packed[0].shape
+
+    def home(low, high):
+        return pl.BlockSpec(
+            (1, 3, rows, width),
+            lambda step: (jnp.clip(step - low, 0, high - low - 1), 0, 0, 0),
+        )
+
     return pl.pallas_call(
-        widen_kernel,
-        grid=(span,),
-        in_specs=[pl.BlockSpec((1, 3, rows, width), lambda step: (step, 0, 0, 0))]
-        + [pl.BlockSpec(memory_space=pl.ANY)] * len(held),
-        out_specs=[pl.BlockSpec((1, rows, width), lambda step: (step + first, 0, 0))] * 3,
-        out_shape=[shape] * 3,
-        input_output_aliases={1 + index: index for index in range(len(held))},
-    )(packed, *held)
+        functools.partial(widen_kernel, edges),
+        grid=(edges[-1],),
+        in_specs=[home(low, high) for low, high in zip(edges[:-1], edges[1:])],
+        out_specs=[pl.BlockSpec((1, rows, width), lambda step: (step, 0, 0))] * 3,
+        out_shape=[jax.ShapeDtypeStruct((edges[-1], rows, width), jnp.float32)] * 3,
+    )(*packed)
 
 
 def shifted_blocks(block, count):
@@ -1125,38 +1136,34 @@
     group_size = local_rows * tp_count
     gathers = 2 if group_size <= 1024 else 1
 
-    moe_grad = (resid_scale * cotangent.astype(jnp.float32)).astype(jnp.bfloat16)
-    moe_grad_blocks = shifted_blocks(moe_grad, tp_count)
     attn_w = lax.all_gather(
-        join([w_query, w_key, w_value, w_out, w_router], used + 128), "fsdp", axis=0, tiled=True
+        join([w_query, w_key, w_value, w_out], w_router.T, used + 128),
+        "fsdp",
+        axis=0,
+        tiled=True,
+    )
+    gain_one = norm1_gain.astype(jnp.float32)[None, :]
+    gain_two = norm2_gain.astype(jnp.float32)[None, :]
+    group_rows, mask, place_cols, place_rows, counts = norm_gather(
+        emb, gain_one, routes, tp_count, 0
     )
     edges = [experts_here * part // gathers for part in range(gathers + 1)]
-    pieces = [
-        lax.all_gather(pack([w_gate, w_up, w_down], low, high), "fsdp", axis=2, tiled=True)
-        for low, high in zip(edges[:-1], edges[1:])
-    ]
-    gain_one = norm1_gain.astype(jnp.float32)[None, :]
-    gain_two = norm2_gain.astype(jnp.float32)[None, :]
-    group_rows = norm_gather(emb, gain_one, tp_count, 0)
-
+    stacks = (w_gate, w_up, w_down)
+    pieces = []
+    for low, high in zip(edges[:-1], edges[1:]):
+        pieces.append(lax.all_gather(pack(stacks, low, high), "fsdp", axis=2, tiled=True))
+        stacks, _ = lax.optimization_barrier((stacks, counts))
+    late_grad, _ = lax.optimization_barrier((cotangent, counts))
+    moe_grad = (resid_scale * late_grad.astype(jnp.float32)).astype(jnp.bfloat16)
+    moe_grad_blocks = shifted_blocks(moe_grad, tp_count)
     capacity = group_size * routes.shape[1] // expert_count * 2
-    lanes = jnp.arange(128, dtype=jnp.int32)
-    member_all = jnp.any(routes[:, :, None] == lanes[None, None, :], axis=1)
-    member = lax.dynamic_slice_in_dim(member_all, tp_index * experts_here, experts_here, 1)
-    ids = jnp.arange(group_size)
-    earlier = (ids[:, None] > ids[None, :]).astype(jnp.bfloat16)
-    ranks = jnp.dot(earlier, member.astype(jnp.bfloat16), preferred_element_type=jnp.float32)
-    places = jnp.where(member, ranks.astype(jnp.int32), -1)
-    meta = jnp.concatenate(
-        [jnp.sum(member.astype(jnp.int32), axis=0), jnp.stack([tp_index * experts_here, tp_index])]
-    )
-    place_rows = places.T[:, None, :]
+    meta = jnp.concatenate([counts[0], jnp.stack([tp_index * experts_here, tp_index])])
 
     tables = attend_tables()
     heads_here, kv_here = q_width // HEAD_DIM, kv_width // HEAD_DIM
     *kept, branch_part = attend(group_rows, attn_w, segment_ids, tables, heads_here, kv_here)
     mid_x, moe_rows, gate_rows, own_gates = find_mid(
-        branch_part, emb, gain_two, attn_w, used, member_all.astype(jnp.float32), tp_count, 1
+        branch_part, emb, gain_two, attn_w, used, mask, tp_count, 1
     )
 
     outs = []
@@ -1169,7 +1176,7 @@
             experts_step(
                 meta,
                 place_rows,
-                places,
+                place_cols,
                 gate_rows,
                 moe_rows,
                 moe_grad_blocks,
@@ -1198,18 +1205,10 @@
     moe_sum = shifted_scatter(y_part, tp_count, tp_index)
     out = (mid_x + resid_scale * moe_sum).astype(jnp.bfloat16)
     dx_one, attn_grads = attend_back(group_rows, attn_w, segment_ids, tables, kept, moe_rows, sent)
-    grad_emb, attn_sum, gain_sums, *expert_sums = finish(
-        dx_one,
-        attn_grads,
-        emb,
-        gain_one,
-        mid_grad,
-        gain_two_grad,
-        grad_sums[:-1],
-        experts_here,
-        3,
+    grad_emb, attn_sum, gain_sums = finish(
+        dx_one, attn_grads, emb, gain_one, mid_grad, gain_two_grad, 3
     )
-    expert_sums = widen(grad_sums[-1], experts_here, runs[-2], expert_sums)
+    expert_sums = widen(grad_sums, runs)
     return (
         out,
         grad_emb,

time: 728 us -> 675 us (0.927)
  Pallas kernels: 623 us -> 602 us
  waiting for transfers between devices: 27.8 us -> 13.2 us
  local copies, waits for them, and re-layouts: 29 us -> 20.6 us
    pallas_call x4, Pallas kernels: 195 us -> 156 us  [the longest x1 86.9 us: finish(): pl.pallas_call(functools.partial(finish_kernel, tp_count, fsdp_count), ou...]
    ppermute x3, waiting for transfers between devices: 27.7 us -> 0.01 us  [shifted_scatter(): lax.ppermute(block, 'tp', [(i, (i + shift) % count) for i in range(count)])]
    pallas_call x1, Pallas kernels: 110 us -> 129 us  [find_mid(): pl.pallas_call(functools.partial(mid_kernel, count), grid=(1,), out_shape...]
    reduce_scatter x3, waiting for transfers between devices: 0.01 us -> 13.1 us  [local(): lax.psum_scatter(part[2], 'fsdp', scatter_dimension=2, tiled=True)]
    unnamed x37, local copies, waits for them, and re-layouts: 17.1 us -> 9.74 us
  transfers between devices with their start and end apart: 12 -> 12, of which waited for: 1 -> 1; matrix products, arithmetic and copies ran while one was open for 4% -> 3% of each run, Pallas kernels for 86% -> 89%
where the time goes in v5:
time: 675 us; the launch traced here: 665 us
  Pallas kernels  602 us (89%)
  local copies, waits for them, and re-layouts  20.6 us (3%)
  between operations  14.9 us (2%)
  waiting for transfers between devices  13.2 us (2%)
  starting transfers between devices  7.94 us (1%)
    pallas_call x1, Pallas kernels, find_mid_grad(): pl.pallas_call(functools.partial(moe_back_kernel, count, runs), grid=(1,)...  134 us
    pallas_call x1, Pallas kernels, find_mid(): pl.pallas_call(functools.partial(mid_kernel, count), grid=(1,), out_shape...  129 us
    pallas_call x3, Pallas kernels, experts_step(): pl.pallas_call(functools.partial(experts_kernel, first, capacity), grid_s...  119 us
    pallas_call x1, Pallas kernels, finish(): pl.pallas_call(functools.partial(finish_kernel, tp_count, fsdp_count), ou...  86.9 us
    pallas_call x1, Pallas kernels, norm_gather(): pl.pallas_call(functools.partial(norm_gather_kernel, count), out_shape=[j...  57.5 us
    pallas_call x1, Pallas kernels, attend_back(): pl.pallas_call(attend_back_kernel, grid=(group // SEQ,), in_specs=[by_row...  39 us
    pallas_call x1, Pallas kernels, attend(): pl.pallas_call(attend_kernel, grid=(seqs,), in_specs=[by_row(width), fixe...  19.7 us
  transfers between devices with their start and end apart: 12, of which 1 were waited for; matrix products, arithmetic and copies ran while one was open for 3% of the time, Pallas kernels for 89%

profile of v5, /device:TPU:0, one launch (start us, length us, event | category | flops | bytes accessed | tf_op | source)
XLA Modules:
  0.0 665.2 jit_solution(15289617680903679305)
XLA Ops:
  7.2 1.9 shard_map.230
  9.2 2.8 shard_map.233
  13.2 57.5 %shard_map.229 = (bf16[1024,1536]{1,0:T(8,128)(2,1)S(1)}, f32[1024,128]{1,0:T(8,128)S(1)}, s32[1024,128]{1,0:T(8,128)S(1)}, s32[128,1024]{1,0:T(8,128)S(1)}, s32[1,128]{1,0:T(1,128)S(1)}) custom-call(bf16[256,1536]{1,0:T(8,128)(2,1)S(1)} %copy-done, f32[1,1536]{1,0:T(1,128)S(1)} %reshape.35.gain_ref.refs_3_, s32[1024,8]{1,0:T(8,128)S(1)} %copy.28.routes_ref), custom_call_target="tpu_custom_call" | custom-call | bytes 150000000 | tf_op jit(solution)/shard_map/pallas_call | solution.py:288
  71.5 1.7 copy-done.3
  73.1 0.8 copy-done.4
  73.9 0.8 copy-done.5
  74.7 2.8 shard_map.236
  77.7 1.0 copy-done.7
  78.9 2.7 collective-permute-start.1
  81.7 1.1 collective-permute-start.2
  84.6 1.0 fusion
  85.6 1.0 pad_maximum_fusion
  86.6 19.7 %shard_map.231 = (bf16[6,1024,64]{2,1,0:T(8,128)(2,1)}, bf16[2,1024,64]{2,1,0:T(8,128)(2,1)}, bf16[2,1024,64]{2,1,0:T(8,128)(2,1)}, bf16[1024,384]{1,0:T(8,128)(...) custom-call(bf16[1024,1536]{1,0:T(8,128)(2,1)} %copy-done.3, ...), custom_call_target="tpu_custom_call" | custom-call | flops 10000000000 | bytes 60000000 | tf_op jit(solution)/shard_map/pallas_call | solution.py:976
  106.3 129.1 %shard_map.232 = (f32[256,1536]{1,0:T(8,128)}, bf16[1024,1536]{1,0:T(8,128)(2,1)}, f32[128,1024]{1,0:T(8,128)}, f32[256,128]{1,0:T(8,128)}) custom-call(bf16[1024,1536]{1,0:T(8,128)(2,1)} %get-tuple-element.53.part_ref, bf16[256,1536]{1,0:T(8,128)(2,1)} %refs_2_.6, f32[1,1536]{1,0:T(1,128)} %reshape.36.gain_ref.refs_9_, ...), custom_call_target="tpu_custom_call" | custom-call | bytes 150000000 | tf_op jit(solution)/shard_map/pallas_call | solution.py:354
  235.5 0.9 copy-done.14
  237.3 26.8 %shard_map.234 = (bf16[1024,1536]{1,0:T(8,128)(2,1)}, bf16[1024,1664]{1,0:T(8,128)(2,1)}, bf16[2,3,1536,512]{3,2,1,0:T(8,128)(2,1)}) custom-call(s32[130]{0:T(256)} %pad_add_fusion.meta, s32[128,1024]{1,0:T(8,128)} %copy-done.5, s32[1024,128]{1,0:T(8,128)} %copy-done.4, f32[128,1024]{1,0:T(8,128)} %get-tuple-element.59.gate_rows, ...), custom_call_target="tpu_custom_call" | custom-call | flops 21818769408 | bytes 18874368 | tf_op jit(solution)/shard_map/pallas_call | solution.py:745
  264.1 42.8 %shard_map.235 = (bf16[1024,1536]{1,0:T(8,128)(2,1)}, bf16[1024,1664]{1,0:T(8,128)(2,1)}, bf16[3,3,1536,512]{3,2,1,0:T(8,128)(2,1)}) custom-call(s32[130]{0:T(256)} %pad_add_fusion.meta, s32[128,1024]{1,0:T(8,128)} %copy-done.5, s32[1024,128]{1,0:T(8,128)} %copy-done.4, f32[128,1024]{1,0:T(8,128)} %get-tuple-element.59.gate_rows, ...), custom_call_target="tpu_custom_call" | custom-call | flops 32728154112 | bytes 28311552 | tf_op jit(solution)/shard_map/pallas_call | solution.py:745
  307.0 49.6 %shard_map.237 = (bf16[1024,1536]{1,0:T(8,128)(2,1)}, bf16[1024,1664]{1,0:T(8,128)(2,1)}, bf16[5,3,1536,512]{3,2,1,0:T(8,128)(2,1)}) custom-call(s32[130]{0:T(256)} %pad_add_fusion.meta, s32[128,1024]{1,0:T(8,128)} %copy-done.5, s32[1024,128]{1,0:T(8,128)} %copy-done.4, f32[128,1024]{1,0:T(8,128)} %get-tuple-element.59.gate_rows, ...), custom_call_target="tpu_custom_call" | custom-call | flops 54546923520 | bytes 47185920 | tf_op jit(solution)/shard_map/pallas_call | solution.py:745
  356.6 134.1 %shard_map.238 = (bf16[1024,1536]{1,0:T(8,128)(2,1)}, f32[256,1536]{1,0:T(8,128)}, f32[1,1536]{1,0:T(1,128)}, bf16[1024,1664]{1,0:T(8,128)(2,1)}) custom-call(bf16[1024,1664]{1,0:T(8,128)(2,1)} %get-tuple-element.62.refs_0_, bf16[1024,1664]{1,0:T(8,128)(2,1)} %get-tuple-element.63.refs_1_, bf16[1024,1664]{1,0:T(8,128)(2,1)} %get-tuple-element.67.refs_2_, ...), custom_call_target="tpu_custom_call" | custom-call | bytes 150000000 | tf_op jit(solution)/shard_map/pallas_call | solution.py:422
  490.8 3.5 constant_dynamic-slice_fusion.2
  494.3 2.8 collective-permute-start.4
  497.1 1.1 collective-permute-start.5
  498.1 39.0 %shard_map.239 = (bf16[1024,1536]{1,0:T(8,128)(2,1)}, bf16[1536,1152]{1,0:T(8,128)(2,1)}) custom-call(bf16[1024,1536]{1,0:T(8,128)(2,1)} %copy-done.3, bf16[1536,1152]{1,0:T(8,128)(2,1)} %all-gather.4.cloned.1.call-done.w_ref.router_ref.refs_10_, s32[2,1,512]{2,1,0:T(1,128)} %broadcast_in_dim.18.seg_row, f32[512,64]{1,0:T(8,128)} %get-tuple-element.128.cos_ref, ...), custom_call_target="tpu_custom_call" | custom-call | flops 20000000000 | bytes 100000000 | tf_op jit(solution)/shard_map/pallas_call | solution.py:1022
  537.2 86.9 %shard_map.240 = (f32[256,1536]{1,0:T(8,128)}, f32[192,1152]{1,0:T(8,128)}, f32[8,1536]{1,0:T(8,128)}) custom-call(bf16[1024,1536]{1,0:T(8,128)(2,1)} %get-tuple-element.79.refs_0_, bf16[1536,1152]{1,0:T(8,128)(2,1)} %get-tuple-element.80.refs_1_, bf16[256,1536]{1,0:T(8,128)(2,1)} %refs_2_.6, f32[1,1536]{1,0:T(1,128)} %copy-done.2, ...), custom_call_target="tpu_custom_call" | custom-call | bytes 150000000 | tf_op jit(solution)/shard_map/pallas_call | solution.py:548
  624.0 1.0 slice.27
  625.8 1.5 slice_reduce_fusion
  627.3 1.7 fusion.2
  629.0 1.9 fusion.1
  630.9 3.3 add_convert_fusion
  634.2 13.1 %reduce-scatter.8.cloned.1.call-done.refs_2_ = bf16[5,3,192,512]{3,2,1,0:T(8,128)(2,1)} async-done(((bf16[5,3,1536,512]{3,2,1,0:T(8,128)(2,1)}), bf16[5,3,192,512]{3,2,1,0:T(8,128)(2,1)}) %reduce-scatter.8.cloned.1.call-update) | async-done | bytes 2949136 | tf_op jit(solution)/shard_map/reduce_scatter | solution.py:1191
  647.3 9.4 %shard_map.241 = (f32[10,192,512]{2,1,0:T(8,128)}, f32[10,192,512]{2,1,0:T(8,128)}, f32[10,192,512]{2,1,0:T(8,128)}) custom-call(bf16[2,3,192,512]{3,2,1,0:T(8,128)(2,1)} %reduce-scatter.4.cloned.1.call-done.refs_0_, bf16[3,3,192,512]{3,2,1,0:T(8,128)(2,1)} %reduce-scatter.6.cloned.1.call-done.refs_1_, ...), custom_call_target="tpu_custom_call" | custom-call | tf_op jit(solution)/shard_map/pallas_call | solution.py:1083
  656.7 1.1 copy.32
  (63 shorter events, 5.9 us)
Async XLA Ops:
  7.2 79.4 %all-gather.4.cloned.1.call-start = ((), (), s32[]{:S(2)}) async-start(), calls=%async_computation.3 | async-start | bytes 3981312 | tf_op jit(solution)/shard_map/all_gather | solution.py:1139
  9.1 227.3 %all-gather.6.cloned.1.call-start = ((), (), s32[]{:S(2)}) async-start(), calls=%async_computation.4 | async-start | bytes 26542080 | tf_op jit(solution)/shard_map/all_gather | solution.py:1154
  12.0 0.7 copy-start.11
  12.0 0.8 copy-start.10
  12.1 1.1 copy-start
  12.1 294.9 %all-gather.8.cloned.1.call-start = ((), (), s32[]{:S(2)}) async-start(), calls=%async_computation.5 | async-start | bytes 26542080 | tf_op jit(solution)/shard_map/all_gather | solution.py:1154
  12.8 64.8 %copy-start.2 = (f32[1,1536]{1,0:T(1,128)}, f32[1,1536]{1,0:T(1,128)S(1)}, u32[]{:S(2)}) copy-start(f32[1,1536]{1,0:T(1,128)S(1)} %reshape.35.gain_ref.refs_3_) | copy-start | bytes 18436
  70.7 0.8 copy-start.1
  71.5 1.7 copy-start.3
  73.1 0.8 copy-start.4
  73.9 0.8 copy-start.5
  77.6 1.1 copy-start.7
  77.6 5.1 copy-start.12
  77.6 5.7 copy-start.13
  77.7 556.6 %reduce-scatter.4.cloned.1.call-start = ((), (), s32[]{:S(2)}) async-start(), calls=%async_computation.6 | async-start | bytes 10616832 | tf_op jit(solution)/shard_map/reduce_scatter | solution.py:1191
  78.9 27.5 %copy-start.9 = (bf16[256,1536]{1,0:T(8,128)(2,1)}, bf16[256,1536]{1,0:T(8,128)(2,1)S(1)}, u32[]{:S(2)}) copy-start(bf16[256,1536]{1,0:T(8,128)(2,1)S(1)} %multiply_convert_fusion.refs_0_) | copy-start | bytes 2359300
  78.9 156.6 %collective-permute-start = (bf16[256,1536]{1,0:T(8,128)(2,1)S(1)}, bf16[256,1536]{1,0:T(8,128)(2,1)S(1)}, u32[]{:S(2)}, u32[]{:S(2)}) collective-permute-start(bf16[256,1536]{1,0:T(8,128)(2,1)S(1)} %multiply_convert_fusion.refs_0_), channel_id=1, source_target_pairs={{0,1},{1,2},{2,3},{3,0},{4,5},{5,6},{6,7},{7,4},{8,9},{9,10},{10,1... | collective-permute-start | bytes 2359304 | tf_op jit(solution)/shard_map/ppermute | solution.py:1094
  78.9 156.6 %collective-permute-start.1 = (bf16[256,1536]{1,0:T(8,128)(2,1)S(1)}, bf16[256,1536]{1,0:T(8,128)(2,1)S(1)}, u32[]{:S(2)}, u32[]{:S(2)}) collective-permute-start(bf16[256,1536]{1,0:T(8,128)(2,1)S(1)} %multiply_convert_fusion.refs_0_), channel_id=1, source_target_pairs={{0,2},{1,3},{2,0},{3,1},{4,6},{5,7},{6,4},{7,5},{8,10},{9,11},{10,... | collective-permute-start | bytes 2359304 | tf_op jit(solution)/shard_map/ppermute | solution.py:1094
  81.7 153.9 %collective-permute-start.2 = (bf16[256,1536]{1,0:T(8,128)(2,1)S(1)}, bf16[256,1536]{1,0:T(8,128)(2,1)S(1)}, u32[]{:S(2)}, u32[]{:S(2)}) collective-permute-start(bf16[256,1536]{1,0:T(8,128)(2,1)S(1)} %multiply_convert_fusion.refs_0_), channel_id=1, source_target_pairs={{0,3},{1,0},{2,1},{3,2},{4,7},{5,4},{6,5},{7,6},{8,11},{9,8},{10,9... | collective-permute-start | bytes 2359304 | tf_op jit(solution)/shard_map/ppermute | solution.py:1094
  235.5 0.9 copy-start.14
  235.5 1.3 copy-start.15
  236.4 0.9 copy-start.16
  264.1 370.2 %reduce-scatter.6.cloned.1.call-start = ((), (), s32[]{:S(2)}) async-start(), calls=%async_computation.7 | async-start | bytes 15925248 | tf_op jit(solution)/shard_map/reduce_scatter | solution.py:1191
  306.9 340.4 %reduce-scatter.8.cloned.1.call-start = ((), (), s32[]{:S(2)}) async-start(), calls=%async_computation.8 | async-start | bytes 26542080 | tf_op jit(solution)/shard_map/reduce_scatter | solution.py:1191
  494.3 136.6 %collective-permute-start.3 = (bf16[256,1536]{1,0:T(8,128)(2,1)}, bf16[256,1536]{1,0:T(8,128)(2,1)S(1)}, u32[]{:S(2)}, u32[]{:S(2)}) collective-permute-start(bf16[256,1536]{1,0:T(8,128)(2,1)} %get-tuple-element.118), channel_id=1, source_target_pairs={{0,1},{1,2},{2,3},{3,0},{4,5},{5,6},{6,7},{7,4},{8,9},{9,10},{10,1... | collective-permute-start | bytes 2359304 | tf_op jit(solution)/shard_map/ppermute | solution.py:1106
  494.3 136.6 %collective-permute-start.4 = (bf16[256,1536]{1,0:T(8,128)(2,1)}, bf16[256,1536]{1,0:T(8,128)(2,1)}, u32[]{:S(2)}, u32[]{:S(2)}) collective-permute-start(bf16[256,1536]{1,0:T(8,128)(2,1)} %get-tuple-element.120), channel_id=1, source_target_pairs={{0,2},{1,3},{2,0},{3,1},{4,6},{5,7},{6,4},{7,5},{8,10},{9,11},{10,... | collective-permute-start | bytes 2359304 | tf_op jit(solution)/shard_map/ppermute | solution.py:1106
  497.1 133.8 %collective-permute-start.5 = (bf16[256,1536]{1,0:T(8,128)(2,1)S(1)}, bf16[256,1536]{1,0:T(8,128)(2,1)}, u32[]{:S(2)}, u32[]{:S(2)}) collective-permute-start(bf16[256,1536]{1,0:T(8,128)(2,1)S(1)} %get-tuple-element.119), channel_id=1, source_target_pairs={{0,3},{1,0},{2,1},{3,2},{4,7},{5,4},{6,5},{7,6},{8,11},{9,8},{10,9... | collective-permute-start | bytes 2359304 | tf_op jit(solution)/shard_map/ppermute | solution.py:1106
  624.0 6.8 %copy-start.6 = (f32[256,1536]{1,0:T(8,128)S(1)}, f32[256,1536]{1,0:T(8,128)}, u32[]{:S(2)}) copy-start(f32[256,1536]{1,0:T(8,128)} %get-tuple-element.55.refs_6_) | copy-start | bytes 4718596
  634.2 22.5 %copy-start.8 = (f32[256,1536]{1,0:T(8,128)S(1)}, f32[256,1536]{1,0:T(8,128)}, u32[]{:S(2)}) copy-start(f32[256,1536]{1,0:T(8,128)} %get-tuple-element.143) | copy-start | bytes 4718596
Sparse Core Ops, SparseCore 0:
  10.4 36.5 all-gather.3
  49.5 118.5 all-gather.5
  170.6 118.5 all-gather.7
  292.5 76.6 reduce-scatter.3
  372.6 99.5 reduce-scatter.5
  475.7 171.5 reduce-scatter.7

commit v6 on v5

--- a/solution.py
+++ b/solution.py
@@ -2,6 +2,7 @@
 
 import jax
 import jax.numpy as jnp
+import numpy as np
 from jax import lax
 from jax.experimental import pallas as pl
 from jax.experimental.pallas import tpu as pltpu
@@ -131,6 +132,160 @@
     ]
 
 
+class PlaneGather:
+    def __init__(self, plane, w_ref, wo_ref, out_send, out_recv, on_send, on_recv, kept_sem):
+        self.plane, self.w_ref, self.wo_ref = plane, w_ref, wo_ref
+        self.out_send, self.out_recv = out_send, out_recv
+        self.on_send, self.on_recv = on_send, on_recv
+        self.rows = w_ref.shape[0]
+        self.kept = pltpu.make_async_copy(w_ref, rows_of(wo_ref, plane.me, self.rows), kept_sem)
+
+    def outward(self, shift, target, source_device):
+        return pltpu.make_async_remote_copy(
+            src_ref=self.w_ref,
+            dst_ref=rows_of(self.wo_ref, source_device, self.rows),
+            send_sem=self.out_send.at[shift],
+            recv_sem=self.out_recv.at[shift],
+            device_id={"fsdp": target},
+        )
+
+    def onward(self, shift, source_device):
+        part = rows_of(self.wo_ref, source_device, self.rows)
+        return pltpu.make_async_remote_copy(
+            src_ref=part,
+            dst_ref=part,
+            send_sem=self.on_send.at[shift - 1],
+            recv_sem=self.on_recv.at[shift - 1],
+            device_id={"fsdp": self.plane.partner},
+        )
+
+    def start(self):
+        plane = self.plane
+        for shift in range(1, plane.chips):
+            self.outward(shift, plane.peer(shift), plane.me).start()
+        self.outward(0, plane.partner, plane.me).start()
+        self.kept.start()
+
+    def forward(self):
+        plane = self.plane
+        for shift in range(1, plane.chips):
+            self.outward(shift, plane.peer(shift), plane.peer(-shift)).wait_recv()
+            self.onward(shift, plane.peer(-shift)).start()
+
+    def finish(self):
+        plane = self.plane
+        self.outward(0, plane.partner, plane.partner).wait_recv()
+        for shift in range(1, plane.chips):
+            self.onward(shift, plane.chip_at(-shift) * 2 + 1 - plane.core).wait_recv()
+        for shift in range(1, plane.chips):
+            self.outward(shift, plane.peer(shift), plane.me).wait_send()
+            self.onward(shift, plane.peer(-shift)).wait_send()
+        self.outward(0, plane.partner, plane.me).wait_send()
+        self.kept.wait()
+
+
+class ExpertSums:
+    def __init__(self, plane, picks, grads_ref, out_ref, *refs):
+        self.plane, self.picks, self.grads_ref, self.out_ref = plane, picks, grads_ref, out_ref
+        (
+            self.got, self.own, self.chip_got, self.held,
+            self.pair_send, self.pair_recv, self.own_sem,
+            self.chip_send, self.chip_recv, self.put_sem,
+        ) = refs
+        self.rows = out_ref.shape[2]
+
+    def area(self, index, dest):
+        low = pl.multiple_of(dest * self.rows, self.rows)
+        return self.grads_ref.at[self.picks[index], :, pl.ds(low, self.rows)]
+
+    def to_pair(self, index, shift):
+        plane = self.plane
+        return pltpu.make_async_remote_copy(
+            src_ref=self.area(index, plane.chip_at(shift) * 2 + 1 - plane.core),
+            dst_ref=self.got.at[index, shift],
+            send_sem=self.pair_send.at[index, shift],
+            recv_sem=self.pair_recv.at[index, shift],
+            device_id={"fsdp": plane.partner},
+        )
+
+    def keep(self, index, shift):
+        return pltpu.make_async_copy(
+            self.area(index, self.plane.peer(shift)),
+            self.own.at[index, shift],
+            self.own_sem.at[index, shift],
+        )
+
+    def to_chip(self, index, shift):
+        return pltpu.make_async_remote_copy(
+            src_ref=self.own.at[index, shift],
+            dst_ref=self.chip_got.at[index, shift - 1],
+            send_sem=self.chip_send.at[index, shift - 1],
+            recv_sem=self.chip_recv.at[index, shift - 1],
+            device_id={"fsdp": self.plane.peer(shift)},
+        )
+
+    def put(self, index):
+        return pltpu.make_async_copy(
+            self.held.at[index], self.out_ref.at[index], self.put_sem.at[index]
+        )
+
+    def order(self):
+        return list(range(1, self.plane.chips)) + [0]
+
+    def begin(self, index):
+        for shift in self.order():
+            self.to_pair(index, shift).start()
+            self.keep(index, shift).start()
+
+    def pass_on(self, index):
+        for shift in self.order():
+            self.to_pair(index, shift).wait_recv()
+            self.keep(index, shift).wait()
+            for slot in range(self.own.shape[2]):
+                both = self.own[index, shift, slot].astype(jnp.float32) + self.got[
+                    index, shift, slot
+                ].astype(jnp.float32)
+                self.own[index, shift, slot] = both.astype(jnp.bfloat16)
+            if shift > 0:
+                self.to_chip(index, shift).start()
+
+    def collect(self, index):
+        chips = self.plane.chips
+        for shift in range(1, chips):
+            self.to_chip(index, shift).wait_recv()
+        for slot in range(self.own.shape[2]):
+            total = self.own[index, 0, slot].astype(jnp.float32)
+            for shift in range(1, chips):
+                total = total + self.chip_got[index, shift - 1, slot].astype(jnp.float32)
+            self.held[index, slot] = total.astype(jnp.bfloat16)
+        self.put(index).start()
+
+    def finish(self):
+        for index in range(len(self.picks)):
+            self.put(index).wait()
+            for shift in self.order():
+                self.to_pair(index, shift).wait_send()
+                if shift > 0:
+                    self.to_chip(index, shift).wait_send()
+
+
+def expert_buffers(count, chips, rows, width):
+    if count == 0:
+        return []
+    return [
+        pltpu.VMEM((count, chips, 3, rows, width), jnp.bfloat16),
+        pltpu.VMEM((count, chips, 3, rows, width), jnp.bfloat16),
+        pltpu.VMEM((count, chips - 1, 3, rows, width), jnp.bfloat16),
+        pltpu.VMEM((count, 3, rows, width), jnp.bfloat16),
+        pltpu.SemaphoreType.DMA((count, chips)),
+        pltpu.SemaphoreType.DMA((count, chips)),
+        pltpu.SemaphoreType.DMA((count, chips)),
+        pltpu.SemaphoreType.DMA((count, chips - 1)),
+        pltpu.SemaphoreType.DMA((count, chips - 1)),
+        pltpu.SemaphoreType.DMA((count,)),
+    ]
+
+
 class LineScatter:
     def __init__(self, count, x_refs, o_ref, recv, send, send_sem, recv_sem):
         self.count, self.x_refs, self.o_ref = count, x_refs, o_ref
@@ -225,9 +380,12 @@
     return inverse * (weighted - scaled * row_inner), gain_grad
 
 
-def enter_kernel(count):
+def enter_kernel(count, plane=None):
     barrier = pltpu.get_barrier_semaphore()
-    pl.semaphore_wait(barrier, line_signal(barrier, lax.axis_index("tp"), count))
+    waits = line_signal(barrier, lax.axis_index("tp"), count)
+    if plane is not None:
+        waits = waits + plane.signal(barrier)
+    pl.semaphore_wait(barrier, waits)
 
 
 def remote_params(ident, limit=60):
@@ -241,19 +399,40 @@
 TRANSFER = pl.CostEstimate(flops=0, transcendentals=0, bytes_accessed=150_000_000)
 
 
-def norm_gather_kernel(
-    count, emb_ref, gain_ref, routes_ref, rows_ref, mask_ref, cols_ref, turned_ref, counts_ref, *sems
-):
-    enter_kernel(count)
-    line = LineGather(count, rows_ref, *sems)
+def norm_gather_kernel(count, fsdp_count, low, *refs):
+    emb_ref, gain_ref, routes_ref, w_ref, *refs = refs
+    stacks, refs = (refs[:3], refs[3:]) if low else ((), refs)
+    rows_ref, mask_ref, cols_ref, turned_ref, counts_ref, wo_ref, *refs = refs
+    packed, refs = (refs[0], refs[1:]) if low else (None, refs)
+    row_send, row_recv, *refs = refs
+    plane = Plane(fsdp_count)
+    if low:
+        held, in_sem, out_sem = refs[5:]
+        gets, puts = pack_copies(low, stacks, packed, held, in_sem, out_sem)
+        for get in gets:
+            get.start()
+    enter_kernel(count, plane)
+    line = LineGather(count, rows_ref, row_send, row_recv)
+    weights = PlaneGather(plane, w_ref, wo_ref, *refs[:5])
     start_x = emb_ref[...].astype(jnp.float32) * emb_scale
     normed = start_x * inverse_norm(start_x) * gain_ref[...]
     rows_ref[own_rows(line.rows), :] = normed.astype(jnp.bfloat16)
     for step in range(count - 1):
         line.start(step)
         if step == 0:
+            weights.start()
             place_routes(line.rows, routes_ref, mask_ref, cols_ref, turned_ref, counts_ref)
+            if low:
+                for get, put in zip(gets, puts):
+                    get.wait()
+                    put.start()
+        if step == count - 2:
+            weights.forward()
         line.arrive(step)
+    if low:
+        for put in puts:
+            put.wait()
+    weights.finish()
     line.finish()
 
 
@@ -282,24 +461,43 @@
         turned_ref[:, area] = places.T.astype(jnp.int32)
 
 
-def norm_gather(emb, gain_row, routes, count, ident):
+def norm_gather(emb, gain_row, routes, weights, stacks, low, count, fsdp_count, ident):
     rows, width = emb.shape
     group = rows * count
+    chips = fsdp_count // 2
+    experts, share, hidden = stacks[0].shape
+    span = experts - low
+    outs = [
+        jax.ShapeDtypeStruct((group, width), jnp.bfloat16),
+        jax.ShapeDtypeStruct((group, 128), jnp.float32),
+        jax.ShapeDtypeStruct((group, 128), jnp.int32),
+        jax.ShapeDtypeStruct((128, group), jnp.int32),
+        jax.ShapeDtypeStruct((1, 128), jnp.int32),
+        jax.ShapeDtypeStruct((weights.shape[0] * fsdp_count, weights.shape[1]), jnp.bfloat16),
+    ]
+    scratch = line_sems(count) + [
+        pltpu.SemaphoreType.DMA((chips,)),
+        pltpu.SemaphoreType.DMA((chips,)),
+        pltpu.SemaphoreType.DMA((chips - 1,)),
+        pltpu.SemaphoreType.DMA((chips - 1,)),
+        pltpu.SemaphoreType.DMA,
+    ]
+    if low:
+        outs.append(jax.ShapeDtypeStruct((span, 3, share, hidden), jnp.bfloat16))
+        scratch += [
+            pltpu.VMEM((3, span, share, hidden), jnp.bfloat16),
+            pltpu.SemaphoreType.DMA((3,)),
+            pltpu.SemaphoreType.DMA((3,)),
+        ]
     return pl.pallas_call(
-        functools.partial(norm_gather_kernel, count),
-        out_shape=[
-            jax.ShapeDtypeStruct((group, width), jnp.bfloat16),
-            jax.ShapeDtypeStruct((group, 128), jnp.float32),
-            jax.ShapeDtypeStruct((group, 128), jnp.int32),
-            jax.ShapeDtypeStruct((128, group), jnp.int32),
-            jax.ShapeDtypeStruct((1, 128), jnp.int32),
-        ],
-        in_specs=[IN_VMEM] * 3,
-        out_specs=[IN_VMEM] * 5,
-        scratch_shapes=line_sems(count),
+        functools.partial(norm_gather_kernel, count, fsdp_count, low),
+        out_shape=outs,
+        in_specs=[IN_VMEM] * 4 + [IN_PLACE] * (3 if low else 0),
+        out_specs=[IN_VMEM] * 5 + [IN_PLACE] * (len(outs) - 5),
+        scratch_shapes=scratch,
         compiler_params=remote_params(ident, 48),
         cost_estimate=TRANSFER,
-    )(emb, gain_row, routes)
+    )(emb, gain_row, routes, weights, *(stacks if low else ()))
 
 
 def mid_kernel(
@@ -374,26 +572,51 @@
     )(part, emb, gain_row, weights, mask)
 
 
-def moe_back_kernel(count, runs, *refs):
-    dx_parts, y_parts, refs = refs[:runs], refs[runs : 2 * runs], refs[2 * runs :]
+def moe_back_kernel(count, fsdp_count, runs, picks, *refs):
+    dx_refs, y_refs, refs = refs[:runs], refs[runs : 2 * runs], refs[2 * runs :]
+    mid_ref, cotangent_ref, own_gates, gain_ref, router_ref, *refs = refs
+    grads_ref, refs = (refs[0], refs[1:]) if picks else (None, refs)
+    y_ref, mid_grad, gain_grad, sent_ref, *refs = refs
+    sums_ref, refs = (refs[0], refs[1:]) if picks else (None, refs)
     (
-        mid_ref, cotangent_ref, own_gates, gain_ref, router_ref,
-        y_ref, mid_grad, gain_grad, sent_ref,
-        sum_ref, recv, send, sum_send, sum_recv, row_send, row_recv,
+        dx_parts, y_parts, load_sem, store_sem,
+        sum_ref, recv, send, sum_send, sum_recv, row_send, row_recv, *refs,
     ) = refs
-    enter_kernel(count)
-    total = LineScatter(count, dx_parts, sum_ref, recv, send, sum_send, sum_recv)
+    loads = []
+    for index, (source, parts) in enumerate(
+        [(ref, dx_parts) for ref in dx_refs] + [(ref, y_parts) for ref in y_refs]
+    ):
+        loads.append(
+            pltpu.make_async_copy(source, parts.at[index % runs], load_sem.at[index])
+        )
+        loads[-1].start()
+    plane = Plane(fsdp_count) if picks else None
+    enter_kernel(count, plane)
+    total = LineScatter(
+        count, [dx_parts.at[run] for run in range(runs)], sum_ref, recv, send, sum_send, sum_recv
+    )
     line = LineGather(count, sent_ref, row_send, row_recv)
+    experts = ExpertSums(plane, picks, grads_ref, sums_ref, *refs) if picks else None
     rows, width = mid_ref.shape
+    store = pltpu.make_async_copy(y_parts.at[0], y_ref, store_sem)
+    for index in range(len(picks)):
+        experts.begin(index)
+    for load in loads[:runs]:
+        load.wait()
     for step in range(count - 1):
         total.start(step)
         if step == 0:
-            for chunk in range(count):
+            for load in loads[runs:]:
+                load.wait()
+            for chunk in range(count if runs > 1 else 0):
                 area = slice(chunk * rows, (chunk + 1) * rows)
-                whole = y_parts[0][area, :].astype(jnp.float32)
-                for y_part in y_parts[1:]:
-                    whole = whole + y_part[area, :].astype(jnp.float32)
-                y_ref[area, :] = whole.astype(y_ref.dtype)
+                whole = y_parts[0, area, :].astype(jnp.float32)
+                for run in range(1, runs):
+                    whole = whole + y_parts[run, area, :].astype(jnp.float32)
+                y_parts[0, area, :] = whole.astype(y_parts.dtype)
+            store.start()
+        if step < len(picks):
+            experts.pass_on(step)
         total.arrive(step)
     total.collect()
     gates = own_gates[...]
@@ -410,42 +633,67 @@
     sent_ref[own, width:] = logits_grad
     for step in range(count - 1):
         line.start(step)
+        if 0 < step <= len(picks):
+            experts.collect(step - 1)
         line.arrive(step)
+    for index in range(count - 2, len(picks)):
+        experts.collect(index)
     line.finish()
     total.finish()
-
-
-def find_mid_grad(dx_parts, y_parts, mid, cotangent, own_gates, gain_row, weights, used, count, ident):
+    store.wait()
+    if picks:
+        experts.finish()
+
+
+def find_mid_grad(
+    dx_parts, y_parts, mid, cotangent, own_gates, gain_row, weights, used, grads, picks,
+    count, fsdp_count, ident,
+):
     rows, width = mid.shape
     runs, group = len(dx_parts), rows * count
     wide = dx_parts[0].shape[1]
+    share = grads.shape[2] // fsdp_count
+    sums = [jax.ShapeDtypeStruct((len(picks), 3, share, grads.shape[3]), jnp.bfloat16)]
+    sums = sums if picks else []
     return pl.pallas_call(
-        functools.partial(moe_back_kernel, count, runs),
+        functools.partial(moe_back_kernel, count, fsdp_count, runs, picks),
         grid=(1,),
         out_shape=[
             jax.ShapeDtypeStruct((group, width), jnp.bfloat16),
             jax.ShapeDtypeStruct((rows, width), jnp.float32),
             jax.ShapeDtypeStruct((1, width), jnp.float32),
             jax.ShapeDtypeStruct((group, wide), jnp.bfloat16),
-        ],
-        in_specs=[IN_VMEM] * (2 * runs + 4)
-        + [pl.BlockSpec((width, 128), lambda step: (0, used // 128))],
-        out_specs=[IN_VMEM] * 4,
-        scratch_shapes=[pltpu.VMEM((rows, wide), jnp.float32)]
+        ]
+        + sums,
+        in_specs=[IN_PLACE] * (2 * runs)
+        + [IN_VMEM] * 4
+        + [pl.BlockSpec((width, 128), lambda step: (0, used // 128))]
+        + [IN_PLACE] * len(sums),
+        out_specs=[IN_PLACE] + [IN_VMEM] * 3 + [IN_PLACE] * len(sums),
+        scratch_shapes=[
+            pltpu.VMEM((runs, group, wide), jnp.bfloat16),
+            pltpu.VMEM((runs, group, width), jnp.bfloat16),
+            pltpu.SemaphoreType.DMA((2 * runs,)),
+            pltpu.SemaphoreType.DMA,
+            pltpu.VMEM((rows, wide), jnp.float32),
+        ]
         + line_buffers(count, rows, wide)
-        + line_sems(count),
-        compiler_params=remote_params(ident, 62),
+        + line_sems(count)
+        + expert_buffers(len(picks), fsdp_count // 2, share, grads.shape[3]),
+        compiler_params=remote_params(ident, 63),
         cost_estimate=TRANSFER,
-    )(*dx_parts, *y_parts, mid, cotangent, own_gates, gain_row, weights)
-
-
-def finish_kernel(tp_count, fsdp_count, *refs):
+    )(*dx_parts, *y_parts, mid, cotangent, own_gates, gain_row, weights, *([grads] if picks else []))
+
+
+def finish_kernel(tp_count, fsdp_count, picks, *refs):
     x_ref, w_ref, emb_ref, gain_ref, mid_grad, gain_two, *refs = refs
+    grads_ref, refs = (refs[0], refs[1:]) if picks else (None, refs)
+    grad_ref, w_sum, gains_ref, *refs = refs
+    sums_ref, refs = (refs[0], refs[1:]) if picks else (None, refs)
     (
-        grad_ref, w_sum, gains_ref,
         line_recv, line_send, line_send_sem, line_recv_sem,
         pair_got, chip_sums, chip_got, pair_send, pair_recv, chip_send, chip_recv,
-        tp_got, fsdp_got, small_send, small_recv,
+        tp_got, fsdp_got, small_send, small_recv, *refs,
     ) = refs
     plane = Plane(fsdp_count)
     tp_me, fsdp_me = lax.axis_index("tp"), plane.me
@@ -505,15 +753,20 @@
             total = total + got[index]
         return total
 
+    experts = ExpertSums(plane, picks, grads_ref, sums_ref, *refs) if picks else None
     line.start(0)
     order = list(range(1, plane.chips)) + [0]
     for shift in order:
         to_pair(shift).start()
+    for index in range(len(picks)):
+        experts.begin(index)
     for shift in order:
         to_pair(shift).wait_recv()
         if shift > 0:
             chip_sums[shift - 1] = both_cores(shift).astype(chip_sums.dtype)
             to_chip(shift).start()
+    for index in range(len(picks)):
+        experts.pass_on(index)
     line.arrive(0)
     for step in range(1, tp_count - 1):
         line.start(step)
@@ -531,6 +784,8 @@
         to_chip(shift).wait_recv()
         total = total + chip_got[shift - 1].astype(jnp.float32)
     w_sum[...] = total
+    for index in range(len(picks)):
+        experts.collect(index)
     gains_ref[...] = exchange("tp", tp_me, tp_count, tp_got, 0)
     gains_ref[...] = exchange("fsdp", fsdp_me, fsdp_count, fsdp_got, tp_count)
     line.finish()
@@ -538,22 +793,28 @@
         to_pair(shift).wait_send()
         if shift > 0:
             to_chip(shift).wait_send()
-
-
-def finish(dx_rows, weight_grads, emb, gain_row, mid_grad, gain_two, ident):
+    if picks:
+        experts.finish()
+
+
+def finish(dx_rows, weight_grads, emb, gain_row, mid_grad, gain_two, grads, picks, ident):
     tp_count, fsdp_count = lax.axis_size("tp"), lax.axis_size("fsdp")
     rows, width = emb.shape
     w_rows, w_width = weight_grads.shape[0] // fsdp_count, weight_grads.shape[1]
     chips = fsdp_count // 2
+    share = grads.shape[2] // fsdp_count
+    sums = [jax.ShapeDtypeStruct((len(picks), 3, share, grads.shape[3]), jnp.bfloat16)]
+    sums = sums if picks else []
     return pl.pallas_call(
-        functools.partial(finish_kernel, tp_count, fsdp_count),
+        functools.partial(finish_kernel, tp_count, fsdp_count, picks),
         out_shape=[
             jax.ShapeDtypeStruct((rows, width), jnp.float32),
             jax.ShapeDtypeStruct((w_rows, w_width), jnp.float32),
             jax.ShapeDtypeStruct((8, width), jnp.float32),
+            *sums,
         ],
-        in_specs=[IN_VMEM] * 6,
-        out_specs=[IN_VMEM] * 3,
+        in_specs=[IN_VMEM] * 6 + [IN_PLACE] * len(sums),
+        out_specs=[IN_VMEM] * 3 + [IN_PLACE] * len(sums),
         scratch_shapes=line_buffers(tp_count, rows, width)
         + [
             pltpu.VMEM((chips, w_rows, w_width), jnp.bfloat16),
@@ -567,14 +828,14 @@
             pltpu.VMEM((fsdp_count, 8, width), jnp.float32),
             pltpu.SemaphoreType.DMA((tp_count + fsdp_count,)),
             pltpu.SemaphoreType.DMA((tp_count + fsdp_count,)),
-        ],
+        ]
+        + expert_buffers(len(picks), chips, share, grads.shape[3]),
         compiler_params=remote_params(ident),
         cost_estimate=TRANSFER,
-    )(dx_rows, weight_grads, emb, gain_row, mid_grad, gain_two)
-
-
-def pack_kernel(low, *refs):
-    sources, target, held, in_sem, out_sem = refs[:-4], *refs[-4:]
+    )(dx_rows, weight_grads, emb, gain_row, mid_grad, gain_two, *([grads] if picks else []))
+
+
+def pack_copies(low, sources, target, held, in_sem, out_sem):
     span = target.shape[0]
     gets = [
         pltpu.make_async_copy(source.at[pl.ds(low, span)], held.at[slot], in_sem.at[slot])
@@ -584,6 +845,12 @@
         pltpu.make_async_copy(held.at[slot], target.at[:, slot], out_sem.at[slot])
         for slot in range(len(sources))
     ]
+    return gets, puts
+
+
+def pack_kernel(low, *refs):
+    sources, target, held, in_sem, out_sem = refs[:-4], *refs[-4:]
+    gets, puts = pack_copies(low, sources, target, held, in_sem, out_sem)
     for get in gets:
         get.start()
     for get, put in zip(gets, puts):
@@ -960,13 +1227,13 @@
 
 def attend_tables():
     half = HEAD_DIM // 2
-    positions = jnp.arange(SEQ).astype(jnp.float32)
-    frequency = rope_base ** (-jnp.arange(half).astype(jnp.float32) * 2.0 / HEAD_DIM)
-    angles = positions[:, None] * frequency[None, :]
-    cosine, sine = jnp.cos(angles), jnp.sin(angles)
+    positions = np.arange(SEQ, dtype=np.float32)
+    frequency = np.float32(rope_base) ** (-np.arange(half, dtype=np.float32) * 2.0 / HEAD_DIM)
+    angles = (positions[:, None] * frequency[None, :].astype(np.float32)).astype(np.float32)
+    cosine, sine = np.cos(angles), np.sin(angles)
     return (
-        jnp.concatenate([cosine, cosine], axis=1),
-        jnp.concatenate([-sine, sine], axis=1),
+        jnp.asarray(np.concatenate([cosine, cosine], axis=1)),
+        jnp.asarray(np.concatenate([-sine, sine], axis=1)),
     )
 
 
@@ -1108,7 +1375,8 @@
     return total
 
 
-RUNS = (0, 2, 5, 10)
+RUNS = (0, 6, 10)
+DIRECT = (2, 2)
 
 
 def local(
@@ -1134,25 +1402,26 @@
     q_width, kv_width = w_query.shape[1], w_key.shape[1]
     used = 2 * (q_width + kv_width)
     group_size = local_rows * tp_count
-    gathers = 2 if group_size <= 1024 else 1
-
-    attn_w = lax.all_gather(
-        join([w_query, w_key, w_value, w_out], w_router.T, used + 128),
-        "fsdp",
-        axis=0,
-        tiled=True,
-    )
+    fsdp_count = lax.axis_size("fsdp")
+    split = group_size <= 1024
+    runs = [edge * experts_here // RUNS[-1] for edge in RUNS] if split else [0, experts_here]
+    stacks = (w_gate, w_up, w_down)
+    pieces = [lax.all_gather(pack(stacks, 0, runs[1]), "fsdp", axis=2, tiled=True)]
     gain_one = norm1_gain.astype(jnp.float32)[None, :]
     gain_two = norm2_gain.astype(jnp.float32)[None, :]
-    group_rows, mask, place_cols, place_rows, counts = norm_gather(
-        emb, gain_one, routes, tp_count, 0
+    group_rows, mask, place_cols, place_rows, counts, attn_w, *packed = norm_gather(
+        emb,
+        gain_one,
+        routes,
+        join([w_query, w_key, w_value, w_out], w_router.T, used + 128),
+        stacks,
+        runs[1] if split else 0,
+        tp_count,
+        fsdp_count,
+        0,
     )
-    edges = [experts_here * part // gathers for part in range(gathers + 1)]
-    stacks = (w_gate, w_up, w_down)
-    pieces = []
-    for low, high in zip(edges[:-1], edges[1:]):
-        pieces.append(lax.all_gather(pack(stacks, low, high), "fsdp", axis=2, tiled=True))
-        stacks, _ = lax.optimization_barrier((stacks, counts))
+    if split:
+        pieces.append(lax.all_gather(packed[0], "fsdp", axis=2, tiled=True))
     late_grad, _ = lax.optimization_barrier((cotangent, counts))
     moe_grad = (resid_scale * late_grad.astype(jnp.float32)).astype(jnp.bfloat16)
     moe_grad_blocks = shifted_blocks(moe_grad, tp_count)
@@ -1167,11 +1436,7 @@
     )
 
     outs = []
-    runs = edges
-    if gathers > 1:
-        runs = sorted({edge * experts_here // RUNS[-1] for edge in RUNS} | set(edges))
-    for first, last in zip(runs[:-1], runs[1:]):
-        home = max(index for index in range(gathers) if edges[index] <= first)
+    for first, last, piece in zip(runs[:-1], runs[1:], pieces):
         outs.append(
             experts_step(
                 meta,
@@ -1180,17 +1445,17 @@
                 gate_rows,
                 moe_rows,
                 moe_grad_blocks,
-                pieces[home],
+                piece,
                 first,
                 last - first,
-                first - edges[home],
+                0,
                 capacity,
             )
         )
-    grad_sums = [
-        lax.psum_scatter(part[2], "fsdp", scatter_dimension=2, tiled=True) for part in outs
-    ]
-    y_part, mid_grad, gain_two_grad, sent = find_mid_grad(
+    grad_sums = [lax.psum_scatter(outs[0][2], "fsdp", scatter_dimension=2, tiled=True)]
+    last_grads = outs[-1][2]
+    picks = (tuple(range(DIRECT[0])), tuple(range(DIRECT[0], sum(DIRECT)))) if split else ((), ())
+    y_part, mid_grad, gain_two_grad, sent, *mid_sums = find_mid_grad(
         [part[1] for part in outs],
         [part[0] for part in outs],
         mid_x,
@@ -1199,16 +1464,23 @@
         gain_two,
         attn_w,
         used,
+        last_grads,
+        picks[0],
         tp_count,
+        fsdp_count,
         2,
     )
     moe_sum = shifted_scatter(y_part, tp_count, tp_index)
     out = (mid_x + resid_scale * moe_sum).astype(jnp.bfloat16)
     dx_one, attn_grads = attend_back(group_rows, attn_w, segment_ids, tables, kept, moe_rows, sent)
-    grad_emb, attn_sum, gain_sums = finish(
-        dx_one, attn_grads, emb, gain_one, mid_grad, gain_two_grad, 3
+    grad_emb, attn_sum, gain_sums, *end_sums = finish(
+        dx_one, attn_grads, emb, gain_one, mid_grad, gain_two_grad, last_grads, picks[1], 3
     )
-    expert_sums = widen(grad_sums, runs)
+    grad_sums = grad_sums + mid_sums + end_sums
+    ends = [0]
+    for part in grad_sums:
+        ends.append(ends[-1] + part.shape[0])
+    expert_sums = widen(grad_sums, ends)
     return (
         out,
         grad_emb,

time: 675 us -> 659 us (0.976)
  waiting for transfers between devices: 13.2 us -> 0.09 us
    pallas_call x3, Pallas kernels: 278 us -> 292 us  [the longest x1 134 us: find_mid_grad(): pl.pallas_call(functools.partial(moe_back_kernel, count, fsdp_count, runs...]
    reduce_scatter x3 -> x1, waiting for transfers between devices: 13.1 us -> 0.01 us  [local(): lax.psum_scatter(outs[0][2], 'fsdp', scatter_dimension=2, tiled=True)]
    pallas_call x3 -> x2, Pallas kernels: 119 us -> 108 us  [experts_step(): pl.pallas_call(functools.partial(experts_kernel, first, capacity), grid_s...]
  transfers between devices with their start and end apart: 12 -> 9, of which waited for: 1 -> 0; matrix products, arithmetic and copies ran while one was open for 3% -> 2% of each run, Pallas kernels for 89% -> 91%
where the time goes in v6:
time: 659 us; the launch traced here: 649 us
  Pallas kernels  603 us (92%)
  local copies, waits for them, and re-layouts  19.2 us (3%)
  between operations  14.2 us (2%)
  starting transfers between devices  8.89 us (1%)
    pallas_call x1, Pallas kernels, find_mid_grad(): pl.pallas_call(functools.partial(moe_back_kernel, count, fsdp_count, runs...  134 us
    pallas_call x1, Pallas kernels, find_mid(): pl.pallas_call(functools.partial(mid_kernel, count), grid=(1,), out_shape...  130 us
    pallas_call x2, Pallas kernels, experts_step(): pl.pallas_call(functools.partial(experts_kernel, first, capacity), grid_s...  108 us
    pallas_call x1, Pallas kernels, finish(): pl.pallas_call(functools.partial(finish_kernel, tp_count, fsdp_count, pic...  96.2 us
    pallas_call x1, Pallas kernels, norm_gather(): pl.pallas_call(functools.partial(norm_gather_kernel, count, fsdp_count, l...  61.5 us
    pallas_call x1, Pallas kernels, attend_back(): pl.pallas_call(attend_back_kernel, grid=(group // SEQ,), in_specs=[by_row...  36.7 us
    pallas_call x1, Pallas kernels, attend(): pl.pallas_call(attend_kernel, grid=(seqs,), in_specs=[by_row(width), fixe...  21.3 us
  transfers between devices with their start and end apart: 9, of which 0 were waited for; matrix products, arithmetic and copies ran while one was open for 2% of the time, Pallas kernels for 91%

profile of v6, /device:TPU:0, one launch (start us, length us, event | category | flops | bytes accessed | tf_op | source)
XLA Modules:
  0.0 649.4 jit_solution(7130573280042089152)
XLA Ops:
  7.2 3.1 shard_map.251
  11.3 1.9 shard_map.247.refs_3_
  13.2 1.0 copy-done.2
  14.2 61.5 %shard_map.248 = (bf16[1024,1536]{1,0:T(8,128)(2,1)}, f32[1024,128]{1,0:T(8,128)S(1)}, s32[1024,128]{1,0:T(8,128)S(1)}, s32[128,1024]{1,0:T(8,128)S(1)}, s32[1,1...) custom-call(bf16[256,1536]{1,0:T(8,128)(2,1)S(1)} %copy-done.1, ...), custom_call_target="tpu_custom_call" | custom-call | bytes 150000000 | tf_op jit(solution)/shard_map/pallas_call | solution.py:492
  75.8 0.8 copy-done.3
  76.5 0.8 copy-done.5
  77.3 0.8 copy-done.6
  78.2 1.1 copy-done.8
  79.5 2.0 collective-permute-start.1
  81.5 1.8 collective-permute-start.2
  83.3 0.6 broadcast_in_dim.16.seg_row
  83.9 0.6 reshape.25.gain_ref.refs_7_
  84.5 21.3 %shard_map.249 = (bf16[6,1024,64]{2,1,0:T(8,128)(2,1)}, bf16[2,1024,64]{2,1,0:T(8,128)(2,1)}, bf16[2,1024,64]{2,1,0:T(8,128)(2,1)}, bf16[1024,384]{1,0:T(8,128)(...) custom-call(bf16[1024,1536]{1,0:T(8,128)(2,1)} %get-tuple-element.50.x_ref, ...), custom_call_target="tpu_custom_call" | custom-call | flops 10000000000 | bytes 60000000 | tf_op jit(solution)/shard_map/pallas_call | solution.py:1243
  105.8 130.2 %shard_map.250 = (f32[256,1536]{1,0:T(8,128)}, bf16[1024,1536]{1,0:T(8,128)(2,1)}, f32[128,1024]{1,0:T(8,128)}, f32[256,128]{1,0:T(8,128)}) custom-call(bf16[1024,1536]{1,0:T(8,128)(2,1)} %get-tuple-element.52.part_ref, bf16[256,1536]{1,0:T(8,128)(2,1)} %refs_2_.6, f32[1,1536]{1,0:T(1,128)} %reshape.25.gain_ref.refs_7_, ...), custom_call_target="tpu_custom_call" | custom-call | bytes 150000000 | tf_op jit(solution)/shard_map/pallas_call | solution.py:552
  236.0 0.6 pad_add_fusion.meta
  236.7 0.9 copy-done.16
  237.6 0.9 copy-done.17
  238.5 63.6 %shard_map.252 = (bf16[1024,1536]{1,0:T(8,128)(2,1)}, bf16[1024,1664]{1,0:T(8,128)(2,1)}, bf16[6,3,1536,512]{3,2,1,0:T(8,128)(2,1)}) custom-call(s32[130]{0:T(256)} %pad_add_fusion.meta, s32[128,1024]{1,0:T(8,128)} %copy-done.6, s32[1024,128]{1,0:T(8,128)} %copy-done.5, f32[128,1024]{1,0:T(8,128)} %get-tuple-element.58.gate_rows, ...), custom_call_target="tpu_custom_call" | custom-call | flops 65456308224 | bytes 56623104 | tf_op jit(solution)/shard_map/pallas_call | solution.py:1012
  302.2 44.6 %shard_map.253 = (bf16[1024,1536]{1,0:T(8,128)(2,1)}, bf16[1024,1664]{1,0:T(8,128)(2,1)}, bf16[4,3,1536,512]{3,2,1,0:T(8,128)(2,1)}) custom-call(s32[130]{0:T(256)} %pad_add_fusion.meta, s32[128,1024]{1,0:T(8,128)} %copy-done.6, s32[1024,128]{1,0:T(8,128)} %copy-done.5, f32[128,1024]{1,0:T(8,128)} %get-tuple-element.58.gate_rows, ...), custom_call_target="tpu_custom_call" | custom-call | flops 43637538816 | bytes 37748736 | tf_op jit(solution)/shard_map/pallas_call | solution.py:1012
  346.8 134.2 %shard_map.254 = (bf16[1024,1536]{1,0:T(8,128)(2,1)}, f32[256,1536]{1,0:T(8,128)}, f32[1,1536]{1,0:T(1,128)}, bf16[1024,1664]{1,0:T(8,128)(2,1)}, bf16[2,3,192,512]{3,2,1,0:T(8,128)(2,1)}) custom-call(bf16[1024,1664]{1,0:T(8,128)(2,1)} %get-tuple-element.61.refs_0_, bf16[1024,1664]{1,0:T(8,128)(2,1)} %get-tuple-element.63.refs_1_, ...), custom_call_target="tpu_custom_call" | custom-call | bytes 150000000 | tf_op jit(solution)/shard_map/pallas_call | solution.py:658
  481.0 2.9 constant_dynamic-slice_fusion.2
  483.9 4.9 collective-permute-start.4
  488.8 36.7 %shard_map.255 = (bf16[1024,1536]{1,0:T(8,128)(2,1)}, bf16[1536,1152]{1,0:T(8,128)(2,1)}) custom-call(bf16[1024,1536]{1,0:T(8,128)(2,1)} %get-tuple-element.50.x_ref, bf16[1536,1152]{1,0:T(8,128)(2,1)} %get-tuple-element.51.w_ref.router_ref.refs_8_, s32[2,1,512]{2,1,0:T(1,128)} %broadcast_in_dim.16.seg_row, f32[512,64]{1,0:T(8,128)} %constant.31.clone.cos_ref, ...), custom_call_target="tpu_custom_call" | custom-call | flops 20000000000 | bytes 100000000 | tf_op jit(solution)/shard_map/pallas_call | solution.py:1289
  525.5 96.2 %shard_map.256 = (f32[256,1536]{1,0:T(8,128)}, f32[192,1152]{1,0:T(8,128)}, f32[8,1536]{1,0:T(8,128)}, bf16[2,3,192,512]{3,2,1,0:T(8,128)(2,1)}) custom-call(bf16[1024,1536]{1,0:T(8,128)(2,1)} %get-tuple-element.75.refs_0_, bf16[1536,1152]{1,0:T(8,128)(2,1)} %get-tuple-element.76.refs_1_, bf16[256,1536]{1,0:T(8,128)(2,1)} %refs_2_.6, f32[1,1536]{1,0:T(1,128)} %copy-done.4, ...), custom_call_target="tpu_custom_call" | custom-call | bytes 150000000 | tf_op jit(solution)/shard_map/pallas_call | solution.py:808
  621.8 1.0 slice.27
  622.8 0.7 copy.29
  623.5 1.5 slice_reduce_fusion
  625.0 1.6 fusion.1
  626.6 1.9 fusion
  628.5 3.0 add_convert_fusion
  631.5 10.0 %shard_map.257 = (f32[10,192,512]{2,1,0:T(8,128)}, f32[10,192,512]{2,1,0:T(8,128)}, f32[10,192,512]{2,1,0:T(8,128)}) custom-call(bf16[6,3,192,512]{3,2,1,0:T(8,128)(2,1)} %reduce-scatter.2.cloned.1.call-done.refs_0_, bf16[2,3,192,512]{3,2,1,0:T(8,128)(2,1)} %get-tuple-element.83.refs_1_, bf16[2,3,192,512]{3,2,1,0:T(8,128)(2,1)} %get-tuple-element.84.refs_2_), custom_call_target="tpu_custom_call" | custom-call | tf_op jit(solution)/shard_map/pallas_call | solution.py:1350
  641.5 1.1 copy.31
  (50 shorter events, 1.3 us)
Async XLA Ops:
  7.2 230.5 %all-gather.3.cloned.1.call-start = ((), (), s32[]{:S(2)}) async-start(), calls=%async_computation.1 | async-start | bytes 31850496 | tf_op jit(solution)/shard_map/all_gather | solution.py:1409
  10.3 0.7 copy-start.12
  10.4 0.8 copy-start.11
  10.4 2.8 copy-start
  10.4 2.8 copy-start.1
  10.4 291.8 %all-gather.5.cloned.1.call-start = ((), (), s32[]{:S(2)}) async-start(), calls=%async_computation.2 | async-start | bytes 21233664 | tf_op jit(solution)/shard_map/all_gather | solution.py:1424
  11.1 64.6 %copy-start.4 = (f32[1,1536]{1,0:T(1,128)}, f32[1,1536]{1,0:T(1,128)S(1)}, u32[]{:S(2)}) copy-start(f32[1,1536]{1,0:T(1,128)S(1)} %reshape.24.refs_1_.refs_3_) | copy-start | bytes 18436
  13.2 1.0 copy-start.2
  75.7 0.8 copy-start.3
  76.5 0.8 copy-start.5
  77.3 0.8 copy-start.6
  78.1 1.1 copy-start.8
  78.1 5.2 copy-start.13
  78.1 5.8 copy-start.14
  78.2 553.4 %reduce-scatter.2.cloned.1.call-start = ((), (), s32[]{:S(2)}) async-start(), calls=%async_computation.3 | async-start | bytes 31850496 | tf_op jit(solution)/shard_map/reduce_scatter | solution.py:1455
  79.4 26.4 %copy-start.10 = (bf16[256,1536]{1,0:T(8,128)(2,1)}, bf16[256,1536]{1,0:T(8,128)(2,1)S(1)}, u32[]{:S(2)}) copy-start(bf16[256,1536]{1,0:T(8,128)(2,1)S(1)} %multiply_convert_fusion.refs_0_) | copy-start | bytes 2359300
  79.4 157.2 %collective-permute-start = (bf16[256,1536]{1,0:T(8,128)(2,1)S(1)}, bf16[256,1536]{1,0:T(8,128)(2,1)S(1)}, u32[]{:S(2)}, u32[]{:S(2)}) collective-permute-start(bf16[256,1536]{1,0:T(8,128)(2,1)S(1)} %multiply_convert_fusion.refs_0_), channel_id=1, source_target_pairs={{0,1},{1,2},{2,3},{3,0},{4,5},{5,6},{6,7},{7,4},{8,9},{9,10},{10,1... | collective-permute-start | bytes 2359304 | tf_op jit(solution)/shard_map/ppermute | solution.py:1361
  79.5 157.2 %collective-permute-start.1 = (bf16[256,1536]{1,0:T(8,128)(2,1)S(1)}, bf16[256,1536]{1,0:T(8,128)(2,1)S(1)}, u32[]{:S(2)}, u32[]{:S(2)}) collective-permute-start(bf16[256,1536]{1,0:T(8,128)(2,1)S(1)} %multiply_convert_fusion.refs_0_), channel_id=1, source_target_pairs={{0,2},{1,3},{2,0},{3,1},{4,6},{5,7},{6,4},{7,5},{8,10},{9,11},{10,... | collective-permute-start | bytes 2359304 | tf_op jit(solution)/shard_map/ppermute | solution.py:1361
  81.5 155.2 %collective-permute-start.2 = (bf16[256,1536]{1,0:T(8,128)(2,1)S(1)}, bf16[256,1536]{1,0:T(8,128)(2,1)S(1)}, u32[]{:S(2)}, u32[]{:S(2)}) collective-permute-start(bf16[256,1536]{1,0:T(8,128)(2,1)S(1)} %multiply_convert_fusion.refs_0_), channel_id=1, source_target_pairs={{0,3},{1,0},{2,1},{3,2},{4,7},{5,4},{6,5},{7,6},{8,11},{9,8},{10,9... | collective-permute-start | bytes 2359304 | tf_op jit(solution)/shard_map/ppermute | solution.py:1361
  236.7 1.9 copy-start.15
  236.7 1.0 copy-start.16
  237.6 0.9 copy-start.17
  483.9 144.6 %collective-permute-start.5 = (bf16[256,1536]{1,0:T(8,128)(2,1)}, bf16[256,1536]{1,0:T(8,128)(2,1)S(1)}, u32[]{:S(2)}, u32[]{:S(2)}) collective-permute-start(bf16[256,1536]{1,0:T(8,128)(2,1)} %get-tuple-element.103), channel_id=1, source_target_pairs={{0,3},{1,0},{2,1},{3,2},{4,7},{5,4},{6,5},{7,6},{8,11},{9,8},{10,9... | collective-permute-start | bytes 2359304 | tf_op jit(solution)/shard_map/ppermute | solution.py:1373
  483.9 144.6 %collective-permute-start.4 = (bf16[256,1536]{1,0:T(8,128)(2,1)}, bf16[256,1536]{1,0:T(8,128)(2,1)}, u32[]{:S(2)}, u32[]{:S(2)}) collective-permute-start(bf16[256,1536]{1,0:T(8,128)(2,1)} %get-tuple-element.104), channel_id=1, source_target_pairs={{0,2},{1,3},{2,0},{3,1},{4,6},{5,7},{6,4},{7,5},{8,10},{9,11},{10,... | collective-permute-start | bytes 2359304 | tf_op jit(solution)/shard_map/ppermute | solution.py:1373
  488.8 139.7 %collective-permute-start.3 = (bf16[256,1536]{1,0:T(8,128)(2,1)S(1)}, bf16[256,1536]{1,0:T(8,128)(2,1)}, u32[]{:S(2)}, u32[]{:S(2)}) collective-permute-start(bf16[256,1536]{1,0:T(8,128)(2,1)S(1)} %get-tuple-element.102), channel_id=1, source_target_pairs={{0,1},{1,2},{2,3},{3,0},{4,5},{5,6},{6,7},{7,4},{8,9},{9,10},{10,1... | collective-permute-start | bytes 2359304 | tf_op jit(solution)/shard_map/ppermute | solution.py:1373
  621.7 6.8 %copy-start.7 = (f32[256,1536]{1,0:T(8,128)S(1)}, f32[256,1536]{1,0:T(8,128)}, u32[]{:S(2)}) copy-start(f32[256,1536]{1,0:T(8,128)} %get-tuple-element.54.refs_4_) | copy-start | bytes 4718596
  631.5 10.0 %copy-start.9 = (f32[256,1536]{1,0:T(8,128)S(1)}, f32[256,1536]{1,0:T(8,128)}, u32[]{:S(2)}) copy-start(f32[256,1536]{1,0:T(8,128)} %get-tuple-element.122) | copy-start | bytes 4718596
Sparse Core Ops, SparseCore 0:
  10.5 152.9 all-gather.2
  165.4 98.5 all-gather.4
  302.3 250.0 reduce-scatter.1

commit v7 on v6

--- a/solution.py
+++ b/solution.py
@@ -287,9 +287,8 @@
 
 
 class LineScatter:
-    def __init__(self, count, x_refs, o_ref, recv, send, send_sem, recv_sem):
-        self.count, self.x_refs, self.o_ref = count, x_refs, o_ref
-        self.recv, self.send = recv, send
+    def __init__(self, count, x_refs, o_ref, recv, send_sem, recv_sem):
+        self.count, self.x_refs, self.o_ref, self.recv = count, x_refs, o_ref, recv
         self.send_sem, self.recv_sem = send_sem, recv_sem
         self.rows = o_ref.shape[0]
         me = self.me = lax.axis_index("tp")
@@ -304,9 +303,9 @@
             total = total + x_ref[area, :].astype(jnp.float32)
         return total
 
-    def hop(self, way, step):
+    def hop(self, way, step, source):
         return pltpu.make_async_remote_copy(
-            src_ref=self.send.at[way, step],
+            src_ref=source,
             dst_ref=self.recv.at[way, step],
             send_sem=self.send_sem.at[way, step],
             recv_sem=self.recv_sem.at[way, step],
@@ -314,30 +313,32 @@
         )
 
     def start(self, step):
-        count, me, send = self.count, self.me, self.send
+        count, me, recv = self.count, self.me, self.recv
         for way in range(2):
             dest = count - 1 - step + me if way == 0 else step - (count - 1 - me)
             active = self.has_next[way] & (step >= self.behind[way])
 
             @pl.when(active & (self.behind[way] == 0))
             def _():
-                send[way, step] = self.block(dest).astype(send.dtype)
-                self.hop(way, step).start()
+                part = rows_of(self.x_refs[0], dest, self.rows)
+                if len(self.x_refs) > 1:
+                    part[...] = self.block(dest).astype(part.dtype)
+                self.hop(way, step, part).start()
 
             if step > 0:
 
                 @pl.when(active & (self.behind[way] > 0))
                 def _():
-                    total = self.block(dest) + self.recv[way, step - 1].astype(jnp.float32)
-                    send[way, step] = total.astype(send.dtype)
-                    self.hop(way, step).start()
+                    total = self.block(dest) + recv[way, step - 1].astype(jnp.float32)
+                    recv[way, step - 1] = total.astype(recv.dtype)
+                    self.hop(way, step, recv.at[way, step - 1]).start()
 
     def arrive(self, step):
         for way in range(2):
 
             @pl.when(self.has_prev[way] & (step >= self.behind[way] - 1))
             def _():
-                self.hop(way, step).wait_recv()
+                self.hop(way, step, self.recv.at[way, step]).wait_recv()
 
     def collect(self):
         self.o_ref[...] = self.block(self.me)
@@ -353,17 +354,14 @@
 
                 @pl.when(self.has_next[way] & (step >= self.behind[way]))
                 def _():
-                    self.hop(way, step).wait_send()
+                    self.hop(way, step, self.recv.at[way, step]).wait_send()
 
 
 def line_buffers(count, rows, width):
-    return [
-        pltpu.VMEM((2, count - 1, rows, width), jnp.bfloat16),
-        pltpu.VMEM((2, count - 1, rows, width), jnp.bfloat16),
-    ] + line_sems(count)
-
-
-def own_rows(rows):
+    return [pltpu.VMEM((2, count - 1, rows, width), jnp.bfloat16)] + line_sems(count)
+
+
+def own_rows(ref, rows):
     return pl.ds(pl.multiple_of(lax.axis_index("tp") * rows, rows), rows)
 
 
@@ -416,7 +414,7 @@
     weights = PlaneGather(plane, w_ref, wo_ref, *refs[:5])
     start_x = emb_ref[...].astype(jnp.float32) * emb_scale
     normed = start_x * inverse_norm(start_x) * gain_ref[...]
-    rows_ref[own_rows(line.rows), :] = normed.astype(jnp.bfloat16)
+    rows_ref[own_rows(rows_ref, line.rows), :] = normed.astype(jnp.bfloat16)
     for step in range(count - 1):
         line.start(step)
         if step == 0:
@@ -501,21 +499,27 @@
 
 
 def mid_kernel(
-    count, part_ref, emb_ref, gain_ref, router_ref, mask_ref,
-    mid_ref, rows_ref, gates_ref, own_gates,
-    recv, send, sum_send, sum_recv, row_send, row_recv,
+    count, part_ref, emb_ref, gain_ref, router_ref, mask_ref, cotangent_ref,
+    mid_ref, rows_ref, gates_ref, own_gates, moe_grads,
+    recv, sum_send, sum_recv, row_send, row_recv, grad_send, grad_recv,
 ):
     enter_kernel(count)
-    total = LineScatter(count, [part_ref], mid_ref, recv, send, sum_send, sum_recv)
+    total = LineScatter(count, [part_ref], mid_ref, recv, sum_send, sum_recv)
     line = LineGather(count, rows_ref, row_send, row_recv)
+    others = LineGather(count, moe_grads, grad_send, grad_recv)
     rows = line.rows
+    moe_grads[own_rows(moe_grads, rows), :] = (
+        resid_scale * cotangent_ref[...].astype(jnp.float32)
+    ).astype(jnp.bfloat16)
     for step in range(count - 1):
         total.start(step)
+        others.start(step)
         total.arrive(step)
+        others.arrive(step)
     total.collect()
     mid = emb_ref[...].astype(jnp.float32) * emb_scale + resid_scale * mid_ref[...]
     mid_ref[...] = mid
-    own = own_rows(rows)
+    own = own_rows(rows_ref, rows)
     rows_ref[own, :] = (mid * inverse_norm(mid) * gain_ref[...]).astype(jnp.bfloat16)
 
     def find_gates(chunk):
@@ -544,9 +548,10 @@
 
     line.finish()
     total.finish()
-
-
-def find_mid(part, emb, gain_row, weights, used, mask, count, ident):
+    others.finish()
+
+
+def find_mid(part, emb, gain_row, weights, used, mask, cotangent, count, ident):
     rows, width = emb.shape
     group = rows * count
     return pl.pallas_call(
@@ -557,6 +562,7 @@
             jax.ShapeDtypeStruct((group, width), jnp.bfloat16),
             jax.ShapeDtypeStruct((128, group), jnp.float32),
             jax.ShapeDtypeStruct((rows, 128), jnp.float32),
+            jax.ShapeDtypeStruct((group, width), jnp.bfloat16),
         ],
         in_specs=[
             IN_VMEM,
@@ -564,23 +570,24 @@
             IN_VMEM,
             pl.BlockSpec((width, 128), lambda step: (0, used // 128)),
             IN_VMEM,
+            IN_VMEM,
         ],
-        out_specs=[IN_VMEM] * 4,
-        scratch_shapes=line_buffers(count, rows, width) + line_sems(count),
+        out_specs=[IN_VMEM] * 5,
+        scratch_shapes=line_buffers(count, rows, width) + line_sems(count) + line_sems(count),
         compiler_params=remote_params(ident),
         cost_estimate=TRANSFER,
-    )(part, emb, gain_row, weights, mask)
+    )(part, emb, gain_row, weights, mask, cotangent)
 
 
 def moe_back_kernel(count, fsdp_count, runs, picks, *refs):
     dx_refs, y_refs, refs = refs[:runs], refs[runs : 2 * runs], refs[2 * runs :]
     mid_ref, cotangent_ref, own_gates, gain_ref, router_ref, *refs = refs
     grads_ref, refs = (refs[0], refs[1:]) if picks else (None, refs)
-    y_ref, mid_grad, gain_grad, sent_ref, *refs = refs
+    out_ref, mid_grad, gain_grad, sent_ref, *refs = refs
     sums_ref, refs = (refs[0], refs[1:]) if picks else (None, refs)
     (
-        dx_parts, y_parts, load_sem, store_sem,
-        sum_ref, recv, send, sum_send, sum_recv, row_send, row_recv, *refs,
+        dx_parts, y_parts, load_sem, sum_ref, moe_ref,
+        recv, sum_send, sum_recv, moe_recv, moe_send, moe_recv_sem, row_send, row_recv, *refs,
     ) = refs
     loads = []
     for index, (source, parts) in enumerate(
@@ -593,28 +600,20 @@
     plane = Plane(fsdp_count) if picks else None
     enter_kernel(count, plane)
     total = LineScatter(
-        count, [dx_parts.at[run] for run in range(runs)], sum_ref, recv, send, sum_send, sum_recv
+        count, [dx_parts.at[run] for run in range(runs)], sum_ref, recv, sum_send, sum_recv
+    )
+    moe = LineScatter(
+        count, [y_parts.at[run] for run in range(runs)], moe_ref, moe_recv, moe_send, moe_recv_sem
     )
     line = LineGather(count, sent_ref, row_send, row_recv)
     experts = ExpertSums(plane, picks, grads_ref, sums_ref, *refs) if picks else None
     rows, width = mid_ref.shape
-    store = pltpu.make_async_copy(y_parts.at[0], y_ref, store_sem)
     for index in range(len(picks)):
         experts.begin(index)
     for load in loads[:runs]:
         load.wait()
     for step in range(count - 1):
         total.start(step)
-        if step == 0:
-            for load in loads[runs:]:
-                load.wait()
-            for chunk in range(count if runs > 1 else 0):
-                area = slice(chunk * rows, (chunk + 1) * rows)
-                whole = y_parts[0, area, :].astype(jnp.float32)
-                for run in range(1, runs):
-                    whole = whole + y_parts[run, area, :].astype(jnp.float32)
-                y_parts[0, area, :] = whole.astype(y_parts.dtype)
-            store.start()
         if step < len(picks):
             experts.pass_on(step)
         total.arrive(step)
@@ -628,19 +627,25 @@
     grad = cotangent_ref[...].astype(jnp.float32) + from_norm
     mid_grad[...] = grad
     gain_grad[...] = gain_part
-    own = own_rows(rows)
+    own = own_rows(sent_ref, rows)
     sent_ref[own, :width] = (resid_scale * grad).astype(jnp.bfloat16)
     sent_ref[own, width:] = logits_grad
+    for load in loads[runs:]:
+        load.wait()
     for step in range(count - 1):
         line.start(step)
+        moe.start(step)
         if 0 < step <= len(picks):
             experts.collect(step - 1)
+        moe.arrive(step)
         line.arrive(step)
+    moe.collect()
+    out_ref[...] = (mid_ref[...] + resid_scale * moe_ref[...]).astype(out_ref.dtype)
     for index in range(count - 2, len(picks)):
         experts.collect(index)
     line.finish()
     total.finish()
-    store.wait()
+    moe.finish()
     if picks:
         experts.finish()
 
@@ -659,7 +664,7 @@
         functools.partial(moe_back_kernel, count, fsdp_count, runs, picks),
         grid=(1,),
         out_shape=[
-            jax.ShapeDtypeStruct((group, width), jnp.bfloat16),
+            jax.ShapeDtypeStruct((rows, width), jnp.bfloat16),
             jax.ShapeDtypeStruct((rows, width), jnp.float32),
             jax.ShapeDtypeStruct((1, width), jnp.float32),
             jax.ShapeDtypeStruct((group, wide), jnp.bfloat16),
@@ -669,15 +674,16 @@
         + [IN_VMEM] * 4
         + [pl.BlockSpec((width, 128), lambda step: (0, used // 128))]
         + [IN_PLACE] * len(sums),
-        out_specs=[IN_PLACE] + [IN_VMEM] * 3 + [IN_PLACE] * len(sums),
+        out_specs=[IN_VMEM] * 4 + [IN_PLACE] * len(sums),
         scratch_shapes=[
             pltpu.VMEM((runs, group, wide), jnp.bfloat16),
             pltpu.VMEM((runs, group, width), jnp.bfloat16),
             pltpu.SemaphoreType.DMA((2 * runs,)),
-            pltpu.SemaphoreType.DMA,
             pltpu.VMEM((rows, wide), jnp.float32),
+            pltpu.VMEM((rows, width), jnp.float32),
         ]
         + line_buffers(count, rows, wide)
+        + line_buffers(count, rows, width)
         + line_sems(count)
         + expert_buffers(len(picks), fsdp_count // 2, share, grads.shape[3]),
         compiler_params=remote_params(ident, 63),
@@ -691,7 +697,7 @@
     grad_ref, w_sum, gains_ref, *refs = refs
     sums_ref, refs = (refs[0], refs[1:]) if picks else (None, refs)
     (
-        line_recv, line_send, line_send_sem, line_recv_sem,
+        line_recv, line_send_sem, line_recv_sem,
         pair_got, chip_sums, chip_got, pair_send, pair_recv, chip_send, chip_recv,
         tp_got, fsdp_got, small_send, small_recv, *refs,
     ) = refs
@@ -706,7 +712,7 @@
         )
     pl.semaphore_wait(barrier, tp_count + fsdp_count - 2)
     line = LineScatter(
-        tp_count, [x_ref], grad_ref, line_recv, line_send, line_send_sem, line_recv_sem
+        tp_count, [x_ref], grad_ref, line_recv, line_send_sem, line_recv_sem
     )
     rows = w_sum.shape[0]
 
@@ -907,10 +913,12 @@
     place_cols,
     gate_rows,
     x_ref,
+    g_ref,
     weights,
-    *refs,
+    y_ref,
+    dx_ref,
+    grads,
 ):
-    g_blocks, (y_ref, dx_ref, grads, g_ref, g_sem) = refs[:-5], refs[-5:]
     step = pl.program_id(0)
     expert = step + first_expert
     group, width = x_ref.shape
@@ -918,18 +926,10 @@
 
     @pl.when(step == 0)
     def _():
-        count, rows = len(g_blocks), g_blocks[0].shape[0]
-        copies = []
-        for shift, block in enumerate(g_blocks):
-            home = lax.rem(meta[meta.shape[0] - 1] + count - shift, count)
-            copies.append(pltpu.make_async_copy(block, rows_of(g_ref, home, rows), g_sem.at[shift]))
-            copies[-1].start()
         y_ref[...] = jnp.zeros_like(y_ref)
         dx_ref[...] = jnp.zeros_like(dx_ref)
-        for copy in copies:
-            copy.wait()
-
-    column = expert + meta[meta.shape[0] - 2]
+
+    column = expert + meta[meta.shape[0] - 1]
     lanes = lax.broadcasted_iota(jnp.int32, place_cols.shape, 1)
     place_col = jnp.sum(jnp.where(lanes == column, place_cols[...], 0), axis=1, keepdims=True)
     place_row = place_rows[pl.ds(column, 1), :]
@@ -996,7 +996,7 @@
             run(base, span)
 
 
-def experts_step(meta, place_rows, place_cols, gate_rows, x_rows, g_blocks, weights, first, count, skip, capacity):
+def experts_step(meta, place_rows, place_cols, gate_rows, x_rows, g_rows, weights, first, count, skip, capacity):
     group, width = x_rows.shape
     hidden = weights.shape[-1]
     tail = 128
@@ -1019,17 +1019,13 @@
                 whole(place_cols.shape),
                 whole(gate_rows.shape),
                 whole(x_rows.shape),
+                whole(g_rows.shape),
                 big(skip),
-            ]
-            + [IN_PLACE] * len(g_blocks),
+            ],
             out_specs=[
                 whole((group, width)),
                 whole((group, width + tail)),
                 big(0),
-            ],
-            scratch_shapes=[
-                pltpu.VMEM((group, width), jnp.bfloat16),
-                pltpu.SemaphoreType.DMA((len(g_blocks),)),
             ],
         ),
         out_shape=[
@@ -1045,7 +1041,7 @@
             transcendentals=count * 408 * hidden,
             bytes_accessed=count * 12 * width * hidden,
         ),
-    )(meta, place_rows, place_cols, gate_rows, x_rows, weights, *g_blocks)
+    )(meta, place_rows, place_cols, gate_rows, x_rows, g_rows, weights)
 
 
 def rotate_head(values, cosine, sine, sign):
@@ -1356,25 +1352,6 @@
     )(*packed)
 
 
-def shifted_blocks(block, count):
-    return [block] + [
-        lax.ppermute(block, "tp", [(i, (i + shift) % count) for i in range(count)])
-        for shift in range(1, count)
-    ]
-
-
-def shifted_scatter(partial_rows, count, me):
-    rows = partial_rows.shape[0] // count
-    total = lax.dynamic_slice_in_dim(partial_rows, me * rows, rows, 0).astype(jnp.float32)
-    for shift in range(1, count):
-        block = lax.dynamic_slice_in_dim(
-            partial_rows, lax.rem(me + shift, count) * rows, rows, 0
-        ).astype(jnp.bfloat16)
-        got = lax.ppermute(block, "tp", [(i, (i + shift) % count) for i in range(count)])
-        total = total + got.astype(jnp.float32)
-    return total
-
-
 RUNS = (0, 6, 10)
 DIRECT = (2, 2)
 
@@ -1395,7 +1372,7 @@
     w_down,
     cotangent,
 ):
-    local_rows, _ = emb.shape
+    local_rows, width = emb.shape
     tp_count, tp_index = lax.axis_size("tp"), lax.axis_index("tp")
     experts_here = w_gate.shape[0]
     expert_count = w_router.shape[1]
@@ -1422,17 +1399,14 @@
     )
     if split:
         pieces.append(lax.all_gather(packed[0], "fsdp", axis=2, tiled=True))
-    late_grad, _ = lax.optimization_barrier((cotangent, counts))
-    moe_grad = (resid_scale * late_grad.astype(jnp.float32)).astype(jnp.bfloat16)
-    moe_grad_blocks = shifted_blocks(moe_grad, tp_count)
     capacity = group_size * routes.shape[1] // expert_count * 2
-    meta = jnp.concatenate([counts[0], jnp.stack([tp_index * experts_here, tp_index])])
+    meta = jnp.concatenate([counts[0], (tp_index * experts_here)[None]])
 
     tables = attend_tables()
     heads_here, kv_here = q_width // HEAD_DIM, kv_width // HEAD_DIM
     *kept, branch_part = attend(group_rows, attn_w, segment_ids, tables, heads_here, kv_here)
-    mid_x, moe_rows, gate_rows, own_gates = find_mid(
-        branch_part, emb, gain_two, attn_w, used, mask, tp_count, 1
+    mid_x, moe_rows, gate_rows, own_gates, moe_grad_rows = find_mid(
+        branch_part, emb, gain_two, attn_w, used, mask, cotangent, tp_count, 1
     )
 
     outs = []
@@ -1444,7 +1418,7 @@
                 place_cols,
                 gate_rows,
                 moe_rows,
-                moe_grad_blocks,
+                moe_grad_rows,
                 piece,
                 first,
                 last - first,
@@ -1455,7 +1429,7 @@
     grad_sums = [lax.psum_scatter(outs[0][2], "fsdp", scatter_dimension=2, tiled=True)]
     last_grads = outs[-1][2]
     picks = (tuple(range(DIRECT[0])), tuple(range(DIRECT[0], sum(DIRECT)))) if split else ((), ())
-    y_part, mid_grad, gain_two_grad, sent, *mid_sums = find_mid_grad(
+    out, mid_grad, gain_two_grad, sent, *mid_sums = find_mid_grad(
         [part[1] for part in outs],
         [part[0] for part in outs],
         mid_x,
@@ -1470,9 +1444,9 @@
         fsdp_count,
         2,
     )
-    moe_sum = shifted_scatter(y_part, tp_count, tp_index)
-    out = (mid_x + resid_scale * moe_sum).astype(jnp.bfloat16)
-    dx_one, attn_grads = attend_back(group_rows, attn_w, segment_ids, tables, kept, moe_rows, sent)
+    dx_one, attn_grads = attend_back(
+        group_rows, attn_w, segment_ids, tables, kept, moe_rows, sent
+    )
     grad_emb, attn_sum, gain_sums, *end_sums = finish(
         dx_one, attn_grads, emb, gain_one, mid_grad, gain_two_grad, last_grads, picks[1], 3
     )

time: 659 us -> 701 us (1.064)
  Pallas kernels: 603 us -> 663 us
  starting transfers between devices: 8.89 us -> 0.12 us
    pallas_call x1, Pallas kernels: 130 us -> 155 us  [find_mid(): pl.pallas_call(functools.partial(mid_kernel, count), grid=(1,), out_shape...]
    pallas_call x1, Pallas kernels: 134 us -> 155 us  [find_mid_grad(): pl.pallas_call(functools.partial(moe_back_kernel, count, fsdp_count, runs...]
    ppermute x6 -> x0, starting transfers between devices: 8.77 us -> none  [the longest x3 4.9 us: shifted_scatter(): lax.ppermute(block, 'tp', [(i, (i + shift) % count) for i in range(count)])]
    pallas_call x2, Pallas kernels: 108 us -> 116 us  [experts_step(): pl.pallas_call(functools.partial(experts_kernel, first, capacity), grid_s...]
  transfers between devices with their start and end apart: 9 -> 3, of which waited for: 0 -> 0; matrix products, arithmetic and copies ran while one was open for 2% -> 1% of each run, Pallas kernels for 91% -> 94%
where the time goes in v7:
time: 701 us; the launch traced here: 692 us
  Pallas kernels  663 us (95%)
  local copies, waits for them, and re-layouts  14.2 us (2%)
  between operations  14.1 us (2%)
    pallas_call x1, Pallas kernels, find_mid(): pl.pallas_call(functools.partial(mid_kernel, count), grid=(1,), out_shape...  155 us
    pallas_call x1, Pallas kernels, find_mid_grad(): pl.pallas_call(functools.partial(moe_back_kernel, count, fsdp_count, runs...  155 us
    pallas_call x2, Pallas kernels, experts_step(): pl.pallas_call(functools.partial(experts_kernel, first, capacity), grid_s...  116 us
    pallas_call x1, Pallas kernels, finish(): pl.pallas_call(functools.partial(finish_kernel, tp_count, fsdp_count, pic...  103 us
    pallas_call x1, Pallas kernels, norm_gather(): pl.pallas_call(functools.partial(norm_gather_kernel, count, fsdp_count, l...  61.5 us
    pallas_call x1, Pallas kernels, attend_back(): pl.pallas_call(attend_back_kernel, grid=(group // SEQ,), in_specs=[by_row...  37 us
    pallas_call x1, Pallas kernels, attend(): pl.pallas_call(attend_kernel, grid=(seqs,), in_specs=[by_row(width), fixe...  19.7 us
  transfers between devices with their start and end apart: 3, of which 0 were waited for; matrix products, arithmetic and copies ran while one was open for 1% of the time, Pallas kernels for 94%

profile of v7, /device:TPU:0, one launch (start us, length us, event | category | flops | bytes accessed | tf_op | source)
XLA Modules:
  0.0 691.6 jit_solution(9688181215698777568)
XLA Ops:
  7.2 0.0 all-gather.3.cloned.1.call-start
  7.2 3.1 shard_map.251
  10.4 0.0 all-gather.5.cloned.1.call-start
  10.5 0.6 copy-done.10
  11.0 0.1 copy-done.9
  11.1 0.2 copy.28.refs_2_
  11.3 1.9 shard_map.247.refs_3_
  13.2 1.0 copy-done.2
  14.2 61.5 %shard_map.248 = (bf16[1024,1536]{1,0:T(8,128)(2,1)}, f32[1024,128]{1,0:T(8,128)S(1)}, s32[1024,128]{1,0:T(8,128)S(1)}, s32[128,1024]{1,0:T(8,128)S(1)}, s32[1,1...) custom-call(bf16[256,1536]{1,0:T(8,128)(2,1)S(1)} %copy-done.1, ...), custom_call_target="tpu_custom_call" | custom-call | bytes 150000000 | tf_op jit(solution)/shard_map/pallas_call | solution.py:490
  75.8 0.8 copy-done.3
  76.5 0.8 copy-done.5
  77.4 0.8 copy-done.6
  78.2 0.0 reduce-scatter.2.cloned.1.call-start
  78.3 0.6 broadcast_in_dim.20.seg_row
  78.9 0.6 reshape.25.gain_ref.refs_7_
  79.5 19.7 %shard_map.249 = (bf16[6,1024,64]{2,1,0:T(8,128)(2,1)}, bf16[2,1024,64]{2,1,0:T(8,128)(2,1)}, bf16[2,1024,64]{2,1,0:T(8,128)(2,1)}, bf16[1024,384]{1,0:T(8,128)(...) custom-call(bf16[1024,1536]{1,0:T(8,128)(2,1)} %get-tuple-element.53.x_ref, ...), custom_call_target="tpu_custom_call" | custom-call | flops 10000000000 | bytes 60000000 | tf_op jit(solution)/shard_map/pallas_call | solution.py:1239
  99.2 155.0 %shard_map.250 = (f32[256,1536]{1,0:T(8,128)}, bf16[1024,1536]{1,0:T(8,128)(2,1)}, f32[128,1024]{1,0:T(8,128)}, f32[256,128]{1,0:T(8,128)}, bf16[1024,1536]{1,0:T(8,128)(2,1)}) custom-call(bf16[1024,1536]{1,0:T(8,128)(2,1)} %get-tuple-element.55.part_ref, bf16[256,1536]{1,0:T(8,128)(2,1)} %refs_2_.6, f32[1,1536]{1,0:T(1,128)} %reshape.25.gain_ref.refs_7_, ...), custom_call_target="tpu_custom_call" | custom-call | bytes 150000000 | tf_op jit(solution)/shard_map/pallas_call | solution.py:557
  254.2 0.6 pad_add_fusion.meta
  254.8 62.6 %shard_map.252 = (bf16[1024,1536]{1,0:T(8,128)(2,1)}, bf16[1024,1664]{1,0:T(8,128)(2,1)}, bf16[6,3,1536,512]{3,2,1,0:T(8,128)(2,1)}) custom-call(s32[129]{0:T(256)} %pad_add_fusion.meta, s32[128,1024]{1,0:T(8,128)} %copy-done.6, s32[1024,128]{1,0:T(8,128)} %copy-done.5, f32[128,1024]{1,0:T(8,128)} %get-tuple-element.57.gate_rows, ...), custom_call_target="tpu_custom_call" | custom-call | flops 65456308224 | bytes 56623104 | tf_op jit(solution)/shard_map/pallas_call | solution.py:1012
  317.4 0.0 all-gather.5.cloned.1.call-done.weights
  317.4 53.7 %shard_map.253 = (bf16[1024,1536]{1,0:T(8,128)(2,1)}, bf16[1024,1664]{1,0:T(8,128)(2,1)}, bf16[4,3,1536,512]{3,2,1,0:T(8,128)(2,1)}) custom-call(s32[129]{0:T(256)} %pad_add_fusion.meta, s32[128,1024]{1,0:T(8,128)} %copy-done.6, s32[1024,128]{1,0:T(8,128)} %copy-done.5, f32[128,1024]{1,0:T(8,128)} %get-tuple-element.57.gate_rows, ...), custom_call_target="tpu_custom_call" | custom-call | flops 43637538816 | bytes 37748736 | tf_op jit(solution)/shard_map/pallas_call | solution.py:1012
  371.2 155.0 %shard_map.254 = (bf16[256,1536]{1,0:T(8,128)(2,1)}, f32[256,1536]{1,0:T(8,128)}, f32[1,1536]{1,0:T(1,128)}, bf16[1024,1664]{1,0:T(8,128)(2,1)}, bf16[2,3,192,512]{3,2,1,0:T(8,128)(2,1)}) custom-call(bf16[1024,1664]{1,0:T(8,128)(2,1)} %get-tuple-element.60.refs_0_, bf16[1024,1664]{1,0:T(8,128)(2,1)} %get-tuple-element.62.refs_1_, ...), custom_call_target="tpu_custom_call" | custom-call | bytes 150000000 | tf_op jit(solution)/shard_map/pallas_call | solution.py:663
  526.2 37.0 %shard_map.255 = (bf16[1024,1536]{1,0:T(8,128)(2,1)}, bf16[1536,1152]{1,0:T(8,128)(2,1)}) custom-call(bf16[1024,1536]{1,0:T(8,128)(2,1)} %get-tuple-element.53.x_ref, bf16[1536,1152]{1,0:T(8,128)(2,1)} %get-tuple-element.54.w_ref.router_ref.refs_8_, s32[2,1,512]{2,1,0:T(1,128)} %broadcast_in_dim.20.seg_row, f32[512,64]{1,0:T(8,128)} %constant.10.clone.cos_ref, ...), custom_call_target="tpu_custom_call" | custom-call | flops 20000000000 | bytes 100000000 | tf_op jit(solution)/shard_map/pallas_call | solution.py:1285
  563.2 103.0 %shard_map.256 = (f32[256,1536]{1,0:T(8,128)}, f32[192,1152]{1,0:T(8,128)}, f32[8,1536]{1,0:T(8,128)}, bf16[2,3,192,512]{3,2,1,0:T(8,128)(2,1)}) custom-call(bf16[1024,1536]{1,0:T(8,128)(2,1)} %get-tuple-element.75.refs_0_, bf16[1536,1152]{1,0:T(8,128)(2,1)} %get-tuple-element.76.refs_1_, bf16[256,1536]{1,0:T(8,128)(2,1)} %refs_2_.6, f32[1,1536]{1,0:T(1,128)} %copy-done.4, ...), custom_call_target="tpu_custom_call" | custom-call | bytes 150000000 | tf_op jit(solution)/shard_map/pallas_call | solution.py:814
  666.2 0.9 slice.27
  667.1 0.7 copy.29
  667.8 1.5 slice_reduce_fusion
  669.3 1.6 fusion.1
  670.9 1.9 fusion
  672.8 10.0 %shard_map.257 = (f32[10,192,512]{2,1,0:T(8,128)}, f32[10,192,512]{2,1,0:T(8,128)}, f32[10,192,512]{2,1,0:T(8,128)}) custom-call(bf16[6,3,192,512]{3,2,1,0:T(8,128)(2,1)} %reduce-scatter.2.cloned.1.call-done.refs_0_, bf16[2,3,192,512]{3,2,1,0:T(8,128)(2,1)} %get-tuple-element.83.refs_1_, bf16[2,3,192,512]{3,2,1,0:T(8,128)(2,1)} %get-tuple-element.84.refs_2_), custom_call_target="tpu_custom_call" | custom-call | tf_op jit(solution)/shard_map/pallas_call | solution.py:1346
  682.8 0.9 copy.32
  683.7 1.1 copy.33
  (26 shorter events, 0.1 us)
Async XLA Ops:
  7.2 247.6 %all-gather.3.cloned.1.call-start = ((), (), s32[]{:S(2)}) async-start(), calls=%async_computation.1 | async-start | bytes 31850496 | tf_op jit(solution)/shard_map/all_gather | solution.py:1386
  10.3 0.7 copy-start.10
  10.4 0.8 copy-start.9
  10.4 2.8 copy-start
  10.4 2.8 copy-start.1
  10.4 307.0 %all-gather.5.cloned.1.call-start = ((), (), s32[]{:S(2)}) async-start(), calls=%async_computation.2 | async-start | bytes 21233664 | tf_op jit(solution)/shard_map/all_gather | solution.py:1401
  11.1 64.6 %copy-start.4 = (f32[1,1536]{1,0:T(1,128)}, f32[1,1536]{1,0:T(1,128)S(1)}, u32[]{:S(2)}) copy-start(f32[1,1536]{1,0:T(1,128)S(1)} %reshape.24.refs_1_.refs_3_) | copy-start | bytes 18436
  13.2 1.0 copy-start.2
  14.2 64.0 %copy-start.11 = (s32[2,512]{1,0:T(2,128)S(1)}, s32[2,512]{1,0:T(2,128)}, u32[]{:S(2)}) copy-start(s32[2,512]{1,0:T(2,128)} %param.17) | copy-start | bytes 12292
  14.2 64.6 %copy-start.12 = (bf16[1536]{0:T(1024)(128)(2,1)S(1)}, bf16[1536]{0:T(1024)(128)(2,1)}, u32[]{:S(2)}) copy-start(bf16[1536]{0:T(1024)(128)(2,1)} %param.24) | copy-start | bytes 9220
  75.7 0.8 copy-start.3
  76.5 0.8 copy-start.5
  77.4 0.8 copy-start.6
  78.2 594.6 %reduce-scatter.2.cloned.1.call-start = ((), (), s32[]{:S(2)}) async-start(), calls=%async_computation.3 | async-start | bytes 31850496 | tf_op jit(solution)/shard_map/reduce_scatter | solution.py:1429
  672.8 10.0 %copy-start.8 = (bf16[256,1536]{1,0:T(8,128)(2,1)S(1)}, bf16[256,1536]{1,0:T(8,128)(2,1)}, u32[]{:S(2)}) copy-start(bf16[256,1536]{1,0:T(8,128)(2,1)} %get-tuple-element.118) | copy-start | bytes 2359300
  672.8 10.9 %copy-start.7 = (f32[256,1536]{1,0:T(8,128)S(1)}, f32[256,1536]{1,0:T(8,128)}, u32[]{:S(2)}) copy-start(f32[256,1536]{1,0:T(8,128)} %get-tuple-element.119) | copy-start | bytes 4718596
Sparse Core Ops, SparseCore 0:
  10.5 152.9 all-gather.2
  165.4 98.5 all-gather.4
  317.5 235.0 reduce-scatter.1

commit v8 on v7

--- a/solution.py
+++ b/solution.py
@@ -237,17 +237,19 @@
             self.to_pair(index, shift).start()
             self.keep(index, shift).start()
 
-    def pass_on(self, index):
-        for shift in self.order():
-            self.to_pair(index, shift).wait_recv()
-            self.keep(index, shift).wait()
-            for slot in range(self.own.shape[2]):
-                both = self.own[index, shift, slot].astype(jnp.float32) + self.got[
-                    index, shift, slot
-                ].astype(jnp.float32)
-                self.own[index, shift, slot] = both.astype(jnp.bfloat16)
-            if shift > 0:
-                self.to_chip(index, shift).start()
+    def items(self):
+        return [(index, shift) for index in range(len(self.picks)) for shift in self.order()]
+
+    def pass_on(self, index, shift):
+        self.to_pair(index, shift).wait_recv()
+        self.keep(index, shift).wait()
+        for slot in range(self.own.shape[2]):
+            both = self.own[index, shift, slot].astype(jnp.float32) + self.got[
+                index, shift, slot
+            ].astype(jnp.float32)
+            self.own[index, shift, slot] = both.astype(jnp.bfloat16)
+        if shift > 0:
+            self.to_chip(index, shift).start()
 
     def collect(self, index):
         chips = self.plane.chips
@@ -511,11 +513,15 @@
     moe_grads[own_rows(moe_grads, rows), :] = (
         resid_scale * cotangent_ref[...].astype(jnp.float32)
     ).astype(jnp.bfloat16)
-    for step in range(count - 1):
-        total.start(step)
-        others.start(step)
-        total.arrive(step)
-        others.arrive(step)
+    for step in range(count):
+        if step < count - 1:
+            others.start(step)
+        if step > 0:
+            total.start(step - 1)
+        if step < count - 1:
+            others.arrive(step)
+        if step > 0:
+            total.arrive(step - 1)
     total.collect()
     mid = emb_ref[...].astype(jnp.float32) * emb_scale + resid_scale * mid_ref[...]
     mid_ref[...] = mid
@@ -612,11 +618,14 @@
         experts.begin(index)
     for load in loads[:runs]:
         load.wait()
+    items = experts.items() if picks else []
+    each = -(-len(items) // (2 * count - 2))
     for step in range(count - 1):
         total.start(step)
-        if step < len(picks):
-            experts.pass_on(step)
+        for item in items[step * each : (step + 1) * each]:
+            experts.pass_on(*item)
         total.arrive(step)
+    items = items[(count - 1) * each :]
     total.collect()
     gates = own_gates[...]
     gates_grad = sum_ref[:, width:]
@@ -632,16 +641,20 @@
     sent_ref[own, width:] = logits_grad
     for load in loads[runs:]:
         load.wait()
-    for step in range(count - 1):
-        line.start(step)
-        moe.start(step)
-        if 0 < step <= len(picks):
-            experts.collect(step - 1)
-        moe.arrive(step)
-        line.arrive(step)
+    for step in range(count):
+        if step < count - 1:
+            line.start(step)
+        if step > 0:
+            moe.start(step - 1)
+        for item in items[step * each : (step + 1) * each]:
+            experts.pass_on(*item)
+        if step < count - 1:
+            line.arrive(step)
+        if step > 0:
+            moe.arrive(step - 1)
     moe.collect()
     out_ref[...] = (mid_ref[...] + resid_scale * moe_ref[...]).astype(out_ref.dtype)
-    for index in range(count - 2, len(picks)):
+    for index in range(len(picks)):
         experts.collect(index)
     line.finish()
     total.finish()
@@ -771,11 +784,13 @@
         if shift > 0:
             chip_sums[shift - 1] = both_cores(shift).astype(chip_sums.dtype)
             to_chip(shift).start()
-    for index in range(len(picks)):
-        experts.pass_on(index)
+    items = experts.items() if picks else []
+    each = -(-len(items) // (tp_count - 2))
     line.arrive(0)
     for step in range(1, tp_count - 1):
         line.start(step)
+        for item in items[(step - 1) * each : step * each]:
+            experts.pass_on(*item)
         line.arrive(step)
     line.collect()
     from_norm, gain_one = rms_back(
@@ -1352,8 +1367,8 @@
     )(*packed)
 
 
-RUNS = (0, 6, 10)
-DIRECT = (2, 2)
+RUNS = (0, 7, 10)
+DIRECT = (2, 1)
 
 
 def local(

time: 701 us -> 647 us (0.923)
  Pallas kernels: 663 us -> 609 us
    pallas_call x1, Pallas kernels: 155 us -> 127 us  [find_mid(): pl.pallas_call(functools.partial(mid_kernel, count), grid=(1,), out_shape...]
    pallas_call x1, Pallas kernels: 103 us -> 84.7 us  [finish(): pl.pallas_call(functools.partial(finish_kernel, tp_count, fsdp_count, pic...]
    pallas_call x1, Pallas kernels: 155 us -> 147 us  [find_mid_grad(): pl.pallas_call(functools.partial(moe_back_kernel, count, fsdp_count, runs...]
  transfers between devices with their start and end apart: 3 -> 3, of which waited for: 0 -> 0; matrix products, arithmetic and copies ran while one was open for 1% -> 1% of each run, Pallas kernels for 94% -> 93%
where the time goes in v8:
time: 647 us; the launch traced here: 638 us
  Pallas kernels  609 us (94%)
  local copies, waits for them, and re-layouts  14.2 us (2%)
  between operations  14.1 us (2%)
    pallas_call x1, Pallas kernels, find_mid_grad(): pl.pallas_call(functools.partial(moe_back_kernel, count, fsdp_count, runs...  147 us
    pallas_call x1, Pallas kernels, find_mid(): pl.pallas_call(functools.partial(mid_kernel, count), grid=(1,), out_shape...  127 us
    pallas_call x2, Pallas kernels, experts_step(): pl.pallas_call(functools.partial(experts_kernel, first, capacity), grid_s...  118 us
    pallas_call x1, Pallas kernels, finish(): pl.pallas_call(functools.partial(finish_kernel, tp_count, fsdp_count, pic...  84.7 us
    pallas_call x1, Pallas kernels, norm_gather(): pl.pallas_call(functools.partial(norm_gather_kernel, count, fsdp_count, l...  61.4 us
    pallas_call x1, Pallas kernels, attend_back(): pl.pallas_call(attend_back_kernel, grid=(group // SEQ,), in_specs=[by_row...  36.7 us
    pallas_call x1, Pallas kernels, attend(): pl.pallas_call(attend_kernel, grid=(seqs,), in_specs=[by_row(width), fixe...  19.7 us
  transfers between devices with their start and end apart: 3, of which 0 were waited for; matrix products, arithmetic and copies ran while one was open for 1% of the time, Pallas kernels for 93%

profile of v8, /device:TPU:0, one launch (start us, length us, event | category | flops | bytes accessed | tf_op | source)
XLA Modules:
  0.0 637.6 jit_solution(6750770506398115930)
XLA Ops:
  7.2 0.0 all-gather.3.cloned.1.call-start
  7.2 3.3 shard_map.251
  10.6 0.0 all-gather.5.cloned.1.call-start
  10.7 0.6 copy-done.9
  11.3 0.1 copy-done.8
  11.3 0.2 copy.28.refs_2_
  11.5 1.9 shard_map.247.refs_3_
  13.4 1.0 copy-done.1
  14.4 61.4 %shard_map.248 = (bf16[1024,1536]{1,0:T(8,128)(2,1)}, f32[1024,128]{1,0:T(8,128)S(1)}, s32[1024,128]{1,0:T(8,128)S(1)}, s32[128,1024]{1,0:T(8,128)S(1)}, s32[1,1...) custom-call(bf16[256,1536]{1,0:T(8,128)(2,1)S(1)} %copy-done, ...), custom_call_target="tpu_custom_call" | custom-call | bytes 150000000 | tf_op jit(solution)/shard_map/pallas_call | solution.py:492
  75.8 0.8 copy-done.2
  76.6 0.8 copy-done.4
  77.4 0.8 copy-done.5
  78.3 0.0 reduce-scatter.2.cloned.1.call-start
  78.3 0.6 broadcast_in_dim.20.seg_row
  78.9 0.6 reshape.25.gain_ref.refs_7_
  79.5 19.7 %shard_map.249 = (bf16[6,1024,64]{2,1,0:T(8,128)(2,1)}, bf16[2,1024,64]{2,1,0:T(8,128)(2,1)}, bf16[2,1024,64]{2,1,0:T(8,128)(2,1)}, bf16[1024,384]{1,0:T(8,128)(...) custom-call(bf16[1024,1536]{1,0:T(8,128)(2,1)} %get-tuple-element.53.x_ref, ...), custom_call_target="tpu_custom_call" | custom-call | flops 10000000000 | bytes 60000000 | tf_op jit(solution)/shard_map/pallas_call | solution.py:1254
  99.2 126.5 %shard_map.250 = (f32[256,1536]{1,0:T(8,128)}, bf16[1024,1536]{1,0:T(8,128)(2,1)}, f32[128,1024]{1,0:T(8,128)}, f32[256,128]{1,0:T(8,128)}, bf16[1024,1536]{1,0:T(8,128)(2,1)}) custom-call(bf16[1024,1536]{1,0:T(8,128)(2,1)} %get-tuple-element.55.part_ref, bf16[256,1536]{1,0:T(8,128)(2,1)} %refs_2_.6, f32[1,1536]{1,0:T(1,128)} %reshape.25.gain_ref.refs_7_, ...), custom_call_target="tpu_custom_call" | custom-call | bytes 150000000 | tf_op jit(solution)/shard_map/pallas_call | solution.py:563
  225.7 0.6 pad_add_fusion.meta
  226.3 83.3 %shard_map.252 = (bf16[1024,1536]{1,0:T(8,128)(2,1)}, bf16[1024,1664]{1,0:T(8,128)(2,1)}, bf16[7,3,1536,512]{3,2,1,0:T(8,128)(2,1)}) custom-call(s32[129]{0:T(256)} %pad_add_fusion.meta, s32[128,1024]{1,0:T(8,128)} %copy-done.5, s32[1024,128]{1,0:T(8,128)} %copy-done.4, f32[128,1024]{1,0:T(8,128)} %get-tuple-element.57.gate_rows, ...), custom_call_target="tpu_custom_call" | custom-call | flops 76365692928 | bytes 66060288 | tf_op jit(solution)/shard_map/pallas_call | solution.py:1027
  309.6 0.0 all-gather.5.cloned.1.call-done.weights
  309.7 34.3 %shard_map.253 = (bf16[1024,1536]{1,0:T(8,128)(2,1)}, bf16[1024,1664]{1,0:T(8,128)(2,1)}, bf16[3,3,1536,512]{3,2,1,0:T(8,128)(2,1)}) custom-call(s32[129]{0:T(256)} %pad_add_fusion.meta, s32[128,1024]{1,0:T(8,128)} %copy-done.5, s32[1024,128]{1,0:T(8,128)} %copy-done.4, f32[128,1024]{1,0:T(8,128)} %get-tuple-element.57.gate_rows, ...), custom_call_target="tpu_custom_call" | custom-call | flops 32728154112 | bytes 28311552 | tf_op jit(solution)/shard_map/pallas_call | solution.py:1027
  344.0 147.1 %shard_map.254 = (bf16[256,1536]{1,0:T(8,128)(2,1)}, f32[256,1536]{1,0:T(8,128)}, f32[1,1536]{1,0:T(1,128)}, bf16[1024,1664]{1,0:T(8,128)(2,1)}, bf16[2,3,192,512]{3,2,1,0:T(8,128)(2,1)}) custom-call(bf16[1024,1664]{1,0:T(8,128)(2,1)} %get-tuple-element.60.refs_0_, bf16[1024,1664]{1,0:T(8,128)(2,1)} %get-tuple-element.62.refs_1_, ...), custom_call_target="tpu_custom_call" | custom-call | bytes 150000000 | tf_op jit(solution)/shard_map/pallas_call | solution.py:676
  491.1 36.7 %shard_map.255 = (bf16[1024,1536]{1,0:T(8,128)(2,1)}, bf16[1536,1152]{1,0:T(8,128)(2,1)}) custom-call(bf16[1024,1536]{1,0:T(8,128)(2,1)} %get-tuple-element.53.x_ref, bf16[1536,1152]{1,0:T(8,128)(2,1)} %get-tuple-element.54.w_ref.router_ref.refs_8_, s32[2,1,512]{2,1,0:T(1,128)} %broadcast_in_dim.20.seg_row, f32[512,64]{1,0:T(8,128)} %constant.10.clone.cos_ref, ...), custom_call_target="tpu_custom_call" | custom-call | flops 20000000000 | bytes 100000000 | tf_op jit(solution)/shard_map/pallas_call | solution.py:1300
  527.8 84.7 %shard_map.256 = (f32[256,1536]{1,0:T(8,128)}, f32[192,1152]{1,0:T(8,128)}, f32[8,1536]{1,0:T(8,128)}, bf16[1,3,192,512]{3,2,1,0:T(8,128)(2,1)}) custom-call(bf16[1024,1536]{1,0:T(8,128)(2,1)} %get-tuple-element.75.refs_0_, bf16[1536,1152]{1,0:T(8,128)(2,1)} %get-tuple-element.76.refs_1_, bf16[256,1536]{1,0:T(8,128)(2,1)} %refs_2_.6, f32[1,1536]{1,0:T(1,128)} %copy-done.3, ...), custom_call_target="tpu_custom_call" | custom-call | bytes 150000000 | tf_op jit(solution)/shard_map/pallas_call | solution.py:829
  612.5 0.9 slice.27
  613.4 0.7 copy.29
  614.1 1.5 slice_reduce_fusion
  615.6 1.6 fusion.1
  617.2 1.9 fusion
  619.1 9.7 %shard_map.257 = (f32[10,192,512]{2,1,0:T(8,128)}, f32[10,192,512]{2,1,0:T(8,128)}, f32[10,192,512]{2,1,0:T(8,128)}) custom-call(bf16[7,3,192,512]{3,2,1,0:T(8,128)(2,1)} %reduce-scatter.2.cloned.1.call-done.refs_0_, bf16[2,3,192,512]{3,2,1,0:T(8,128)(2,1)} %get-tuple-element.83.refs_1_, bf16[1,3,192,512]{3,2,1,0:T(8,128)(2,1)} %get-tuple-element.84.refs_2_), custom_call_target="tpu_custom_call" | custom-call | tf_op jit(solution)/shard_map/pallas_call | solution.py:1361
  628.9 0.9 copy.32
  629.7 1.1 copy.33
  (24 shorter events, 0.1 us)
Async XLA Ops:
  7.2 219.1 %all-gather.3.cloned.1.call-start = ((), (), s32[]{:S(2)}) async-start(), calls=%async_computation.1 | async-start | bytes 37158912 | tf_op jit(solution)/shard_map/all_gather | solution.py:1401
  10.6 0.7 copy-start.9
  10.6 0.8 copy-start.8
  10.6 2.8 copy-start
  10.6 299.0 %all-gather.5.cloned.1.call-start = ((), (), s32[]{:S(2)}) async-start(), calls=%async_computation.2 | async-start | bytes 15925248 | tf_op jit(solution)/shard_map/all_gather | solution.py:1416
  11.3 64.5 %copy-start.3 = (f32[1,1536]{1,0:T(1,128)}, f32[1,1536]{1,0:T(1,128)S(1)}, u32[]{:S(2)}) copy-start(f32[1,1536]{1,0:T(1,128)S(1)} %reshape.24.refs_1_.refs_3_) | copy-start | bytes 18436
  13.4 1.0 copy-start.1
  14.4 63.9 %copy-start.10 = (s32[2,512]{1,0:T(2,128)S(1)}, s32[2,512]{1,0:T(2,128)}, u32[]{:S(2)}) copy-start(s32[2,512]{1,0:T(2,128)} %param.17) | copy-start | bytes 12292
  14.4 64.5 %copy-start.11 = (bf16[1536]{0:T(1024)(128)(2,1)S(1)}, bf16[1536]{0:T(1024)(128)(2,1)}, u32[]{:S(2)}) copy-start(bf16[1536]{0:T(1024)(128)(2,1)} %param.24) | copy-start | bytes 9220
  75.8 0.8 copy-start.2
  76.6 0.8 copy-start.4
  77.4 0.8 copy-start.5
  78.3 540.9 %reduce-scatter.2.cloned.1.call-start = ((), (), s32[]{:S(2)}) async-start(), calls=%async_computation.3 | async-start | bytes 37158912 | tf_op jit(solution)/shard_map/reduce_scatter | solution.py:1444
  619.1 9.7 %copy-start.7 = (bf16[256,1536]{1,0:T(8,128)(2,1)S(1)}, bf16[256,1536]{1,0:T(8,128)(2,1)}, u32[]{:S(2)}) copy-start(bf16[256,1536]{1,0:T(8,128)(2,1)} %get-tuple-element.118) | copy-start | bytes 2359300
  619.1 10.6 %copy-start.6 = (f32[256,1536]{1,0:T(8,128)S(1)}, f32[256,1536]{1,0:T(8,128)}, u32[]{:S(2)}) copy-start(f32[256,1536]{1,0:T(8,128)} %get-tuple-element.119) | copy-start | bytes 4718596
Sparse Core Ops, SparseCore 0:
  10.7 172.1 all-gather.2
  184.8 78.6 all-gather.4
  309.7 281.5 reduce-scatter.1

commit v9 on v8

--- a/solution.py
+++ b/solution.py
@@ -185,43 +185,60 @@
 
 
 class ExpertSums:
+    NEAR = {0: (1, 0), 1: (3, 0), 2: (2, 1), 3: (3, 1), 4: (2, 0), 5: (1, 1)}
+
     def __init__(self, plane, picks, grads_ref, out_ref, *refs):
         self.plane, self.picks, self.grads_ref, self.out_ref = plane, picks, grads_ref, out_ref
         (
-            self.got, self.own, self.chip_got, self.held,
+            self.got, self.own, self.hop_got, self.held,
             self.pair_send, self.pair_recv, self.own_sem,
-            self.chip_send, self.chip_recv, self.put_sem,
+            self.hop_send, self.hop_recv, self.put_sem,
         ) = refs
         self.rows = out_ref.shape[2]
+        self.half = self.rows // 2
+
+    def chip_by(self, way):
+        chip = self.plane.chip
+        low, high = lax.rem(chip, 2), lax.div(chip, 2)
+        if way % 2:
+            low = 1 - low
+        if way >= 2:
+            high = 1 - high
+        return high * 2 + low
 
     def area(self, index, dest):
         low = pl.multiple_of(dest * self.rows, self.rows)
         return self.grads_ref.at[self.picks[index], :, pl.ds(low, self.rows)]
 
-    def to_pair(self, index, shift):
-        plane = self.plane
+    def part(self, index, way, half):
+        return self.own.at[index, way, :, pl.ds(half * self.half, self.half)]
+
+    def to_pair(self, index, way):
         return pltpu.make_async_remote_copy(
-            src_ref=self.area(index, plane.chip_at(shift) * 2 + 1 - plane.core),
-            dst_ref=self.got.at[index, shift],
-            send_sem=self.pair_send.at[index, shift],
-            recv_sem=self.pair_recv.at[index, shift],
-            device_id={"fsdp": plane.partner},
+            src_ref=self.area(index, self.chip_by(way) * 2 + 1 - self.plane.core),
+            dst_ref=self.got.at[index, way],
+            send_sem=self.pair_send.at[index, way],
+            recv_sem=self.pair_recv.at[index, way],
+            device_id={"fsdp": self.plane.partner},
         )
 
-    def keep(self, index, shift):
+    def keep(self, index, way):
         return pltpu.make_async_copy(
-            self.area(index, self.plane.peer(shift)),
-            self.own.at[index, shift],
-            self.own_sem.at[index, shift],
+            self.area(index, self.chip_by(way) * 2 + self.plane.core),
+            self.own.at[index, way],
+            self.own_sem.at[index, way],
         )
 
-    def to_chip(self, index, shift):
+    def hop(self, index, slot):
+        way, half = self.NEAR[slot]
+        source = self.part(index, way, half) if slot < 4 else self.hop_got.at[index, 2 * slot - 7]
+        target = (1, 1, 2, 2, 2, 1)[slot]
         return pltpu.make_async_remote_copy(
-            src_ref=self.own.at[index, shift],
-            dst_ref=self.chip_got.at[index, shift - 1],
-            send_sem=self.chip_send.at[index, shift - 1],
-            recv_sem=self.chip_recv.at[index, shift - 1],
-            device_id={"fsdp": self.plane.peer(shift)},
+            src_ref=source,
+            dst_ref=self.hop_got.at[index, slot],
+            send_sem=self.hop_send.at[index, slot],
+            recv_sem=self.hop_recv.at[index, slot],
+            device_id={"fsdp": self.chip_by(target) * 2 + self.plane.core},
         )
 
     def put(self, index):
@@ -229,61 +246,89 @@
             self.held.at[index], self.out_ref.at[index], self.put_sem.at[index]
         )
 
-    def order(self):
-        return list(range(1, self.plane.chips)) + [0]
-
     def begin(self, index):
-        for shift in self.order():
-            self.to_pair(index, shift).start()
-            self.keep(index, shift).start()
+        for way in (3, 1, 2, 0):
+            self.to_pair(index, way).start()
+            self.keep(index, way).start()
+
+    def both_cores(self, index, way):
+        self.to_pair(index, way).wait_recv()
+        self.keep(index, way).wait()
+        for slot in range(self.own.shape[2]):
+            both = self.own[index, way, slot].astype(jnp.float32) + self.got[
+                index, way, slot
+            ].astype(jnp.float32)
+            self.own[index, way, slot] = both.astype(jnp.bfloat16)
 
     def items(self):
-        return [(index, shift) for index in range(len(self.picks)) for shift in self.order()]
-
-    def pass_on(self, index, shift):
-        self.to_pair(index, shift).wait_recv()
-        self.keep(index, shift).wait()
-        for slot in range(self.own.shape[2]):
-            both = self.own[index, shift, slot].astype(jnp.float32) + self.got[
-                index, shift, slot
-            ].astype(jnp.float32)
-            self.own[index, shift, slot] = both.astype(jnp.bfloat16)
-        if shift > 0:
-            self.to_chip(index, shift).start()
+        count = len(self.picks)
+        order = []
+        for index in range(count + 1):
+            if index < count:
+                order += [(index, 0), (index, 1)]
+            if index > 0:
+                order += [(index - 1, 2), (index - 1, 3)]
+        return order
+
+    def do(self, index, stage):
+        if stage == 0:
+            self.both_cores(index, 3)
+            self.hop(index, 1).start()
+            self.hop(index, 3).start()
+        elif stage == 1:
+            self.both_cores(index, 1)
+            self.hop(index, 0).start()
+            self.both_cores(index, 2)
+            self.hop(index, 2).start()
+        elif stage == 2:
+            for slot in (4, 5):
+                behind = 2 * slot - 7
+                way, half = self.NEAR[slot]
+                self.hop(index, behind).wait_recv()
+                for layer in range(self.own.shape[2]):
+                    mine = self.own[
+                        index, way, layer, half * self.half : (half + 1) * self.half, :
+                    ].astype(jnp.float32)
+                    total = mine + self.hop_got[index, behind, layer].astype(jnp.float32)
+                    self.hop_got[index, behind, layer] = total.astype(jnp.bfloat16)
+                self.hop(index, slot).start()
+        else:
+            self.both_cores(index, 0)
 
     def collect(self, index):
-        chips = self.plane.chips
-        for shift in range(1, chips):
-            self.to_chip(index, shift).wait_recv()
-        for slot in range(self.own.shape[2]):
-            total = self.own[index, 0, slot].astype(jnp.float32)
-            for shift in range(1, chips):
-                total = total + self.chip_got[index, shift - 1, slot].astype(jnp.float32)
-            self.held[index, slot] = total.astype(jnp.bfloat16)
+        for half, slots in ((0, (0, 4)), (1, (2, 5))):
+            area = slice(half * self.half, (half + 1) * self.half)
+            for slot in slots:
+                self.hop(index, slot).wait_recv()
+            for layer in range(self.own.shape[2]):
+                total = self.own[index, 0, layer, area, :].astype(jnp.float32)
+                for slot in slots:
+                    total = total + self.hop_got[index, slot, layer].astype(jnp.float32)
+                self.held[index, layer, area, :] = total.astype(jnp.bfloat16)
         self.put(index).start()
 
     def finish(self):
         for index in range(len(self.picks)):
             self.put(index).wait()
-            for shift in self.order():
-                self.to_pair(index, shift).wait_send()
-                if shift > 0:
-                    self.to_chip(index, shift).wait_send()
-
-
-def expert_buffers(count, chips, rows, width):
+            for way in range(4):
+                self.to_pair(index, way).wait_send()
+            for slot in range(6):
+                self.hop(index, slot).wait_send()
+
+
+def expert_buffers(count, rows, width):
     if count == 0:
         return []
     return [
-        pltpu.VMEM((count, chips, 3, rows, width), jnp.bfloat16),
-        pltpu.VMEM((count, chips, 3, rows, width), jnp.bfloat16),
-        pltpu.VMEM((count, chips - 1, 3, rows, width), jnp.bfloat16),
+        pltpu.VMEM((count, 4, 3, rows, width), jnp.bfloat16),
+        pltpu.VMEM((count, 4, 3, rows, width), jnp.bfloat16),
+        pltpu.VMEM((count, 6, 3, rows // 2, width), jnp.bfloat16),
         pltpu.VMEM((count, 3, rows, width), jnp.bfloat16),
-        pltpu.SemaphoreType.DMA((count, chips)),
-        pltpu.SemaphoreType.DMA((count, chips)),
-        pltpu.SemaphoreType.DMA((count, chips)),
-        pltpu.SemaphoreType.DMA((count, chips - 1)),
-        pltpu.SemaphoreType.DMA((count, chips - 1)),
+        pltpu.SemaphoreType.DMA((count, 4)),
+        pltpu.SemaphoreType.DMA((count, 4)),
+        pltpu.SemaphoreType.DMA((count, 4)),
+        pltpu.SemaphoreType.DMA((count, 6)),
+        pltpu.SemaphoreType.DMA((count, 6)),
         pltpu.SemaphoreType.DMA((count,)),
     ]
 
@@ -623,7 +668,7 @@
     for step in range(count - 1):
         total.start(step)
         for item in items[step * each : (step + 1) * each]:
-            experts.pass_on(*item)
+            experts.do(*item)
         total.arrive(step)
     items = items[(count - 1) * each :]
     total.collect()
@@ -647,7 +692,7 @@
         if step > 0:
             moe.start(step - 1)
         for item in items[step * each : (step + 1) * each]:
-            experts.pass_on(*item)
+            experts.do(*item)
         if step < count - 1:
             line.arrive(step)
         if step > 0:
@@ -698,7 +743,7 @@
         + line_buffers(count, rows, wide)
         + line_buffers(count, rows, width)
         + line_sems(count)
-        + expert_buffers(len(picks), fsdp_count // 2, share, grads.shape[3]),
+        + expert_buffers(len(picks), share, grads.shape[3]),
         compiler_params=remote_params(ident, 63),
         cost_estimate=TRANSFER,
     )(*dx_parts, *y_parts, mid, cotangent, own_gates, gain_row, weights, *([grads] if picks else []))
@@ -790,7 +835,7 @@
     for step in range(1, tp_count - 1):
         line.start(step)
         for item in items[(step - 1) * each : step * each]:
-            experts.pass_on(*item)
+            experts.do(*item)
         line.arrive(step)
     line.collect()
     from_norm, gain_one = rms_back(
@@ -850,7 +895,7 @@
             pltpu.SemaphoreType.DMA((tp_count + fsdp_count,)),
             pltpu.SemaphoreType.DMA((tp_count + fsdp_count,)),
         ]
-        + expert_buffers(len(picks), chips, share, grads.shape[3]),
+        + expert_buffers(len(picks), share, grads.shape[3]),
         compiler_params=remote_params(ident),
         cost_estimate=TRANSFER,
     )(dx_rows, weight_grads, emb, gain_row, mid_grad, gain_two, *([grads] if picks else []))
@@ -930,10 +975,9 @@
     x_ref,
     g_ref,
     weights,
-    y_ref,
-    dx_ref,
-    grads,
+    *refs,
 ):
+    *held, y_ref, dx_ref, grads, load_sem = refs
     step = pl.program_id(0)
     expert = step + first_expert
     group, width = x_ref.shape
@@ -941,8 +985,18 @@
 
     @pl.when(step == 0)
     def _():
-        y_ref[...] = jnp.zeros_like(y_ref)
-        dx_ref[...] = jnp.zeros_like(dx_ref)
+        if held:
+            loads = [
+                pltpu.make_async_copy(source, target, load_sem.at[index])
+                for index, (source, target) in enumerate(zip(held, (y_ref, dx_ref)))
+            ]
+            for load in loads:
+                load.start()
+            for load in loads:
+                load.wait()
+        else:
+            y_ref[...] = jnp.zeros_like(y_ref)
+            dx_ref[...] = jnp.zeros_like(dx_ref)
 
     column = expert + meta[meta.shape[0] - 1]
     lanes = lax.broadcasted_iota(jnp.int32, place_cols.shape, 1)
@@ -1011,7 +1065,7 @@
             run(base, span)
 
 
-def experts_step(meta, place_rows, place_cols, gate_rows, x_rows, g_rows, weights, first, count, skip, capacity):
+def experts_step(meta, place_rows, place_cols, gate_rows, x_rows, g_rows, weights, held, first, count, skip, capacity):
     group, width = x_rows.shape
     hidden = weights.shape[-1]
     tail = 128
@@ -1036,12 +1090,14 @@
                 whole(x_rows.shape),
                 whole(g_rows.shape),
                 big(skip),
-            ],
+            ]
+            + [IN_PLACE] * len(held),
             out_specs=[
                 whole((group, width)),
                 whole((group, width + tail)),
                 big(0),
             ],
+            scratch_shapes=[pltpu.SemaphoreType.DMA((2,))],
         ),
         out_shape=[
             jax.ShapeDtypeStruct((group, width), jnp.bfloat16),
@@ -1056,7 +1112,7 @@
             transcendentals=count * 408 * hidden,
             bytes_accessed=count * 12 * width * hidden,
         ),
-    )(meta, place_rows, place_cols, gate_rows, x_rows, g_rows, weights)
+    )(meta, place_rows, place_cols, gate_rows, x_rows, g_rows, weights, *held)
 
 
 def rotate_head(values, cosine, sine, sign):
@@ -1367,8 +1423,8 @@
     )(*packed)
 
 
-RUNS = (0, 7, 10)
-DIRECT = (2, 1)
+RUNS = (0, 5, 10)
+DIRECT = (3, 2)
 
 
 def local(
@@ -1435,6 +1491,7 @@
                 moe_rows,
                 moe_grad_rows,
                 piece,
+                outs[-1][:2] if outs else (),
                 first,
                 last - first,
                 0,
@@ -1445,8 +1502,8 @@
     last_grads = outs[-1][2]
     picks = (tuple(range(DIRECT[0])), tuple(range(DIRECT[0], sum(DIRECT)))) if split else ((), ())
     out, mid_grad, gain_two_grad, sent, *mid_sums = find_mid_grad(
-        [part[1] for part in outs],
-        [part[0] for part in outs],
+        outs[-1][1:2],
+        outs[-1][0:1],
         mid_x,
         cotangent,
         own_gates,

time: 647 us -> 656 us (1.014); the launches traced: 638 us -> 654 us
  Pallas kernels: 609 us -> 625 us
    pallas_call x2, Pallas kernels: 118 us -> 148 us  [experts_step(): pl.pallas_call(functools.partial(experts_kernel, first, capacity), grid_s...]
    pallas_call x1, Pallas kernels: 147 us -> 137 us  [find_mid_grad(): pl.pallas_call(functools.partial(moe_back_kernel, count, fsdp_count, runs...]
    pallas_call x1, Pallas kernels: 84.7 us -> 77.7 us  [finish(): pl.pallas_call(functools.partial(finish_kernel, tp_count, fsdp_count, pic...]
  transfers between devices with their start and end apart: 3 -> 3, of which waited for: 0 -> 0; matrix products, arithmetic and copies ran while one was open for 1% -> 1% of each run, Pallas kernels for 93% -> 94%
where the time goes in v9:
time: 656 us; the launch traced here: 654 us
  Pallas kernels  625 us (95%)
  between operations  14.4 us (2%)
  local copies, waits for them, and re-layouts  13.5 us (2%)
    pallas_call x2, Pallas kernels, experts_step(): pl.pallas_call(functools.partial(experts_kernel, first, capacity), grid_s...  148 us
    pallas_call x1, Pallas kernels, find_mid_grad(): pl.pallas_call(functools.partial(moe_back_kernel, count, fsdp_count, runs...  137 us
    pallas_call x1, Pallas kernels, find_mid(): pl.pallas_call(functools.partial(mid_kernel, count), grid=(1,), out_shape...  129 us
    pallas_call x1, Pallas kernels, finish(): pl.pallas_call(functools.partial(finish_kernel, tp_count, fsdp_count, pic...  77.7 us
    pallas_call x1, Pallas kernels, norm_gather(): pl.pallas_call(functools.partial(norm_gather_kernel, count, fsdp_count, l...  61.7 us
    pallas_call x1, Pallas kernels, attend_back(): pl.pallas_call(attend_back_kernel, grid=(group // SEQ,), in_specs=[by_row...  36.5 us
    pallas_call x1, Pallas kernels, attend(): pl.pallas_call(attend_kernel, grid=(seqs,), in_specs=[by_row(width), fixe...  19.9 us
  transfers between devices with their start and end apart: 3, of which 0 were waited for; matrix products, arithmetic and copies ran while one was open for 1% of the time, Pallas kernels for 94%

profile of v9, /device:TPU:0, one launch (start us, length us, event | category | flops | bytes accessed | tf_op | source)
XLA Modules:
  0.0 653.6 jit_solution(11814995190287700221)
XLA Ops:
  7.2 0.0 all-gather.5.cloned.1.call-start
  7.2 2.8 shard_map.251
  10.1 0.0 all-gather.5.cloned.1.call-update
  10.1 0.0 all-gather.3.cloned.1.call-start
  10.2 0.2 copy.28.refs_2_
  10.4 2.1 shard_map.247.refs_3_
  12.5 1.0 copy-done.2
  13.5 61.7 %shard_map.248 = (bf16[1024,1536]{1,0:T(8,128)(2,1)}, f32[1024,128]{1,0:T(8,128)S(1)}, s32[1024,128]{1,0:T(8,128)S(1)}, s32[128,1024]{1,0:T(8,128)S(1)}, s32[1,1...) custom-call(bf16[256,1536]{1,0:T(8,128)(2,1)S(1)} %copy-done.1, ...), custom_call_target="tpu_custom_call" | custom-call | bytes 150000000 | tf_op jit(solution)/shard_map/pallas_call | solution.py:537
  75.2 0.8 copy-done.3
  76.0 0.8 copy-done.5
  76.8 0.8 copy-done.6
  77.7 0.0 reduce-scatter.2.cloned.1.call-start
  77.7 0.6 broadcast_in_dim.20.seg_row
  78.3 0.6 reshape.25.gain_ref.refs_5_
  78.9 19.9 %shard_map.249 = (bf16[6,1024,64]{2,1,0:T(8,128)(2,1)}, bf16[2,1024,64]{2,1,0:T(8,128)(2,1)}, bf16[2,1024,64]{2,1,0:T(8,128)(2,1)}, bf16[1024,384]{1,0:T(8,128)(...) custom-call(bf16[1024,1536]{1,0:T(8,128)(2,1)} %get-tuple-element.53.x_ref, ...), custom_call_target="tpu_custom_call" | custom-call | flops 10000000000 | bytes 60000000 | tf_op jit(solution)/shard_map/pallas_call | solution.py:1310
  98.8 128.7 %shard_map.250 = (f32[256,1536]{1,0:T(8,128)}, bf16[1024,1536]{1,0:T(8,128)(2,1)}, f32[128,1024]{1,0:T(8,128)}, f32[256,128]{1,0:T(8,128)}, bf16[1024,1536]{1,0:T(8,128)(2,1)}) custom-call(bf16[1024,1536]{1,0:T(8,128)(2,1)} %get-tuple-element.55.part_ref, bf16[256,1536]{1,0:T(8,128)(2,1)} %refs_2_.6, f32[1,1536]{1,0:T(1,128)} %reshape.25.gain_ref.refs_5_, ...), custom_call_target="tpu_custom_call" | custom-call | bytes 150000000 | tf_op jit(solution)/shard_map/pallas_call | solution.py:608
  227.5 0.6 pad_add_fusion.meta
  228.0 70.6 %shard_map.252 = (bf16[1024,1536]{1,0:T(8,128)(2,1)}, bf16[1024,1664]{1,0:T(8,128)(2,1)}, bf16[5,3,1536,512]{3,2,1,0:T(8,128)(2,1)}) custom-call(s32[129]{0:T(256)} %pad_add_fusion.meta, s32[128,1024]{1,0:T(8,128)} %copy-done.6, s32[1024,128]{1,0:T(8,128)} %copy-done.5, f32[128,1024]{1,0:T(8,128)} %get-tuple-element.57.gate_rows, ...), custom_call_target="tpu_custom_call" | custom-call | flops 54546923520 | bytes 47185920 | tf_op jit(solution)/shard_map/pallas_call | solution.py:1081
  298.7 0.0 reduce-scatter.2.cloned.1.call-update
  298.7 0.0 all-gather.3.cloned.1.call-done.weights
  298.7 77.5 %shard_map.253 = (bf16[1024,1536]{1,0:T(8,128)(2,1)}, bf16[1024,1664]{1,0:T(8,128)(2,1)}, bf16[5,3,1536,512]{3,2,1,0:T(8,128)(2,1)}) custom-call(s32[129]{0:T(256)} %pad_add_fusion.meta, s32[128,1024]{1,0:T(8,128)} %copy-done.6, s32[1024,128]{1,0:T(8,128)} %copy-done.5, f32[128,1024]{1,0:T(8,128)} %get-tuple-element.57.gate_rows, ...), custom_call_target="tpu_custom_call" | custom-call | flops 54546923520 | bytes 47185920 | tf_op jit(solution)/shard_map/pallas_call | solution.py:1081
  376.2 137.5 %shard_map.254 = (bf16[256,1536]{1,0:T(8,128)(2,1)}, f32[256,1536]{1,0:T(8,128)}, f32[1,1536]{1,0:T(1,128)}, bf16[1024,1664]{1,0:T(8,128)(2,1)}, bf16[3,3,192,512]{3,2,1,0:T(8,128)(2,1)}) custom-call(bf16[1024,1664]{1,0:T(8,128)(2,1)} %get-tuple-element.63.refs_0_, bf16[1024,1536]{1,0:T(8,128)(2,1)} %get-tuple-element.64.refs_1_, ...), custom_call_target="tpu_custom_call" | custom-call | bytes 150000000 | tf_op jit(solution)/shard_map/pallas_call | solution.py:721
  513.7 36.5 %shard_map.255 = (bf16[1024,1536]{1,0:T(8,128)(2,1)}, bf16[1536,1152]{1,0:T(8,128)(2,1)}) custom-call(bf16[1024,1536]{1,0:T(8,128)(2,1)} %get-tuple-element.53.x_ref, bf16[1536,1152]{1,0:T(8,128)(2,1)} %get-tuple-element.54.w_ref.router_ref.refs_6_, s32[2,1,512]{2,1,0:T(1,128)} %broadcast_in_dim.20.seg_row, f32[512,64]{1,0:T(8,128)} %constant.10.clone.cos_ref, ...), custom_call_target="tpu_custom_call" | custom-call | flops 20000000000 | bytes 100000000 | tf_op jit(solution)/shard_map/pallas_call | solution.py:1356
  550.2 77.7 %shard_map.256 = (f32[256,1536]{1,0:T(8,128)}, f32[192,1152]{1,0:T(8,128)}, f32[8,1536]{1,0:T(8,128)}, bf16[2,3,192,512]{3,2,1,0:T(8,128)(2,1)}) custom-call(bf16[1024,1536]{1,0:T(8,128)(2,1)} %get-tuple-element.75.refs_0_, bf16[1536,1152]{1,0:T(8,128)(2,1)} %get-tuple-element.76.refs_1_, bf16[256,1536]{1,0:T(8,128)(2,1)} %refs_2_.6, f32[1,1536]{1,0:T(1,128)} %copy-done.4, ...), custom_call_target="tpu_custom_call" | custom-call | bytes 150000000 | tf_op jit(solution)/shard_map/pallas_call | solution.py:874
  627.9 0.9 slice.27
  628.8 0.7 copy.29
  629.5 1.5 slice_reduce_fusion
  631.0 1.6 fusion.1
  632.7 1.9 fusion
  634.6 10.0 %shard_map.257 = (f32[10,192,512]{2,1,0:T(8,128)}, f32[10,192,512]{2,1,0:T(8,128)}, f32[10,192,512]{2,1,0:T(8,128)}) custom-call(bf16[5,3,192,512]{3,2,1,0:T(8,128)(2,1)} %reduce-scatter.2.cloned.1.call-done.refs_0_, bf16[3,3,192,512]{3,2,1,0:T(8,128)(2,1)} %get-tuple-element.83.refs_1_, bf16[2,3,192,512]{3,2,1,0:T(8,128)(2,1)} %get-tuple-element.84.refs_2_), custom_call_target="tpu_custom_call" | custom-call | tf_op jit(solution)/shard_map/pallas_call | solution.py:1417
  644.6 0.9 copy.32
  645.5 1.1 copy.33
  (26 shorter events, 0.1 us)
Async XLA Ops:
  7.2 3.0 copy-start.10
  7.2 3.0 copy-start.9
  7.2 220.9 %all-gather.5.cloned.1.call-start = ((), (), s32[]{:S(2)}) async-start(), calls=%async_computation.2 | async-start | bytes 26542080 | tf_op jit(solution)/shard_map/all_gather | solution.py:1457
  10.1 2.4 copy-start
  10.1 2.4 copy-start.1
  10.1 288.6 %all-gather.3.cloned.1.call-start = ((), (), s32[]{:S(2)}) async-start(), calls=%async_computation.1 | async-start | bytes 26542080 | tf_op jit(solution)/shard_map/all_gather | solution.py:1472
  10.2 65.0 %copy-start.4 = (f32[1,1536]{1,0:T(1,128)}, f32[1,1536]{1,0:T(1,128)S(1)}, u32[]{:S(2)}) copy-start(f32[1,1536]{1,0:T(1,128)S(1)} %reshape.24.refs_1_.refs_3_) | copy-start | bytes 18436
  12.5 1.0 copy-start.2
  13.5 64.2 %copy-start.11 = (s32[2,512]{1,0:T(2,128)S(1)}, s32[2,512]{1,0:T(2,128)}, u32[]{:S(2)}) copy-start(s32[2,512]{1,0:T(2,128)} %param.17) | copy-start | bytes 12292
  13.5 64.8 %copy-start.12 = (bf16[1536]{0:T(1024)(128)(2,1)S(1)}, bf16[1536]{0:T(1024)(128)(2,1)}, u32[]{:S(2)}) copy-start(bf16[1536]{0:T(1024)(128)(2,1)} %param.24) | copy-start | bytes 9220
  75.2 0.8 copy-start.3
  76.0 0.8 copy-start.5
  76.8 0.8 copy-start.6
  77.7 556.9 %reduce-scatter.2.cloned.1.call-start = ((), (), s32[]{:S(2)}) async-start(), calls=%async_computation.3 | async-start | bytes 26542080 | tf_op jit(solution)/shard_map/reduce_scatter | solution.py:1501
  634.6 10.0 %copy-start.8 = (bf16[256,1536]{1,0:T(8,128)(2,1)S(1)}, bf16[256,1536]{1,0:T(8,128)(2,1)}, u32[]{:S(2)}) copy-start(bf16[256,1536]{1,0:T(8,128)(2,1)} %get-tuple-element.118) | copy-start | bytes 2359300
  634.6 10.9 %copy-start.7 = (f32[256,1536]{1,0:T(8,128)S(1)}, f32[256,1536]{1,0:T(8,128)}, u32[]{:S(2)}) copy-start(f32[256,1536]{1,0:T(8,128)} %get-tuple-element.119) | copy-start | bytes 4718596
Sparse Core Ops, SparseCore 0:
  10.5 133.2 all-gather.4
  145.7 118.5 all-gather.2
  298.8 219.5 reduce-scatter.1

commit v10 on v9

--- a/solution.py
+++ b/solution.py
@@ -445,12 +445,14 @@
 
 
 def norm_gather_kernel(count, fsdp_count, low, *refs):
-    emb_ref, gain_ref, routes_ref, w_ref, *refs = refs
+    emb_ref, gain_ref, routes_ref, *refs = refs
+    parts, refs = refs[:5], refs[5:]
     stacks, refs = (refs[:3], refs[3:]) if low else ((), refs)
     rows_ref, mask_ref, cols_ref, turned_ref, counts_ref, wo_ref, *refs = refs
     packed, refs = (refs[0], refs[1:]) if low else (None, refs)
-    row_send, row_recv, *refs = refs
+    w_ref, row_send, row_recv, *refs = refs
     plane = Plane(fsdp_count)
+    join(parts, w_ref)
     if low:
         held, in_sem, out_sem = refs[5:]
         gets, puts = pack_copies(low, stacks, packed, held, in_sem, out_sem)
@@ -506,21 +508,22 @@
         turned_ref[:, area] = places.T.astype(jnp.int32)
 
 
-def norm_gather(emb, gain_row, routes, weights, stacks, low, count, fsdp_count, ident):
+def norm_gather(emb, gain_row, routes, parts, w_width, stacks, low, count, fsdp_count, ident):
     rows, width = emb.shape
     group = rows * count
     chips = fsdp_count // 2
     experts, share, hidden = stacks[0].shape
     span = experts - low
+    w_rows = parts[0].shape[0]
     outs = [
         jax.ShapeDtypeStruct((group, width), jnp.bfloat16),
         jax.ShapeDtypeStruct((group, 128), jnp.float32),
         jax.ShapeDtypeStruct((group, 128), jnp.int32),
         jax.ShapeDtypeStruct((128, group), jnp.int32),
         jax.ShapeDtypeStruct((1, 128), jnp.int32),
-        jax.ShapeDtypeStruct((weights.shape[0] * fsdp_count, weights.shape[1]), jnp.bfloat16),
+        jax.ShapeDtypeStruct((w_rows * fsdp_count, w_width), jnp.bfloat16),
     ]
-    scratch = line_sems(count) + [
+    scratch = [pltpu.VMEM((w_rows, w_width), jnp.bfloat16)] + line_sems(count) + [
         pltpu.SemaphoreType.DMA((chips,)),
         pltpu.SemaphoreType.DMA((chips,)),
         pltpu.SemaphoreType.DMA((chips - 1,)),
@@ -537,12 +540,12 @@
     return pl.pallas_call(
         functools.partial(norm_gather_kernel, count, fsdp_count, low),
         out_shape=outs,
-        in_specs=[IN_VMEM] * 4 + [IN_PLACE] * (3 if low else 0),
+        in_specs=[IN_VMEM] * (3 + len(parts)) + [IN_PLACE] * (3 if low else 0),
         out_specs=[IN_VMEM] * 5 + [IN_PLACE] * (len(outs) - 5),
         scratch_shapes=scratch,
         compiler_params=remote_params(ident, 48),
         cost_estimate=TRANSFER,
-    )(emb, gain_row, routes, weights, *(stacks if low else ()))
+    )(emb, gain_row, routes, *parts, *(stacks if low else ()))
 
 
 def mid_kernel(
@@ -942,8 +945,8 @@
     )(*stacks)
 
 
-def join_kernel(*refs):
-    *sources, last, target = refs
+def join(parts, target):
+    *sources, last = parts
     low = 0
     for source in sources:
         target[:, low : low + source.shape[1]] = source[...]
@@ -951,15 +954,6 @@
     router = last[...].astype(jnp.float32).T.astype(jnp.bfloat16)
     target[:, low:] = jnp.zeros((target.shape[0], target.shape[1] - low), jnp.bfloat16)
     target[:, low : low + router.shape[1]] = router
-
-
-def join(parts, last_turned, width):
-    return pl.pallas_call(
-        join_kernel,
-        in_specs=[IN_VMEM] * (len(parts) + 1),
-        out_specs=IN_VMEM,
-        out_shape=jax.ShapeDtypeStruct((parts[0].shape[0], width), jnp.bfloat16),
-    )(*parts, last_turned)
 
 
 SLOTS = 256
@@ -1394,9 +1388,22 @@
       queries, keys, values, mixed, logsum, moe_rows, branch_grad)
 
 
-def widen_kernel(edges, *refs):
+def outputs_kernel(edges, attn_ref, gains_ref, *refs):
     step = pl.program_id(0)
-    packed, targets = refs[:-3], refs[-3:]
+    packed, refs = refs[: len(edges) - 1], refs[len(edges) - 1 :]
+    *small, router_ref, gain_one, gain_two = refs[:7]
+    targets = refs[7:]
+
+    @pl.when(step == 0)
+    def _():
+        low = 0
+        for target in small:
+            target[...] = attn_ref[:, low : low + target.shape[1]]
+            low += target.shape[1]
+        router_ref[...] = attn_ref[:, low:].T[: router_ref.shape[0], :]
+        gain_one[...] = gains_ref[0:1, :]
+        gain_two[...] = gains_ref[1:2, :]
+
     for part, low, high in zip(packed, edges[:-1], edges[1:]):
 
         @pl.when((step >= low) & (step < high))
@@ -1405,8 +1412,9 @@
                 target[0] = part[0, slot].astype(jnp.float32)
 
 
-def widen(packed, edges):
+def outputs(attn_sum, gains, packed, edges, widths, expert_count):
     _, _, rows, width = packed[0].shape
+    shapes = [(rows, span) for span in widths] + [(expert_count, rows)] + [(1, gains.shape[1])] * 2
 
     def home(low, high):
         return pl.BlockSpec(
@@ -1414,17 +1422,23 @@
             lambda step: (jnp.clip(step - low, 0, high - low - 1), 0, 0, 0),
         )
 
+    def still(shape):
+        return pl.BlockSpec(shape, lambda step: (0,) * len(shape))
+
     return pl.pallas_call(
-        functools.partial(widen_kernel, edges),
+        functools.partial(outputs_kernel, edges),
         grid=(edges[-1],),
-        in_specs=[home(low, high) for low, high in zip(edges[:-1], edges[1:])],
-        out_specs=[pl.BlockSpec((1, rows, width), lambda step: (step, 0, 0))] * 3,
-        out_shape=[jax.ShapeDtypeStruct((edges[-1], rows, width), jnp.float32)] * 3,
-    )(*packed)
-
-
-RUNS = (0, 5, 10)
-DIRECT = (3, 2)
+        in_specs=[still(attn_sum.shape), still(gains.shape)]
+        + [home(low, high) for low, high in zip(edges[:-1], edges[1:])],
+        out_specs=[still(shape) for shape in shapes]
+        + [pl.BlockSpec((1, rows, width), lambda step: (step, 0, 0))] * 3,
+        out_shape=[jax.ShapeDtypeStruct(shape, jnp.float32) for shape in shapes]
+        + [jax.ShapeDtypeStruct((edges[-1], rows, width), jnp.float32)] * 3,
+    )(attn_sum, gains, *packed)
+
+
+RUNS = (0, 6, 10)
+DIRECT = (3, 1)
 
 
 def local(
@@ -1461,7 +1475,8 @@
         emb,
         gain_one,
         routes,
-        join([w_query, w_key, w_value, w_out], w_router.T, used + 128),
+        [w_query, w_key, w_value, w_out, w_router.T],
+        used + 128,
         stacks,
         runs[1] if split else 0,
         tp_count,
@@ -1526,18 +1541,20 @@
     ends = [0]
     for part in grad_sums:
         ends.append(ends[-1] + part.shape[0])
-    expert_sums = widen(grad_sums, ends)
+    widths = [q_width, kv_width, kv_width, q_width]
+    *attn_outs, router_turned, gain_one_sum, gain_two_sum, gate_sum, up_sum, down_sum = outputs(
+        attn_sum, gain_sums, grad_sums, ends, widths, expert_count
+    )
     return (
         out,
         grad_emb,
-        gain_sums[0],
-        attn_sum[:, :q_width],
-        attn_sum[:, q_width : q_width + kv_width],
-        attn_sum[:, q_width + kv_width : q_width + 2 * kv_width],
-        attn_sum[:, q_width + 2 * kv_width : used],
-        gain_sums[1],
-        attn_sum[:, used : used + expert_count],
-        *expert_sums,
+        gain_one_sum[0],
+        *attn_outs,
+        gain_two_sum[0],
+        router_turned.T,
+        gate_sum,
+        up_sum,
+        down_sum,
     )
 
 

time: 656 us -> 654 us (level); the launches traced: 654 us -> 644 us
  Pallas kernels: 625 us -> 616 us
    pallas_call x1, Pallas kernels: 137 us -> 156 us  [find_mid_grad(): pl.pallas_call(functools.partial(moe_back_kernel, count, fsdp_count, runs...]
    pallas_call x2, Pallas kernels: 148 us -> 129 us  [experts_step(): pl.pallas_call(functools.partial(experts_kernel, first, capacity), grid_s...]
where the time goes in v10:
time: 654 us; the launch traced here: 644 us
  Pallas kernels  616 us (94%)
  between operations  14.5 us (2%)
  local copies, waits for them, and re-layouts  9.69 us (1%)
    pallas_call x1, Pallas kernels, find_mid_grad(): pl.pallas_call(functools.partial(moe_back_kernel, count, fsdp_count, runs...  156 us
    pallas_call x2, Pallas kernels, experts_step(): pl.pallas_call(functools.partial(experts_kernel, first, capacity), grid_s...  129 us
    pallas_call x1, Pallas kernels, find_mid(): pl.pallas_call(functools.partial(mid_kernel, count), grid=(1,), out_shape...  125 us
    pallas_call x1, Pallas kernels, finish(): pl.pallas_call(functools.partial(finish_kernel, tp_count, fsdp_count, pic...  73.2 us
    pallas_call x1, Pallas kernels, norm_gather(): pl.pallas_call(functools.partial(norm_gather_kernel, count, fsdp_count, l...  61.6 us
    pallas_call x1, Pallas kernels, attend_back(): pl.pallas_call(attend_back_kernel, grid=(group // SEQ,), in_specs=[by_row...  36.9 us
    pallas_call x1, Pallas kernels, attend(): pl.pallas_call(attend_kernel, grid=(seqs,), in_specs=[by_row(width), fixe...  20.7 us
  transfers between devices with their start and end apart: 3, of which 0 were waited for; matrix products, arithmetic and copies ran while one was open for 1% of the time, Pallas kernels for 94%

profile of v10, /device:TPU:0, one launch (start us, length us, event | category | flops | bytes accessed | tf_op | source)
XLA Modules:
  0.0 643.7 jit_solution(12646786665665819287)
XLA Ops:
  7.2 0.0 all-gather.5.cloned.1.call-start
  7.2 3.1 shard_map.250
  10.4 0.0 copy-start
  10.4 0.0 all-gather.5.cloned.1.call-update
  10.5 0.0 all-gather.3.cloned.1.call-start
  10.5 0.5 copy-done.13
  11.0 1.2 copy.28.refs_2_
  12.3 0.9 copy-done.4
  13.2 61.6 %shard_map.247 = (bf16[1024,1536]{1,0:T(8,128)(2,1)}, f32[1024,128]{1,0:T(8,128)S(1)}, s32[1024,128]{1,0:T(8,128)S(1)}, s32[128,1024]{1,0:T(8,128)S(1)}, s32[1,1...) custom-call(bf16[256,1536]{1,0:T(8,128)(2,1)S(1)} %copy-done.1, ...), custom_call_target="tpu_custom_call" | custom-call | bytes 150000000 | tf_op jit(solution)/shard_map/pallas_call | solution.py:540
  74.8 0.8 copy-done.2
  75.6 0.8 copy-done.9
  76.5 0.8 copy-done.10
  77.2 0.0 all-gather.3.cloned.1.call-update
  77.3 0.0 reduce-scatter.2.cloned.1.call-start
  77.3 1.3 broadcast_in_dim.20.seg_row
  78.6 1.3 reshape.25.gain_ref.refs_5_
  79.9 20.7 %shard_map.248 = (bf16[6,1024,64]{2,1,0:T(8,128)(2,1)}, bf16[2,1024,64]{2,1,0:T(8,128)(2,1)}, bf16[2,1024,64]{2,1,0:T(8,128)(2,1)}, bf16[1024,384]{1,0:T(8,128)(...) custom-call(bf16[1024,1536]{1,0:T(8,128)(2,1)} %get-tuple-element.60.x_ref, ...), custom_call_target="tpu_custom_call" | custom-call | flops 10000000000 | bytes 60000000 | tf_op jit(solution)/shard_map/pallas_call | solution.py:1304
  100.6 124.8 %shard_map.249 = (f32[256,1536]{1,0:T(8,128)}, bf16[1024,1536]{1,0:T(8,128)(2,1)}, f32[128,1024]{1,0:T(8,128)}, f32[256,128]{1,0:T(8,128)}, bf16[1024,1536]{1,0:T(8,128)(2,1)}) custom-call(bf16[1024,1536]{1,0:T(8,128)(2,1)} %get-tuple-element.62.part_ref, bf16[256,1536]{1,0:T(8,128)(2,1)} %refs_2_.4, f32[1,1536]{1,0:T(1,128)} %reshape.25.gain_ref.refs_5_, ...), custom_call_target="tpu_custom_call" | custom-call | bytes 150000000 | tf_op jit(solution)/shard_map/pallas_call | solution.py:611
  225.4 0.6 pad_add_fusion.meta
  226.0 77.9 %shard_map.251 = (bf16[1024,1536]{1,0:T(8,128)(2,1)}, bf16[1024,1664]{1,0:T(8,128)(2,1)}, bf16[6,3,1536,512]{3,2,1,0:T(8,128)(2,1)}) custom-call(s32[129]{0:T(256)} %pad_add_fusion.meta, s32[128,1024]{1,0:T(8,128)} %copy-done.10, s32[1024,128]{1,0:T(8,128)} %copy-done.9, f32[128,1024]{1,0:T(8,128)} %get-tuple-element.64.gate_rows, ...), custom_call_target="tpu_custom_call" | custom-call | flops 65456308224 | bytes 56623104 | tf_op jit(solution)/shard_map/pallas_call | solution.py:1075
  303.9 0.0 reduce-scatter.2.cloned.1.call-update
  303.9 0.0 all-gather.3.cloned.1.call-done.weights
  304.0 51.3 %shard_map.252 = (bf16[1024,1536]{1,0:T(8,128)(2,1)}, bf16[1024,1664]{1,0:T(8,128)(2,1)}, bf16[4,3,1536,512]{3,2,1,0:T(8,128)(2,1)}) custom-call(s32[129]{0:T(256)} %pad_add_fusion.meta, s32[128,1024]{1,0:T(8,128)} %copy-done.10, s32[1024,128]{1,0:T(8,128)} %copy-done.9, f32[128,1024]{1,0:T(8,128)} %get-tuple-element.64.gate_rows, ...), custom_call_target="tpu_custom_call" | custom-call | flops 43637538816 | bytes 37748736 | tf_op jit(solution)/shard_map/pallas_call | solution.py:1075
  355.2 156.5 %shard_map.253 = (bf16[256,1536]{1,0:T(8,128)(2,1)}, f32[256,1536]{1,0:T(8,128)}, f32[1,1536]{1,0:T(1,128)}, bf16[1024,1664]{1,0:T(8,128)(2,1)}, bf16[3,3,192,512]{3,2,1,0:T(8,128)(2,1)}) custom-call(bf16[1024,1664]{1,0:T(8,128)(2,1)} %get-tuple-element.70.refs_0_, bf16[1024,1536]{1,0:T(8,128)(2,1)} %get-tuple-element.71.refs_1_, ...), custom_call_target="tpu_custom_call" | custom-call | bytes 150000000 | tf_op jit(solution)/shard_map/pallas_call | solution.py:724
  511.7 36.9 %shard_map.254 = (bf16[1024,1536]{1,0:T(8,128)(2,1)}, bf16[1536,1152]{1,0:T(8,128)(2,1)}) custom-call(bf16[1024,1536]{1,0:T(8,128)(2,1)} %get-tuple-element.60.x_ref, bf16[1536,1152]{1,0:T(8,128)(2,1)} %get-tuple-element.61.w_ref.router_ref.refs_6_, s32[2,1,512]{2,1,0:T(1,128)} %broadcast_in_dim.20.seg_row, f32[512,64]{1,0:T(8,128)} %constant.10.clone.cos_ref, ...), custom_call_target="tpu_custom_call" | custom-call | flops 20000000000 | bytes 100000000 | tf_op jit(solution)/shard_map/pallas_call | solution.py:1350
  548.6 73.2 %shard_map.255 = (f32[256,1536]{1,0:T(8,128)}, f32[192,1152]{1,0:T(8,128)}, f32[8,1536]{1,0:T(8,128)}, bf16[1,3,192,512]{3,2,1,0:T(8,128)(2,1)}) custom-call(bf16[1024,1536]{1,0:T(8,128)(2,1)} %get-tuple-element.82.refs_0_, bf16[1536,1152]{1,0:T(8,128)(2,1)} %get-tuple-element.83.refs_1_, bf16[256,1536]{1,0:T(8,128)(2,1)} %refs_2_.4, f32[1,1536]{1,0:T(1,128)} %copy-done.5, ...), custom_call_target="tpu_custom_call" | custom-call | bytes 150000000 | tf_op jit(solution)/shard_map/pallas_call | solution.py:877
  621.9 0.0 reduce-scatter.2.cloned.1.call-done.refs_0_
  621.9 10.2 %shard_map.256 = (f32[192,384]{1,0:T(8,128)}, f32[192,128]{1,0:T(8,128)}, f32[192,128]{1,0:T(8,128)}, f32[192,384]{1,0:T(8,128)}, f32[40,192]{1,0:T(8,128)}, /*i...) custom-call(f32[192,1152]{1,0:T(8,128)} %get-tuple-element.87.attn_r, ...), custom_call_target="tpu_custom_call" | custom-call | tf_op jit(solution)/shard_map/pallas_call | solution.py:1428
  632.1 1.3 reduce
  633.4 1.3 reduce.1
  634.7 0.9 copy.31
  635.6 1.1 copy.32
  (24 shorter events, 0.1 us)
Async XLA Ops:
  7.2 218.8 %all-gather.5.cloned.1.call-start = ((), (), s32[]{:S(2)}) async-start(), calls=%async_computation.2 | async-start | bytes 31850496 | tf_op jit(solution)/shard_map/all_gather | solution.py:1471
  10.3 0.7 copy-start.13
  10.4 1.9 copy-start
  10.4 1.9 copy-start.1
  10.4 1.9 copy-start.3
  10.4 1.9 copy-start.6
  10.4 1.9 copy-start.7
  10.4 1.9 copy-start.8
  10.5 293.5 %all-gather.3.cloned.1.call-start = ((), (), s32[]{:S(2)}) async-start(), calls=%async_computation.1 | async-start | bytes 21233664 | tf_op jit(solution)/shard_map/all_gather | solution.py:1487
  11.0 63.8 %copy-start.5 = (f32[1,1536]{1,0:T(1,128)}, f32[1,1536]{1,0:T(1,128)S(1)}, u32[]{:S(2)}) copy-start(f32[1,1536]{1,0:T(1,128)S(1)} %reshape.24.refs_1_.refs_3_) | copy-start | bytes 18436
  12.3 0.9 copy-start.4
  74.8 0.8 copy-start.2
  75.6 0.8 copy-start.9
  76.5 0.8 copy-start.10
  77.3 544.6 %reduce-scatter.2.cloned.1.call-start = ((), (), s32[]{:S(2)}) async-start(), calls=%async_computation.3 | async-start | bytes 31850496 | tf_op jit(solution)/shard_map/reduce_scatter | solution.py:1516
  621.9 12.8 %copy-start.12 = (bf16[256,1536]{1,0:T(8,128)(2,1)S(1)}, bf16[256,1536]{1,0:T(8,128)(2,1)}, u32[]{:S(2)}) copy-start(bf16[256,1536]{1,0:T(8,128)(2,1)} %get-tuple-element.114) | copy-start | bytes 2359300
  621.9 13.7 %copy-start.11 = (f32[256,1536]{1,0:T(8,128)S(1)}, f32[256,1536]{1,0:T(8,128)}, u32[]{:S(2)}) copy-start(f32[256,1536]{1,0:T(8,128)} %get-tuple-element.115) | copy-start | bytes 4718596
Sparse Core Ops, SparseCore 0:
  10.6 151.9 all-gather.4
  164.5 98.5 all-gather.2
  304.1 228.7 reduce-scatter.1
